TPU v7x, 32 devices: a whole 2x2x4 slice. The times are simulated.
32 devices in a mesh: seq: 8 (over z, core), fsdp: 4 (over y, x).
Axes of the slice: x: 2, y: 2, z: 4, core: 2. Of those that a mesh axis runs over, the one named last changes fastest.
Arguments:
- inputs: bfloat16 [4, 1024, 2048], P('fsdp', 'seq'), may hold values from -6 to 6
- query_weight: bfloat16 [2048, 2048], P(('seq', 'fsdp')), may hold values from -0.125 to 0.125
- key_weight: bfloat16 [2048, 2048], P(('seq', 'fsdp')), may hold values from -0.125 to 0.125
- value_weight: bfloat16 [2048, 2048], P(('seq', 'fsdp')), may hold values from -0.125 to 0.125
- output_weight: bfloat16 [2048, 2048], P(('seq', 'fsdp')), may hold values from -0.125 to 0.125
- query_gain: bfloat16 [2048], P(('seq', 'fsdp')), may hold values from 0.5 to 7
- key_gain: bfloat16 [2048], P(('seq', 'fsdp')), may hold values from 0.5 to 7
- attention_gain: bfloat16 [2048], P(('seq', 'fsdp')), may hold values from 0.25 to 1.75
- gate_weight: bfloat16 [2048, 8192], P(('seq', 'fsdp')), may hold values from -0.125 to 0.125
- up_weight: bfloat16 [2048, 8192], P(('seq', 'fsdp')), may hold values from -0.125 to 0.125
- down_weight: bfloat16 [2048, 8192], P(('seq', 'fsdp')), may hold values from -0.0625 to 0.0625
- feedforward_gain: bfloat16 [2048], P(('seq', 'fsdp')), may hold values from 0.25 to 1.75
- segments: int32 [4, 1024], P('fsdp'), may hold values from 0 to 2, never falling along the last dimension, each value on 1 to 682 neighbouring positions
- cotangent: bfloat16 [4, 1024, 2048], P('fsdp', 'seq'), may hold values from -6 to 6
Outputs:
- result: bfloat16 [4, 1024, 2048], P('fsdp', 'seq')
- input_grad: float32 [4, 1024, 2048], P('fsdp', 'seq')
- query_weight_grad: float32 [2048, 2048], P(('seq', 'fsdp'))
- key_weight_grad: float32 [2048, 2048], P(('seq', 'fsdp'))
- value_weight_grad: float32 [2048, 2048], P(('seq', 'fsdp'))
- output_weight_grad: float32 [2048, 2048], P(('seq', 'fsdp'))
- query_gain_grad: float32 [2048], P(('seq', 'fsdp'))
- key_gain_grad: float32 [2048], P(('seq', 'fsdp'))
- attention_gain_grad: float32 [2048], P(('seq', 'fsdp'))
- gate_weight_grad: float32 [2048, 8192], P(('seq', 'fsdp'))
- up_weight_grad: float32 [2048, 8192], P(('seq', 'fsdp'))
- down_weight_grad: float32 [2048, 8192], P(('seq', 'fsdp'))
- feedforward_gain_grad: float32 [2048], P(('seq', 'fsdp'))
Inputs may be any that keep to these rules, and one draw needn't show every extreme that they name: `segments`: segment numbers never fall along a pack; each document holds at most 682 tokens and one holds exactly that many.
All inputs are finite; a program needn't handle non-finite values.
Results may differ from a plain program's by a relative error of at most 0.025.
The roundings to bfloat16 on the way count: a program that leaves them out, or rounds other values in their place, can miss the bound.
Values may be sent and summed in bfloat16 or wider, within the bound.
A program may use at most 320 MiB of HBM per device.

v0:
```python
import jax
import jax.numpy as jnp
from jax import lax
from jax.sharding import PartitionSpec as P

HEADS = 16
DH = 128


eps_norm = 1e-06
rope_base = 500000.0
neg_fill = -1e30


def rms_scale(tensor, gain):
    return tensor * lax.rsqrt(jnp.mean(tensor * tensor, axis=-1, keepdims=True) + eps_norm) * gain


def rotary(tensor, positions):
    row_count = tensor.shape[0]
    grouped = tensor.reshape(row_count, HEADS, DH)
    half_width = DH // 2
    frequency = rope_base ** (-jnp.arange(half_width, dtype=jnp.float32) * 2.0 / DH)
    angles = positions.astype(jnp.float32)[:, None] * frequency[None, :]
    cosine = jnp.cos(angles)[:, None, :]
    sine_table = jnp.sin(angles)[:, None, :]
    first_half = grouped[..., :half_width]
    second_half = grouped[..., half_width:]
    turned = jnp.concatenate(
        [
            first_half * cosine - second_half * sine_table,
            second_half * cosine + first_half * sine_table,
        ],
        axis=-1,
    )
    return turned.reshape(tensor.shape)


def norm_rotary(tensor, gain, positions):
    return rotary(rms_scale(tensor, gain), positions)


def swiglu_act(gate_linear, up_linear):
    return jax.nn.silu(gate_linear) * up_linear


def contract_rows(left, right):
    return lax.dot_general(
        left, right, (((0,), (0,)), ((), ())), preferred_element_type=jnp.float32
    )


def contract_cols(left, right):
    return lax.dot_general(
        left, right, (((1,), (1,)), ((), ())), preferred_element_type=jnp.float32
    )


def swap_blocks(tensor, outer, inner):
    block_rows = tensor.shape[0] // (outer * inner)
    return (
        tensor.reshape(outer, inner, block_rows, tensor.shape[1])
        .transpose(1, 0, 2, 3)
        .reshape(tensor.shape)
    )


def masked_scores(query_block, key_heads, first_row, segment_row, score_scale):
    block_rows = query_block.shape[0]
    sequence_rows = key_heads.shape[0]
    scores = (
        jnp.einsum("qhd,khd->hqk", query_block, key_heads, preferred_element_type=jnp.float32)
        * score_scale
    )
    query_pos = first_row + jnp.arange(block_rows, dtype=jnp.int32)
    key_pos = jnp.arange(sequence_rows, dtype=jnp.int32)
    query_seg = lax.dynamic_slice_in_dim(segment_row, first_row, block_rows, 0)
    allowed = (key_pos[None, :] <= query_pos[:, None]) & (
        segment_row[None, :] == query_seg[:, None]
    )
    return jnp.where(allowed[None], scores, neg_fill)


def per_device(
    inputs,
    query_weight,
    key_weight,
    value_weight,
    output_weight,
    query_gain,
    key_gain,
    attention_gain,
    gate_weight,
    up_weight,
    down_weight,
    feedforward_gain,
    segments,
    cotangent,
):
    token_count = inputs.shape[1]
    width_all = inputs.shape[2]
    local_in = inputs.reshape(token_count, width_all)
    positions = lax.axis_index("seq") * token_count + jnp.arange(token_count, dtype=jnp.int32)
    segment_row = segments[0]
    score_scale = DH ** (-0.5)
    seq_count = lax.axis_size("seq")
    fsdp_count = lax.axis_size("fsdp")
    attention_set = (
        lax.all_gather(query_weight, ("seq", "fsdp"), axis=0, tiled=True),
        lax.all_gather(key_weight, ("seq", "fsdp"), axis=0, tiled=True),
        lax.all_gather(value_weight, ("seq", "fsdp"), axis=0, tiled=True),
        lax.all_gather(output_weight, ("seq", "fsdp"), axis=0, tiled=True),
        lax.all_gather(query_gain, ("seq", "fsdp"), axis=0, tiled=True),
        lax.all_gather(key_gain, ("seq", "fsdp"), axis=0, tiled=True),
        lax.all_gather(attention_gain, ("seq", "fsdp"), axis=0, tiled=True),
        lax.all_gather(feedforward_gain, ("seq", "fsdp"), axis=0, tiled=True),
    )
    query_full, key_full, value_full, output_full = (
        attention_set[0],
        attention_set[1],
        attention_set[2],
        attention_set[3],
    )
    query_scale = attention_set[4].astype(jnp.float32)
    key_scale = attention_set[5].astype(jnp.float32)
    attention_scale = attention_set[6].astype(jnp.float32)
    feedforward_scale = attention_set[7].astype(jnp.float32)
    query_pre = jnp.dot(local_in, query_full, preferred_element_type=jnp.float32)
    key_pre = jnp.dot(local_in, key_full, preferred_element_type=jnp.float32)
    values_low = jnp.dot(local_in, value_full, preferred_element_type=jnp.float32).astype(
        jnp.bfloat16
    )
    queries_low = norm_rotary(query_pre, query_scale, positions).astype(jnp.bfloat16)
    keys_low = norm_rotary(key_pre, key_scale, positions).astype(jnp.bfloat16)
    heads_query, heads_key, heads_value = (
        lax.all_to_all(queries_low, "seq", split_axis=1, concat_axis=0, tiled=True),
        lax.all_to_all(keys_low, "seq", split_axis=1, concat_axis=0, tiled=True),
        lax.all_to_all(values_low, "seq", split_axis=1, concat_axis=0, tiled=True),
    )
    sequence_rows = heads_query.shape[0]
    local_heads = heads_query.shape[1] // DH
    query_heads = heads_query.reshape(sequence_rows, local_heads, DH)
    key_heads = heads_key.reshape(sequence_rows, local_heads, DH)
    value_heads = heads_value.reshape(sequence_rows, local_heads, DH)
    block_rows = min(512, sequence_rows)
    block_count = sequence_rows // block_rows
    block_ids = jnp.arange(block_count, dtype=jnp.int32)

    def attend_block(loop_state, block_index):
        first_row = block_index * block_rows
        query_block = lax.dynamic_slice_in_dim(query_heads, first_row, block_rows, 0)
        scores = masked_scores(query_block, key_heads, first_row, segment_row, score_scale)
        row_max = jnp.max(scores, axis=-1, keepdims=True)
        expanded = jnp.exp(scores - row_max)
        row_total = jnp.sum(expanded, axis=-1, keepdims=True)
        softmax_low = (expanded / row_total).astype(jnp.bfloat16)
        block_out = jnp.einsum(
            "hqk,khd->qhd", softmax_low, value_heads, preferred_element_type=jnp.float32
        )
        log_total = (row_max + jnp.log(row_total))[..., 0]
        return (loop_state, (block_out.astype(jnp.bfloat16), log_total))

    _, (out_blocks, log_totals) = lax.scan(attend_block, jnp.zeros((), jnp.int32), block_ids)
    attended_heads = out_blocks.reshape(sequence_rows, local_heads * DH)
    attended = lax.all_to_all(attended_heads, "seq", split_axis=0, concat_axis=1, tiled=True)
    projected = jnp.dot(attended, output_full, preferred_element_type=jnp.float32)
    hidden = local_in.astype(jnp.float32) + rms_scale(projected, attention_scale)
    hidden_low = hidden.astype(jnp.bfloat16)
    column_parts = (
        lax.all_to_all(gate_weight, "seq", split_axis=1, concat_axis=0, tiled=True),
        lax.all_to_all(up_weight, "seq", split_axis=1, concat_axis=0, tiled=True),
        lax.all_to_all(down_weight, "seq", split_axis=1, concat_axis=0, tiled=True),
    )
    column_all = (
        lax.all_gather(column_parts[0], "fsdp", axis=0, tiled=True),
        lax.all_gather(column_parts[1], "fsdp", axis=0, tiled=True),
        lax.all_gather(column_parts[2], "fsdp", axis=0, tiled=True),
    )
    gate_cols = swap_blocks(column_all[0], fsdp_count, seq_count)
    up_cols = swap_blocks(column_all[1], fsdp_count, seq_count)
    down_cols = swap_blocks(column_all[2], fsdp_count, seq_count)
    hidden_all = lax.all_gather(hidden_low, "seq", axis=0, tiled=True)
    gate_linear = jnp.dot(hidden_all, gate_cols, preferred_element_type=jnp.float32)
    up_linear = jnp.dot(hidden_all, up_cols, preferred_element_type=jnp.float32)
    activated = swiglu_act(gate_linear, up_linear).astype(jnp.bfloat16)
    mixed_pre = lax.psum_scatter(
        contract_cols(activated, down_cols).astype(jnp.bfloat16),
        "seq",
        scatter_dimension=0,
        tiled=True,
    ).astype(jnp.float32)
    result = (
        (hidden + rms_scale(mixed_pre, feedforward_scale))
        .astype(jnp.bfloat16)
        .reshape(1, token_count, width_all)
    )
    grad_result = cotangent.reshape(token_count, width_all).astype(jnp.float32)
    _, mixed_pull = jax.vjp(rms_scale, mixed_pre, feedforward_scale)
    grad_mixed, grad_feedforward_gain = mixed_pull(grad_result)
    grad_mixed_low = grad_mixed.astype(jnp.bfloat16)
    grad_all = lax.all_gather(grad_mixed_low, "seq", axis=0, tiled=True)
    grad_activated = jnp.dot(grad_all, down_cols, preferred_element_type=jnp.float32)
    _, swiglu_pull = jax.vjp(swiglu_act, gate_linear, up_linear)
    grad_gate, grad_upward = swiglu_pull(grad_activated)
    grad_gate_low = grad_gate.astype(jnp.bfloat16)
    grad_upward_low = grad_upward.astype(jnp.bfloat16)
    grad_hidden = grad_result + lax.psum_scatter(
        (contract_cols(grad_gate_low, gate_cols) + contract_cols(grad_upward_low, up_cols)).astype(
            jnp.bfloat16
        ),
        "seq",
        scatter_dimension=0,
        tiled=True,
    ).astype(jnp.float32)
    gate_term = swap_blocks(contract_rows(hidden_all, grad_gate_low), seq_count, fsdp_count)
    up_term = swap_blocks(contract_rows(hidden_all, grad_upward_low), seq_count, fsdp_count)
    down_term = swap_blocks(contract_rows(grad_all, activated), seq_count, fsdp_count)
    summed_terms = (
        lax.psum_scatter(
            gate_term.astype(jnp.bfloat16), "fsdp", scatter_dimension=0, tiled=True
        ).astype(jnp.float32),
        lax.psum_scatter(
            up_term.astype(jnp.bfloat16), "fsdp", scatter_dimension=0, tiled=True
        ).astype(jnp.float32),
        lax.psum_scatter(
            down_term.astype(jnp.bfloat16), "fsdp", scatter_dimension=0, tiled=True
        ).astype(jnp.float32),
    )
    gate_weight_grad, up_weight_grad, down_weight_grad = (
        lax.all_to_all(
            summed_terms[0].astype(jnp.bfloat16), "seq", split_axis=0, concat_axis=1, tiled=True
        ).astype(jnp.float32),
        lax.all_to_all(
            summed_terms[1].astype(jnp.bfloat16), "seq", split_axis=0, concat_axis=1, tiled=True
        ).astype(jnp.float32),
        lax.all_to_all(
            summed_terms[2].astype(jnp.bfloat16), "seq", split_axis=0, concat_axis=1, tiled=True
        ).astype(jnp.float32),
    )
    _, branch_pull = jax.vjp(rms_scale, projected, attention_scale)
    grad_projected, grad_attention_gain = branch_pull(grad_hidden)
    grad_projected_low = grad_projected.astype(jnp.bfloat16)
    query_back, key_back, value_back, output_back = (
        lax.all_gather(query_weight, ("seq", "fsdp"), axis=0, tiled=True),
        lax.all_gather(key_weight, ("seq", "fsdp"), axis=0, tiled=True),
        lax.all_gather(value_weight, ("seq", "fsdp"), axis=0, tiled=True),
        lax.all_gather(output_weight, ("seq", "fsdp"), axis=0, tiled=True),
    )
    output_weight_grad = contract_rows(attended, grad_projected_low)
    grad_attended = contract_cols(grad_projected_low, output_back).astype(jnp.bfloat16)
    grad_heads = lax.all_to_all(grad_attended, "seq", split_axis=1, concat_axis=0, tiled=True)
    grad_out_heads = grad_heads.reshape(sequence_rows, local_heads, DH)

    def attend_back(loop_state, block_index):
        key_total, value_total = loop_state
        first_row = block_index * block_rows
        query_block = lax.dynamic_slice_in_dim(query_heads, first_row, block_rows, 0)
        grad_block = lax.dynamic_slice_in_dim(grad_out_heads, first_row, block_rows, 0)
        log_block = lax.dynamic_index_in_dim(log_totals, block_index, 0, keepdims=False)
        scores = masked_scores(query_block, key_heads, first_row, segment_row, score_scale)
        probabilities = jnp.exp(scores - log_block[..., None])
        softmax_low = probabilities.astype(jnp.bfloat16)
        value_total = value_total + jnp.einsum(
            "hqk,qhd->khd", softmax_low, grad_block, preferred_element_type=jnp.float32
        )
        grad_softmax = jnp.einsum(
            "qhd,khd->hqk", grad_block, value_heads, preferred_element_type=jnp.float32
        )
        row_dot = jnp.sum(probabilities * grad_softmax, axis=-1, keepdims=True)
        grad_scores = (probabilities * (grad_softmax - row_dot)).astype(jnp.bfloat16)
        grad_query_block = (
            jnp.einsum("hqk,khd->qhd", grad_scores, key_heads, preferred_element_type=jnp.float32)
            * score_scale
        )
        key_total = (
            key_total
            + jnp.einsum(
                "hqk,qhd->khd", grad_scores, query_block, preferred_element_type=jnp.float32
            )
            * score_scale
        )
        return ((key_total, value_total), grad_query_block.astype(jnp.bfloat16))

    zero_heads = jnp.zeros((sequence_rows, local_heads, DH), jnp.float32)
    (key_total, value_total), grad_query_blocks = lax.scan(
        attend_back, (zero_heads, zero_heads), block_ids
    )
    grad_queries_heads = grad_query_blocks.reshape(sequence_rows, local_heads * DH)
    grad_keys_heads = key_total.astype(jnp.bfloat16).reshape(sequence_rows, local_heads * DH)
    grad_values_heads = value_total.astype(jnp.bfloat16).reshape(sequence_rows, local_heads * DH)
    grad_queries, grad_keys, grad_values = (
        lax.all_to_all(grad_queries_heads, "seq", split_axis=0, concat_axis=1, tiled=True),
        lax.all_to_all(grad_keys_heads, "seq", split_axis=0, concat_axis=1, tiled=True),
        lax.all_to_all(grad_values_heads, "seq", split_axis=0, concat_axis=1, tiled=True),
    )
    _, query_pull = jax.vjp(
        lambda tensor, gain: norm_rotary(tensor, gain, positions), query_pre, query_scale
    )
    grad_query_pre, grad_query_gain = query_pull(grad_queries.astype(jnp.float32))
    _, key_pull = jax.vjp(
        lambda tensor, gain: norm_rotary(tensor, gain, positions), key_pre, key_scale
    )
    grad_key_pre, grad_key_gain = key_pull(grad_keys.astype(jnp.float32))
    grad_query_low = grad_query_pre.astype(jnp.bfloat16)
    grad_key_low = grad_key_pre.astype(jnp.bfloat16)
    grad_input = (
        grad_hidden
        + contract_cols(grad_query_low, query_back)
        + contract_cols(grad_key_low, key_back)
        + contract_cols(grad_values, value_back)
    )
    query_weight_grad = contract_rows(local_in, grad_query_low)
    key_weight_grad = contract_rows(local_in, grad_key_low)
    value_weight_grad = contract_rows(local_in, grad_values)
    shares = (
        lax.psum_scatter(query_weight_grad, ("seq", "fsdp"), scatter_dimension=0, tiled=True),
        lax.psum_scatter(key_weight_grad, ("seq", "fsdp"), scatter_dimension=0, tiled=True),
        lax.psum_scatter(value_weight_grad, ("seq", "fsdp"), scatter_dimension=0, tiled=True),
        lax.psum_scatter(output_weight_grad, ("seq", "fsdp"), scatter_dimension=0, tiled=True),
        lax.psum_scatter(grad_query_gain, ("seq", "fsdp"), scatter_dimension=0, tiled=True),
        lax.psum_scatter(grad_key_gain, ("seq", "fsdp"), scatter_dimension=0, tiled=True),
        lax.psum_scatter(grad_attention_gain, ("seq", "fsdp"), scatter_dimension=0, tiled=True),
        lax.psum_scatter(grad_feedforward_gain, ("seq", "fsdp"), scatter_dimension=0, tiled=True),
    )
    return (
        result,
        grad_input.reshape(1, token_count, width_all),
        shares[0],
        shares[1],
        shares[2],
        shares[3],
        shares[4],
        shares[5],
        shares[6],
        gate_weight_grad,
        up_weight_grad,
        down_weight_grad,
        shares[7],
    )


def solution(mesh):
    in_specs = (
        P("fsdp", "seq", None),
        P(("seq", "fsdp"), None),
        P(("seq", "fsdp"), None),
        P(("seq", "fsdp"), None),
        P(("seq", "fsdp"), None),
        P(("seq", "fsdp")),
        P(("seq", "fsdp")),
        P(("seq", "fsdp")),
        P(("seq", "fsdp"), None),
        P(("seq", "fsdp"), None),
        P(("seq", "fsdp"), None),
        P(("seq", "fsdp")),
        P("fsdp", None),
        P("fsdp", "seq", None),
    )
    out_specs = (
        P("fsdp", "seq", None),
        P("fsdp", "seq", None),
        P(("seq", "fsdp"), None),
        P(("seq", "fsdp"), None),
        P(("seq", "fsdp"), None),
        P(("seq", "fsdp"), None),
        P(("seq", "fsdp")),
        P(("seq", "fsdp")),
        P(("seq", "fsdp")),
        P(("seq", "fsdp"), None),
        P(("seq", "fsdp"), None),
        P(("seq", "fsdp"), None),
        P(("seq", "fsdp")),
    )
    return jax.shard_map(
        per_device, mesh=mesh, in_specs=in_specs, out_specs=out_specs, check_vma=False
    )
```

profile of v0, /device:TPU:0, one launch (start us, length us, event | category | flops | bytes accessed | tf_op | source)
XLA Modules:
  0.0 2398.0 jit_solution(3982378241102895781)
XLA Ops:
  11.4 41.7 %all_to_all.218 = bf16[64,8,1024]{2,0,1:T(8,128)(2,1)} all-to-all(bf16[64,8,1024]{2,0,1:T(8,128)(2,1)S(1)} %bitcast.267), channel_id=1, replica_groups=mesh['seq'=8,'fsdp'=4] {'seq'}, dimensions={1} | all-to-all | bytes 2097152 | tf_op jit(solution)/shard_map/all_to_all | solution.py:170
  53.2 49.4 %all_to_all.219 = bf16[64,8,1024]{2,0,1:T(8,128)(2,1)} all-to-all(bf16[64,8,1024]{2,0,1:T(8,128)(2,1)S(1)} %bitcast.268), channel_id=1, replica_groups=mesh['seq'=8,'fsdp'=4] {'seq'}, dimensions={1} | all-to-all | bytes 2097152 | tf_op jit(solution)/shard_map/all_to_all | solution.py:171
  103.8 4.3 all-to-all-start.6
  109.1 50.9 %all-reduce.13 = (bf16[2048]{0:T(1024)(128)(2,1)S(1)}, bf16[2048]{0:T(1024)(128)(2,1)S(1)}, bf16[2048]{0:T(1024)(128)(2,1)S(1)}, bf16[2048]{0:T(1024)(128)(2,1)S(1)}) all-reduce(bf16[2048]{0:T(1024)(128)(2,1)S(1)} %dynamic-update-slice, bf16[2048]{0:T(1024)(128)(2,1)S(1)} %dynamic-update-slice.1, ...), channel_id=1, replica_groups=mesh['seq'=8,'fsdp'=4] {'seq','fsdp'}, use_global_device_ids=true, to_apply=%add.4 | all-reduce | flops 8192 | bytes 32768
  160.3 4.7 multiply_reduce_fusion.8
  166.6 27.5 %all-gather.10.cloned.1.call-done = bf16[2048,2048]{1,0:T(8,128)(2,1)} async-done(((bf16[64,2048]{1,0:T(8,128)(2,1)}), bf16[2048,2048]{1,0:T(8,128)(2,1)}) %all-gather.10.cloned.1.call-update) | async-done | bytes 8388624 | tf_op jit(solution)/shard_map/all_gather | solution.py:109
  194.1 4.7 multiply_reduce_fusion.9
  208.0 18.0 all-to-all-done
  229.5 53.1 %all-gather.14.cloned.1.call-done = bf16[2048,2048]{1,0:T(8,128)(2,1)} async-done(((bf16[64,2048]{1,0:T(8,128)(2,1)}), bf16[2048,2048]{1,0:T(8,128)(2,1)}) %all-gather.14.cloned.1.call-update) | async-done | bytes 8388624 | tf_op jit(solution)/shard_map/all_gather | solution.py:111
  282.6 4.6 convolution_convert_fusion.5
  294.9 17.6 all-to-all-done.2
  314.5 16.2 while.27
  335.4 29.5 %all-to-all-done.3 = bf16[8,128,256]{2,1,0:T(8,128)(2,1)S(1)} async-done(((bf16[8,128,256]{2,1,0:T(8,128)(2,1)}), bf16[8,128,256]{2,1,0:T(8,128)(2,1)S(1)}, u32[]{:S(2)}, u32[]{:S(2)}) %all-to-all-start.3) | async-done | bytes 524320 | tf_op jit(solution)/shard_map/all_to_all | solution.py:165
  365.2 9.3 all-gather.16.cloned.1.call-done
  374.5 4.7 multiply_reduce_fusion.7
  380.8 46.8 %all-gather.20.cloned.1.call-done = bf16[2048,1024]{1,0:T(8,128)(2,1)} async-done(((bf16[512,1024]{1,0:T(8,128)(2,1)}), bf16[2048,1024]{1,0:T(8,128)(2,1)}) %all-gather.20.cloned.1.call-update) | async-done | bytes 4194320 | tf_op jit(solution)/shard_map/all_gather | solution.py:175
  427.5 4.9 copy.113
  432.4 49.4 %all-gather.22.cloned.1.call-done = bf16[2048,1024]{1,0:T(8,128)(2,1)} async-done(((bf16[512,1024]{1,0:T(8,128)(2,1)}), bf16[2048,1024]{1,0:T(8,128)(2,1)}) %all-gather.22.cloned.1.call-update) | async-done | bytes 4194320 | tf_op jit(solution)/shard_map/all_gather | solution.py:176
  481.8 4.8 copy.115
  486.7 49.6 %all-gather.24.cloned.1.call-done = bf16[2048,1024]{1,0:T(8,128)(2,1)} async-done(((bf16[512,1024]{1,0:T(8,128)(2,1)}), bf16[2048,1024]{1,0:T(8,128)(2,1)}) %all-gather.24.cloned.1.call-update) | async-done | bytes 4194320 | tf_op jit(solution)/shard_map/all_gather | solution.py:177
  536.3 4.8 copy.117
  541.1 44.2 %all-gather.18.cloned.1.call-done = bf16[1024,2048]{1,0:T(8,128)(2,1)} async-done(((bf16[128,2048]{1,0:T(8,128)(2,1)}), bf16[1024,2048]{1,0:T(8,128)(2,1)}) %all-gather.18.cloned.1.call-update) | async-done | bytes 4194320 | tf_op jit(solution)/shard_map/all_gather | solution.py:182
  585.3 7.7 fusion.71
  593.0 6.5 multiply_convert_fusion.2
  600.8 6.1 convolution_convert_fusion.3
  607.1 48.8 %reduce-scatter.16.cloned.1.call-done = bf16[128,2048]{1,0:T(8,128)(2,1)} async-done(((bf16[1024,2048]{1,0:T(8,128)(2,1)}), bf16[128,2048]{1,0:T(8,128)(2,1)}) %reduce-scatter.16.cloned.1.call-update) | async-done | bytes 524304 | tf_op jit(solution)/shard_map/reduce_scatter | solution.py:186
  661.7 45.3 %all-gather.26.cloned.1.call-done = bf16[1024,2048]{1,0:T(8,128)(2,1)} async-done(((bf16[128,2048]{1,0:T(8,128)(2,1)}), bf16[1024,2048]{1,0:T(8,128)(2,1)}) %all-gather.26.cloned.1.call-update) | async-done | bytes 4194320 | tf_op jit(solution)/shard_map/all_gather | solution.py:201
  707.0 11.7 multiply_convert_fusion.1
  718.7 4.5 fusion.72
  723.3 6.2 add_convert_fusion
  729.8 7.4 convolution_convert_fusion.2
  739.8 7.5 convolution_convert_fusion.1
  750.2 7.5 convolution_convert_fusion
  760.2 18.2 reduce-scatter.18.cloned.1.call-done
  783.2 8.5 fusion.73
  792.7 6.4 convolution_convert_fusion.4
  800.1 3.7 all-to-all-start.7
  803.8 15.2 all-to-all-done.7
  821.5 43.6 %while.28 = (s32[]{:T(128)}, f32[1024,2,128]{0,2,1:T(8,128)}, f32[1024,2,128]{0,2,1:T(8,128)}, bf16[2,512,2,128]{3,2,1,0:T(2,128)(2,1)}, s32[2]{0:T(128)S(1)}, /...) while((s32[]{:T(128)}, f32[1024,2,128]{0,2,1:T(8,128)}, ...), condition=%wide.region_14.15_spmd.clone, body=%wide.region_12.14_spmd.clone.sunk | while | flops 1361051136 | bytes 78948760 | solution.py:285
  828.9 4.5 multiply_reduce_fusion.11
  850.2 4.7 multiply_reduce_fusion.11
  859.5 3.8 fusion.155
  873.1 12.9 all-to-all-done.8
  890.2 14.6 all-to-all-done.9
  909.0 8.3 convolution_bitcast_fusion.2
  917.3 17.8 copy.145
  938.1 8.1 convolution_bitcast_fusion.1
  946.2 17.7 copy.147
  965.5 20.4 all_to_all.220
  985.9 8.2 convolution_bitcast_fusion
  994.1 17.7 copy.149
  1011.8 4.4 all-to-all-start.11
  1016.3 31.4 %all-to-all-done.11 = bf16[8,64,1024]{2,1,0:T(8,128)(2,1)} async-done(((bf16[8,64,1024]{2,1,0:T(8,128)(2,1)}), bf16[8,64,1024]{2,1,0:T(8,128)(2,1)}, u32[]{:S(2)}, u32[]{:S(2)}) %all-to-all-start.11) | async-done | bytes 1048608 | tf_op jit(solution)/shard_map/all_to_all | solution.py:230
  1047.7 5.2 all-to-all-start.12
  1052.9 32.4 %all-to-all-done.12 = bf16[8,64,1024]{2,1,0:T(8,128)(2,1)} async-done(((bf16[8,64,1024]{2,1,0:T(8,128)(2,1)}), bf16[8,64,1024]{2,1,0:T(8,128)(2,1)}, u32[]{:S(2)}, u32[]{:S(2)}) %all-to-all-start.12) | async-done | bytes 1048608 | tf_op jit(solution)/shard_map/all_to_all | solution.py:233
  1085.3 4.5 all-to-all-start.13
  1089.8 7.3 convolution_add_fusion.2
  1097.2 52.2 %all-reduce.12 = (f32[2048]{0:T(1024)S(1)}, f32[2048]{0:T(1024)S(1)}, f32[2048]{0:T(1024)S(1)}, f32[2048]{0:T(1024)S(1)}) all-reduce(f32[2048]{0:T(1024)S(1)} %get-tuple-element.288, f32[2048]{0:T(1024)S(1)} %get-tuple-element.286, f32[2048]{0:T(1024)S(1)} %get-tuple-element.284, ...), channel_id=8, replica_groups=mesh['seq'=8,'fsdp'=4] {'seq','fsdp'}, use_global_device_ids=true, to_apply=%region_22.23.clone | all-reduce | flops 8192 | bytes 65536
  1151.7 6.6 convolution_add_fusion.1
  1158.2 7.3 fusion.45
  1174.4 131.1 %reduce-scatter.20.cloned.1.call-done = f32[64,2048]{1,0:T(8,128)} async-done(((f32[2048,2048]{1,0:T(8,128)}), f32[64,2048]{1,0:T(8,128)}) %reduce-scatter.20.cloned.1.call-update) | async-done | bytes 524304 | tf_op jit(solution)/shard_map/reduce_scatter | solution.py:319
  1305.5 361.7 %reduce-scatter.28.cloned.1.call-done = f32[64,2048]{1,0:T(8,128)} async-done(((f32[2048,2048]{1,0:T(8,128)}), f32[64,2048]{1,0:T(8,128)}) %reduce-scatter.28.cloned.1.call-update) | async-done | bytes 524304
  1667.2 361.7 %reduce-scatter.30.cloned.1.call-done = f32[64,2048]{1,0:T(8,128)} async-done(((f32[2048,2048]{1,0:T(8,128)}), f32[64,2048]{1,0:T(8,128)}) %reduce-scatter.30.cloned.1.call-update) | async-done | bytes 524304
  2029.0 361.8 %reduce-scatter.32.cloned.1.call-done = f32[64,2048]{1,0:T(8,128)} async-done(((f32[2048,2048]{1,0:T(8,128)}), f32[64,2048]{1,0:T(8,128)}) %reduce-scatter.32.cloned.1.call-update) | async-done | bytes 524304
  (296 shorter events, 132.9 us)
Async XLA Ops:
  7.2 45.9 %copy-start.25 = (bf16[64,8192]{1,0:T(8,128)(2,1)S(1)}, bf16[64,8192]{1,0:T(8,128)(2,1)}, u32[]{:S(2)}) copy-start(bf16[64,8192]{1,0:T(8,128)(2,1)} %param.27) | copy-start | bytes 3145732
  7.2 153.1 %all-gather.12.cloned.1.call-start = ((), (), s32[]{:S(2)}) async-start(), calls=%async_computation.24 | async-start | bytes 8650752 | tf_op jit(solution)/shard_map/all_gather | solution.py:110
  7.9 186.2 %all-gather.10.cloned.1.call-start = ((), (), s32[]{:S(2)}) async-start(), calls=%async_computation.23 | async-start | bytes 8650752 | tf_op jit(solution)/shard_map/all_gather | solution.py:109
  8.7 273.9 %all-gather.14.cloned.1.call-start = ((), (), s32[]{:S(2)}) async-start(), calls=%async_computation.25 | async-start | bytes 8650752 | tf_op jit(solution)/shard_map/all_gather | solution.py:111
  9.4 365.1 %all-gather.16.cloned.1.call-start = ((), (), s32[]{:S(2)}) async-start(), calls=%async_computation.26 | async-start | bytes 8650752 | tf_op jit(solution)/shard_map/all_gather | solution.py:112
  10.0 417.5 %all-gather.20.cloned.1.call-start = ((), (), s32[]{:S(2)}) async-start(), calls=%async_computation.28 | async-start | bytes 5242880 | tf_op jit(solution)/shard_map/all_gather | solution.py:175
  11.3 91.4 %copy-start.26 = (bf16[64,8192]{1,0:T(8,128)(2,1)S(1)}, bf16[64,8192]{1,0:T(8,128)(2,1)}, u32[]{:S(2)}) copy-start(bf16[64,8192]{1,0:T(8,128)(2,1)} %param.28) | copy-start | bytes 3145732
  53.0 428.8 %all-gather.22.cloned.1.call-start = ((), (), s32[]{:S(2)}) async-start(), calls=%async_computation.29 | async-start | bytes 5242880 | tf_op jit(solution)/shard_map/all_gather | solution.py:176
  53.2 54.9 %copy-start.46 = (bf16[64]{0:T(256)(128)(2,1)S(1)}, bf16[64]{0:T(256)(128)(2,1)}, u32[]{:S(2)}) copy-start(bf16[64]{0:T(256)(128)(2,1)} %param.23) | copy-start | bytes 388
  53.2 55.2 %copy-start.47 = (bf16[64]{0:T(256)(128)(2,1)S(1)}, bf16[64]{0:T(256)(128)(2,1)}, u32[]{:S(2)}) copy-start(bf16[64]{0:T(256)(128)(2,1)} %param.24) | copy-start | bytes 388
  53.2 55.4 %copy-start.48 = (bf16[64]{0:T(256)(128)(2,1)S(1)}, bf16[64]{0:T(256)(128)(2,1)}, u32[]{:S(2)}) copy-start(bf16[64]{0:T(256)(128)(2,1)} %param.25) | copy-start | bytes 388
  53.2 55.7 %copy-start.49 = (bf16[64]{0:T(256)(128)(2,1)S(1)}, bf16[64]{0:T(256)(128)(2,1)}, u32[]{:S(2)}) copy-start(bf16[64]{0:T(256)(128)(2,1)} %param.29) | copy-start | bytes 388
  53.2 107.1 %copy-start.2 = (bf16[1,128,2048]{2,1,0:T(8,128)(2,1)S(1)}, bf16[1,128,2048]{2,1,0:T(8,128)(2,1)}, u32[]{:S(2)}) copy-start(bf16[1,128,2048]{2,1,0:T(8,128)(2,1)} %param.18) | copy-start | bytes 1572868
  103.8 99.9 %all-to-all-start.6 = ((bf16[64,8,1024]{2,0,1:T(8,128)(2,1)}), bf16[64,8,1024]{2,0,1:T(8,128)(2,1)}, u32[]{:S(2)}, u32[]{:S(2)}) async-start(bf16[64,8,1024]{2,0,1:T(8,128)(2,1)} %bitcast.207), calls=%async_computation.6 | async-start | bytes 2097152 | tf_op jit(solution)/shard_map/all_to_all | solution.py:172
  160.0 5.1 copy-start.32
  160.0 38.8 %copy-start.34 = (f32[2048]{0:T(1024)}, f32[2048]{0:T(1024)S(1)}, u32[]{:S(2)}) copy-start(f32[2048]{0:T(1024)S(1)} %convert_element_type.203) | copy-start | bytes 24580
  160.3 42.2 %copy-start.28 = (f32[128,64]{0,1:T(8,128)}, f32[128,64]{0,1:T(8,128)S(1)}, u32[]{:S(2)}) copy-start(f32[128,64]{0,1:T(8,128)S(1)} %get-tuple-element.362) | copy-start | bytes 98308
  160.3 42.2 %copy-start.30 = (f32[128,64]{0,1:T(8,128)}, f32[128,64]{0,1:T(8,128)S(1)}, u32[]{:S(2)}) copy-start(f32[128,64]{0,1:T(8,128)S(1)} %get-tuple-element.363) | copy-start | bytes 98308
  165.1 33.7 %copy-start.41 = (f32[128]{0:T(128)}, f32[128]{0:T(128)S(1)}, u32[]{:S(2)}) copy-start(f32[128]{0:T(128)S(1)} %get-tuple-element.364) | copy-start | bytes 1540
  165.1 33.7 %copy-start.37 = (f32[128]{0:T(128)}, f32[128]{0:T(128)S(1)}, u32[]{:S(2)}) copy-start(f32[128]{0:T(128)S(1)} %fusion.68) | copy-start | bytes 1540
  203.7 22.4 all-to-all-start
  226.0 62.2 %all-to-all-start.1 = ((bf16[128,8,256]{0,2,1:T(8,128)(2,1)}), bf16[128,8,256]{0,2,1:T(8,128)(2,1)S(1)}, u32[]{:S(2)}, u32[]{:S(2)}) async-start(bf16[128,8,256]{0,2,1:T(8,128)(2,1)} %bitcast.9), calls=%async_computation.1 | async-start | bytes 1048576 | tf_op jit(solution)/shard_map/all_to_all | solution.py:137
  288.2 24.4 %all-to-all-start.2 = ((bf16[128,8,256]{0,2,1:T(8,128)(2,1)}), bf16[128,8,256]{0,2,1:T(8,128)(2,1)S(1)}, u32[]{:S(2)}, u32[]{:S(2)}) async-start(bf16[128,8,256]{0,2,1:T(8,128)(2,1)} %bitcast.11), calls=%async_computation.2 | async-start | bytes 1048576 | tf_op jit(solution)/shard_map/all_to_all | solution.py:138
  291.7 244.5 %all-gather.24.cloned.1.call-start = ((), (), s32[]{:S(2)}) async-start(), calls=%async_computation.30 | async-start | bytes 5242880 | tf_op jit(solution)/shard_map/all_gather | solution.py:177
  293.1 21.4 copy-start.27
  331.8 33.1 %all-to-all-start.3 = ((bf16[8,128,256]{2,1,0:T(8,128)(2,1)}), bf16[8,128,256]{2,1,0:T(8,128)(2,1)S(1)}, u32[]{:S(2)}, u32[]{:S(2)}) async-start(bf16[8,128,256]{2,1,0:T(8,128)(2,1)} %all_to_all.171), calls=%async_computation.3 | async-start | bytes 1048576 | tf_op jit(solution)/shard_map/all_to_all | solution.py:165
  335.3 250.0 %all-gather.18.cloned.1.call-start = ((), (), s32[]{:S(2)}) async-start(), calls=%async_computation.27 | async-start | bytes 4718592 | tf_op jit(solution)/shard_map/all_gather | solution.py:182
  365.2 14.1 copy-start.11
  380.3 275.6 %reduce-scatter.16.cloned.1.call-start = ((), (), s32[]{:S(2)}) async-start(), calls=%async_computation.31 | async-start | bytes 4718592 | tf_op jit(solution)/shard_map/reduce_scatter | solution.py:186
  585.3 7.7 copy-start.19
  585.3 7.7 copy-start.45
  593.0 6.5 copy-start.50
  593.0 7.8 copy-start.21
  607.0 50.1 %copy-start.8 = (bf16[1,128,2048]{2,1,0:T(8,128)(2,1)S(1)}, bf16[1,128,2048]{2,1,0:T(8,128)(2,1)}, u32[]{:S(2)}) copy-start(bf16[1,128,2048]{2,1,0:T(8,128)(2,1)} %param.31) | copy-start | bytes 1572868
  607.0 100.0 %all-gather.26.cloned.1.call-start = ((), (), s32[]{:S(2)}) async-start(), calls=%async_computation.32 | async-start | bytes 4718592 | tf_op jit(solution)/shard_map/all_gather | solution.py:201
  661.5 116.9 %reduce-scatter.18.cloned.1.call-start = ((), (), s32[]{:S(2)}) async-start(), calls=%async_computation.33 | async-start | bytes 4718592 | tf_op jit(solution)/shard_map/reduce_scatter | solution.py:207
  707.0 11.7 copy-start.18
  718.7 4.6 copy-start.51
  718.7 4.6 copy-start.53
  718.7 4.6 copy-start.20
  729.5 282.3 %reduce-scatter.22.cloned.1.call-start = ((), (), s32[]{:S(2)}) async-start(), calls=%async_computation.35 | async-start | bytes 5242880 | tf_op jit(solution)/shard_map/reduce_scatter | solution.py:219
  739.7 276.5 %reduce-scatter.24.cloned.1.call-start = ((), (), s32[]{:S(2)}) async-start(), calls=%async_computation.36 | async-start | bytes 5242880 | tf_op jit(solution)/shard_map/reduce_scatter | solution.py:222
  749.7 303.2 %reduce-scatter.26.cloned.1.call-start = ((), (), s32[]{:S(2)}) async-start(), calls=%async_computation.37 | async-start | bytes 5242880 | tf_op jit(solution)/shard_map/reduce_scatter | solution.py:225
  760.1 19.8 copy-start.10
  760.1 545.4 %reduce-scatter.20.cloned.1.call-start = ((), (), s32[]{:S(2)}) async-start(), calls=%async_computation.34 | async-start | bytes 17301504 | tf_op jit(solution)/shard_map/reduce_scatter | solution.py:319
  778.4 4.7 copy-start.12
  800.1 18.9 all-to-all-start.7
  828.9 4.5 copy-start
  850.2 4.7 copy-start
  859.5 4.5 copy-start.22
  867.3 18.8 all-to-all-start.8
  872.1 32.8 %copy-start.29 = (f32[128,64]{0,1:T(8,128)S(1)}, f32[128,64]{0,1:T(8,128)}, u32[]{:S(2)}) copy-start(f32[128,64]{0,1:T(8,128)} %copy-done.28) | copy-start | bytes 98308
  872.1 32.8 %copy-start.31 = (f32[128,64]{0,1:T(8,128)S(1)}, f32[128,64]{0,1:T(8,128)}, u32[]{:S(2)}) copy-start(f32[128,64]{0,1:T(8,128)} %copy-done.30) | copy-start | bytes 98308
  886.0 18.8 all-to-all-start.9
  889.5 777.7 %reduce-scatter.28.cloned.1.call-start = ((), (), s32[]{:S(2)}) async-start(), calls=%async_computation.38 | async-start | bytes 17301504
  935.1 1093.9 %reduce-scatter.30.cloned.1.call-start = ((), (), s32[]{:S(2)}) async-start(), calls=%async_computation.39 | async-start | bytes 17301504
  964.0 1426.8 %reduce-scatter.32.cloned.1.call-start = ((), (), s32[]{:S(2)}) async-start(), calls=%async_computation.40 | async-start | bytes 17301504
  1011.8 78.0 %copy-start.9 = (bf16[1,128,2048]{2,1,0:T(8,128)(2,1)S(1)}, bf16[1,128,2048]{2,1,0:T(8,128)(2,1)}, u32[]{:S(2)}) copy-start(bf16[1,128,2048]{2,1,0:T(8,128)(2,1)} %param.31) | copy-start | bytes 1572868
  1011.8 78.0 %copy-start.17 = (bf16[128,2048]{1,0:T(8,128)(2,1)S(1)}, bf16[128,2048]{1,0:T(8,128)(2,1)}, u32[]{:S(2)}) copy-start(bf16[128,2048]{1,0:T(8,128)(2,1)} %reduce-scatter.18.cloned.1.call-done) | copy-start | bytes 1572868
  1011.8 35.8 %all-to-all-start.11 = ((bf16[8,64,1024]{2,1,0:T(8,128)(2,1)}), bf16[8,64,1024]{2,1,0:T(8,128)(2,1)}, u32[]{:S(2)}, u32[]{:S(2)}) async-start(bf16[8,64,1024]{2,1,0:T(8,128)(2,1)} %bitcast.290), calls=%async_computation.15 | async-start | bytes 2097152 | tf_op jit(solution)/shard_map/all_to_all | solution.py:230
  1047.7 37.6 %all-to-all-start.12 = ((bf16[8,64,1024]{2,1,0:T(8,128)(2,1)}), bf16[8,64,1024]{2,1,0:T(8,128)(2,1)}, u32[]{:S(2)}, u32[]{:S(2)}) async-start(bf16[8,64,1024]{2,1,0:T(8,128)(2,1)} %bitcast.289), calls=%async_computation.17 | async-start | bytes 2097152 | tf_op jit(solution)/shard_map/all_to_all | solution.py:233
  1085.3 86.1 %all-to-all-start.13 = ((bf16[8,64,1024]{2,1,0:T(8,128)(2,1)}), bf16[8,64,1024]{2,1,0:T(8,128)(2,1)}, u32[]{:S(2)}, u32[]{:S(2)}) async-start(bf16[8,64,1024]{2,1,0:T(8,128)(2,1)} %bitcast.288), calls=%async_computation.19 | async-start | bytes 2097152 | tf_op jit(solution)/shard_map/all_to_all | solution.py:236
  1089.8 7.3 copy-start.36
  1089.8 61.8 %copy-start.14 = (bf16[128,2048]{1,0:T(8,128)(2,1)S(1)}, bf16[128,2048]{1,0:T(8,128)(2,1)}, u32[]{:S(2)}) copy-start(bf16[128,2048]{1,0:T(8,128)(2,1)} %copy-done.13) | copy-start | bytes 1572868
  (23 other events, 48.4 us)
Sparse Core Ops, SparseCore 0:
  10.9 99.2 all-gather.11
  113.0 81.0 all-gather.9
  197.0 85.5 all-gather.13
  285.3 89.1 all-gather.15
  376.2 51.2 all-gather.19
  429.2 52.5 all-gather.21
  483.7 52.5 all-gather.23
  538.4 46.8 all-gather.17
  607.1 48.7 reduce-scatter.15
  661.6 45.3 all-gather.25
  729.7 48.7 reduce-scatter.17
  781.2 51.0 reduce-scatter.21
  835.3 52.6 reduce-scatter.23
  890.8 52.5 reduce-scatter.25
  946.2 359.3 reduce-scatter.19
  1308.2 358.9 reduce-scatter.27
  1669.9 358.9 reduce-scatter.29
  2031.7 359.0 reduce-scatter.31
where the time goes:
time: 2410 us; the launch traced here: 2400 us
  waiting for transfers between devices  1780 us (74%)
  blocking collectives  215 us (9%)
  matrix products  185 us (8%)
  local copies, waits for them, and re-layouts  117 us (5%)
  starting transfers between devices  45.4 us (2%)
  other arithmetic  30 us (1%)
    unnamed x21, waiting for transfers between devices  1090 us
    reduce_scatter x1, waiting for transfers between devices, per_device(): lax.psum_scatter(output_weight_grad, ('seq', 'fsdp'), scatter_dimension=0...  131 us
    unnamed x2, blocking collectives  103 us
    unnamed x117, local copies, waits for them, and re-layouts  63.8 us
    dot_general x7, matrix products, contract_rows(): lax.dot_general(left, right, (((0,), (0,)), ((), ())), preferred_element_...  55.5 us
    all_gather x1, waiting for transfers between devices, per_device(): lax.all_gather(value_weight, ('seq', 'fsdp'), axis=0, tiled=True)  53.1 us
    all_gather x1, waiting for transfers between devices, per_device(): lax.all_gather(column_parts[2], 'fsdp', axis=0, tiled=True)  49.6 us
    all_to_all x1, blocking collectives, per_device(): lax.all_to_all(up_weight, 'seq', split_axis=1, concat_axis=0, tiled=True)  49.4 us
  transfers between devices with their start and end apart: 29, of which 22 were waited for; matrix products, arithmetic and copies ran while one was open for 11% of the time, Pallas kernels for 0%

commit v1 on v0

v1 whole, which is shorter than its diff:
```python
import jax
import jax.numpy as jnp
from jax import lax
from jax.sharding import PartitionSpec as P

HEADS = 16
DH = 128


eps_norm = 1e-06
rope_base = 500000.0
neg_fill = -1e30


def rms_scale(tensor, gain):
    return tensor * lax.rsqrt(jnp.mean(tensor * tensor, axis=-1, keepdims=True) + eps_norm) * gain


def rotary(tensor, positions):
    row_count = tensor.shape[0]
    grouped = tensor.reshape(row_count, HEADS, DH)
    half_width = DH // 2
    frequency = rope_base ** (-jnp.arange(half_width, dtype=jnp.float32) * 2.0 / DH)
    angles = positions.astype(jnp.float32)[:, None] * frequency[None, :]
    cosine = jnp.cos(angles)[:, None, :]
    sine_table = jnp.sin(angles)[:, None, :]
    first_half = grouped[..., :half_width]
    second_half = grouped[..., half_width:]
    turned = jnp.concatenate(
        [
            first_half * cosine - second_half * sine_table,
            second_half * cosine + first_half * sine_table,
        ],
        axis=-1,
    )
    return turned.reshape(tensor.shape)


def norm_rotary(tensor, gain, positions):
    return rotary(rms_scale(tensor, gain), positions)


def swiglu_act(gate_linear, up_linear):
    return jax.nn.silu(gate_linear) * up_linear


def contract_rows(left, right):
    return lax.dot_general(
        left, right, (((0,), (0,)), ((), ())), preferred_element_type=jnp.float32
    )


def contract_cols(left, right):
    return lax.dot_general(
        left, right, (((1,), (1,)), ((), ())), preferred_element_type=jnp.float32
    )


def swap_blocks(tensor, outer, inner):
    block_rows = tensor.shape[0] // (outer * inner)
    return (
        tensor.reshape(outer, inner, block_rows, tensor.shape[1])
        .transpose(1, 0, 2, 3)
        .reshape(tensor.shape)
    )


def masked_scores(query_block, key_heads, first_row, segment_row, score_scale):
    block_rows = query_block.shape[0]
    sequence_rows = key_heads.shape[0]
    scores = (
        jnp.einsum("qhd,khd->hqk", query_block, key_heads, preferred_element_type=jnp.float32)
        * score_scale
    )
    query_pos = first_row + jnp.arange(block_rows, dtype=jnp.int32)
    key_pos = jnp.arange(sequence_rows, dtype=jnp.int32)
    query_seg = lax.dynamic_slice_in_dim(segment_row, first_row, block_rows, 0)
    allowed = (key_pos[None, :] <= query_pos[:, None]) & (
        segment_row[None, :] == query_seg[:, None]
    )
    return jnp.where(allowed[None], scores, neg_fill)


def gather_seq(tensor):
    return lax.all_gather(tensor, "seq", axis=0, tiled=True)


def scatter_seq(tensor):
    return lax.psum_scatter(tensor, "seq", scatter_dimension=0, tiled=True)


def columns_in(weight):
    seq_count = lax.axis_size("seq")
    fsdp_count = lax.axis_size("fsdp")
    part = lax.all_to_all(weight, "seq", split_axis=1, concat_axis=0, tiled=True)
    whole = lax.all_gather(part, "fsdp", axis=0, tiled=True)
    return swap_blocks(whole, fsdp_count, seq_count)


def columns_out(term):
    seq_count = lax.axis_size("seq")
    fsdp_count = lax.axis_size("fsdp")
    swapped = swap_blocks(term, seq_count, fsdp_count).astype(jnp.bfloat16)
    summed = lax.psum_scatter(swapped, "fsdp", scatter_dimension=0, tiled=True)
    return lax.all_to_all(summed, "seq", split_axis=0, concat_axis=1, tiled=True).astype(
        jnp.float32
    )


def rope_tables(row_count):
    half_width = DH // 2
    frequency = rope_base ** (-jnp.arange(half_width, dtype=jnp.float32) * 2.0 / DH)
    angles = jnp.arange(row_count, dtype=jnp.int32).astype(jnp.float32)[:, None] * frequency[None, :]
    return jnp.cos(angles), jnp.sin(angles)


def rotate(tensor, cosine, sine_table):
    row_count = tensor.shape[0]
    half_width = DH // 2
    grouped = tensor.reshape(row_count, -1, DH)
    first_half = grouped[..., :half_width]
    second_half = grouped[..., half_width:]
    cosine = cosine[:, None, :]
    sine_table = sine_table[:, None, :]
    turned = jnp.concatenate(
        [
            first_half * cosine - second_half * sine_table,
            second_half * cosine + first_half * sine_table,
        ],
        axis=-1,
    )
    return turned.reshape(tensor.shape)


def per_device(
    inputs,
    query_weight,
    key_weight,
    value_weight,
    output_weight,
    query_gain,
    key_gain,
    attention_gain,
    gate_weight,
    up_weight,
    down_weight,
    feedforward_gain,
    segments,
    cotangent,
):
    token_count = inputs.shape[1]
    width_all = inputs.shape[2]
    local_in = inputs.reshape(token_count, width_all)
    segment_row = segments[0]
    score_scale = DH ** (-0.5)
    seq_index = lax.axis_index("seq")
    inputs_all = gather_seq(local_in)
    sequence_rows = inputs_all.shape[0]
    query_cols = columns_in(query_weight)
    key_cols = columns_in(key_weight)
    value_cols = columns_in(value_weight)
    head_width = query_cols.shape[1]
    local_heads = head_width // DH
    output_rows = lax.all_gather(output_weight, "fsdp", axis=0, tiled=True)
    gains = lax.all_gather(
        jnp.stack([query_gain, key_gain, attention_gain, feedforward_gain]),
        ("seq", "fsdp"),
        axis=1,
        tiled=True,
    ).astype(jnp.float32)
    query_scale = lax.dynamic_slice_in_dim(gains[0], seq_index * head_width, head_width, 0)
    key_scale = lax.dynamic_slice_in_dim(gains[1], seq_index * head_width, head_width, 0)
    attention_scale = gains[2]
    feedforward_scale = gains[3]
    query_pre = jnp.dot(inputs_all, query_cols, preferred_element_type=jnp.float32)
    key_pre = jnp.dot(inputs_all, key_cols, preferred_element_type=jnp.float32)
    values_low = jnp.dot(inputs_all, value_cols, preferred_element_type=jnp.float32).astype(
        jnp.bfloat16
    )
    squares = lax.psum(
        jnp.stack([jnp.sum(query_pre * query_pre, axis=-1), jnp.sum(key_pre * key_pre, axis=-1)]),
        "seq",
    )
    inverse = lax.rsqrt(squares / width_all + eps_norm)
    query_unit = query_pre * inverse[0][:, None]
    key_unit = key_pre * inverse[1][:, None]
    cosine, sine_table = rope_tables(sequence_rows)
    queries_low = rotate(query_unit * query_scale, cosine, sine_table).astype(jnp.bfloat16)
    keys_low = rotate(key_unit * key_scale, cosine, sine_table).astype(jnp.bfloat16)
    query_heads = queries_low.reshape(sequence_rows, local_heads, DH)
    key_heads = keys_low.reshape(sequence_rows, local_heads, DH)
    value_heads = values_low.reshape(sequence_rows, local_heads, DH)
    block_rows = min(512, sequence_rows)
    block_count = sequence_rows // block_rows
    block_ids = jnp.arange(block_count, dtype=jnp.int32)

    def attend_block(loop_state, block_index):
        first_row = block_index * block_rows
        query_block = lax.dynamic_slice_in_dim(query_heads, first_row, block_rows, 0)
        scores = masked_scores(query_block, key_heads, first_row, segment_row, score_scale)
        row_max = jnp.max(scores, axis=-1, keepdims=True)
        expanded = jnp.exp(scores - row_max)
        row_total = jnp.sum(expanded, axis=-1, keepdims=True)
        softmax_low = (expanded / row_total).astype(jnp.bfloat16)
        block_out = jnp.einsum(
            "hqk,khd->qhd", softmax_low, value_heads, preferred_element_type=jnp.float32
        )
        log_total = (row_max + jnp.log(row_total))[..., 0]
        return (loop_state, (block_out.astype(jnp.bfloat16), log_total))

    _, (out_blocks, log_totals) = lax.scan(attend_block, jnp.zeros((), jnp.int32), block_ids)
    attended_heads = out_blocks.reshape(sequence_rows, head_width)
    projected = scatter_seq(
        jnp.dot(attended_heads, output_rows, preferred_element_type=jnp.float32).astype(
            jnp.bfloat16
        )
    ).astype(jnp.float32)
    hidden = local_in.astype(jnp.float32) + rms_scale(projected, attention_scale)
    hidden_low = hidden.astype(jnp.bfloat16)
    gate_cols = columns_in(gate_weight)
    up_cols = columns_in(up_weight)
    down_cols = columns_in(down_weight)
    hidden_all = gather_seq(hidden_low)
    gate_linear = jnp.dot(hidden_all, gate_cols, preferred_element_type=jnp.float32)
    up_linear = jnp.dot(hidden_all, up_cols, preferred_element_type=jnp.float32)
    activated = swiglu_act(gate_linear, up_linear).astype(jnp.bfloat16)
    mixed_pre = scatter_seq(contract_cols(activated, down_cols).astype(jnp.bfloat16)).astype(
        jnp.float32
    )
    result = (
        (hidden + rms_scale(mixed_pre, feedforward_scale))
        .astype(jnp.bfloat16)
        .reshape(1, token_count, width_all)
    )
    grad_result = cotangent.reshape(token_count, width_all).astype(jnp.float32)
    _, mixed_pull = jax.vjp(rms_scale, mixed_pre, feedforward_scale)
    grad_mixed, grad_feedforward_gain = mixed_pull(grad_result)
    grad_mixed_low = grad_mixed.astype(jnp.bfloat16)
    grad_all = gather_seq(grad_mixed_low)
    grad_activated = jnp.dot(grad_all, down_cols, preferred_element_type=jnp.float32)
    _, swiglu_pull = jax.vjp(swiglu_act, gate_linear, up_linear)
    grad_gate, grad_upward = swiglu_pull(grad_activated)
    grad_gate_low = grad_gate.astype(jnp.bfloat16)
    grad_upward_low = grad_upward.astype(jnp.bfloat16)
    grad_hidden = grad_result + scatter_seq(
        (contract_cols(grad_gate_low, gate_cols) + contract_cols(grad_upward_low, up_cols)).astype(
            jnp.bfloat16
        )
    ).astype(jnp.float32)
    gate_weight_grad = columns_out(contract_rows(hidden_all, grad_gate_low))
    up_weight_grad = columns_out(contract_rows(hidden_all, grad_upward_low))
    down_weight_grad = columns_out(contract_rows(grad_all, activated))
    _, branch_pull = jax.vjp(rms_scale, projected, attention_scale)
    grad_projected, grad_attention_gain = branch_pull(grad_hidden)
    grad_projected_all = gather_seq(grad_projected.astype(jnp.bfloat16))
    output_weight_grad = lax.psum_scatter(
        contract_rows(attended_heads, grad_projected_all).astype(jnp.bfloat16),
        "fsdp",
        scatter_dimension=0,
        tiled=True,
    ).astype(jnp.float32)
    grad_attended = contract_cols(grad_projected_all, output_rows).astype(jnp.bfloat16)
    grad_out_heads = grad_attended.reshape(sequence_rows, local_heads, DH)

    def attend_back(loop_state, block_index):
        key_total, value_total = loop_state
        first_row = block_index * block_rows
        query_block = lax.dynamic_slice_in_dim(query_heads, first_row, block_rows, 0)
        grad_block = lax.dynamic_slice_in_dim(grad_out_heads, first_row, block_rows, 0)
        log_block = lax.dynamic_index_in_dim(log_totals, block_index, 0, keepdims=False)
        scores = masked_scores(query_block, key_heads, first_row, segment_row, score_scale)
        probabilities = jnp.exp(scores - log_block[..., None])
        softmax_low = probabilities.astype(jnp.bfloat16)
        value_total = value_total + jnp.einsum(
            "hqk,qhd->khd", softmax_low, grad_block, preferred_element_type=jnp.float32
        )
        grad_softmax = jnp.einsum(
            "qhd,khd->hqk", grad_block, value_heads, preferred_element_type=jnp.float32
        )
        row_dot = jnp.sum(probabilities * grad_softmax, axis=-1, keepdims=True)
        grad_scores = (probabilities * (grad_softmax - row_dot)).astype(jnp.bfloat16)
        grad_query_block = (
            jnp.einsum("hqk,khd->qhd", grad_scores, key_heads, preferred_element_type=jnp.float32)
            * score_scale
        )
        key_total = (
            key_total
            + jnp.einsum(
                "hqk,qhd->khd", grad_scores, query_block, preferred_element_type=jnp.float32
            )
            * score_scale
        )
        return ((key_total, value_total), grad_query_block.astype(jnp.bfloat16))

    zero_heads = jnp.zeros((sequence_rows, local_heads, DH), jnp.float32)
    (key_total, value_total), grad_query_blocks = lax.scan(
        attend_back, (zero_heads, zero_heads), block_ids
    )
    grad_queries = grad_query_blocks.reshape(sequence_rows, head_width).astype(jnp.float32)
    grad_keys = (
        key_total.astype(jnp.bfloat16).reshape(sequence_rows, head_width).astype(jnp.float32)
    )
    grad_values = value_total.astype(jnp.bfloat16).reshape(sequence_rows, head_width)
    query_error = rotate(grad_queries, cosine, -sine_table)
    key_error = rotate(grad_keys, cosine, -sine_table)
    grad_query_gain = jnp.sum(query_error * query_unit, axis=0)
    grad_key_gain = jnp.sum(key_error * key_unit, axis=0)
    query_error = query_error * query_scale
    key_error = key_error * key_scale
    means = (
        lax.psum(
            jnp.stack(
                [
                    jnp.sum(query_error * query_unit, axis=-1),
                    jnp.sum(key_error * key_unit, axis=-1),
                ]
            ),
            "seq",
        )
        / width_all
    )
    grad_query_low = (
        inverse[0][:, None] * (query_error - query_unit * means[0][:, None])
    ).astype(jnp.bfloat16)
    grad_key_low = (inverse[1][:, None] * (key_error - key_unit * means[1][:, None])).astype(
        jnp.bfloat16
    )
    grad_input = grad_hidden + scatter_seq(
        (
            contract_cols(grad_query_low, query_cols)
            + contract_cols(grad_key_low, key_cols)
            + contract_cols(grad_values, value_cols)
        ).astype(jnp.bfloat16)
    ).astype(jnp.float32)
    query_weight_grad = columns_out(contract_rows(inputs_all, grad_query_low))
    key_weight_grad = columns_out(contract_rows(inputs_all, grad_key_low))
    value_weight_grad = columns_out(contract_rows(inputs_all, grad_values))
    head_gains = lax.psum_scatter(
        jnp.stack([grad_query_gain, grad_key_gain]), "fsdp", scatter_dimension=1, tiled=True
    )
    token_gains = lax.psum_scatter(
        jnp.stack([grad_attention_gain, grad_feedforward_gain]),
        ("seq", "fsdp"),
        scatter_dimension=1,
        tiled=True,
    )
    return (
        result,
        grad_input.reshape(1, token_count, width_all),
        query_weight_grad,
        key_weight_grad,
        value_weight_grad,
        output_weight_grad,
        head_gains[0],
        head_gains[1],
        token_gains[0],
        gate_weight_grad,
        up_weight_grad,
        down_weight_grad,
        token_gains[1],
    )


def solution(mesh):
    in_specs = (
        P("fsdp", "seq", None),
        P(("seq", "fsdp"), None),
        P(("seq", "fsdp"), None),
        P(("seq", "fsdp"), None),
        P(("seq", "fsdp"), None),
        P(("seq", "fsdp")),
        P(("seq", "fsdp")),
        P(("seq", "fsdp")),
        P(("seq", "fsdp"), None),
        P(("seq", "fsdp"), None),
        P(("seq", "fsdp"), None),
        P(("seq", "fsdp")),
        P("fsdp", None),
        P("fsdp", "seq", None),
    )
    out_specs = (
        P("fsdp", "seq", None),
        P("fsdp", "seq", None),
        P(("seq", "fsdp"), None),
        P(("seq", "fsdp"), None),
        P(("seq", "fsdp"), None),
        P(("seq", "fsdp"), None),
        P(("seq", "fsdp")),
        P(("seq", "fsdp")),
        P(("seq", "fsdp")),
        P(("seq", "fsdp"), None),
        P(("seq", "fsdp"), None),
        P(("seq", "fsdp"), None),
        P(("seq", "fsdp")),
    )
    return jax.shard_map(
        per_device, mesh=mesh, in_specs=in_specs, out_specs=out_specs, check_vma=False
    )
```

time: 2410 us -> 1280 us (0.53)
  waiting for transfers between devices: 1780 us -> 703 us
  matrix products: 185 us -> 143 us
  local copies, waits for them, and re-layouts: 117 us -> 76.1 us
  blocking collectives: 215 us -> 254 us
    unnamed x21 -> x26, waiting for transfers between devices: 1090 us -> 148 us
    all_to_all x11 -> x6, waiting for transfers between devices: 172 us -> 46.1 us  [columns_out(): lax.all_to_all(summed, 'seq', split_axis=0, concat_axis=1, tiled=True)]
    unnamed x2 -> x0, blocking collectives: 103 us -> none
    all_gather x9 -> x11, waiting for transfers between devices: 325 us -> 252 us  [the longest x4 128 us: gather_seq(): return lax.all_gather(tensor, 'seq', axis=0, tiled=True)]
    all_gather x0 -> x1, blocking collectives: none -> 66.3 us  [per_device(): lax.all_gather(jnp.stack([query_gain, key_gain, attention_gain, feedforwa...]
    reduce_scatter x6 -> x11, waiting for transfers between devices: 198 us -> 257 us  [the longest x4 135 us: scatter_seq(): return lax.psum_scatter(tensor, 'seq', scatter_dimension=0, tiled=True)]
    unnamed x117 -> x116, local copies, waits for them, and re-layouts: 63.8 us -> 13.6 us
    all_to_all x3 -> x6, blocking collectives: 112 us -> 157 us  [columns_in(): lax.all_to_all(weight, 'seq', split_axis=1, concat_axis=0, tiled=True)]
  transfers between devices with their start and end apart: 29 -> 30, of which waited for: 22 -> 20; matrix products, arithmetic and copies ran while one was open for 11% -> 16% of each run, Pallas kernels for 0% -> 0%
where the time goes in v1:
time: 1280 us; the launch traced here: 1270 us
  waiting for transfers between devices  703 us (55%)
  blocking collectives  254 us (20%)
  matrix products  143 us (11%)
  local copies, waits for them, and re-layouts  76.1 us (6%)
  other arithmetic  43.9 us (3%)
  starting transfers between devices  26.9 us (2%)
  between operations  15.7 us (1%)
    all_to_all x6, blocking collectives, columns_in(): lax.all_to_all(weight, 'seq', split_axis=1, concat_axis=0, tiled=True)  157 us
    unnamed x26, waiting for transfers between devices  148 us
    reduce_scatter x4, waiting for transfers between devices, scatter_seq(): return lax.psum_scatter(tensor, 'seq', scatter_dimension=0, tiled=True)  135 us
    all_gather x4, waiting for transfers between devices, gather_seq(): return lax.all_gather(tensor, 'seq', axis=0, tiled=True)  128 us
    all_gather x6, waiting for transfers between devices, columns_in(): whole = lax.all_gather(part, 'fsdp', axis=0, tiled=True)  124 us
    reduce_scatter x6, waiting for transfers between devices, columns_out(): summed = lax.psum_scatter(swapped, 'fsdp', scatter_dimension=0, tiled=True)  93.7 us
    all_gather x1, blocking collectives, per_device(): lax.all_gather(jnp.stack([query_gain, key_gain, attention_gain, feedforwa...  66.3 us
    all_to_all x6, waiting for transfers between devices, columns_out(): lax.all_to_all(summed, 'seq', split_axis=0, concat_axis=1, tiled=True)  46.1 us
  transfers between devices with their start and end apart: 30, of which 20 were waited for; matrix products, arithmetic and copies ran while one was open for 16% of the time, Pallas kernels for 0%

profile of v1, /device:TPU:0, one launch (start us, length us, event | category | flops | bytes accessed | tf_op | source)
XLA Modules:
  0.0 1268.5 jit_solution(9031191432619376328)
XLA Ops:
  8.2 16.0 %all_to_all.192 = bf16[64,8,256]{2,0,1:T(8,128)(2,1)} all-to-all(bf16[64,8,256]{2,0,1:T(8,128)(2,1)S(1)} %bitcast.402), channel_id=1, replica_groups=mesh['seq'=8,'fsdp'=4] {'seq'}, dimensions={1} | all-to-all | bytes 524288 | tf_op jit(solution)/shard_map/all_to_all | solution.py:95
  25.3 12.8 %all_to_all.193 = bf16[64,8,256]{2,0,1:T(8,128)(2,1)} all-to-all(bf16[64,8,256]{2,0,1:T(8,128)(2,1)S(1)} %bitcast.403), channel_id=1, replica_groups=mesh['seq'=8,'fsdp'=4] {'seq'}, dimensions={1} | all-to-all | bytes 524288 | tf_op jit(solution)/shard_map/all_to_all | solution.py:95
  39.1 12.8 %all_to_all.194 = bf16[64,8,256]{2,0,1:T(8,128)(2,1)} all-to-all(bf16[64,8,256]{2,0,1:T(8,128)(2,1)S(1)} %bitcast.404), channel_id=1, replica_groups=mesh['seq'=8,'fsdp'=4] {'seq'}, dimensions={1} | all-to-all | bytes 524288 | tf_op jit(solution)/shard_map/all_to_all | solution.py:95
  53.2 66.3 %all-gather.1 = bf16[32,64,4]{1,2,0:T(4,128)(2,1)S(1)} all-gather(bf16[1,64,4]{1,2,0:T(4,128)(2,1)S(1)} %maximum_bitcast_fusion), channel_id=1, replica_groups=mesh['seq'=8,'fsdp'=4] {'seq','fsdp'}, dimensions={0}, use_global_device_ids=true | all-gather | bytes 16896 | tf_op jit(solution)/shard_map/all_gather | solution.py:165
  119.6 3.1 fusion.102
  129.2 25.9 %all-gather.34.cloned.1.call-done = bf16[1,1024,2048]{2,1,0:T(8,128)(2,1)} async-done(((bf16[1,128,2048]{2,1,0:T(8,128)(2,1)}), bf16[1,1024,2048]{2,1,0:T(8,128)(2,1)}) %all-gather.34.cloned.1.call-update) | async-done | bytes 4194320 | tf_op jit(solution)/shard_map/all_gather | solution.py:85
  155.1 3.6 multiply_reduce_fusion.4
  160.2 15.2 %psum.14 = f32[2,1024]{1,0:T(2,128)S(1)} all-reduce(f32[2,1024]{1,0:T(2,128)S(1)} %pad_maximum_fusion.5), channel_id=1, replica_groups=mesh['seq'=8,'fsdp'=4] {'seq'}, use_global_device_ids=true, to_apply=%region_2.0 | all-reduce | flops 2048 | bytes 16384 | tf_op jit(solution)/shard_map/psum | solution.py:180
  181.7 4.4 fusion.76
  190.7 12.2 while.27
  202.9 4.7 convolution_convert_fusion
  207.8 47.5 %all_to_all.195 = bf16[64,8,1024]{2,0,1:T(8,128)(2,1)} all-to-all(bf16[64,8,1024]{2,0,1:T(8,128)(2,1)S(1)} %bitcast.377), channel_id=1, replica_groups=mesh['seq'=8,'fsdp'=4] {'seq'}, dimensions={1} | all-to-all | bytes 2097152 | tf_op jit(solution)/shard_map/all_to_all | solution.py:95
  256.8 38.2 %all_to_all.196 = bf16[64,8,1024]{2,0,1:T(8,128)(2,1)} all-to-all(bf16[64,8,1024]{2,0,1:T(8,128)(2,1)S(1)} %bitcast.378), channel_id=1, replica_groups=mesh['seq'=8,'fsdp'=4] {'seq'}, dimensions={1} | all-to-all | bytes 2097152 | tf_op jit(solution)/shard_map/all_to_all | solution.py:95
  295.1 29.8 %all_to_all.197 = bf16[64,8,1024]{2,0,1:T(8,128)(2,1)} all-to-all(bf16[64,8,1024]{2,0,1:T(8,128)(2,1)S(1)} %bitcast.379), channel_id=1, replica_groups=mesh['seq'=8,'fsdp'=4] {'seq'}, dimensions={1} | all-to-all | bytes 2097152 | tf_op jit(solution)/shard_map/all_to_all | solution.py:95
  328.6 24.5 %all-gather.24.cloned.1.call-done = bf16[2048,1024]{1,0:T(8,128)(2,1)} async-done(((bf16[512,1024]{1,0:T(8,128)(2,1)}), bf16[2048,1024]{1,0:T(8,128)(2,1)}) %all-gather.24.cloned.1.call-update) | async-done | bytes 4194320 | tf_op jit(solution)/shard_map/all_gather | solution.py:96
  353.2 4.9 copy.166
  358.1 49.5 %all-gather.26.cloned.1.call-done = bf16[2048,1024]{1,0:T(8,128)(2,1)} async-done(((bf16[512,1024]{1,0:T(8,128)(2,1)}), bf16[2048,1024]{1,0:T(8,128)(2,1)}) %all-gather.26.cloned.1.call-update) | async-done | bytes 4194320 | tf_op jit(solution)/shard_map/all_gather | solution.py:96
  407.6 5.0 copy.168
  412.6 49.5 %all-gather.28.cloned.1.call-done = bf16[2048,1024]{1,0:T(8,128)(2,1)} async-done(((bf16[512,1024]{1,0:T(8,128)(2,1)}), bf16[2048,1024]{1,0:T(8,128)(2,1)}) %all-gather.28.cloned.1.call-update) | async-done | bytes 4194320 | tf_op jit(solution)/shard_map/all_gather | solution.py:96
  462.1 5.0 copy.170
  467.1 43.9 %all-gather.22.cloned.1.call-done = bf16[1024,2048]{1,0:T(8,128)(2,1)} async-done(((bf16[128,2048]{1,0:T(8,128)(2,1)}), bf16[1024,2048]{1,0:T(8,128)(2,1)}) %all-gather.22.cloned.1.call-update) | async-done | bytes 4194320 | tf_op jit(solution)/shard_map/all_gather | solution.py:85
  511.0 7.7 fusion.112
  518.7 6.6 multiply_convert_fusion.2
  526.6 6.1 convolution_convert_fusion.4
  532.8 48.8 %reduce-scatter.20.cloned.1.call-done = bf16[128,2048]{1,0:T(8,128)(2,1)} async-done(((bf16[1024,2048]{1,0:T(8,128)(2,1)}), bf16[128,2048]{1,0:T(8,128)(2,1)}) %reduce-scatter.20.cloned.1.call-update) | async-done | bytes 524304 | tf_op jit(solution)/shard_map/reduce_scatter | solution.py:89
  587.1 45.0 %all-gather.30.cloned.1.call-done = bf16[1024,2048]{1,0:T(8,128)(2,1)} async-done(((bf16[128,2048]{1,0:T(8,128)(2,1)}), bf16[1024,2048]{1,0:T(8,128)(2,1)}) %all-gather.30.cloned.1.call-update) | async-done | bytes 4194320 | tf_op jit(solution)/shard_map/all_gather | solution.py:85
  632.1 11.7 multiply_convert_fusion.1
  643.9 4.6 fusion.113
  648.5 6.2 add_convert_fusion.1
  654.8 48.8 %reduce-scatter.22.cloned.1.call-done = bf16[128,2048]{1,0:T(8,128)(2,1)} async-done(((bf16[1024,2048]{1,0:T(8,128)(2,1)}), bf16[128,2048]{1,0:T(8,128)(2,1)}) %reduce-scatter.22.cloned.1.call-update) | async-done | bytes 524304 | tf_op jit(solution)/shard_map/reduce_scatter | solution.py:89
  708.3 7.4 convolution_convert_fusion.1
  718.3 7.5 convolution_convert_fusion.3
  728.4 7.5 convolution_convert_fusion.2
  740.3 13.3 %all-gather.32.cloned.1.call-done = bf16[1024,2048]{1,0:T(8,128)(2,1)} async-done(((bf16[128,2048]{1,0:T(8,128)(2,1)}), bf16[1024,2048]{1,0:T(8,128)(2,1)}) %all-gather.32.cloned.1.call-update) | async-done | bytes 4194320 | tf_op jit(solution)/shard_map/all_gather | solution.py:85
  753.6 3.8 convolution_convert_fusion.6
  757.4 40.7 %while.28 = (s32[]{:T(128)}, f32[1024,2,128]{0,2,1:T(8,128)}, f32[1024,2,128]{0,2,1:T(8,128)}, bf16[2,512,2,128]{3,1,0,2:T(8,128)(2,1)}, s32[2]{0:T(128)S(1)}, /...) while((s32[]{:T(128)}, f32[1024,2,128]{0,2,1:T(8,128)}, ...), condition=%wide.region_16.17_spmd.clone, body=%wide.region_14.16_spmd.clone.sunk | while | flops 1361051136 | bytes 86813704 | solution.py:296
  764.1 4.2 multiply_reduce_fusion.6
  773.8 3.5 fusion.195
  784.0 4.3 multiply_reduce_fusion.6
  789.8 3.0 fusion.194
  794.2 3.9 fusion.195
  813.1 15.1 %psum.15 = f32[2,1024]{1,0:T(2,128)S(1)} all-reduce(f32[2,1024]{1,0:T(2,128)S(1)} %pad_maximum_fusion.6), channel_id=1, replica_groups=mesh['seq'=8,'fsdp'=4] {'seq'}, use_global_device_ids=true, to_apply=%region_19.20 | all-reduce | flops 2048 | bytes 16384 | tf_op jit(solution)/shard_map/psum | solution.py:311
  829.8 4.4 fusion.70
  839.4 4.5 fusion.73
  847.5 5.2 convolution_convert_fusion.5
  854.8 4.5 fusion.67
  864.7 3.4 add_convert_fusion
  868.2 3.6 all-to-all-start.11
  871.8 26.5 %all-to-all-done.11 = bf16[8,64,1024]{2,1,0:T(8,128)(2,1)S(1)} async-done(((bf16[8,64,1024]{2,1,0:T(8,128)(2,1)}), bf16[8,64,1024]{2,1,0:T(8,128)(2,1)S(1)}, u32[]{:S(2)}, u32[]{:S(2)}) %all-to-all-start.11) | async-done | bytes 1048608 | tf_op jit(solution)/shard_map/all_to_all | solution.py:105
  898.3 3.6 all-to-all-start.9
  901.8 16.9 %reduce-scatter.36.cloned.1.call-done = bf16[512,1024]{1,0:T(8,128)(2,1)} async-done(((bf16[2048,1024]{1,0:T(8,128)(2,1)}), bf16[512,1024]{1,0:T(8,128)(2,1)}) %reduce-scatter.36.cloned.1.call-update) | async-done | bytes 1048592 | tf_op jit(solution)/shard_map/reduce_scatter | solution.py:104
  918.7 9.6 all-to-all-done.9
  929.3 3.6 all-to-all-start.10
  932.8 125.1 %reduce-scatter.42.cloned.1.call-done = f32[64,2]{1,0:T(8,128)} async-done(((f32[2048,2]{1,0:T(8,128)}), f32[64,2]{1,0:T(8,128)}) %reduce-scatter.42.cloned.1.call-update) | async-done | bytes 528
  1060.1 25.0 %reduce-scatter.28.cloned.1.call-done = bf16[512,256]{1,0:T(8,128)(2,1)} async-done(((bf16[2048,256]{1,0:T(8,128)(2,1)}), bf16[512,256]{1,0:T(8,128)(2,1)}) %reduce-scatter.28.cloned.1.call-update) | async-done | bytes 262160 | tf_op jit(solution)/shard_map/reduce_scatter | solution.py:104
  1085.1 4.6 all-to-all-start.7
  1093.1 22.7 %reduce-scatter.26.cloned.1.call-done = bf16[512,256]{1,0:T(8,128)(2,1)} async-done(((bf16[2048,256]{1,0:T(8,128)(2,1)}), bf16[512,256]{1,0:T(8,128)(2,1)}) %reduce-scatter.26.cloned.1.call-update) | async-done | bytes 262160 | tf_op jit(solution)/shard_map/reduce_scatter | solution.py:104
  1115.8 4.6 all-to-all-start.6
  1122.1 21.1 %reduce-scatter.40.cloned.1.call-done = f32[64,2]{1,0:T(8,128)} async-done(((f32[256,2]{1,0:T(8,128)}), f32[64,2]{1,0:T(8,128)}) %reduce-scatter.40.cloned.1.call-update) | async-done | bytes 528
  1145.3 28.8 %reduce-scatter.32.cloned.1.call-done = bf16[64,2048]{1,0:T(8,128)(2,1)} async-done(((bf16[256,2048]{1,0:T(8,128)(2,1)}), bf16[64,2048]{1,0:T(8,128)(2,1)}) %reduce-scatter.32.cloned.1.call-update) | async-done | bytes 262160 | tf_op jit(solution)/shard_map/reduce_scatter | solution.py:256
  1175.9 29.1 %reduce-scatter.30.cloned.1.call-done = bf16[512,256]{1,0:T(8,128)(2,1)} async-done(((bf16[2048,256]{1,0:T(8,128)(2,1)}), bf16[512,256]{1,0:T(8,128)(2,1)}) %reduce-scatter.30.cloned.1.call-update) | async-done | bytes 262160 | tf_op jit(solution)/shard_map/reduce_scatter | solution.py:104
  1205.0 4.6 all-to-all-start.8
  1211.3 10.1 all-to-all-done.8
  1222.3 36.9 %reduce-scatter.24.cloned.1.call-done = bf16[128,2048]{1,0:T(8,128)(2,1)} async-done(((bf16[1024,2048]{1,0:T(8,128)(2,1)}), bf16[128,2048]{1,0:T(8,128)(2,1)}) %reduce-scatter.24.cloned.1.call-update) | async-done | bytes 524304 | tf_op jit(solution)/shard_map/reduce_scatter | solution.py:89
  (332 shorter events, 126.3 us)
Async XLA Ops:
  7.2 46.0 %copy-start.54 = (bf16[64]{0:T(256)(128)(2,1)S(1)}, bf16[64]{0:T(256)(128)(2,1)}, u32[]{:S(2)}) copy-start(bf16[64]{0:T(256)(128)(2,1)} %param.23) | copy-start | bytes 388
  7.2 46.0 %copy-start.53 = (bf16[64]{0:T(256)(128)(2,1)S(1)}, bf16[64]{0:T(256)(128)(2,1)}, u32[]{:S(2)}) copy-start(bf16[64]{0:T(256)(128)(2,1)} %param.24) | copy-start | bytes 388
  7.2 46.0 %copy-start.52 = (bf16[64]{0:T(256)(128)(2,1)S(1)}, bf16[64]{0:T(256)(128)(2,1)}, u32[]{:S(2)}) copy-start(bf16[64]{0:T(256)(128)(2,1)} %param.25) | copy-start | bytes 388
  7.2 46.0 %copy-start.51 = (bf16[64]{0:T(256)(128)(2,1)S(1)}, bf16[64]{0:T(256)(128)(2,1)}, u32[]{:S(2)}) copy-start(bf16[64]{0:T(256)(128)(2,1)} %param.29) | copy-start | bytes 388
  7.2 115.5 %all-gather.14.cloned.1.call-start = ((), (), s32[]{:S(2)}) async-start(), calls=%async_computation.25 | async-start | bytes 1310720 | tf_op jit(solution)/shard_map/all_gather | solution.py:96
  24.2 100.0 %all-gather.16.cloned.1.call-start = ((), (), s32[]{:S(2)}) async-start(), calls=%async_computation.26 | async-start | bytes 1310720 | tf_op jit(solution)/shard_map/all_gather | solution.py:96
  38.0 88.9 %all-gather.18.cloned.1.call-start = ((), (), s32[]{:S(2)}) async-start(), calls=%async_computation.27 | async-start | bytes 1310720 | tf_op jit(solution)/shard_map/all_gather | solution.py:96
  51.9 103.2 %all-gather.34.cloned.1.call-start = ((), (), s32[]{:S(2)}) async-start(), calls=%async_computation.46 | async-start | bytes 4718592 | tf_op jit(solution)/shard_map/all_gather | solution.py:85
  52.4 150.5 %all-gather.20.cloned.1.call-start = ((), (), s32[]{:S(2)}) async-start(), calls=%async_computation.28 | async-start | bytes 1310720 | tf_op jit(solution)/shard_map/all_gather | solution.py:164
  53.0 272.0 %reduce-scatter.18.cloned.1.call-start = ((), (), s32[]{:S(2)}) async-start(), calls=%async_computation.29 | async-start | bytes 4718592 | tf_op jit(solution)/shard_map/reduce_scatter | solution.py:89
  122.7 64.7 %copy-start.15 = (f32[1024,64]{1,0:T(8,128)}, f32[1024,64]{1,0:T(8,128)S(1)}, u32[]{:S(2)}) copy-start(f32[1024,64]{1,0:T(8,128)S(1)} %get-tuple-element.362) | copy-start | bytes 786436
  122.7 52.8 %copy-start.47 = (f32[1,256]{1,0:T(1,128)}, f32[1,256]{1,0:T(1,128)S(1)}, u32[]{:S(2)}) copy-start(f32[1,256]{1,0:T(1,128)S(1)} %get-tuple-element.370) | copy-start | bytes 3076
  122.7 56.1 %copy-start.49 = (f32[1,256]{1,0:T(1,128)}, f32[1,256]{1,0:T(1,128)S(1)}, u32[]{:S(2)}) copy-start(f32[1,256]{1,0:T(1,128)S(1)} %get-tuple-element.369) | copy-start | bytes 3076
  124.2 34.6 %copy-start.19 = (bf16[4,8,64,256]{3,2,0,1:T(8,128)(2,1)}, bf16[4,8,64,256]{3,2,0,1:T(8,128)(2,1)S(1)}, u32[]{:S(2)}) copy-start(bf16[4,8,64,256]{3,2,0,1:T(8,128)(2,1)S(1)} %copy.153) | copy-start | bytes 3145732
  158.8 16.8 %copy-start.8 = (f32[1024,256]{0,1:T(8,128)}, f32[1024,256]{0,1:T(8,128)S(1)}, u32[]{:S(2)}) copy-start(f32[1024,256]{0,1:T(8,128)S(1)} %get-tuple-element.366) | copy-start | bytes 3145732
  160.2 18.8 %copy-start.10 = (f32[1024,256]{0,1:T(8,128)}, f32[1024,256]{0,1:T(8,128)S(1)}, u32[]{:S(2)}) copy-start(f32[1024,256]{0,1:T(8,128)S(1)} %get-tuple-element.364) | copy-start | bytes 3145732
  181.7 5.7 copy-start.27
  202.9 4.8 copy-start.40
  207.7 145.5 %all-gather.24.cloned.1.call-start = ((), (), s32[]{:S(2)}) async-start(), calls=%async_computation.31 | async-start | bytes 5242880 | tf_op jit(solution)/shard_map/all_gather | solution.py:96
  207.8 87.2 %copy-start.41 = (bf16[64,8192]{1,0:T(8,128)(2,1)S(1)}, bf16[64,8192]{1,0:T(8,128)(2,1)}, u32[]{:S(2)}) copy-start(bf16[64,8192]{1,0:T(8,128)(2,1)} %param.28) | copy-start | bytes 3145732
  255.4 152.2 %all-gather.26.cloned.1.call-start = ((), (), s32[]{:S(2)}) async-start(), calls=%async_computation.32 | async-start | bytes 5242880 | tf_op jit(solution)/shard_map/all_gather | solution.py:96
  256.8 69.5 %copy-start.17 = (bf16[1,128,2048]{2,1,0:T(8,128)(2,1)S(1)}, bf16[1,128,2048]{2,1,0:T(8,128)(2,1)}, u32[]{:S(2)}) copy-start(bf16[1,128,2048]{2,1,0:T(8,128)(2,1)} %param.18) | copy-start | bytes 1572868
  295.0 167.1 %all-gather.28.cloned.1.call-start = ((), (), s32[]{:S(2)}) async-start(), calls=%async_computation.33 | async-start | bytes 5242880 | tf_op jit(solution)/shard_map/all_gather | solution.py:96
  324.9 186.1 %all-gather.22.cloned.1.call-start = ((), (), s32[]{:S(2)}) async-start(), calls=%async_computation.30 | async-start | bytes 4718592 | tf_op jit(solution)/shard_map/all_gather | solution.py:85
  328.4 253.3 %reduce-scatter.20.cloned.1.call-start = ((), (), s32[]{:S(2)}) async-start(), calls=%async_computation.34 | async-start | bytes 4718592 | tf_op jit(solution)/shard_map/reduce_scatter | solution.py:89
  511.0 7.7 copy-start.29
  511.0 7.7 copy-start.56
  518.7 6.6 copy-start.57
  518.7 7.9 copy-start.31
  532.7 50.1 %copy-start.6 = (bf16[1,128,2048]{2,1,0:T(8,128)(2,1)S(1)}, bf16[1,128,2048]{2,1,0:T(8,128)(2,1)}, u32[]{:S(2)}) copy-start(bf16[1,128,2048]{2,1,0:T(8,128)(2,1)} %param.31) | copy-start | bytes 1572868
  532.8 99.4 %all-gather.30.cloned.1.call-start = ((), (), s32[]{:S(2)}) async-start(), calls=%async_computation.35 | async-start | bytes 4718592 | tf_op jit(solution)/shard_map/all_gather | solution.py:85
  586.7 116.9 %reduce-scatter.22.cloned.1.call-start = ((), (), s32[]{:S(2)}) async-start(), calls=%async_computation.36 | async-start | bytes 4718592 | tf_op jit(solution)/shard_map/reduce_scatter | solution.py:89
  632.1 11.7 copy-start.28
  654.7 48.9 %copy-start.13 = (bf16[128,2048]{1,0:T(8,128)(2,1)S(1)}, bf16[128,2048]{1,0:T(8,128)(2,1)}, u32[]{:S(2)}) copy-start(bf16[128,2048]{1,0:T(8,128)(2,1)} %reduce-scatter.18.cloned.1.call-done) | copy-start | bytes 1572868
  654.7 50.5 %copy-start.14 = (bf16[128,2048]{1,0:T(8,128)(2,1)S(1)}, bf16[128,2048]{1,0:T(8,128)(2,1)}, u32[]{:S(2)}) copy-start(bf16[128,2048]{1,0:T(8,128)(2,1)} %reduce-scatter.20.cloned.1.call-done) | copy-start | bytes 1572868
  654.7 98.9 %all-gather.32.cloned.1.call-start = ((), (), s32[]{:S(2)}) async-start(), calls=%async_computation.37 | async-start | bytes 4718592 | tf_op jit(solution)/shard_map/all_gather | solution.py:85
  708.1 160.1 %reduce-scatter.38.cloned.1.call-start = ((), (), s32[]{:S(2)}) async-start(), calls=%async_computation.45 | async-start | bytes 5242880 | tf_op jit(solution)/shard_map/reduce_scatter | solution.py:104
  718.3 153.5 %reduce-scatter.34.cloned.1.call-start = ((), (), s32[]{:S(2)}) async-start(), calls=%async_computation.43 | async-start | bytes 5242880 | tf_op jit(solution)/shard_map/reduce_scatter | solution.py:104
  728.4 190.4 %reduce-scatter.36.cloned.1.call-start = ((), (), s32[]{:S(2)}) async-start(), calls=%async_computation.44 | async-start | bytes 5242880 | tf_op jit(solution)/shard_map/reduce_scatter | solution.py:104
  738.3 319.7 %reduce-scatter.42.cloned.1.call-start = ((), (), s32[]{:S(2)}) async-start(), calls=%async_computation.48 | async-start | bytes 1081344
  739.9 345.2 %reduce-scatter.28.cloned.1.call-start = ((), (), s32[]{:S(2)}) async-start(), calls=%async_computation.40 | async-start | bytes 1310720 | tf_op jit(solution)/shard_map/reduce_scatter | solution.py:104
  757.4 10.9 copy-start.2
  757.4 10.9 copy-start.4
  757.4 10.9 copy-start.32
  777.4 11.0 copy-start.2
  777.4 11.0 copy-start.4
  777.4 11.0 copy-start.32
  804.5 7.1 copy-start.11
  804.5 7.1 copy-start.46
  804.5 7.1 copy-start.50
  834.2 5.0 copy-start.12
  838.9 276.9 %reduce-scatter.26.cloned.1.call-start = ((), (), s32[]{:S(2)}) async-start(), calls=%async_computation.39 | async-start | bytes 1310720 | tf_op jit(solution)/shard_map/reduce_scatter | solution.py:104
  846.5 296.8 %reduce-scatter.40.cloned.1.call-start = ((), (), s32[]{:S(2)}) async-start(), calls=%async_computation.47 | async-start | bytes 163840
  847.4 326.7 %reduce-scatter.32.cloned.1.call-start = ((), (), s32[]{:S(2)}) async-start(), calls=%async_computation.42 | async-start | bytes 1310720 | tf_op jit(solution)/shard_map/reduce_scatter | solution.py:256
  852.7 352.3 %reduce-scatter.30.cloned.1.call-start = ((), (), s32[]{:S(2)}) async-start(), calls=%async_computation.41 | async-start | bytes 1310720 | tf_op jit(solution)/shard_map/reduce_scatter | solution.py:104
  862.0 397.2 %reduce-scatter.24.cloned.1.call-start = ((), (), s32[]{:S(2)}) async-start(), calls=%async_computation.38 | async-start | bytes 4718592 | tf_op jit(solution)/shard_map/reduce_scatter | solution.py:89
  868.2 30.1 %all-to-all-start.11 = ((bf16[8,64,1024]{2,1,0:T(8,128)(2,1)}), bf16[8,64,1024]{2,1,0:T(8,128)(2,1)S(1)}, u32[]{:S(2)}, u32[]{:S(2)}) async-start(bf16[8,64,1024]{2,1,0:T(8,128)(2,1)} %bitcast.394), calls=%async_computation.22 | async-start | bytes 2097152 | tf_op jit(solution)/shard_map/all_to_all | solution.py:105
  898.3 30.1 %all-to-all-start.9 = ((bf16[8,64,1024]{2,1,0:T(8,128)(2,1)}), bf16[8,64,1024]{2,1,0:T(8,128)(2,1)S(1)}, u32[]{:S(2)}, u32[]{:S(2)}) async-start(bf16[8,64,1024]{2,1,0:T(8,128)(2,1)} %bitcast.395), calls=%async_computation.18 | async-start | bytes 2097152 | tf_op jit(solution)/shard_map/all_to_all | solution.py:105
  929.3 130.8 %all-to-all-start.10 = ((bf16[8,64,1024]{2,1,0:T(8,128)(2,1)}), bf16[8,64,1024]{2,1,0:T(8,128)(2,1)S(1)}, u32[]{:S(2)}, u32[]{:S(2)}) async-start(bf16[8,64,1024]{2,1,0:T(8,128)(2,1)} %bitcast.393), calls=%async_computation.20 | async-start | bytes 2097152 | tf_op jit(solution)/shard_map/all_to_all | solution.py:105
  1085.1 30.7 %all-to-all-start.7 = ((bf16[8,64,256]{2,1,0:T(8,128)(2,1)}), bf16[8,64,256]{2,1,0:T(8,128)(2,1)S(1)}, u32[]{:S(2)}, u32[]{:S(2)}) async-start(bf16[8,64,256]{2,1,0:T(8,128)(2,1)} %bitcast.418), calls=%async_computation.13 | async-start | bytes 524288 | tf_op jit(solution)/shard_map/all_to_all | solution.py:105
  1115.8 89.2 %all-to-all-start.6 = ((bf16[8,64,256]{2,1,0:T(8,128)(2,1)}), bf16[8,64,256]{2,1,0:T(8,128)(2,1)S(1)}, u32[]{:S(2)}, u32[]{:S(2)}) async-start(bf16[8,64,256]{2,1,0:T(8,128)(2,1)} %bitcast.417), calls=%async_computation.11 | async-start | bytes 524288 | tf_op jit(solution)/shard_map/all_to_all | solution.py:105
  1122.1 137.1 %copy-start.7 = (bf16[1,128,2048]{2,1,0:T(8,128)(2,1)S(1)}, bf16[1,128,2048]{2,1,0:T(8,128)(2,1)}, u32[]{:S(2)}) copy-start(bf16[1,128,2048]{2,1,0:T(8,128)(2,1)} %param.31) | copy-start | bytes 1572868
  1122.1 137.1 %copy-start.18 = (bf16[128,2048]{1,0:T(8,128)(2,1)S(1)}, bf16[128,2048]{1,0:T(8,128)(2,1)}, u32[]{:S(2)}) copy-start(bf16[128,2048]{1,0:T(8,128)(2,1)} %reduce-scatter.22.cloned.1.call-done) | copy-start | bytes 1572868
  1205.0 16.5 %all-to-all-start.8 = ((bf16[8,64,256]{2,1,0:T(8,128)(2,1)}), bf16[8,64,256]{2,1,0:T(8,128)(2,1)S(1)}, u32[]{:S(2)}, u32[]{:S(2)}) async-start(bf16[8,64,256]{2,1,0:T(8,128)(2,1)} %bitcast.419), calls=%async_computation.15 | async-start | bytes 524288 | tf_op jit(solution)/shard_map/all_to_all | solution.py:105
  (35 other events, 106.3 us)
Sparse Core Ops, SparseCore 0:
  24.3 25.4 all-gather.13
  51.7 26.5 all-gather.15
  80.1 26.5 all-gather.17
  108.2 46.8 all-gather.33
  156.8 25.2 all-gather.19
  207.8 77.5 reduce-scatter.17
  287.2 65.9 all-gather.23
  355.0 52.5 all-gather.25
  409.5 52.5 all-gather.27
  464.1 46.8 all-gather.21
  532.9 48.7 reduce-scatter.19
  586.8 45.3 all-gather.29
  654.8 48.7 reduce-scatter.21
  708.2 45.3 all-gather.31
  756.4 51.3 reduce-scatter.37
  810.6 52.5 reduce-scatter.33
  866.1 52.5 reduce-scatter.35
  920.8 137.0 reduce-scatter.41
  1060.9 24.1 reduce-scatter.27
  1087.8 27.9 reduce-scatter.25
  1119.1 24.1 reduce-scatter.39
  1146.2 27.9 reduce-scatter.31
  1177.0 27.9 reduce-scatter.29
  1207.1 52.0 reduce-scatter.23

commit v2 on v1

--- a/solution.py
+++ b/solution.py
@@ -1,6 +1,10 @@
+import functools
+
 import jax
 import jax.numpy as jnp
 from jax import lax
+from jax.experimental import pallas as pl
+from jax.experimental.pallas import tpu as pltpu
 from jax.sharding import PartitionSpec as P
 
 HEADS = 16
@@ -79,6 +83,584 @@
         segment_row[None, :] == query_seg[:, None]
     )
     return jnp.where(allowed[None], scores, neg_fill)
+
+MESH = pl.DeviceIdType.MESH
+RS_PARTS = 4
+
+
+class Line:
+    def __init__(self, chips):
+        index = lax.axis_index("seq")
+        self.chips = chips
+        self.fsdp = lax.axis_index("fsdp")
+        self.place = index // 2
+        self.core = index % 2
+
+    def device(self, place, core):
+        return (place * 2 + core, self.fsdp)
+
+    @property
+    def partner(self):
+        return self.device(self.place, 1 - self.core)
+
+    @property
+    def above(self):
+        return self.device(jnp.minimum(self.place + 1, self.chips - 1), self.core)
+
+    @property
+    def below(self):
+        return self.device(jnp.maximum(self.place - 1, 0), self.core)
+
+    @property
+    def has_above(self):
+        return self.place < self.chips - 1
+
+    @property
+    def has_below(self):
+        return self.place > 0
+
+    def greet(self):
+        barrier = pltpu.get_barrier_semaphore()
+        pl.semaphore_signal(barrier, inc=1, device_id=self.partner, device_id_type=MESH)
+
+        @pl.when(self.has_above)
+        def _():
+            pl.semaphore_signal(barrier, inc=1, device_id=self.above, device_id_type=MESH)
+
+        @pl.when(self.has_below)
+        def _():
+            pl.semaphore_signal(barrier, inc=1, device_id=self.below, device_id_type=MESH)
+
+        peers = (
+            1 + jnp.minimum(self.place, 1) + jnp.minimum(self.chips - 1 - self.place, 1)
+        )
+        pl.semaphore_wait(barrier, peers)
+
+    def order(self, step):
+        place, last = self.place, self.chips - 1
+        near = jnp.minimum(place, last - place)
+        both = jnp.where(step % 2 == 1, place - (step + 1) // 2, place + step // 2)
+        rest = jnp.where(place <= last - place, step, last - step)
+        return jnp.where(step <= 2 * near, both, rest)
+
+    def paired(self, step):
+        near = jnp.minimum(self.place, self.chips - 1 - self.place)
+        return (step % 2 == 1) & (step <= 2 * near)
+
+    def second_of_pair(self, step):
+        near = jnp.minimum(self.place, self.chips - 1 - self.place)
+        return (step % 2 == 0) & (step > 0) & (step <= 2 * near)
+
+
+class Gather:
+    def __init__(self, line, blocks, arrive, up_sem, down_sem, side_sem):
+        self.line, self.blocks, self.arrive = line, blocks, arrive
+        self.up_sem, self.down_sem, self.side_sem = up_sem, down_sem, side_sem
+
+    @staticmethod
+    def scratch(chips, rows, width):
+        return [
+            pltpu.VMEM((2 * chips, rows, width), jnp.bfloat16),
+            pltpu.SemaphoreType.DMA((2 * chips,)),
+            pltpu.SemaphoreType.DMA((chips,)),
+            pltpu.SemaphoreType.DMA((chips,)),
+            pltpu.SemaphoreType.DMA((chips,)),
+        ]
+
+    def copy(self, chip, sem, target):
+        slot = chip * 2 + self.line.core
+        return pltpu.make_async_remote_copy(
+            src_ref=self.blocks.at[slot],
+            dst_ref=self.blocks.at[slot],
+            send_sem=sem.at[chip],
+            recv_sem=self.arrive.at[slot],
+            device_id=target,
+            device_id_type=MESH,
+        )
+
+    def wait_slot(self, slot):
+        pltpu.make_async_remote_copy(
+            src_ref=self.blocks.at[slot],
+            dst_ref=self.blocks.at[slot],
+            send_sem=self.side_sem.at[0],
+            recv_sem=self.arrive.at[slot],
+            device_id=self.line.partner,
+            device_id_type=MESH,
+        ).wait_recv()
+
+    def send(self, chip):
+        line = self.line
+
+        @pl.when((chip <= line.place) & line.has_above)
+        def _():
+            self.copy(chip, self.up_sem, line.above).start()
+
+        @pl.when((chip >= line.place) & line.has_below)
+        def _():
+            self.copy(chip, self.down_sem, line.below).start()
+
+        self.copy(chip, self.side_sem, line.partner).start()
+
+    def take(self, chip):
+        self.wait_slot(chip * 2 + self.line.core)
+        self.send(chip)
+
+    def step(self, step):
+        line = self.line
+        chip = line.order(step)
+
+        @pl.when((step > 0) & jnp.logical_not(line.second_of_pair(step)))
+        def _():
+            self.take(chip)
+
+        @pl.when(line.paired(step))
+        def _():
+            self.take(line.order(step + 1))
+
+        self.wait_slot(chip * 2 + 1 - line.core)
+        return chip
+
+    def finish(self):
+        line = self.line
+
+        @pl.loop(0, line.chips)
+        def _(chip):
+            @pl.when((chip <= line.place) & line.has_above)
+            def _():
+                self.copy(chip, self.up_sem, line.above).wait_send()
+
+            @pl.when((chip >= line.place) & line.has_below)
+            def _():
+                self.copy(chip, self.down_sem, line.below).wait_send()
+
+            self.copy(chip, self.side_sem, line.partner).wait_send()
+
+
+class Scatter:
+    def __init__(self, line, fresh, terms, side_out, side_in, out, inward, side_send, side_recv, send_sem, recv_sem):
+        self.line, self.fresh, self.terms = line, fresh, terms
+        self.side_out, self.side_in = side_out, side_in
+        self.out, self.inward = out, inward
+        self.side_send, self.side_recv = side_send, side_recv
+        self.send_sem, self.recv_sem = send_sem, recv_sem
+        self.rows = terms.shape[1] // RS_PARTS
+
+    @staticmethod
+    def scratch(chips, rows, width):
+        return [
+            pltpu.VMEM((2, rows, width), jnp.float32),
+            pltpu.VMEM((chips, rows, width), jnp.float32),
+            pltpu.VMEM((chips, rows, width), jnp.bfloat16),
+            pltpu.VMEM((chips, rows, width), jnp.bfloat16),
+            pltpu.VMEM((chips, rows, width), jnp.bfloat16),
+            pltpu.VMEM((2, chips, rows, width), jnp.bfloat16),
+            pltpu.SemaphoreType.DMA((chips,)),
+            pltpu.SemaphoreType.DMA((chips,)),
+            pltpu.SemaphoreType.DMA((chips, RS_PARTS)),
+            pltpu.SemaphoreType.DMA((2, chips, RS_PARTS)),
+        ]
+
+    def side(self, chip):
+        return pltpu.make_async_remote_copy(
+            src_ref=self.side_out.at[chip],
+            dst_ref=self.side_in.at[chip],
+            send_sem=self.side_send.at[chip],
+            recv_sem=self.side_recv.at[chip],
+            device_id=self.line.partner,
+            device_id_type=MESH,
+        )
+
+    def part(self, chip, part, upward, target):
+        rows = pl.ds(part * self.rows, self.rows)
+        return pltpu.make_async_remote_copy(
+            src_ref=self.out.at[chip, rows],
+            dst_ref=self.inward.at[upward, chip, rows],
+            send_sem=self.send_sem.at[chip, part],
+            recv_sem=self.recv_sem.at[upward, chip, part],
+            device_id=target,
+            device_id_type=MESH,
+        )
+
+    def share(self, chip):
+        self.side_out[chip] = self.fresh[1 - self.line.core].astype(jnp.bfloat16)
+        self.side(chip).start()
+        self.terms[chip] = self.fresh[self.line.core]
+
+    def total(self, chip, part, ways):
+        rows = pl.ds(part * self.rows, self.rows)
+        total = self.terms[chip, rows] + self.side_in[chip, rows].astype(jnp.float32)
+        for way in ways:
+            total = total + self.inward[way, chip, rows].astype(jnp.float32)
+        return rows, total
+
+    def pass_on(self, chip, upward, first):
+        target = self.line.above if upward else self.line.below
+        self.side(chip).wait_recv()
+
+        @pl.loop(0, RS_PARTS)
+        def _(part):
+            if not first:
+                self.part(chip, part, upward, target).wait_recv()
+            rows, total = self.total(chip, part, () if first else (upward,))
+            self.out[chip, rows] = total.astype(jnp.bfloat16)
+            self.part(chip, part, upward, target).start()
+
+    def after_term(self, chip):
+        line = self.line
+        self.share(chip)
+
+        @pl.when((chip < line.place) & jnp.logical_not(line.has_above))
+        def _():
+            self.pass_on(chip, 0, True)
+
+        @pl.when((chip > line.place) & jnp.logical_not(line.has_below))
+        def _():
+            self.pass_on(chip, 1, True)
+
+    def finish(self, result):
+        line = self.line
+        lower = line.place * 2 < line.chips
+
+        @pl.loop(0, line.chips)
+        def _(step):
+            up_chip, down_chip = step, line.chips - 1 - step
+            go_up = (up_chip > line.place) & line.has_below
+            go_down = (down_chip < line.place) & line.has_above
+
+            @pl.when(go_up & lower)
+            def _():
+                self.pass_on(up_chip, 1, False)
+
+            @pl.when(go_down)
+            def _():
+                self.pass_on(down_chip, 0, False)
+
+            @pl.when(go_up & jnp.logical_not(lower))
+            def _():
+                self.pass_on(up_chip, 1, False)
+
+        place = line.place
+        self.side(place).wait_recv()
+
+        @pl.loop(0, RS_PARTS)
+        def _(part):
+            @pl.when(line.has_above)
+            def _():
+                self.part(place, part, 0, line.below).wait_recv()
+
+            @pl.when(line.has_below)
+            def _():
+                self.part(place, part, 1, line.above).wait_recv()
+
+            @pl.when(line.has_above & line.has_below)
+            def _():
+                rows, total = self.total(place, part, (0, 1))
+                result[rows] = total
+
+            @pl.when(line.has_above & jnp.logical_not(line.has_below))
+            def _():
+                rows, total = self.total(place, part, (0,))
+                result[rows] = total
+
+            @pl.when(line.has_below & jnp.logical_not(line.has_above))
+            def _():
+                rows, total = self.total(place, part, (1,))
+                result[rows] = total
+
+        @pl.loop(0, line.chips)
+        def _(chip):
+            self.side(chip).wait_send()
+
+            @pl.when(chip != place)
+            def _():
+                @pl.loop(0, RS_PARTS)
+                def _(part):
+                    self.part(chip, part, 0, line.below).wait_send()
+
+
+def tile_of(extent):
+    return min(256, extent)
+
+
+def dot_cols(left, right):
+    return lax.dot_general(
+        left, right, (((1,), (1,)), ((), ())), preferred_element_type=jnp.float32
+    )
+
+
+def load(pairs):
+    copies = [pltpu.make_async_copy(src, dst, sem) for src, dst, sem in pairs]
+    for copy in copies:
+        copy.start()
+    return copies
+
+
+def feed_forward_kernel(
+    chips,
+    hidden_ref,
+    gate_hbm,
+    up_hbm,
+    down_hbm,
+    mixed_ref,
+    gate_out,
+    up_out,
+    act_out,
+    all_out,
+    gate_w,
+    up_w,
+    down_w,
+    gate_keep,
+    up_keep,
+    act_keep,
+    load_sem,
+    store_sem,
+    *comm,
+):
+    line = Line(chips)
+    gather = Gather(line, *comm[:5])
+    scatter = Scatter(line, *comm[5:])
+    blocks, fresh = gather.blocks, scatter.fresh
+    _, rows, width = blocks.shape
+    units = gate_w.shape[1]
+    copies = load(
+        [
+            (gate_hbm, gate_w, load_sem.at[0]),
+            (up_hbm, up_w, load_sem.at[1]),
+            (down_hbm, down_w, load_sem.at[2]),
+        ]
+    )
+    line.greet()
+    blocks[line.place * 2 + line.core] = hidden_ref[...]
+    gather.send(line.place)
+
+    def stores(chip):
+        pair = pl.ds(chip * 2, 2)
+        return [
+            pltpu.make_async_copy(gate_keep.at[pair], gate_out.at[pair], store_sem.at[0, chip]),
+            pltpu.make_async_copy(up_keep.at[pair], up_out.at[pair], store_sem.at[1, chip]),
+            pltpu.make_async_copy(act_keep.at[pair], act_out.at[pair], store_sem.at[2, chip]),
+            pltpu.make_async_copy(blocks.at[pair], all_out.at[pair], store_sem.at[3, chip]),
+        ]
+
+    for copy in copies:
+        copy.wait()
+
+    @pl.loop(0, chips)
+    def _(step):
+        chip = gather.step(step)
+        pair = pl.ds(chip * 2, 2)
+
+        @pl.loop(0, units // tile_of(units))
+        def _(tile):
+            columns = pl.ds(pl.multiple_of(tile * tile_of(units), 128), tile_of(units))
+            tokens = blocks[pair].reshape(2 * rows, width)
+            gate = jnp.dot(tokens, gate_w[:, columns], preferred_element_type=jnp.float32)
+            up = jnp.dot(tokens, up_w[:, columns], preferred_element_type=jnp.float32)
+            gate_keep[pair, :, columns] = gate.reshape(2, rows, -1)
+            up_keep[pair, :, columns] = up.reshape(2, rows, -1)
+            act_keep[pair, :, columns] = (
+                (gate / (1.0 + jnp.exp(-gate)) * up).astype(jnp.bfloat16).reshape(2, rows, -1)
+            )
+
+        @pl.loop(0, width // tile_of(width))
+        def _(tile):
+            columns = pl.ds(pl.multiple_of(tile * tile_of(width), 128), tile_of(width))
+            act = act_keep[pair].reshape(2 * rows, units)
+            fresh[:, :, columns] = dot_cols(act, down_w[columns, :]).reshape(2, rows, -1)
+
+        for copy in stores(chip):
+            copy.start()
+        scatter.after_term(chip)
+
+    scatter.finish(mixed_ref)
+    gather.finish()
+
+    @pl.loop(0, chips)
+    def _(chip):
+        for copy in stores(chip):
+            copy.wait()
+
+
+def feed_forward_back_kernel(
+    chips,
+    grad_ref,
+    gate_hbm,
+    up_hbm,
+    down_hbm,
+    gate_lin_hbm,
+    up_lin_hbm,
+    hidden_grad_ref,
+    gate_out,
+    up_out,
+    all_out,
+    gate_w,
+    up_w,
+    down_w,
+    gate_lin,
+    up_lin,
+    gate_keep,
+    up_keep,
+    load_sem,
+    store_sem,
+    *comm,
+):
+    line = Line(chips)
+    gather = Gather(line, *comm[:5])
+    scatter = Scatter(line, *comm[5:])
+    blocks, fresh = gather.blocks, scatter.fresh
+    _, rows, width = blocks.shape
+    units = gate_w.shape[1]
+    copies = load(
+        [
+            (down_hbm, down_w, load_sem.at[0]),
+            (gate_lin_hbm, gate_lin, load_sem.at[1]),
+            (up_lin_hbm, up_lin, load_sem.at[2]),
+            (gate_hbm, gate_w, load_sem.at[3]),
+            (up_hbm, up_w, load_sem.at[4]),
+        ]
+    )
+    line.greet()
+    blocks[line.place * 2 + line.core] = grad_ref[...]
+    gather.send(line.place)
+
+    def stores(chip):
+        pair = pl.ds(chip * 2, 2)
+        return [
+            pltpu.make_async_copy(gate_keep.at[pair], gate_out.at[pair], store_sem.at[0, chip]),
+            pltpu.make_async_copy(up_keep.at[pair], up_out.at[pair], store_sem.at[1, chip]),
+            pltpu.make_async_copy(blocks.at[pair], all_out.at[pair], store_sem.at[2, chip]),
+        ]
+
+    for copy in copies:
+        copy.wait()
+
+    @pl.loop(0, chips)
+    def _(step):
+        chip = gather.step(step)
+        pair = pl.ds(chip * 2, 2)
+
+        @pl.loop(0, units // tile_of(units))
+        def _(tile):
+            columns = pl.ds(pl.multiple_of(tile * tile_of(units), 128), tile_of(units))
+            tokens = blocks[pair].reshape(2 * rows, width)
+            grad = jnp.dot(tokens, down_w[:, columns], preferred_element_type=jnp.float32)
+            gate = gate_lin[pair, :, columns].reshape(2 * rows, -1)
+            up = up_lin[pair, :, columns].reshape(2 * rows, -1)
+            sig = 1.0 / (1.0 + jnp.exp(-gate))
+            gate_keep[pair, :, columns] = (
+                (grad * up * sig * (1.0 + gate * (1.0 - sig)))
+                .astype(jnp.bfloat16)
+                .reshape(2, rows, -1)
+            )
+            up_keep[pair, :, columns] = (
+                (grad * (gate * sig)).astype(jnp.bfloat16).reshape(2, rows, -1)
+            )
+
+        @pl.loop(0, width // tile_of(width))
+        def _(tile):
+            columns = pl.ds(pl.multiple_of(tile * tile_of(width), 128), tile_of(width))
+            gate = gate_keep[pair].reshape(2 * rows, units)
+            up = up_keep[pair].reshape(2 * rows, units)
+            fresh[:, :, columns] = (
+                dot_cols(gate, gate_w[columns, :]) + dot_cols(up, up_w[columns, :])
+            ).reshape(2, rows, -1)
+
+        for copy in stores(chip):
+            copy.start()
+        scatter.after_term(chip)
+
+    scatter.finish(hidden_grad_ref)
+    gather.finish()
+
+    @pl.loop(0, chips)
+    def _(chip):
+        for copy in stores(chip):
+            copy.wait()
+
+
+def whole_spec():
+    return pl.BlockSpec(memory_space=pltpu.VMEM)
+
+
+def far_spec():
+    return pl.BlockSpec(memory_space=pl.ANY)
+
+
+def line_params(collective_id):
+    return pltpu.CompilerParams(
+        collective_id=collective_id, has_side_effects=True, vmem_limit_bytes=60 * 2**20
+    )
+
+
+def feed_forward(hidden_low, gate_cols, up_cols, down_cols):
+    rows, width = hidden_low.shape
+    units = gate_cols.shape[1]
+    slots = lax.axis_size("seq")
+    chips = slots // 2
+    weights = [pltpu.VMEM((width, units), jnp.bfloat16)] * 3
+    mixed, gate, up, act, every = pl.pallas_call(
+        functools.partial(feed_forward_kernel, chips),
+        out_shape=(
+            jax.ShapeDtypeStruct((rows, width), jnp.float32),
+            jax.ShapeDtypeStruct((slots, rows, units), jnp.float32),
+            jax.ShapeDtypeStruct((slots, rows, units), jnp.float32),
+            jax.ShapeDtypeStruct((slots, rows, units), jnp.bfloat16),
+            jax.ShapeDtypeStruct((slots, rows, width), jnp.bfloat16),
+        ),
+        in_specs=[whole_spec()] + [far_spec()] * 3,
+        out_specs=(whole_spec(),) + (far_spec(),) * 4,
+        scratch_shapes=weights
+        + [
+            pltpu.VMEM((slots, rows, units), jnp.float32),
+            pltpu.VMEM((slots, rows, units), jnp.float32),
+            pltpu.VMEM((slots, rows, units), jnp.bfloat16),
+            pltpu.SemaphoreType.DMA((3,)),
+            pltpu.SemaphoreType.DMA((4, chips)),
+        ]
+        + Gather.scratch(chips, rows, width)
+        + Scatter.scratch(chips, rows, width),
+        compiler_params=line_params(1),
+        name="feed_forward",
+    )(hidden_low, gate_cols, up_cols, down_cols)
+    return mixed, gate, up, act.reshape(-1, units), every.reshape(-1, width)
+
+
+def feed_forward_back(grad_low, gate_cols, up_cols, down_cols, gate, up):
+    rows, width = grad_low.shape
+    units = gate_cols.shape[1]
+    slots = lax.axis_size("seq")
+    chips = slots // 2
+    weights = [pltpu.VMEM((width, units), jnp.bfloat16)] * 3
+    hidden_grad, gate_grad, up_grad, every = pl.pallas_call(
+        functools.partial(feed_forward_back_kernel, chips),
+        out_shape=(
+            jax.ShapeDtypeStruct((rows, width), jnp.float32),
+            jax.ShapeDtypeStruct((slots, rows, units), jnp.bfloat16),
+            jax.ShapeDtypeStruct((slots, rows, units), jnp.bfloat16),
+            jax.ShapeDtypeStruct((slots, rows, width), jnp.bfloat16),
+        ),
+        in_specs=[whole_spec()] + [far_spec()] * 5,
+        out_specs=(whole_spec(),) + (far_spec(),) * 3,
+        scratch_shapes=weights
+        + [
+            pltpu.VMEM((slots, rows, units), jnp.float32),
+            pltpu.VMEM((slots, rows, units), jnp.float32),
+            pltpu.VMEM((slots, rows, units), jnp.bfloat16),
+            pltpu.VMEM((slots, rows, units), jnp.bfloat16),
+            pltpu.SemaphoreType.DMA((5,)),
+            pltpu.SemaphoreType.DMA((3, chips)),
+        ]
+        + Gather.scratch(chips, rows, width)
+        + Scatter.scratch(chips, rows, width),
+        compiler_params=line_params(2),
+        name="feed_forward_back",
+    )(grad_low, gate_cols, up_cols, down_cols, gate, up)
+    return (
+        hidden_grad,
+        gate_grad.reshape(-1, units),
+        up_grad.reshape(-1, units),
+        every.reshape(-1, width),
+    )
 
 
 def gather_seq(tensor):
@@ -220,12 +802,8 @@
     gate_cols = columns_in(gate_weight)
     up_cols = columns_in(up_weight)
     down_cols = columns_in(down_weight)
-    hidden_all = gather_seq(hidden_low)
-    gate_linear = jnp.dot(hidden_all, gate_cols, preferred_element_type=jnp.float32)
-    up_linear = jnp.dot(hidden_all, up_cols, preferred_element_type=jnp.float32)
-    activated = swiglu_act(gate_linear, up_linear).astype(jnp.bfloat16)
-    mixed_pre = scatter_seq(contract_cols(activated, down_cols).astype(jnp.bfloat16)).astype(
-        jnp.float32
+    mixed_pre, gate_linear, up_linear, activated, hidden_all = feed_forward(
+        hidden_low, gate_cols, up_cols, down_cols
     )
     result = (
         (hidden + rms_scale(mixed_pre, feedforward_scale))
@@ -236,17 +814,10 @@
     _, mixed_pull = jax.vjp(rms_scale, mixed_pre, feedforward_scale)
     grad_mixed, grad_feedforward_gain = mixed_pull(grad_result)
     grad_mixed_low = grad_mixed.astype(jnp.bfloat16)
-    grad_all = gather_seq(grad_mixed_low)
-    grad_activated = jnp.dot(grad_all, down_cols, preferred_element_type=jnp.float32)
-    _, swiglu_pull = jax.vjp(swiglu_act, gate_linear, up_linear)
-    grad_gate, grad_upward = swiglu_pull(grad_activated)
-    grad_gate_low = grad_gate.astype(jnp.bfloat16)
-    grad_upward_low = grad_upward.astype(jnp.bfloat16)
-    grad_hidden = grad_result + scatter_seq(
-        (contract_cols(grad_gate_low, gate_cols) + contract_cols(grad_upward_low, up_cols)).astype(
-            jnp.bfloat16
-        )
-    ).astype(jnp.float32)
+    hidden_term, grad_gate_low, grad_upward_low, grad_all = feed_forward_back(
+        grad_mixed_low, gate_cols, up_cols, down_cols, gate_linear, up_linear
+    )
+    grad_hidden = grad_result + hidden_term
     gate_weight_grad = columns_out(contract_rows(hidden_all, grad_gate_low))
     up_weight_grad = columns_out(contract_rows(hidden_all, grad_upward_low))
     down_weight_grad = columns_out(contract_rows(grad_all, activated))

time: 1280 us -> 1230 us (0.961)
  Pallas kernels: 0 us -> 157 us
  waiting for transfers between devices: 703 us -> 585 us
  blocking collectives: 254 us -> 198 us
  matrix products: 143 us -> 94.9 us
  local copies, waits for them, and re-layouts: 76.1 us -> 92.8 us
    pallas_call x0 -> x2, Pallas kernels: none -> 157 us  [the longest x1 78.3 us: feed_forward(): pl.pallas_call(functools.partial(feed_forward_kernel, chips), out_shape=(...]
    all_to_all x6 -> x4, blocking collectives: 157 us -> 71.5 us  [columns_in(): lax.all_to_all(weight, 'seq', split_axis=1, concat_axis=0, tiled=True)]
    all_gather x4 -> x2, waiting for transfers between devices: 128 us -> 45.1 us  [gather_seq(): return lax.all_gather(tensor, 'seq', axis=0, tiled=True)]
    reduce_scatter x6, waiting for transfers between devices: 93.7 us -> 149 us  [columns_out(): summed = lax.psum_scatter(swapped, 'fsdp', scatter_dimension=0, tiled=True)]
    all_gather x6, waiting for transfers between devices: 124 us -> 74.5 us  [columns_in(): whole = lax.all_gather(part, 'fsdp', axis=0, tiled=True)]
    reduce_scatter x4 -> x2, waiting for transfers between devices: 135 us -> 88.8 us  [scatter_seq(): return lax.psum_scatter(tensor, 'seq', scatter_dimension=0, tiled=True)]
    all_gather x1, blocking collectives: 66.3 us -> 97.2 us  [per_device(): lax.all_gather(jnp.stack([query_gain, key_gain, attention_gain, feedforwa...]
    all_to_all x6, waiting for transfers between devices: 46.1 us -> 16.5 us  [columns_out(): lax.all_to_all(summed, 'seq', split_axis=0, concat_axis=1, tiled=True)]
  transfers between devices with their start and end apart: 30 -> 28, of which waited for: 20 -> 15; matrix products, arithmetic and copies ran while one was open for 16% -> 12% of each run, Pallas kernels for 0% -> 0%
where the time goes in v2:
time: 1230 us
  waiting for transfers between devices  585 us (48%)
  blocking collectives  198 us (16%)
  Pallas kernels  157 us (13%)
  matrix products  94.9 us (8%)
  local copies, waits for them, and re-layouts  92.8 us (8%)
  other arithmetic  44.1 us (4%)
  starting transfers between devices  32.6 us (3%)
  between operations  15.5 us (1%)
    unnamed x22, waiting for transfers between devices  157 us
    reduce_scatter x6, waiting for transfers between devices, columns_out(): summed = lax.psum_scatter(swapped, 'fsdp', scatter_dimension=0, tiled=True)  149 us
    all_gather x1, blocking collectives, per_device(): lax.all_gather(jnp.stack([query_gain, key_gain, attention_gain, feedforwa...  97.2 us
    reduce_scatter x2, waiting for transfers between devices, scatter_seq(): return lax.psum_scatter(tensor, 'seq', scatter_dimension=0, tiled=True)  88.8 us
    pallas_call x1, Pallas kernels, feed_forward(): pl.pallas_call(functools.partial(feed_forward_kernel, chips), out_shape=(...  78.3 us
    pallas_call x1, Pallas kernels, feed_forward_back(): pl.pallas_call(functools.partial(feed_forward_back_kernel, chips), out_sh...  78.3 us
    all_gather x6, waiting for transfers between devices, columns_in(): whole = lax.all_gather(part, 'fsdp', axis=0, tiled=True)  74.5 us
    all_to_all x4, blocking collectives, columns_in(): lax.all_to_all(weight, 'seq', split_axis=1, concat_axis=0, tiled=True)  71.5 us
  transfers between devices with their start and end apart: 28, of which 15 were waited for; matrix products, arithmetic and copies ran while one was open for 12% of the time, Pallas kernels for 0%

profile of v2, /device:TPU:0, one launch (start us, length us, event | category | flops | bytes accessed | tf_op | source)
XLA Modules:
  0.0 1226.2 jit_solution(18423049894402340208)
XLA Ops:
  8.3 16.0 %all_to_all.192 = bf16[64,8,256]{2,0,1:T(8,128)(2,1)} all-to-all(bf16[64,8,256]{2,0,1:T(8,128)(2,1)S(1)} %bitcast.415), channel_id=1, replica_groups=mesh['seq'=8,'fsdp'=4] {'seq'}, dimensions={1} | all-to-all | bytes 524288 | tf_op jit(solution)/shard_map/all_to_all | solution.py:677
  25.3 12.9 %all_to_all.193 = bf16[64,8,256]{2,0,1:T(8,128)(2,1)} all-to-all(bf16[64,8,256]{2,0,1:T(8,128)(2,1)S(1)} %bitcast.416), channel_id=1, replica_groups=mesh['seq'=8,'fsdp'=4] {'seq'}, dimensions={1} | all-to-all | bytes 524288 | tf_op jit(solution)/shard_map/all_to_all | solution.py:677
  39.3 12.8 %all_to_all.194 = bf16[64,8,256]{2,0,1:T(8,128)(2,1)} all-to-all(bf16[64,8,256]{2,0,1:T(8,128)(2,1)S(1)} %bitcast.417), channel_id=1, replica_groups=mesh['seq'=8,'fsdp'=4] {'seq'}, dimensions={1} | all-to-all | bytes 524288 | tf_op jit(solution)/shard_map/all_to_all | solution.py:677
  53.7 3.7 all-to-all-start.3
  58.1 25.9 %all-to-all-done.3 = bf16[64,8,1024]{2,0,1:T(8,128)(2,1)S(1)} async-done(((bf16[64,8,1024]{2,0,1:T(8,128)(2,1)}), bf16[64,8,1024]{2,0,1:T(8,128)(2,1)S(1)}, u32[]{:S(2)}, u32[]{:S(2)}) %all-to-all-start.3) | async-done | bytes 1048608 | tf_op jit(solution)/shard_map/all_to_all | solution.py:677
  85.2 29.8 %all_to_all.195 = bf16[64,8,1024]{2,0,1:T(8,128)(2,1)} all-to-all(bf16[64,8,1024]{2,0,1:T(8,128)(2,1)S(1)} %bitcast.392), channel_id=1, replica_groups=mesh['seq'=8,'fsdp'=4] {'seq'}, dimensions={1} | all-to-all | bytes 2097152 | tf_op jit(solution)/shard_map/all_to_all | solution.py:677
  116.1 3.6 all-to-all-start.5
  119.8 97.2 %all-gather.1 = bf16[32,64,4]{1,2,0:T(4,128)(2,1)S(1)} all-gather(bf16[1,64,4]{1,2,0:T(4,128)(2,1)S(1)} %maximum_bitcast_fusion), channel_id=1, replica_groups=mesh['seq'=8,'fsdp'=4] {'seq','fsdp'}, dimensions={0}, use_global_device_ids=true | all-gather | bytes 16896 | tf_op jit(solution)/shard_map/all_gather | solution.py:747
  217.1 3.0 fusion.95
  222.5 2.7 copy.163
  227.5 3.6 multiply_reduce_fusion.5
  232.6 14.0 %psum.14 = f32[2,1024]{1,0:T(2,128)S(1)} all-reduce(f32[2,1024]{1,0:T(2,128)S(1)} %pad_maximum_fusion.5), channel_id=1, replica_groups=mesh['seq'=8,'fsdp'=4] {'seq'}, use_global_device_ids=true, to_apply=%region_2.0 | all-reduce | flops 2048 | bytes 16384 | tf_op jit(solution)/shard_map/psum | solution.py:762
  257.7 3.5 fusion.72
  261.5 2.7 subtract_convert_fusion
  264.8 13.8 %while.27 = (s32[]{:T(128)}, bf16[2,512,2,128]{3,2,1,0:T(2,128)(2,1)}, f32[2,2,512]{2,1,0:T(2,128)S(1)}, s32[2]{0:T(128)S(1)}, s32[1,1024]{1,0:T(1,128)S(1)}, /*...) while((s32[]{:T(128)}, ...), condition=%wide.region_6.7_spmd, body=%wide.region_3.6_spmd.sunk | while | flops 551157248 | bytes 21018884 | solution.py:793
  278.6 4.7 convolution_convert_fusion
  283.4 4.9 copy.174
  288.3 24.9 %all-gather.22.cloned.1.call-done = bf16[2048,1024]{1,0:T(8,128)(2,1)} async-done(((bf16[512,1024]{1,0:T(8,128)(2,1)}), bf16[2048,1024]{1,0:T(8,128)(2,1)}) %all-gather.22.cloned.1.call-update) | async-done | bytes 4194320 | tf_op jit(solution)/shard_map/all_gather | solution.py:678
  313.2 4.9 copy.176
  318.1 49.5 %all-gather.24.cloned.1.call-done = bf16[2048,1024]{1,0:T(8,128)(2,1)} async-done(((bf16[512,1024]{1,0:T(8,128)(2,1)}), bf16[2048,1024]{1,0:T(8,128)(2,1)}) %all-gather.24.cloned.1.call-update) | async-done | bytes 4194320 | tf_op jit(solution)/shard_map/all_gather | solution.py:678
  367.7 5.0 copy.178
  372.6 47.3 %reduce-scatter.16.cloned.1.call-done = bf16[128,2048]{1,0:T(8,128)(2,1)} async-done(((bf16[1024,2048]{1,0:T(8,128)(2,1)}), bf16[128,2048]{1,0:T(8,128)(2,1)}) %reduce-scatter.16.cloned.1.call-update) | async-done | bytes 524304 | tf_op jit(solution)/shard_map/reduce_scatter | solution.py:671
  423.3 78.3 %feed_forward.1 = (f32[128,2048]{1,0:T(8,128)}, f32[8,128,1024]{2,1,0:T(8,128)}, f32[8,128,1024]{2,1,0:T(8,128)}, bf16[8,128,1024]{2,1,0:T(8,128)(2,1)}, bf16[8,128,2048]{2,1,0:T(8,128)(2,1)}) custom-call(bf16[128,2048]{1,0:T(8,128)(2,1)} %fusion.89.hidden_ref, bf16[2048,1024]{1,0:T(8,128)(2,1)} %bitcast.359, bf16[2048,1024]{1,0:T(8,128)(2,1)} %bitcast.361, ...), custom_call_target="tpu_custom_call" | custom-call | tf_op jit(solution)/shard_map/feed_forward/pallas_call | solution.py:601
  504.6 2.9 fusion.82
  507.5 78.3 %feed_forward_back.1 = (f32[128,2048]{1,0:T(8,128)}, bf16[8,128,1024]{2,1,0:T(8,128)(2,1)}, bf16[8,128,1024]{2,1,0:T(8,128)(2,1)}, bf16[8,128,2048]{2,1,0:T(8,128)(2,1)}) custom-call(bf16[128,2048]{1,0:T(8,128)(2,1)} %get-tuple-element.354.grad_ref, bf16[2048,1024]{1,0:T(8,128)(2,1)} %bitcast.360, bf16[2048,1024]{1,0:T(8,128)(2,1)} %bitcast.362, ...), custom_call_target="tpu_custom_call" | custom-call | tf_op jit(solution)/shard_map/feed_forward_back/pallas_call | solution.py:634
  590.0 45.1 %all-gather.26.cloned.1.call-done = bf16[1024,2048]{1,0:T(8,128)(2,1)} async-done(((bf16[128,2048]{1,0:T(8,128)(2,1)}), bf16[1024,2048]{1,0:T(8,128)(2,1)}) %all-gather.26.cloned.1.call-update) | async-done | bytes 4194320 | tf_op jit(solution)/shard_map/all_gather | solution.py:667
  635.0 3.8 convolution_convert_fusion.2
  638.8 40.4 %while.28 = (s32[]{:T(128)}, f32[1024,2,128]{0,2,1:T(8,128)}, f32[1024,2,128]{0,2,1:T(8,128)}, bf16[2,512,2,128]{3,1,0,2:T(8,128)(2,1)}, s32[2]{0:T(128)S(1)}, /...) while((s32[]{:T(128)}, f32[1024,2,128]{0,2,1:T(8,128)}, ...), condition=%wide.region_14.15_spmd.clone, body=%wide.region_12.14_spmd.clone.sunk | while | flops 1361051136 | bytes 86813704 | solution.py:867
  640.8 2.7 fusion.171
  645.5 4.2 multiply_reduce_fusion.7
  651.1 2.6 fusion.173
  655.2 3.5 fusion.174
  660.7 2.7 fusion.171
  665.4 4.2 multiply_reduce_fusion.7
  671.0 3.0 fusion.173
  675.4 3.9 fusion.174
  685.5 2.9 pad_maximum_fusion.1
  692.5 15.1 %psum.15 = f32[2,1024]{1,0:T(2,128)S(1)} all-reduce(f32[2,1024]{1,0:T(2,128)S(1)} %pad_maximum_fusion.6), channel_id=1, replica_groups=mesh['seq'=8,'fsdp'=4] {'seq'}, use_global_device_ids=true, to_apply=%region_17.18 | all-reduce | flops 2048 | bytes 16384 | tf_op jit(solution)/shard_map/psum | solution.py:882
  709.8 4.4 fusion.66
  717.3 3.6 fusion.69
  724.6 3.6 fusion.63
  729.9 6.6 copy.194
  736.5 6.9 convert_bitcast_fusion.1
  745.9 6.6 copy.199
  752.5 6.9 convert_bitcast_fusion
  763.6 6.9 convert_bitcast_fusion.2
  775.6 4.5 convolution_convert_fusion.1
  782.9 3.4 add_convert_fusion
  786.3 3.4 all-to-all-start.7
  789.8 9.6 all-to-all-done.7
  799.4 3.4 all-to-all-start.6
  802.8 2.7 reduce-scatter.24.cloned.1.call-done
  805.5 6.9 all-to-all-done.6
  812.5 3.4 all-to-all-start.8
  815.9 45.1 %reduce-scatter.30.cloned.1.call-done = bf16[512,1024]{1,0:T(8,128)(2,1)} async-done(((bf16[2048,1024]{1,0:T(8,128)(2,1)}), bf16[512,1024]{1,0:T(8,128)(2,1)}) %reduce-scatter.30.cloned.1.call-update) | async-done | bytes 1048592 | tf_op jit(solution)/shard_map/reduce_scatter | solution.py:686
  861.7 4.6 all-to-all-start.10
  866.3 50.1 %reduce-scatter.32.cloned.1.call-done = bf16[512,1024]{1,0:T(8,128)(2,1)} async-done(((bf16[2048,1024]{1,0:T(8,128)(2,1)}), bf16[512,1024]{1,0:T(8,128)(2,1)}) %reduce-scatter.32.cloned.1.call-update) | async-done | bytes 1048592 | tf_op jit(solution)/shard_map/reduce_scatter | solution.py:686
  916.4 4.6 all-to-all-start.11
  921.1 50.8 %reduce-scatter.28.cloned.1.call-done = bf16[512,1024]{1,0:T(8,128)(2,1)} async-done(((bf16[2048,1024]{1,0:T(8,128)(2,1)}), bf16[512,1024]{1,0:T(8,128)(2,1)}) %reduce-scatter.28.cloned.1.call-update) | async-done | bytes 1048592 | tf_op jit(solution)/shard_map/reduce_scatter | solution.py:686
  971.9 4.6 all-to-all-start.9
  976.5 134.6 %reduce-scatter.36.cloned.1.call-done = f32[64,2]{1,0:T(8,128)} async-done(((f32[2048,2]{1,0:T(8,128)}), f32[64,2]{1,0:T(8,128)}) %reduce-scatter.36.cloned.1.call-update) | async-done | bytes 528
  1113.2 20.8 %reduce-scatter.34.cloned.1.call-done = f32[64,2]{1,0:T(8,128)} async-done(((f32[256,2]{1,0:T(8,128)}), f32[64,2]{1,0:T(8,128)}) %reduce-scatter.34.cloned.1.call-update) | async-done | bytes 528
  1136.1 28.8 %reduce-scatter.26.cloned.1.call-done = bf16[64,2048]{1,0:T(8,128)(2,1)} async-done(((bf16[256,2048]{1,0:T(8,128)(2,1)}), bf16[64,2048]{1,0:T(8,128)(2,1)}) %reduce-scatter.26.cloned.1.call-update) | async-done | bytes 262160 | tf_op jit(solution)/shard_map/reduce_scatter | solution.py:827
  1175.4 41.6 %reduce-scatter.18.cloned.1.call-done = bf16[128,2048]{1,0:T(8,128)(2,1)} async-done(((bf16[1024,2048]{1,0:T(8,128)(2,1)}), bf16[128,2048]{1,0:T(8,128)(2,1)}) %reduce-scatter.18.cloned.1.call-update) | async-done | bytes 524304 | tf_op jit(solution)/shard_map/reduce_scatter | solution.py:671
  (308 shorter events, 109.6 us)
Async XLA Ops:
  7.2 45.5 %copy-start.41 = (bf16[64,8192]{1,0:T(8,128)(2,1)S(1)}, bf16[64,8192]{1,0:T(8,128)(2,1)}, u32[]{:S(2)}) copy-start(bf16[64,8192]{1,0:T(8,128)(2,1)} %param.26) | copy-start | bytes 3145732
  7.2 214.0 %all-gather.12.cloned.1.call-start = ((), (), s32[]{:S(2)}) async-start(), calls=%async_computation.23 | async-start | bytes 1310720 | tf_op jit(solution)/shard_map/all_gather | solution.py:678
  24.3 198.2 %all-gather.14.cloned.1.call-start = ((), (), s32[]{:S(2)}) async-start(), calls=%async_computation.24 | async-start | bytes 1310720 | tf_op jit(solution)/shard_map/all_gather | solution.py:678
  25.3 59.7 %copy-start.42 = (bf16[64,8192]{1,0:T(8,128)(2,1)S(1)}, bf16[64,8192]{1,0:T(8,128)(2,1)}, u32[]{:S(2)}) copy-start(bf16[64,8192]{1,0:T(8,128)(2,1)} %param.27) | copy-start | bytes 3145732
  38.2 186.9 %all-gather.16.cloned.1.call-start = ((), (), s32[]{:S(2)}) async-start(), calls=%async_computation.25 | async-start | bytes 1310720 | tf_op jit(solution)/shard_map/all_gather | solution.py:678
  52.1 175.4 %all-gather.28.cloned.1.call-start = ((), (), s32[]{:S(2)}) async-start(), calls=%async_computation.40 | async-start | bytes 4718592 | tf_op jit(solution)/shard_map/all_gather | solution.py:667
  53.7 61.3 %copy-start.43 = (bf16[64,8192]{1,0:T(8,128)(2,1)S(1)}, bf16[64,8192]{1,0:T(8,128)(2,1)}, u32[]{:S(2)}) copy-start(bf16[64,8192]{1,0:T(8,128)(2,1)} %param.28) | copy-start | bytes 3145732
  53.7 30.2 %all-to-all-start.3 = ((bf16[64,8,1024]{2,0,1:T(8,128)(2,1)}), bf16[64,8,1024]{2,0,1:T(8,128)(2,1)S(1)}, u32[]{:S(2)}, u32[]{:S(2)}) async-start(bf16[64,8,1024]{2,0,1:T(8,128)(2,1)} %bitcast.321), calls=%async_computation.4 | async-start | bytes 2097152 | tf_op jit(solution)/shard_map/all_to_all | solution.py:677
  57.4 221.2 %all-gather.18.cloned.1.call-start = ((), (), s32[]{:S(2)}) async-start(), calls=%async_computation.26 | async-start | bytes 1310720 | tf_op jit(solution)/shard_map/all_gather | solution.py:746
  58.0 225.4 %all-gather.20.cloned.1.call-start = ((), (), s32[]{:S(2)}) async-start(), calls=%async_computation.28 | async-start | bytes 5242880 | tf_op jit(solution)/shard_map/all_gather | solution.py:678
  85.0 228.3 %all-gather.22.cloned.1.call-start = ((), (), s32[]{:S(2)}) async-start(), calls=%async_computation.29 | async-start | bytes 5242880 | tf_op jit(solution)/shard_map/all_gather | solution.py:678
  85.1 34.6 %copy-start.45 = (bf16[64]{0:T(256)(128)(2,1)S(1)}, bf16[64]{0:T(256)(128)(2,1)}, u32[]{:S(2)}) copy-start(bf16[64]{0:T(256)(128)(2,1)} %param.29) | copy-start | bytes 388
  85.1 34.6 %copy-start.46 = (bf16[64]{0:T(256)(128)(2,1)S(1)}, bf16[64]{0:T(256)(128)(2,1)}, u32[]{:S(2)}) copy-start(bf16[64]{0:T(256)(128)(2,1)} %param.25) | copy-start | bytes 388
  85.1 34.6 %copy-start.47 = (bf16[64]{0:T(256)(128)(2,1)S(1)}, bf16[64]{0:T(256)(128)(2,1)}, u32[]{:S(2)}) copy-start(bf16[64]{0:T(256)(128)(2,1)} %param.24) | copy-start | bytes 388
  85.1 34.6 %copy-start.48 = (bf16[64]{0:T(256)(128)(2,1)S(1)}, bf16[64]{0:T(256)(128)(2,1)}, u32[]{:S(2)}) copy-start(bf16[64]{0:T(256)(128)(2,1)} %param.23) | copy-start | bytes 388
  116.1 104.0 %all-to-all-start.5 = ((bf16[64,8,1024]{2,0,1:T(8,128)(2,1)}), bf16[64,8,1024]{2,0,1:T(8,128)(2,1)S(1)}, u32[]{:S(2)}, u32[]{:S(2)}) async-start(bf16[64,8,1024]{2,0,1:T(8,128)(2,1)} %bitcast.319), calls=%async_computation.6 | async-start | bytes 2097152 | tf_op jit(solution)/shard_map/all_to_all | solution.py:677
  119.6 248.1 %all-gather.24.cloned.1.call-start = ((), (), s32[]{:S(2)}) async-start(), calls=%async_computation.30 | async-start | bytes 5242880 | tf_op jit(solution)/shard_map/all_gather | solution.py:678
  220.1 41.4 %copy-start.14 = (f32[1024,64]{1,0:T(8,128)}, f32[1024,64]{1,0:T(8,128)S(1)}, u32[]{:S(2)}) copy-start(f32[1024,64]{1,0:T(8,128)S(1)} %get-tuple-element.378) | copy-start | bytes 786436
  221.1 198.8 %reduce-scatter.16.cloned.1.call-start = ((), (), s32[]{:S(2)}) async-start(), calls=%async_computation.27 | async-start | bytes 4718592 | tf_op jit(solution)/shard_map/reduce_scatter | solution.py:671
  222.5 8.7 copy-start.17
  231.1 15.5 %copy-start.10 = (f32[1024,256]{0,1:T(8,128)}, f32[1024,256]{0,1:T(8,128)S(1)}, u32[]{:S(2)}) copy-start(f32[1024,256]{0,1:T(8,128)S(1)} %get-tuple-element.382) | copy-start | bytes 3145732
  232.6 16.7 %copy-start.12 = (f32[1024,256]{0,1:T(8,128)}, f32[1024,256]{0,1:T(8,128)S(1)}, u32[]{:S(2)}) copy-start(f32[1024,256]{0,1:T(8,128)S(1)} %get-tuple-element.380) | copy-start | bytes 3145732
  248.1 9.6 copy-start.21
  249.2 7.1 copy-start.34
  283.3 351.7 %all-gather.26.cloned.1.call-start = ((), (), s32[]{:S(2)}) async-start(), calls=%async_computation.31 | async-start | bytes 4718592 | tf_op jit(solution)/shard_map/all_gather | solution.py:667
  367.7 53.5 %copy-start.16 = (bf16[1,128,2048]{2,1,0:T(8,128)(2,1)S(1)}, bf16[1,128,2048]{2,1,0:T(8,128)(2,1)}, u32[]{:S(2)}) copy-start(bf16[1,128,2048]{2,1,0:T(8,128)(2,1)} %param.18) | copy-start | bytes 1572868
  423.3 79.7 %copy-start.7 = (bf16[1,128,2048]{2,1,0:T(8,128)(2,1)S(1)}, bf16[1,128,2048]{2,1,0:T(8,128)(2,1)}, u32[]{:S(2)}) copy-start(bf16[1,128,2048]{2,1,0:T(8,128)(2,1)} %param.31) | copy-start | bytes 1572868
  423.3 81.3 %copy-start.6 = (bf16[128,2048]{1,0:T(8,128)(2,1)S(1)}, bf16[128,2048]{1,0:T(8,128)(2,1)}, u32[]{:S(2)}) copy-start(bf16[128,2048]{1,0:T(8,128)(2,1)} %reduce-scatter.16.cloned.1.call-done) | copy-start | bytes 1572868
  589.9 196.4 %reduce-scatter.22.cloned.1.call-start = ((), (), s32[]{:S(2)}) async-start(), calls=%async_computation.34 | async-start | bytes 1310720 | tf_op jit(solution)/shard_map/reduce_scatter | solution.py:686
  638.8 10.9 copy-start.2
  638.9 10.9 copy-start.4
  638.9 10.9 copy-start.25
  645.5 4.3 copy-start
  651.1 4.1 copy-start.1
  658.7 10.9 copy-start.2
  658.7 10.9 copy-start.4
  658.7 10.9 copy-start.25
  665.4 4.3 copy-start
  671.0 4.4 copy-start.1
  685.3 5.7 copy-start.13
  716.8 73.0 %reduce-scatter.20.cloned.1.call-start = ((), (), s32[]{:S(2)}) async-start(), calls=%async_computation.33 | async-start | bytes 1310720 | tf_op jit(solution)/shard_map/reduce_scatter | solution.py:686
  717.2 4.2 copy-start.29
  722.5 83.0 %reduce-scatter.24.cloned.1.call-start = ((), (), s32[]{:S(2)}) async-start(), calls=%async_computation.35 | async-start | bytes 1310720 | tf_op jit(solution)/shard_map/reduce_scatter | solution.py:686
  729.8 131.1 %reduce-scatter.30.cloned.1.call-start = ((), (), s32[]{:S(2)}) async-start(), calls=%async_computation.38 | async-start | bytes 5242880 | tf_op jit(solution)/shard_map/reduce_scatter | solution.py:686
  729.9 6.6 copy-start.52
  745.9 170.5 %reduce-scatter.32.cloned.1.call-start = ((), (), s32[]{:S(2)}) async-start(), calls=%async_computation.39 | async-start | bytes 5242880 | tf_op jit(solution)/shard_map/reduce_scatter | solution.py:686
  745.9 6.6 copy-start.50
  762.0 209.9 %reduce-scatter.28.cloned.1.call-start = ((), (), s32[]{:S(2)}) async-start(), calls=%async_computation.37 | async-start | bytes 5242880 | tf_op jit(solution)/shard_map/reduce_scatter | solution.py:686
  772.9 338.2 %reduce-scatter.36.cloned.1.call-start = ((), (), s32[]{:S(2)}) async-start(), calls=%async_computation.42 | async-start | bytes 1081344
  774.6 5.6 copy-start.20
  774.6 5.6 copy-start.28
  774.6 359.4 %reduce-scatter.34.cloned.1.call-start = ((), (), s32[]{:S(2)}) async-start(), calls=%async_computation.41 | async-start | bytes 163840
  775.5 389.3 %reduce-scatter.26.cloned.1.call-start = ((), (), s32[]{:S(2)}) async-start(), calls=%async_computation.36 | async-start | bytes 1310720 | tf_op jit(solution)/shard_map/reduce_scatter | solution.py:827
  780.1 436.8 %reduce-scatter.18.cloned.1.call-start = ((), (), s32[]{:S(2)}) async-start(), calls=%async_computation.32 | async-start | bytes 4718592 | tf_op jit(solution)/shard_map/reduce_scatter | solution.py:671
  786.3 13.1 %all-to-all-start.7 = ((bf16[8,64,256]{2,1,0:T(8,128)(2,1)}), bf16[8,64,256]{2,1,0:T(8,128)(2,1)S(1)}, u32[]{:S(2)}, u32[]{:S(2)}) async-start(bf16[8,64,256]{2,1,0:T(8,128)(2,1)} %bitcast.430), calls=%async_computation.11 | async-start | bytes 524288 | tf_op jit(solution)/shard_map/all_to_all | solution.py:687
  799.4 13.1 %all-to-all-start.6 = ((bf16[8,64,256]{2,1,0:T(8,128)(2,1)}), bf16[8,64,256]{2,1,0:T(8,128)(2,1)S(1)}, u32[]{:S(2)}, u32[]{:S(2)}) async-start(bf16[8,64,256]{2,1,0:T(8,128)(2,1)} %bitcast.431), calls=%async_computation.9 | async-start | bytes 524288 | tf_op jit(solution)/shard_map/all_to_all | solution.py:687
  812.4 48.5 %copy-start.38 = (bf16[8,64,256]{2,1,0:T(8,128)(2,1)}, bf16[8,64,256]{2,1,0:T(8,128)(2,1)S(1)}, u32[]{:S(2)}) copy-start(bf16[8,64,256]{2,1,0:T(8,128)(2,1)S(1)} %all-to-all-done.6) | copy-start | bytes 786436
  812.5 48.5 %all-to-all-start.8 = ((bf16[8,64,256]{2,1,0:T(8,128)(2,1)}), bf16[8,64,256]{2,1,0:T(8,128)(2,1)S(1)}, u32[]{:S(2)}, u32[]{:S(2)}) async-start(bf16[8,64,256]{2,1,0:T(8,128)(2,1)} %bitcast.432), calls=%async_computation.13 | async-start | bytes 524288 | tf_op jit(solution)/shard_map/all_to_all | solution.py:687
  861.7 54.7 %all-to-all-start.10 = ((bf16[8,64,1024]{2,1,0:T(8,128)(2,1)}), bf16[8,64,1024]{2,1,0:T(8,128)(2,1)S(1)}, u32[]{:S(2)}, u32[]{:S(2)}) async-start(bf16[8,64,1024]{2,1,0:T(8,128)(2,1)} %bitcast.407), calls=%async_computation.18 | async-start | bytes 2097152 | tf_op jit(solution)/shard_map/all_to_all | solution.py:687
  916.4 55.5 %all-to-all-start.11 = ((bf16[8,64,1024]{2,1,0:T(8,128)(2,1)}), bf16[8,64,1024]{2,1,0:T(8,128)(2,1)S(1)}, u32[]{:S(2)}, u32[]{:S(2)}) async-start(bf16[8,64,1024]{2,1,0:T(8,128)(2,1)} %bitcast.409), calls=%async_computation.20 | async-start | bytes 2097152 | tf_op jit(solution)/shard_map/all_to_all | solution.py:687
  971.9 201.8 %all-to-all-start.9 = ((bf16[8,64,1024]{2,1,0:T(8,128)(2,1)}), bf16[8,64,1024]{2,1,0:T(8,128)(2,1)S(1)}, u32[]{:S(2)}, u32[]{:S(2)}) async-start(bf16[8,64,1024]{2,1,0:T(8,128)(2,1)} %bitcast.406), calls=%async_computation.16 | async-start | bytes 2097152 | tf_op jit(solution)/shard_map/all_to_all | solution.py:687
  1164.8 4.5 copy-start.40
  1173.7 43.3 %copy-start.8 = (bf16[1,128,2048]{2,1,0:T(8,128)(2,1)S(1)}, bf16[1,128,2048]{2,1,0:T(8,128)(2,1)}, u32[]{:S(2)}) copy-start(bf16[1,128,2048]{2,1,0:T(8,128)(2,1)} %param.31) | copy-start | bytes 1572868
  1173.7 43.3 %copy-start.9 = (f32[128,2048]{1,0:T(8,128)S(1)}, f32[128,2048]{1,0:T(8,128)}, u32[]{:S(2)}) copy-start(f32[128,2048]{1,0:T(8,128)} %get-tuple-element.138) | copy-start | bytes 3145732
  (27 other events, 58.9 us)
Sparse Core Ops, SparseCore 0:
  24.4 25.4 all-gather.11
  51.7 26.4 all-gather.13
  80.1 26.4 all-gather.15
  108.1 69.3 all-gather.27
  179.2 25.2 all-gather.17
  206.1 52.5 all-gather.19
  260.6 52.5 all-gather.21
  315.1 52.5 all-gather.23
  370.0 49.8 reduce-scatter.15
  590.0 45.0 all-gather.25
  716.9 25.8 reduce-scatter.21
  746.1 27.9 reduce-scatter.19
  777.6 27.9 reduce-scatter.23
  808.3 52.5 reduce-scatter.29
  863.8 52.5 reduce-scatter.31
  919.3 52.5 reduce-scatter.27
  974.0 137.1 reduce-scatter.35
  1113.7 20.2 reduce-scatter.33
  1136.9 27.9 reduce-scatter.25
  1167.0 49.9 reduce-scatter.17

commit v3 on v2

--- a/solution.py
+++ b/solution.py
@@ -663,20 +663,532 @@
     )
 
 
-def gather_seq(tensor):
-    return lax.all_gather(tensor, "seq", axis=0, tiled=True)
-
-
-def scatter_seq(tensor):
-    return lax.psum_scatter(tensor, "seq", scatter_dimension=0, tiled=True)
-
-
-def columns_in(weight):
-    seq_count = lax.axis_size("seq")
+def peers_of(axis, size):
+    me = lax.axis_index(axis)
+    return me, lambda step: (me + step) % size
+
+
+def greet_cross(seq_count, fsdp_count):
+    seq, seq_peer = peers_of("seq", seq_count)
+    fsdp, fsdp_peer = peers_of("fsdp", fsdp_count)
+    barrier = pltpu.get_barrier_semaphore()
+    for step in range(1, seq_count):
+        pl.semaphore_signal(
+            barrier, inc=1, device_id=(seq_peer(step), fsdp), device_id_type=MESH
+        )
+    for step in range(1, fsdp_count):
+        pl.semaphore_signal(
+            barrier, inc=1, device_id=(seq, fsdp_peer(step)), device_id_type=MESH
+        )
+    pl.semaphore_wait(barrier, seq_count + fsdp_count - 2)
+
+
+def bring_in_kernel(
+    chips,
+    fsdp_count,
+    inputs_ref,
+    query_ref,
+    key_ref,
+    value_ref,
+    output_ref,
+    gains_ref,
+    inputs_out,
+    weights_out,
+    output_out,
+    gains_out,
+    weights,
+    outputs,
+    gains,
+    row_send,
+    row_recv,
+    column_send,
+    column_recv,
+    gain_row_send,
+    gain_row_recv,
+    gain_column_send,
+    gain_column_recv,
+    output_send,
+    output_recv,
+    store_sem,
+    *comm,
+):
+    line = Line(chips)
+    gather = Gather(line, *comm)
+    seq_count = 2 * chips
+    seq, seq_peer = peers_of("seq", seq_count)
+    fsdp, fsdp_peer = peers_of("fsdp", fsdp_count)
+    columns = weights.shape[-1]
+    sources = (query_ref, key_ref, value_ref)
+
+    def block(owner):
+        return pl.ds(pl.multiple_of(owner * columns, 128), columns)
+
+    def row_copy(which, step):
+        peer = seq_peer(step)
+        return pltpu.make_async_remote_copy(
+            src_ref=sources[which].at[:, block(peer)],
+            dst_ref=weights.at[which, seq, fsdp],
+            send_sem=row_send.at[which, step],
+            recv_sem=row_recv.at[which, step],
+            device_id=(peer, fsdp),
+            device_id_type=MESH,
+        )
+
+    def column_copy(owner, step):
+        return pltpu.make_async_remote_copy(
+            src_ref=weights.at[:, owner, fsdp],
+            dst_ref=weights.at[:, owner, fsdp],
+            send_sem=column_send.at[owner, step],
+            recv_sem=column_recv.at[owner, step],
+            device_id=(seq, fsdp_peer(step)),
+            device_id_type=MESH,
+        )
+
+    def gain_row_copy(step):
+        return pltpu.make_async_remote_copy(
+            src_ref=gains_ref,
+            dst_ref=gains.at[seq, fsdp],
+            send_sem=gain_row_send.at[step],
+            recv_sem=gain_row_recv.at[step],
+            device_id=(seq_peer(step), fsdp),
+            device_id_type=MESH,
+        )
+
+    def gain_column_copy(owner, step):
+        return pltpu.make_async_remote_copy(
+            src_ref=gains.at[owner, fsdp],
+            dst_ref=gains.at[owner, fsdp],
+            send_sem=gain_column_send.at[owner, step],
+            recv_sem=gain_column_recv.at[owner, step],
+            device_id=(seq, fsdp_peer(step)),
+            device_id_type=MESH,
+        )
+
+    def output_copy(step):
+        return pltpu.make_async_remote_copy(
+            src_ref=output_ref,
+            dst_ref=outputs.at[fsdp],
+            send_sem=output_send.at[step],
+            recv_sem=output_recv.at[step],
+            device_id=(seq, fsdp_peer(step)),
+            device_id_type=MESH,
+        )
+
+    greet_cross(seq_count, fsdp_count)
+    for step in range(1, seq_count):
+        for which in range(3):
+            row_copy(which, step).start()
+        gain_row_copy(step).start()
+    gather.blocks[line.place * 2 + line.core] = inputs_ref[...]
+    gather.send(line.place)
+    for which in range(3):
+        weights[which, seq, fsdp] = sources[which][:, block(seq)]
+    gains[seq, fsdp] = gains_ref[...]
+    outputs[fsdp] = output_ref[...]
+
+    def forward(owner):
+        for step in range(1, fsdp_count):
+            column_copy(owner, step).start()
+            gain_column_copy(owner, step).start()
+
+    forward(seq)
+
+    @pl.loop(1, seq_count)
+    def _(step):
+        for which in range(3):
+            row_copy(which, step).wait_recv()
+        gain_row_copy(step).wait_recv()
+        forward((seq - step + seq_count) % seq_count)
+
+    for step in range(1, fsdp_count):
+        output_copy(step).start()
+
+    @pl.loop(0, chips)
+    def _(step):
+        gather.step(step)
+
+    inputs_store = pltpu.make_async_copy(gather.blocks, inputs_out, store_sem.at[0])
+    inputs_store.start()
+
+    @pl.loop(0, seq_count)
+    def _(owner):
+        for step in range(1, fsdp_count):
+            column_copy(owner, step).wait_recv()
+            gain_column_copy(owner, step).wait_recv()
+
+    weights_store = pltpu.make_async_copy(weights, weights_out, store_sem.at[1])
+    weights_store.start()
+    for step in range(1, fsdp_count):
+        output_copy(step).wait_recv()
+    output_store = pltpu.make_async_copy(outputs, output_out, store_sem.at[2])
+    output_store.start()
+    gains_out[...] = gains[...]
+
+    gather.finish()
+
+    @pl.loop(1, seq_count)
+    def _(step):
+        for which in range(3):
+            row_copy(which, step).wait_send()
+        gain_row_copy(step).wait_send()
+
+    @pl.loop(0, seq_count)
+    def _(owner):
+        for step in range(1, fsdp_count):
+            column_copy(owner, step).wait_send()
+            gain_column_copy(owner, step).wait_send()
+
+    for step in range(1, fsdp_count):
+        output_copy(step).wait_send()
+    inputs_store.wait()
+    weights_store.wait()
+    output_store.wait()
+
+
+def bring_in(local_in, query_weight, key_weight, value_weight, output_weight, gains):
+    rows, width = local_in.shape
+    slots = lax.axis_size("seq")
     fsdp_count = lax.axis_size("fsdp")
-    part = lax.all_to_all(weight, "seq", split_axis=1, concat_axis=0, tiled=True)
+    chips = slots // 2
+    own_rows, columns = query_weight.shape[0], query_weight.shape[1] // slots
+    bf16, dma = jnp.bfloat16, pltpu.SemaphoreType.DMA
+    lanes = pl.cdiv(gains.shape[1], 128) * 128
+    padded = jnp.pad(gains, ((0, 16 - gains.shape[0]), (0, lanes - gains.shape[1])))
+    weight_shape = (3, slots, fsdp_count, own_rows, columns)
+    inputs_all, weights, outputs, gains_all = pl.pallas_call(
+        functools.partial(bring_in_kernel, chips, fsdp_count),
+        out_shape=(
+            jax.ShapeDtypeStruct((slots, rows, width), bf16),
+            jax.ShapeDtypeStruct(weight_shape, bf16),
+            jax.ShapeDtypeStruct((fsdp_count, own_rows, width), bf16),
+            jax.ShapeDtypeStruct((slots, fsdp_count, 16, lanes), bf16),
+        ),
+        in_specs=[whole_spec()] * 6,
+        out_specs=(far_spec(),) * 3 + (whole_spec(),),
+        scratch_shapes=[
+            pltpu.VMEM(weight_shape, bf16),
+            pltpu.VMEM((fsdp_count, own_rows, width), bf16),
+            pltpu.VMEM((slots, fsdp_count, 16, lanes), bf16),
+            dma((3, slots)),
+            dma((3, slots)),
+            dma((slots, fsdp_count)),
+            dma((slots, fsdp_count)),
+            dma((slots,)),
+            dma((slots,)),
+            dma((slots, fsdp_count)),
+            dma((slots, fsdp_count)),
+            dma((fsdp_count,)),
+            dma((fsdp_count,)),
+            dma((3,)),
+        ]
+        + Gather.scratch(chips, rows, width),
+        compiler_params=line_params(3),
+        name="bring_in",
+    )(local_in, query_weight, key_weight, value_weight, output_weight, padded)
+    gains_all = gains_all[:, :, : gains.shape[0], : gains.shape[1]]
+    return (
+        inputs_all.reshape(-1, width),
+        weights.reshape(3, -1, columns),
+        outputs.reshape(-1, width),
+        gains_all.transpose(2, 0, 1, 3).reshape(gains.shape[0], -1),
+    )
+
+
+def take_out_kernel(
+    chips,
+    fsdp_count,
+    terms_ref,
+    output_ref,
+    gains_ref,
+    query_ref,
+    key_ref,
+    value_ref,
+    output_out,
+    gains_out,
+    column_in,
+    row_out,
+    row_in,
+    output_in,
+    gain_in,
+    gain_out,
+    gain_row,
+    column_send,
+    column_recv,
+    row_send,
+    row_recv,
+    output_send,
+    output_recv,
+    gain_send,
+    gain_recv,
+    gain_row_send,
+    gain_row_recv,
+):
+    seq_count = 2 * chips
+    seq, seq_peer = peers_of("seq", seq_count)
+    fsdp, fsdp_peer = peers_of("fsdp", fsdp_count)
+    columns = terms_ref.shape[-1]
+    f32 = jnp.float32
+
+    def column_copy(owner, step):
+        peer = fsdp_peer(step)
+        return pltpu.make_async_remote_copy(
+            src_ref=terms_ref.at[:, owner, peer],
+            dst_ref=column_in.at[owner, step],
+            send_sem=column_send.at[owner, step],
+            recv_sem=column_recv.at[owner, step],
+            device_id=(seq, peer),
+            device_id_type=MESH,
+        )
+
+    def row_copy(step):
+        peer = seq_peer(step)
+        return pltpu.make_async_remote_copy(
+            src_ref=row_out.at[step],
+            dst_ref=row_in.at[step],
+            send_sem=row_send.at[step],
+            recv_sem=row_recv.at[step],
+            device_id=(peer, fsdp),
+            device_id_type=MESH,
+        )
+
+    def output_copy(step):
+        peer = fsdp_peer(step)
+        return pltpu.make_async_remote_copy(
+            src_ref=output_ref.at[peer],
+            dst_ref=output_in.at[step],
+            send_sem=output_send.at[step],
+            recv_sem=output_recv.at[step],
+            device_id=(seq, peer),
+            device_id_type=MESH,
+        )
+
+    def gain_copy(step):
+        peer = fsdp_peer(step)
+        return pltpu.make_async_remote_copy(
+            src_ref=gains_ref.at[peer],
+            dst_ref=gain_in.at[step],
+            send_sem=gain_send.at[step],
+            recv_sem=gain_recv.at[step],
+            device_id=(seq, peer),
+            device_id_type=MESH,
+        )
+
+    def gain_row_copy(step):
+        peer = seq_peer(step)
+        return pltpu.make_async_remote_copy(
+            src_ref=gain_out.at[peer],
+            dst_ref=gain_row.at[step],
+            send_sem=gain_row_send.at[step],
+            recv_sem=gain_row_recv.at[step],
+            device_id=(peer, fsdp),
+            device_id_type=MESH,
+        )
+
+    greet_cross(seq_count, fsdp_count)
+    for step in range(1, fsdp_count):
+        gain_copy(step).start()
+
+    @pl.loop(1, seq_count + 1)
+    def _(turn):
+        owner = (seq + turn) % seq_count
+        for step in range(1, fsdp_count):
+            column_copy(owner, step).start()
+
+    for step in range(1, fsdp_count):
+        output_copy(step).start()
+    total = gains_ref[fsdp]
+    for step in range(1, fsdp_count):
+        gain_copy(step).wait_recv()
+        total = total + gain_in[step]
+    gain_out[...] = total
+    for step in range(1, seq_count):
+        gain_row_copy(step).start()
+
+    def summed(owner):
+        for step in range(1, fsdp_count):
+            column_copy(owner, step).wait_recv()
+        total = terms_ref[:, owner, fsdp].astype(f32)
+        for step in range(1, fsdp_count):
+            total = total + column_in[owner, step].astype(f32)
+        return total
+
+    @pl.loop(1, seq_count)
+    def _(turn):
+        row_out[turn] = summed((seq + turn) % seq_count).astype(jnp.bfloat16)
+        row_copy(turn).start()
+
+    def put(owner, value):
+        block = pl.ds(pl.multiple_of(owner * columns, 128), columns)
+        query_ref[:, block] = value[0]
+        key_ref[:, block] = value[1]
+        value_ref[:, block] = value[2]
+
+    put(seq, summed(seq))
+    total = output_ref[fsdp].astype(f32)
+    for step in range(1, fsdp_count):
+        output_copy(step).wait_recv()
+        total = total + output_in[step].astype(f32)
+    output_out[...] = total
+    total = gain_out[seq]
+    for step in range(1, seq_count):
+        gain_row_copy(step).wait_recv()
+        total = total + gain_row[step]
+    gains_out[...] = total
+
+    @pl.loop(1, seq_count)
+    def _(step):
+        row_copy(step).wait_recv()
+        put((seq - step + seq_count) % seq_count, row_in[step].astype(f32))
+
+    @pl.loop(0, seq_count)
+    def _(owner):
+        for step in range(1, fsdp_count):
+            column_copy(owner, step).wait_send()
+
+    @pl.loop(1, seq_count)
+    def _(step):
+        row_copy(step).wait_send()
+        gain_row_copy(step).wait_send()
+
+    for step in range(1, fsdp_count):
+        output_copy(step).wait_send()
+        gain_copy(step).wait_send()
+
+
+def take_out(terms, output_term, gain_terms):
+    slots = lax.axis_size("seq")
+    fsdp_count = lax.axis_size("fsdp")
+    chips = slots // 2
+    _, width, columns = terms.shape
+    own = width // (slots * fsdp_count)
+    kinds = gain_terms.shape[0]
+    bf16, f32, dma = jnp.bfloat16, jnp.float32, pltpu.SemaphoreType.DMA
+    gains = gain_terms.reshape(kinds, slots, fsdp_count, own).transpose(2, 1, 0, 3)
+    lanes = pl.cdiv(own, 128) * 128
+    gains = jnp.pad(gains, ((0, 0), (0, 0), (0, 8 - kinds), (0, lanes - own)))
+    block = (3, own, columns)
+    query, key, value, output, gains = pl.pallas_call(
+        functools.partial(take_out_kernel, chips, fsdp_count),
+        out_shape=(jax.ShapeDtypeStruct((own, width), f32),) * 4
+        + (jax.ShapeDtypeStruct((8, lanes), f32),),
+        in_specs=[whole_spec()] * 3,
+        out_specs=(whole_spec(),) * 5,
+        scratch_shapes=[
+            pltpu.VMEM((slots, fsdp_count) + block, bf16),
+            pltpu.VMEM((slots,) + block, bf16),
+            pltpu.VMEM((slots,) + block, bf16),
+            pltpu.VMEM((fsdp_count, own, width), bf16),
+            pltpu.VMEM((fsdp_count, slots, 8, lanes), f32),
+            pltpu.VMEM((slots, 8, lanes), f32),
+            pltpu.VMEM((slots, 8, lanes), f32),
+            dma((slots, fsdp_count)),
+            dma((slots, fsdp_count)),
+            dma((slots,)),
+            dma((slots,)),
+            dma((fsdp_count,)),
+            dma((fsdp_count,)),
+            dma((fsdp_count,)),
+            dma((fsdp_count,)),
+            dma((slots,)),
+            dma((slots,)),
+        ],
+        compiler_params=line_params(4),
+        name="take_out",
+    )(
+        terms.reshape(3, slots, fsdp_count, own, columns),
+        output_term.reshape(fsdp_count, own, width),
+        gains,
+    )
+    return query, key, value, output, gains[:kinds, :own]
+
+
+def scatter_product_kernel(chips, count, *refs):
+    lefts, rights = refs[:count], refs[count : 2 * count]
+    result, comm = refs[2 * count], refs[2 * count + 1 :]
+    line = Line(chips)
+    scatter = Scatter(line, *comm)
+    _, rows, width = scatter.fresh.shape
+    line.greet()
+
+    @pl.loop(0, chips)
+    def _(step):
+        chip = line.order(chips - 1 - step)
+        pair = pl.ds(chip * 2, 2)
+
+        @pl.loop(0, width // tile_of(width))
+        def _(tile):
+            columns = pl.ds(pl.multiple_of(tile * tile_of(width), 128), tile_of(width))
+            total = None
+            for left, right in zip(lefts, rights):
+                term = dot_cols(left[pair].reshape(2 * rows, -1), right[columns, :])
+                total = term if total is None else total + term
+            scatter.fresh[:, :, columns] = total.reshape(2, rows, -1)
+
+        scatter.after_term(chip)
+
+    scatter.finish(result)
+
+
+def scatter_product(collective_id, name, pairs):
+    slots = lax.axis_size("seq")
+    chips = slots // 2
+    rows = pairs[0][0].shape[0] // slots
+    width = pairs[0][1].shape[0]
+    return pl.pallas_call(
+        functools.partial(scatter_product_kernel, chips, len(pairs)),
+        out_shape=jax.ShapeDtypeStruct((rows, width), jnp.float32),
+        in_specs=[whole_spec()] * (2 * len(pairs)),
+        out_specs=whole_spec(),
+        scratch_shapes=Scatter.scratch(chips, rows, width),
+        compiler_params=line_params(collective_id),
+        name=name,
+    )(*[left.reshape(slots, rows, -1) for left, _ in pairs], *[right for _, right in pairs])
+
+
+def gather_kernel(chips, local_ref, out, store_sem, *comm):
+    line = Line(chips)
+    gather = Gather(line, *comm)
+    line.greet()
+    gather.blocks[line.place * 2 + line.core] = local_ref[...]
+    gather.send(line.place)
+
+    def store(chip):
+        pair = pl.ds(chip * 2, 2)
+        return pltpu.make_async_copy(gather.blocks.at[pair], out.at[pair], store_sem.at[chip])
+
+    @pl.loop(0, chips)
+    def _(step):
+        store(gather.step(step)).start()
+
+    gather.finish()
+
+    @pl.loop(0, chips)
+    def _(chip):
+        store(chip).wait()
+
+
+def gather_line(collective_id, name, local):
+    rows, width = local.shape
+    slots = lax.axis_size("seq")
+    chips = slots // 2
+    return pl.pallas_call(
+        functools.partial(gather_kernel, chips),
+        out_shape=jax.ShapeDtypeStruct((slots, rows, width), jnp.bfloat16),
+        in_specs=[whole_spec()],
+        out_specs=far_spec(),
+        scratch_shapes=[pltpu.SemaphoreType.DMA((chips,))] + Gather.scratch(chips, rows, width),
+        compiler_params=line_params(collective_id),
+        name=name,
+    )(local).reshape(-1, width)
+
+
+def row_exchange(weight):
+    return lax.all_to_all(weight, "seq", split_axis=1, concat_axis=0, tiled=True)
+
+
+def columns_in(part):
     whole = lax.all_gather(part, "fsdp", axis=0, tiled=True)
-    return swap_blocks(whole, fsdp_count, seq_count)
+    return swap_blocks(whole, lax.axis_size("fsdp"), lax.axis_size("seq"))
 
 
 def columns_out(term):
@@ -736,20 +1248,28 @@
     segment_row = segments[0]
     score_scale = DH ** (-0.5)
     seq_index = lax.axis_index("seq")
-    inputs_all = gather_seq(local_in)
+    gate_part, up_part, down_part, local_in, output_own = lax.optimization_barrier(
+        (
+            row_exchange(gate_weight),
+            row_exchange(up_weight),
+            row_exchange(down_weight),
+            local_in,
+            output_weight,
+        )
+    )
+    inputs_all, attention_cols, output_rows, gains = bring_in(
+        local_in,
+        query_weight,
+        key_weight,
+        value_weight,
+        output_own,
+        jnp.stack([query_gain, key_gain, attention_gain, feedforward_gain]),
+    )
+    query_cols, key_cols, value_cols = attention_cols[0], attention_cols[1], attention_cols[2]
+    gains = gains.astype(jnp.float32)
     sequence_rows = inputs_all.shape[0]
-    query_cols = columns_in(query_weight)
-    key_cols = columns_in(key_weight)
-    value_cols = columns_in(value_weight)
     head_width = query_cols.shape[1]
     local_heads = head_width // DH
-    output_rows = lax.all_gather(output_weight, "fsdp", axis=0, tiled=True)
-    gains = lax.all_gather(
-        jnp.stack([query_gain, key_gain, attention_gain, feedforward_gain]),
-        ("seq", "fsdp"),
-        axis=1,
-        tiled=True,
-    ).astype(jnp.float32)
     query_scale = lax.dynamic_slice_in_dim(gains[0], seq_index * head_width, head_width, 0)
     key_scale = lax.dynamic_slice_in_dim(gains[1], seq_index * head_width, head_width, 0)
     attention_scale = gains[2]
@@ -792,16 +1312,12 @@
 
     _, (out_blocks, log_totals) = lax.scan(attend_block, jnp.zeros((), jnp.int32), block_ids)
     attended_heads = out_blocks.reshape(sequence_rows, head_width)
-    projected = scatter_seq(
-        jnp.dot(attended_heads, output_rows, preferred_element_type=jnp.float32).astype(
-            jnp.bfloat16
-        )
-    ).astype(jnp.float32)
+    projected = scatter_product(5, "project", [(attended_heads, output_rows.T)])
     hidden = local_in.astype(jnp.float32) + rms_scale(projected, attention_scale)
     hidden_low = hidden.astype(jnp.bfloat16)
-    gate_cols = columns_in(gate_weight)
-    up_cols = columns_in(up_weight)
-    down_cols = columns_in(down_weight)
+    gate_cols = columns_in(gate_part)
+    up_cols = columns_in(up_part)
+    down_cols = columns_in(down_part)
     mixed_pre, gate_linear, up_linear, activated, hidden_all = feed_forward(
         hidden_low, gate_cols, up_cols, down_cols
     )
@@ -823,13 +1339,8 @@
     down_weight_grad = columns_out(contract_rows(grad_all, activated))
     _, branch_pull = jax.vjp(rms_scale, projected, attention_scale)
     grad_projected, grad_attention_gain = branch_pull(grad_hidden)
-    grad_projected_all = gather_seq(grad_projected.astype(jnp.bfloat16))
-    output_weight_grad = lax.psum_scatter(
-        contract_rows(attended_heads, grad_projected_all).astype(jnp.bfloat16),
-        "fsdp",
-        scatter_dimension=0,
-        tiled=True,
-    ).astype(jnp.float32)
+    grad_projected_all = gather_line(6, "gather_projected", grad_projected.astype(jnp.bfloat16))
+    output_term = contract_rows(attended_heads, grad_projected_all).astype(jnp.bfloat16)
     grad_attended = contract_cols(grad_projected_all, output_rows).astype(jnp.bfloat16)
     grad_out_heads = grad_attended.reshape(sequence_rows, local_heads, DH)
 
@@ -896,24 +1407,29 @@
     grad_key_low = (inverse[1][:, None] * (key_error - key_unit * means[1][:, None])).astype(
         jnp.bfloat16
     )
-    grad_input = grad_hidden + scatter_seq(
-        (
-            contract_cols(grad_query_low, query_cols)
-            + contract_cols(grad_key_low, key_cols)
-            + contract_cols(grad_values, value_cols)
-        ).astype(jnp.bfloat16)
-    ).astype(jnp.float32)
-    query_weight_grad = columns_out(contract_rows(inputs_all, grad_query_low))
-    key_weight_grad = columns_out(contract_rows(inputs_all, grad_key_low))
-    value_weight_grad = columns_out(contract_rows(inputs_all, grad_values))
-    head_gains = lax.psum_scatter(
-        jnp.stack([grad_query_gain, grad_key_gain]), "fsdp", scatter_dimension=1, tiled=True
-    )
-    token_gains = lax.psum_scatter(
-        jnp.stack([grad_attention_gain, grad_feedforward_gain]),
-        ("seq", "fsdp"),
-        scatter_dimension=1,
-        tiled=True,
+    grad_input = grad_hidden + scatter_product(
+        7,
+        "input_back",
+        [(grad_query_low, query_cols), (grad_key_low, key_cols), (grad_values, value_cols)],
+    )
+    attention_terms = jnp.stack(
+        [
+            contract_rows(inputs_all, grad_query_low).astype(jnp.bfloat16),
+            contract_rows(inputs_all, grad_key_low).astype(jnp.bfloat16),
+            contract_rows(inputs_all, grad_values).astype(jnp.bfloat16),
+        ]
+    )
+    head_gains = lax.dynamic_update_slice_in_dim(
+        jnp.zeros((2, width_all), jnp.float32),
+        jnp.stack([grad_query_gain, grad_key_gain]),
+        seq_index * head_width,
+        1,
+    )
+    gain_terms = jnp.concatenate(
+        [head_gains, jnp.stack([grad_attention_gain, grad_feedforward_gain])], axis=0
+    )
+    query_weight_grad, key_weight_grad, value_weight_grad, output_weight_grad, gain_grads = (
+        take_out(attention_terms, output_term, gain_terms)
     )
     return (
         result,
@@ -922,13 +1438,13 @@
         key_weight_grad,
         value_weight_grad,
         output_weight_grad,
-        head_gains[0],
-        head_gains[1],
-        token_gains[0],
+        gain_grads[0],
+        gain_grads[1],
+        gain_grads[2],
         gate_weight_grad,
         up_weight_grad,
         down_weight_grad,
-        token_gains[1],
+        gain_grads[3],
     )
 
 

time: 1230 us -> 825 us (0.67)
  waiting for transfers between devices: 585 us -> 65.2 us
  Pallas kernels: 157 us -> 439 us
  blocking collectives: 198 us -> 64.2 us
  local copies, waits for them, and re-layouts: 92.8 us -> 76.5 us
  matrix products: 94.9 us -> 78.8 us
    pallas_call x0 -> x5, Pallas kernels: none -> 284 us  [the longest x2 103 us: scatter_product(): pl.pallas_call(functools.partial(scatter_product_kernel, chips, len(pairs...]
    unnamed x22 -> x6, waiting for transfers between devices: 157 us -> 0.79 us
    reduce_scatter x6 -> x3, waiting for transfers between devices: 149 us -> 0.04 us  [columns_out(): summed = lax.psum_scatter(swapped, 'fsdp', scatter_dimension=0, tiled=True)]
    reduce_scatter x3 -> x0, waiting for transfers between devices: 118 us -> none  [the longest x2 88.8 us: scatter_seq(): return lax.psum_scatter(tensor, 'seq', scatter_dimension=0, tiled=True)]
    all_gather x1 -> x0, blocking collectives: 97.2 us -> none  [per_device(): lax.all_gather(jnp.stack([query_gain, key_gain, attention_gain, feedforwa...]
    all_gather x6 -> x3, waiting for transfers between devices: 74.5 us -> 0.01 us  [columns_in(): whole = lax.all_gather(part, 'fsdp', axis=0, tiled=True)]
    all_gather x3 -> x0, waiting for transfers between devices: 45.1 us -> none  [the longest x2 45.1 us: gather_seq(): return lax.all_gather(tensor, 'seq', axis=0, tiled=True)]
    all_to_all x4 -> x1, blocking collectives: 71.5 us -> 29.7 us  [row_exchange(): lax.all_to_all(weight, 'seq', split_axis=1, concat_axis=0, tiled=True)]
  transfers between devices with their start and end apart: 28 -> 11, of which waited for: 15 -> 3; matrix products, arithmetic and copies ran while one was open for 12% -> 20% of each run, Pallas kernels for 0% -> 35%
where the time goes in v3:
time: 825 us; the launch traced here: 817 us
  Pallas kernels  439 us (53%)
  matrix products  78.8 us (10%)
  local copies, waits for them, and re-layouts  76.5 us (9%)
  waiting for transfers between devices  65.2 us (8%)
  blocking collectives  64.2 us (8%)
  other arithmetic  45.2 us (5%)
  starting transfers between devices  25.8 us (3%)
  between operations  15.3 us (2%)
    pallas_call x2, Pallas kernels, scatter_product(): pl.pallas_call(functools.partial(scatter_product_kernel, chips, len(pairs...  103 us
    pallas_call x1, Pallas kernels, bring_in(): pl.pallas_call(functools.partial(bring_in_kernel, chips, fsdp_count), out...  81.9 us
    pallas_call x1, Pallas kernels, feed_forward_back(): pl.pallas_call(functools.partial(feed_forward_back_kernel, chips), out_sh...  78 us
    pallas_call x1, Pallas kernels, feed_forward(): pl.pallas_call(functools.partial(feed_forward_kernel, chips), out_shape=(...  77 us
    pallas_call x1, Pallas kernels, take_out(): pl.pallas_call(functools.partial(take_out_kernel, chips, fsdp_count), out...  57.8 us
    all_to_all x2, waiting for transfers between devices, row_exchange(): lax.all_to_all(weight, 'seq', split_axis=1, concat_axis=0, tiled=True)  50.6 us
    pallas_call x1, Pallas kernels, gather_line(): pl.pallas_call(functools.partial(gather_kernel, chips), out_shape=jax.Sha...  41 us
    dot_general x7, matrix products, contract_rows(): lax.dot_general(left, right, (((0,), (0,)), ((), ())), preferred_element_...  33.2 us
  transfers between devices with their start and end apart: 11, of which 3 were waited for; matrix products, arithmetic and copies ran while one was open for 20% of the time, Pallas kernels for 35%

profile of v3, /device:TPU:0, one launch (start us, length us, event | category | flops | bytes accessed | tf_op | source)
XLA Modules:
  0.0 816.5 jit_solution(16591798663226341390)
XLA Ops:
  7.2 2.4 copy.177
  9.6 6.4 all-to-all-start.2
  17.0 25.5 %all-to-all-done.2 = bf16[64,8,1024]{2,0,1:T(8,128)(2,1)S(1)} async-done(((bf16[64,8,1024]{2,0,1:T(8,128)(2,1)}), bf16[64,8,1024]{2,0,1:T(8,128)(2,1)S(1)}, u32[]{:S(2)}, u32[]{:S(2)}) %all-to-all-start.2) | async-done | bytes 1048608 | tf_op jit(solution)/shard_map/all_to_all | solution.py:1186
  42.5 3.7 all-to-all-start
  47.6 25.1 %all-to-all-done = bf16[64,8,1024]{2,0,1:T(8,128)(2,1)S(1)} async-done(((bf16[64,8,1024]{2,0,1:T(8,128)(2,1)}), bf16[64,8,1024]{2,0,1:T(8,128)(2,1)S(1)}, u32[]{:S(2)}, u32[]{:S(2)}) %all-to-all-start) | async-done | bytes 1048608 | tf_op jit(solution)/shard_map/all_to_all | solution.py:1186
  72.7 29.7 %all_to_all.96 = bf16[64,8,1024]{2,0,1:T(8,128)(2,1)} all-to-all(bf16[64,8,1024]{2,0,1:T(8,128)(2,1)S(1)} %bitcast.293), channel_id=1, replica_groups=mesh['seq'=8,'fsdp'=4] {'seq'}, dimensions={1} | all-to-all | bytes 2097152 | tf_op jit(solution)/shard_map/all_to_all | solution.py:1186
  103.9 2.9 fusion.54
  106.9 81.9 %bring_in.1 = (bf16[8,128,2048]{2,1,0:T(8,128)(2,1)}, bf16[3,8,4,64,256]{4,3,2,1,0:T(8,128)(2,1)}, bf16[4,64,2048]{2,1,0:T(8,128)(2,1)}, bf16[8,4,16,128]{3,2,1,0:T(8,128)(2,1)}) custom-call(bf16[128,2048]{1,0:T(8,128)(2,1)} %bitcast.276, bf16[64,2048]{1,0:T(8,128)(2,1)} %query_ref.1, bf16[64,2048]{1,0:T(8,128)(2,1)} %key_ref.1, bf16[64,2048]{1,0:T(8,128)(2,1)} %value_ref.1, ...), custom_call_target="tpu_custom_call" | custom-call | tf_op jit(solution)/shard_map/bring_in/pallas_call | solution.py:858
  190.0 3.3 fusion.69
  196.0 15.3 %psum.14 = f32[2,1024]{1,0:T(2,128)S(1)} all-reduce(f32[2,1024]{1,0:T(2,128)S(1)} %pad_maximum_fusion.5), channel_id=1, replica_groups=mesh['seq'=8,'fsdp'=4] {'seq'}, use_global_device_ids=true, to_apply=%region_2.3 | all-reduce | flops 2048 | bytes 16384 | tf_op jit(solution)/shard_map/psum | solution.py:1282
  217.5 3.9 convolution_convert_fusion.5
  222.0 2.6 subtract_convert_fusion
  225.3 13.8 %while.27 = (s32[]{:T(128)}, bf16[2,512,2,128]{3,2,1,0:T(2,128)(2,1)}, f32[2,2,512]{2,1,0:T(2,128)S(1)}, s32[2]{0:T(128)S(1)}, s32[1,1024]{1,0:T(1,128)S(1)}, /*...) while((s32[]{:T(128)}, ...), condition=%wide.region_6.7_spmd, body=%wide.region_3.6_spmd.sunk | while | flops 551157248 | bytes 21018884 | solution.py:1313
  229.4 1.7 fusion.127
  236.3 1.7 fusion.127
  239.0 2.2 reshape_reshape.6.refs_0_
  241.3 2.3 copy.120
  243.7 49.7 %project.1 = f32[128,2048]{1,0:T(8,128)} custom-call(bf16[8,128,256]{2,1,0:T(8,128)(2,1)} %reshape_reshape.6.refs_0_, bf16[2048,256]{1,0:T(8,128)(2,1)} %bitcast.292), custom_call_target="tpu_custom_call" | custom-call | tf_op jit(solution)/shard_map/project/pallas_call | solution.py:1137
  294.7 2.2 fusion.50.hidden_ref
  297.0 4.8 copy.121
  301.8 4.9 copy.122
  306.7 4.9 copy.123
  311.6 77.0 %feed_forward.1 = (f32[128,2048]{1,0:T(8,128)}, f32[8,128,1024]{2,1,0:T(8,128)}, f32[8,128,1024]{2,1,0:T(8,128)}, bf16[8,128,1024]{2,1,0:T(8,128)(2,1)}, bf16[8,128,2048]{2,1,0:T(8,128)(2,1)}) custom-call(bf16[128,2048]{1,0:T(8,128)(2,1)} %fusion.50.hidden_ref, bf16[2048,1024]{1,0:T(8,128)(2,1)} %bitcast.267, bf16[2048,1024]{1,0:T(8,128)(2,1)} %bitcast.269, ...), custom_call_target="tpu_custom_call" | custom-call | tf_op jit(solution)/shard_map/feed_forward/pallas_call | solution.py:601
  390.0 1.6 fusion.47
  391.6 2.3 fusion.45.grad_ref
  393.9 78.0 %feed_forward_back.1 = (f32[128,2048]{1,0:T(8,128)}, bf16[8,128,1024]{2,1,0:T(8,128)(2,1)}, bf16[8,128,1024]{2,1,0:T(8,128)(2,1)}, bf16[8,128,2048]{2,1,0:T(8,128)(2,1)}) custom-call(bf16[128,2048]{1,0:T(8,128)(2,1)} %fusion.45.grad_ref, bf16[2048,1024]{1,0:T(8,128)(2,1)} %bitcast.268, bf16[2048,1024]{1,0:T(8,128)(2,1)} %bitcast.270, ...), custom_call_target="tpu_custom_call" | custom-call | tf_op jit(solution)/shard_map/feed_forward_back/pallas_call | solution.py:634
  471.8 6.4 copy.142
  478.3 7.4 convert_bitcast_fusion
  485.7 2.4 copy.143
  488.2 6.5 copy.137
  494.7 7.4 convert_bitcast_fusion.1
  502.1 2.4 copy.140
  504.7 7.4 convert_bitcast_fusion.2
  512.2 2.5 copy.138
  515.4 1.6 fusion.46
  516.9 41.0 %gather_projected.1 = bf16[8,128,2048]{2,1,0:T(8,128)(2,1)} custom-call(bf16[128,2048]{1,0:T(8,128)(2,1)} %get-tuple-element.368.local_ref), custom_call_target="tpu_custom_call" | custom-call | tf_op jit(solution)/shard_map/gather_projected/pallas_call | solution.py:1174
  557.9 3.9 convolution_convert_fusion.4
  561.9 40.6 %while.28 = (s32[]{:T(128)}, f32[1024,2,128]{0,2,1:T(8,128)}, f32[1024,2,128]{0,2,1:T(8,128)}, bf16[2,512,2,128]{3,1,0,2:T(8,128)(2,1)}, s32[2]{0:T(128)S(1)}, /...) while((s32[]{:T(128)}, f32[1024,2,128]{0,2,1:T(8,128)}, ...), condition=%wide.region_13.14_spmd.clone, body=%wide.region_11.13_spmd.clone.sunk | while | flops 1361051136 | bytes 86813704 | solution.py:1378
  563.9 2.7 fusion.137
  568.6 4.2 multiply_reduce_fusion.10
  574.2 2.6 fusion.139
  578.3 3.6 fusion.140
  583.9 2.7 fusion.137
  588.6 4.2 multiply_reduce_fusion.10
  594.2 3.0 fusion.139
  598.6 3.9 fusion.140
  602.5 1.9 copy.128
  604.5 5.2 all-to-all-start.5
  609.8 2.7 multiply_subtract_fusion
  614.2 2.6 pad_maximum_fusion.2
  616.9 1.6 copy.129
  618.5 1.5 fusion.49
  620.3 19.2 %psum.15 = f32[2,1024]{1,0:T(2,128)S(1)} all-reduce(f32[2,1024]{1,0:T(2,128)S(1)} %pad_maximum_fusion.6), channel_id=1, replica_groups=mesh['seq'=8,'fsdp'=4] {'seq'}, use_global_device_ids=true, to_apply=%region_16.17 | all-reduce | flops 2048 | bytes 16384 | tf_op jit(solution)/shard_map/psum | solution.py:1393
  639.5 6.4 all-to-all-start.4
  645.9 2.3 multiply_convert_fusion.2
  650.1 3.7 convolution_convert_fusion.3
  656.7 2.0 pad_maximum_fusion.terms_ref
  658.7 13.8 %all-to-all-done.4 = bf16[8,64,1024]{2,1,0:T(8,128)(2,1)} async-done(((bf16[8,64,1024]{2,1,0:T(8,128)(2,1)}), bf16[8,64,1024]{2,1,0:T(8,128)(2,1)}, u32[]{:S(2)}, u32[]{:S(2)}) %all-to-all-start.4) | async-done | bytes 1048608 | tf_op jit(solution)/shard_map/all_to_all | solution.py:1199
  672.5 3.6 all-to-all-start.3
  678.8 4.5 convolution_convert_fusion
  683.3 57.8 %take_out.1 = (f32[64,2048]{1,0:T(8,128)}, f32[64,2048]{1,0:T(8,128)}, f32[64,2048]{1,0:T(8,128)}, f32[64,2048]{1,0:T(8,128)}, f32[8,128]{1,0:T(8,128)}) custom-call(bf16[3,8,4,64,256]{4,3,2,1,0:T(8,128)(2,1)} %pad_maximum_fusion.terms_ref, bf16[4,64,2048]{2,1,0:T(8,128)(2,1)} %bitcast.319, f32[4,8,8,128]{3,2,1,0:T(8,128)} %pad.9.gains_ref), custom_call_target="tpu_custom_call" | custom-call | tf_op jit(solution)/shard_map/take_out/pallas_call | solution.py:1070
  742.4 53.4 %input_back.1 = f32[128,2048]{1,0:T(8,128)} custom-call(bf16[8,128,256]{2,1,0:T(8,128)(2,1)} %bitcast.310, bf16[8,128,256]{2,1,0:T(8,128)(2,1)} %bitcast.309, bf16[8,128,256]{2,1,0:T(8,128)(2,1)} %copy.150.refs_2_, bf16[2048,256]{1,0:T(8,128)(2,1)} %bitcast.301, bf16[2048,256]{1,0:T(8,128)(2,1)} %bitcast.299, bf16[2048,256]{1,0:T(8,128)(2,1)} %bitcast.297), custom_call_target="tpu_custom_call" | custom-call | tf_op jit(solution)/shard_map/input_back/pallas_call | solution.py:1137
  796.3 2.4 add_bitcast_fusion
  798.7 1.5 convert_bitcast_fusion.3
  (260 shorter events, 56.9 us)
Async XLA Ops:
  7.2 8.7 %copy-start.31 = (bf16[64,8192]{1,0:T(8,128)(2,1)S(1)}, bf16[64,8192]{1,0:T(8,128)(2,1)}, u32[]{:S(2)}) copy-start(bf16[64,8192]{1,0:T(8,128)(2,1)} %param.26) | copy-start | bytes 3145732
  9.6 32.9 %all-to-all-start.2 = ((bf16[64,8,1024]{2,0,1:T(8,128)(2,1)}), bf16[64,8,1024]{2,0,1:T(8,128)(2,1)S(1)}, u32[]{:S(2)}, u32[]{:S(2)}) async-start(bf16[64,8,1024]{2,0,1:T(8,128)(2,1)} %bitcast.230), calls=%async_computation.2 | async-start | bytes 2097152 | tf_op jit(solution)/shard_map/all_to_all | solution.py:1186
  42.5 60.7 %copy-start.20 = (bf16[64,8,1024]{2,0,1:T(8,128)(2,1)}, bf16[64,8,1024]{2,0,1:T(8,128)(2,1)S(1)}, u32[]{:S(2)}) copy-start(bf16[64,8,1024]{2,0,1:T(8,128)(2,1)S(1)} %all-to-all-done.2) | copy-start | bytes 3145732
  42.5 60.8 %copy-start.50 = (bf16[64]{0:T(256)(128)(2,1)S(1)}, bf16[64]{0:T(256)(128)(2,1)}, u32[]{:S(2)}) copy-start(bf16[64]{0:T(256)(128)(2,1)} %param.29) | copy-start | bytes 388
  42.5 60.8 %copy-start.51 = (bf16[64]{0:T(256)(128)(2,1)S(1)}, bf16[64]{0:T(256)(128)(2,1)}, u32[]{:S(2)}) copy-start(bf16[64]{0:T(256)(128)(2,1)} %param.25) | copy-start | bytes 388
  42.5 60.8 %copy-start.52 = (bf16[64]{0:T(256)(128)(2,1)S(1)}, bf16[64]{0:T(256)(128)(2,1)}, u32[]{:S(2)}) copy-start(bf16[64]{0:T(256)(128)(2,1)} %param.24) | copy-start | bytes 388
  42.5 60.8 %copy-start.53 = (bf16[64]{0:T(256)(128)(2,1)S(1)}, bf16[64]{0:T(256)(128)(2,1)}, u32[]{:S(2)}) copy-start(bf16[64]{0:T(256)(128)(2,1)} %param.23) | copy-start | bytes 388
  42.5 30.2 %all-to-all-start = ((bf16[64,8,1024]{2,0,1:T(8,128)(2,1)}), bf16[64,8,1024]{2,0,1:T(8,128)(2,1)S(1)}, u32[]{:S(2)}, u32[]{:S(2)}) async-start(bf16[64,8,1024]{2,0,1:T(8,128)(2,1)} %bitcast.232), calls=%async_computation | async-start | bytes 2097152 | tf_op jit(solution)/shard_map/all_to_all | solution.py:1186
  46.2 250.8 %all-gather.4.cloned.1.call-start = ((), (), s32[]{:S(2)}) async-start(), calls=%async_computation.9 | async-start | bytes 5242880 | tf_op jit(solution)/shard_map/all_gather | solution.py:1190
  72.7 29.7 %copy-start.21 = (bf16[64,8,1024]{2,0,1:T(8,128)(2,1)}, bf16[64,8,1024]{2,0,1:T(8,128)(2,1)S(1)}, u32[]{:S(2)}) copy-start(bf16[64,8,1024]{2,0,1:T(8,128)(2,1)S(1)} %all-to-all-done) | copy-start | bytes 3145732
  102.4 199.4 %all-gather.6.cloned.1.call-start = ((), (), s32[]{:S(2)}) async-start(), calls=%async_computation.10 | async-start | bytes 5242880 | tf_op jit(solution)/shard_map/all_gather | solution.py:1190
  103.2 203.5 %all-gather.8.cloned.1.call-start = ((), (), s32[]{:S(2)}) async-start(), calls=%async_computation.11 | async-start | bytes 5242880 | tf_op jit(solution)/shard_map/all_gather | solution.py:1190
  106.8 115.1 %copy-start.16 = (f32[1024,64]{1,0:T(8,128)}, f32[1024,64]{1,0:T(8,128)S(1)}, u32[]{:S(2)}) copy-start(f32[1024,64]{1,0:T(8,128)S(1)} %get-tuple-element.384) | copy-start | bytes 786436
  190.0 3.3 copy-start.54
  194.6 16.8 %copy-start.12 = (f32[1024,256]{0,1:T(8,128)}, f32[1024,256]{0,1:T(8,128)S(1)}, u32[]{:S(2)}) copy-start(f32[1024,256]{0,1:T(8,128)S(1)} %get-tuple-element.392) | copy-start | bytes 3145732
  195.9 18.9 %copy-start.10 = (f32[1024,256]{0,1:T(8,128)}, f32[1024,256]{0,1:T(8,128)S(1)}, u32[]{:S(2)}) copy-start(f32[1024,256]{0,1:T(8,128)S(1)} %get-tuple-element.390) | copy-start | bytes 3145732
  211.3 3.5 copy-start.45
  211.4 3.4 copy-start.41
  217.5 4.4 copy-start.19
  221.7 382.8 %reduce-scatter.8.cloned.1.call-start = ((), (), s32[]{:S(2)}) async-start(), calls=%async_computation.14 | async-start | bytes 5242880 | tf_op jit(solution)/shard_map/reduce_scatter | solution.py:1198
  222.0 3.3 copy-start.32
  239.0 55.7 %copy-start.18 = (bf16[1,128,2048]{2,1,0:T(8,128)(2,1)S(1)}, bf16[1,128,2048]{2,1,0:T(8,128)(2,1)}, u32[]{:S(2)}) copy-start(bf16[1,128,2048]{2,1,0:T(8,128)(2,1)} %param.18) | copy-start | bytes 1572868
  311.6 78.4 %copy-start.8 = (bf16[1,128,2048]{2,1,0:T(8,128)(2,1)S(1)}, bf16[1,128,2048]{2,1,0:T(8,128)(2,1)}, u32[]{:S(2)}) copy-start(bf16[1,128,2048]{2,1,0:T(8,128)(2,1)} %param.31) | copy-start | bytes 1572868
  488.1 151.4 %reduce-scatter.6.cloned.1.call-start = ((), (), s32[]{:S(2)}) async-start(), calls=%async_computation.13 | async-start | bytes 5242880 | tf_op jit(solution)/shard_map/reduce_scatter | solution.py:1198
  504.5 154.2 %reduce-scatter.4.cloned.1.call-start = ((), (), s32[]{:S(2)}) async-start(), calls=%async_computation.12 | async-start | bytes 5242880 | tf_op jit(solution)/shard_map/reduce_scatter | solution.py:1198
  512.2 3.2 copy-start.7
  561.9 10.9 %copy-start.2 = (bf16[1024,2,128]{2,0,1:T(8,128)(2,1)}, bf16[1024,2,128]{2,0,1:T(8,128)(2,1)S(1)}, u32[]{:S(2)}) copy-start(bf16[1024,2,128]{2,0,1:T(8,128)(2,1)S(1)} %get-tuple-element.609) | copy-start | bytes 1572868 | tf_op jit(solution)/shard_map/while
  561.9 10.9 %copy-start.5 = (bf16[1024,2,128]{2,0,1:T(8,128)(2,1)}, bf16[1024,2,128]{2,0,1:T(8,128)(2,1)S(1)}, u32[]{:S(2)}) copy-start(bf16[1024,2,128]{2,0,1:T(8,128)(2,1)S(1)} %get-tuple-element.615) | copy-start | bytes 1572868 | tf_op jit(solution)/shard_map/while
  561.9 10.9 %copy-start.24 = (bf16[1024,2,128]{0,2,1:T(8,128)(2,1)}, bf16[1024,2,128]{0,2,1:T(8,128)(2,1)S(1)}, u32[]{:S(2)}) copy-start(bf16[1024,2,128]{0,2,1:T(8,128)(2,1)S(1)} %get-tuple-element.614) | copy-start | bytes 1572868 | tf_op jit(solution)/shard_map/while
  568.6 4.2 copy-start
  574.2 4.1 copy-start.1
  578.3 3.6 copy-start.3
  578.3 3.6 copy-start.6
  578.3 3.6 copy-start.25
  581.9 10.9 %copy-start.2 = (bf16[1024,2,128]{2,0,1:T(8,128)(2,1)}, bf16[1024,2,128]{2,0,1:T(8,128)(2,1)S(1)}, u32[]{:S(2)}) copy-start(bf16[1024,2,128]{2,0,1:T(8,128)(2,1)S(1)} %get-tuple-element.609) | copy-start | bytes 1572868 | tf_op jit(solution)/shard_map/while
  581.9 10.9 %copy-start.5 = (bf16[1024,2,128]{2,0,1:T(8,128)(2,1)}, bf16[1024,2,128]{2,0,1:T(8,128)(2,1)S(1)}, u32[]{:S(2)}) copy-start(bf16[1024,2,128]{2,0,1:T(8,128)(2,1)S(1)} %get-tuple-element.615) | copy-start | bytes 1572868 | tf_op jit(solution)/shard_map/while
  581.9 10.9 %copy-start.24 = (bf16[1024,2,128]{0,2,1:T(8,128)(2,1)}, bf16[1024,2,128]{0,2,1:T(8,128)(2,1)S(1)}, u32[]{:S(2)}) copy-start(bf16[1024,2,128]{0,2,1:T(8,128)(2,1)S(1)} %get-tuple-element.614) | copy-start | bytes 1572868 | tf_op jit(solution)/shard_map/while
  588.5 4.3 copy-start
  594.2 4.4 copy-start.1
  598.6 3.9 copy-start.3
  598.6 3.9 copy-start.6
  598.6 3.9 copy-start.25
  602.5 7.2 copy-start.33
  602.5 7.3 copy-start.17
  604.5 35.0 %all-to-all-start.5 = ((bf16[8,64,1024]{2,1,0:T(8,128)(2,1)}), bf16[8,64,1024]{2,1,0:T(8,128)(2,1)}, u32[]{:S(2)}, u32[]{:S(2)}) async-start(bf16[8,64,1024]{2,1,0:T(8,128)(2,1)} %bitcast.318), calls=%async_computation.8 | async-start | bytes 2097152 | tf_op jit(solution)/shard_map/all_to_all | solution.py:1199
  612.9 5.6 copy-start.13
  612.9 5.6 copy-start.44
  612.9 5.6 copy-start.48
  614.2 5.7 copy-start.11
  614.2 5.7 copy-start.42
  614.2 5.7 copy-start.46
  639.5 33.0 %all-to-all-start.4 = ((bf16[8,64,1024]{2,1,0:T(8,128)(2,1)}), bf16[8,64,1024]{2,1,0:T(8,128)(2,1)}, u32[]{:S(2)}, u32[]{:S(2)}) async-start(bf16[8,64,1024]{2,1,0:T(8,128)(2,1)} %bitcast.317), calls=%async_computation.6 | async-start | bytes 2097152 | tf_op jit(solution)/shard_map/all_to_all | solution.py:1199
  649.9 5.4 copy-start.27
  650.1 5.2 copy-start.29
  650.1 3.8 copy-start.55
  656.7 19.4 %copy-start.30 = (bf16[1024,256]{0,1:T(8,128)(2,1)S(1)}, bf16[1024,256]{0,1:T(8,128)(2,1)}, u32[]{:S(2)}) copy-start(bf16[1024,256]{0,1:T(8,128)(2,1)} %copy-done.29) | copy-start | bytes 1572868
  656.7 22.1 %copy-start.36 = (bf16[2,512,2,128]{3,2,1,0:T(2,128)(2,1)S(1)}, bf16[2,512,2,128]{3,2,1,0:T(2,128)(2,1)}, u32[]{:S(2)}) copy-start(bf16[2,512,2,128]{3,2,1,0:T(2,128)(2,1)} %get-tuple-element.153) | copy-start | bytes 1572868
  672.5 132.1 %all-to-all-start.3 = ((bf16[8,64,1024]{2,1,0:T(8,128)(2,1)}), bf16[8,64,1024]{2,1,0:T(8,128)(2,1)S(1)}, u32[]{:S(2)}, u32[]{:S(2)}) async-start(bf16[8,64,1024]{2,1,0:T(8,128)(2,1)} %bitcast.316), calls=%async_computation.4 | async-start | bytes 2097152 | tf_op jit(solution)/shard_map/all_to_all | solution.py:1199
  678.8 62.3 %copy-start.28 = (bf16[1024,2,128]{0,2,1:T(8,128)(2,1)S(1)}, bf16[1024,2,128]{0,2,1:T(8,128)(2,1)}, u32[]{:S(2)}) copy-start(bf16[1024,2,128]{0,2,1:T(8,128)(2,1)} %copy-done.27) | copy-start | bytes 1572868
  741.1 54.7 %copy-start.49 = (f32[8,128]{1,0:T(8,128)S(1)}, f32[8,128]{1,0:T(8,128)}, u32[]{:S(2)}) copy-start(f32[8,128]{1,0:T(8,128)} %get-tuple-element.170) | copy-start | bytes 12292
  741.1 55.2 %copy-start.9 = (bf16[1,128,2048]{2,1,0:T(8,128)(2,1)S(1)}, bf16[1,128,2048]{2,1,0:T(8,128)(2,1)}, u32[]{:S(2)}) copy-start(bf16[1,128,2048]{2,1,0:T(8,128)(2,1)} %param.31) | copy-start | bytes 1572868
  741.1 55.2 %copy-start.15 = (f32[128,2048]{1,0:T(8,128)S(1)}, f32[128,2048]{1,0:T(8,128)}, u32[]{:S(2)}) copy-start(f32[128,2048]{1,0:T(8,128)} %get-tuple-element.161) | copy-start | bytes 3145732
  804.6 3.3 copy-start.38
  804.8 3.9 copy-start.37
  (13 other events, 20.0 us)
Sparse Core Ops, SparseCore 0:
  102.5 90.1 all-gather.3
  194.5 52.1 all-gather.5
  248.5 52.5 all-gather.7
  488.2 50.1 reduce-scatter.7
  541.3 52.5 reduce-scatter.5
  596.7 52.6 reduce-scatter.3

commit v4 on v2

--- a/solution.py
+++ b/solution.py
@@ -60,15 +60,6 @@
     )
 
 
-def swap_blocks(tensor, outer, inner):
-    block_rows = tensor.shape[0] // (outer * inner)
-    return (
-        tensor.reshape(outer, inner, block_rows, tensor.shape[1])
-        .transpose(1, 0, 2, 3)
-        .reshape(tensor.shape)
-    )
-
-
 def masked_scores(query_block, key_heads, first_row, segment_row, score_scale):
     block_rows = query_block.shape[0]
     sequence_rows = key_heads.shape[0]
@@ -83,6 +74,7 @@
         segment_row[None, :] == query_seg[:, None]
     )
     return jnp.where(allowed[None], scores, neg_fill)
+
 
 MESH = pl.DeviceIdType.MESH
 RS_PARTS = 4
@@ -317,28 +309,27 @@
         def _():
             self.pass_on(chip, 1, True)
 
-    def finish(self, result):
+    def hop(self, step):
         line = self.line
         lower = line.place * 2 < line.chips
-
-        @pl.loop(0, line.chips)
-        def _(step):
-            up_chip, down_chip = step, line.chips - 1 - step
-            go_up = (up_chip > line.place) & line.has_below
-            go_down = (down_chip < line.place) & line.has_above
-
-            @pl.when(go_up & lower)
-            def _():
-                self.pass_on(up_chip, 1, False)
-
-            @pl.when(go_down)
-            def _():
-                self.pass_on(down_chip, 0, False)
-
-            @pl.when(go_up & jnp.logical_not(lower))
-            def _():
-                self.pass_on(up_chip, 1, False)
-
+        up_chip, down_chip = step, line.chips - 1 - step
+        go_up = (up_chip > line.place) & line.has_below
+        go_down = (down_chip < line.place) & line.has_above
+
+        @pl.when(go_up & lower)
+        def _():
+            self.pass_on(up_chip, 1, False)
+
+        @pl.when(go_down)
+        def _():
+            self.pass_on(down_chip, 0, False)
+
+        @pl.when(go_up & jnp.logical_not(lower))
+        def _():
+            self.pass_on(up_chip, 1, False)
+
+    def settle(self, result):
+        line = self.line
         place = line.place
         self.side(place).wait_recv()
 
@@ -367,11 +358,19 @@
                 rows, total = self.total(place, part, (1,))
                 result[rows] = total
 
+    def hops(self):
+        @pl.loop(0, self.line.chips)
+        def _(step):
+            self.hop(step)
+
+    def finish(self):
+        line = self.line
+
         @pl.loop(0, line.chips)
         def _(chip):
             self.side(chip).wait_send()
 
-            @pl.when(chip != place)
+            @pl.when(chip != line.place)
             def _():
                 @pl.loop(0, RS_PARTS)
                 def _(part):
@@ -472,7 +471,9 @@
             copy.start()
         scatter.after_term(chip)
 
-    scatter.finish(mixed_ref)
+    scatter.hops()
+    scatter.settle(mixed_ref)
+    scatter.finish()
     gather.finish()
 
     @pl.loop(0, chips)
@@ -569,7 +570,9 @@
             copy.start()
         scatter.after_term(chip)
 
-    scatter.finish(hidden_grad_ref)
+    scatter.hops()
+    scatter.settle(hidden_grad_ref)
+    scatter.finish()
     gather.finish()
 
     @pl.loop(0, chips)
@@ -663,30 +666,920 @@
     )
 
 
-def gather_seq(tensor):
-    return lax.all_gather(tensor, "seq", axis=0, tiled=True)
-
-
-def scatter_seq(tensor):
-    return lax.psum_scatter(tensor, "seq", scatter_dimension=0, tiled=True)
-
-
-def columns_in(weight):
-    seq_count = lax.axis_size("seq")
+def peers_of(axis, size):
+    me = lax.axis_index(axis)
+    return me, lambda step: (me + step) % size
+
+
+def greet_cross(seq_count, fsdp_count):
+    seq, seq_peer = peers_of("seq", seq_count)
+    fsdp, fsdp_peer = peers_of("fsdp", fsdp_count)
+    barrier = pltpu.get_barrier_semaphore()
+    for step in range(1, seq_count):
+        pl.semaphore_signal(
+            barrier, inc=1, device_id=(seq_peer(step), fsdp), device_id_type=MESH
+        )
+    for step in range(1, fsdp_count):
+        pl.semaphore_signal(
+            barrier, inc=1, device_id=(seq, fsdp_peer(step)), device_id_type=MESH
+        )
+    pl.semaphore_wait(barrier, seq_count + fsdp_count - 2)
+
+
+class Cross:
+    def __init__(self, seq_count, fsdp_count):
+        self.seq_count, self.fsdp_count = seq_count, fsdp_count
+        self.seq, self.seq_peer = peers_of("seq", seq_count)
+        self.fsdp, self.fsdp_peer = peers_of("fsdp", fsdp_count)
+        self.square = fsdp_count == 4
+        if self.square:
+            row, place = self.fsdp // 2, self.fsdp % 2
+            self.sides = (row * 2 + 1 - place, (1 - row) * 2 + place)
+            self.corner = (1 - row) * 2 + 1 - place
+        else:
+            self.sides = tuple(self.fsdp_peer(step) for step in range(1, fsdp_count))
+
+    def remote(self, src, dst, send, recv, seq, fsdp):
+        return pltpu.make_async_remote_copy(
+            src_ref=src,
+            dst_ref=dst,
+            send_sem=send,
+            recv_sem=recv,
+            device_id=(seq, fsdp),
+            device_id_type=MESH,
+        )
+
+
+class Spread:
+    def __init__(self, cross, sources, weights, row_send, row_recv, side_send, side_recv, half_send, half_recv):
+        self.cross, self.sources, self.weights = cross, sources, weights
+        self.row_send, self.row_recv = row_send, row_recv
+        self.side_send, self.side_recv = side_send, side_recv
+        self.half_send, self.half_recv = half_send, half_recv
+        self.kinds, self.columns = len(sources), weights.shape[-1]
+        self.rows = weights.shape[-2]
+
+    @staticmethod
+    def scratch(kinds, seq_count, fsdp_count, rows, columns):
+        dma = pltpu.SemaphoreType.DMA
+        sides = 2 if fsdp_count == 4 else fsdp_count - 1
+        return [
+            pltpu.VMEM((kinds, seq_count, fsdp_count, rows, columns), jnp.bfloat16),
+            dma((kinds, seq_count)),
+            dma((kinds, seq_count)),
+            dma((seq_count, sides)),
+            dma((seq_count, sides)),
+            dma((seq_count, 2)),
+            dma((seq_count, 2)),
+        ]
+
+    def block(self, owner):
+        return pl.ds(pl.multiple_of(owner * self.columns, 128), self.columns)
+
+    def row(self, kind, step):
+        cross = self.cross
+        peer = cross.seq_peer(step)
+        return cross.remote(
+            self.sources[kind].at[:, self.block(peer)],
+            self.weights.at[kind, cross.seq, cross.fsdp],
+            self.row_send.at[kind, step],
+            self.row_recv.at[kind, step],
+            peer,
+            cross.fsdp,
+        )
+
+    def side(self, owner, side):
+        cross = self.cross
+        ref = self.weights.at[:, owner, cross.fsdp]
+        return cross.remote(
+            ref,
+            ref,
+            self.side_send.at[owner, side],
+            self.side_recv.at[owner, side],
+            cross.seq,
+            cross.sides[side],
+        )
+
+    def half(self, owner, side):
+        cross = self.cross
+        rows = pl.ds(side * (self.rows // 2), self.rows // 2)
+        ref = self.weights.at[:, owner, cross.sides[side], rows]
+        return cross.remote(
+            ref,
+            ref,
+            self.half_send.at[owner, side],
+            self.half_recv.at[owner, side],
+            cross.seq,
+            cross.sides[1 - side],
+        )
+
+    def start(self):
+        cross = self.cross
+        for step in range(1, cross.seq_count):
+            for kind in range(self.kinds):
+                self.row(kind, step).start()
+
+    def own(self):
+        cross = self.cross
+        for kind in range(self.kinds):
+            self.weights[kind, cross.seq, cross.fsdp] = self.sources[kind][:, self.block(cross.seq)]
+        self.pass_on(0)
+
+    def owner(self, step):
+        return (self.cross.seq - step + self.cross.seq_count) % self.cross.seq_count
+
+    def take(self, step):
+        for kind in range(self.kinds):
+            self.row(kind, step).wait_recv()
+        self.pass_on(step)
+
+    def pass_on(self, step):
+        for side in range(len(self.cross.sides)):
+            self.side(self.owner(step), side).start()
+
+    def relay(self, step):
+        owner = self.owner(step)
+        for side in range(len(self.cross.sides)):
+            self.side(owner, side).wait_recv()
+            if self.cross.square:
+                self.half(owner, side).start()
+
+    def settle(self, step):
+        if self.cross.square:
+            for side in range(2):
+                self.half(self.owner(step), side).wait_recv()
+
+    def finish(self):
+        cross = self.cross
+
+        @pl.loop(1, cross.seq_count)
+        def _(step):
+            for kind in range(self.kinds):
+                self.row(kind, step).wait_send()
+
+        @pl.loop(0, cross.seq_count)
+        def _(owner):
+            for side in range(len(cross.sides)):
+                self.side(owner, side).wait_send()
+                if cross.square:
+                    self.half(owner, side).wait_send()
+
+
+class Collect:
+    def __init__(self, cross, terms, side_in, half_out, half_in, row_out, row_in, side_send, side_recv, half_send, half_recv, row_send, row_recv):
+        self.cross, self.terms = cross, terms
+        self.side_in, self.half_out, self.half_in = side_in, half_out, half_in
+        self.row_out, self.row_in = row_out, row_in
+        self.side_send, self.side_recv = side_send, side_recv
+        self.half_send, self.half_recv = half_send, half_recv
+        self.row_send, self.row_recv = row_send, row_recv
+        self.rows, self.columns = terms.shape[-2:]
+        self.kinds = terms.shape[:-4]
+
+    @staticmethod
+    def scratch(seq_count, fsdp_count, rows, columns):
+        dma = pltpu.SemaphoreType.DMA
+        vmem = pltpu.VMEM
+        bf16 = jnp.bfloat16
+        if fsdp_count == 4:
+            arrays = [
+                vmem((seq_count, 2, 2, rows // 2, columns), bf16),
+                vmem((seq_count, 2, rows // 2, columns), bf16),
+                vmem((seq_count, 2, rows // 2, columns), bf16),
+            ]
+            sides = (2, 2)
+        else:
+            arrays = [
+                vmem((seq_count, fsdp_count - 1, rows, columns), bf16),
+                vmem((1, 1, 16, 128), bf16),
+                vmem((1, 1, 16, 128), bf16),
+            ]
+            sides = (fsdp_count - 1, 1)
+        return arrays + [
+            vmem((seq_count, rows, columns), bf16),
+            vmem((seq_count, rows, columns), bf16),
+            dma((seq_count,) + sides),
+            dma((seq_count,) + sides),
+            dma((seq_count, 2)),
+            dma((seq_count, 2)),
+            dma((seq_count,)),
+            dma((seq_count,)),
+        ]
+
+    def half_rows(self, side):
+        return pl.ds(side * (self.rows // 2), self.rows // 2)
+
+    def side(self, owner, side, which):
+        cross = self.cross
+        if not cross.square:
+            return cross.remote(
+                self.terms.at[owner, cross.sides[side]],
+                self.side_in.at[owner, side],
+                self.side_send.at[owner, side, 0],
+                self.side_recv.at[owner, side, 0],
+                cross.seq,
+                cross.sides[side],
+            )
+        target = cross.sides[side] if which == 0 else cross.corner
+        return cross.remote(
+            self.terms.at[owner, target, self.half_rows(side)],
+            self.side_in.at[owner, side, which],
+            self.side_send.at[owner, side, which],
+            self.side_recv.at[owner, side, which],
+            cross.seq,
+            cross.sides[side],
+        )
+
+    def half(self, owner, side):
+        cross = self.cross
+        return cross.remote(
+            self.half_out.at[owner, side],
+            self.half_in.at[owner, side],
+            self.half_send.at[owner, side],
+            self.half_recv.at[owner, side],
+            cross.seq,
+            cross.sides[1 - side],
+        )
+
+    def row(self, step):
+        cross = self.cross
+        return cross.remote(
+            self.row_out.at[step],
+            self.row_in.at[step],
+            self.row_send.at[step],
+            self.row_recv.at[step],
+            cross.seq_peer(step),
+            cross.fsdp,
+        )
+
+    def owner(self, turn):
+        return self.cross.seq_peer(turn + 1)
+
+    @property
+    def ways(self):
+        return range(2) if self.cross.square else range(1)
+
+    def send(self, turn):
+        owner = self.owner(turn)
+        for which in reversed(self.ways):
+            for side in range(len(self.cross.sides)):
+                self.side(owner, side, which).start()
+
+    def middle(self, turn):
+        if not self.cross.square:
+            return
+        cross, owner = self.cross, self.owner(turn)
+        for side in range(2):
+            self.side(owner, side, 1).wait_recv()
+            mine = self.terms[owner, cross.sides[1 - side], self.half_rows(side)]
+            self.half_out[owner, side] = (
+                mine.astype(jnp.float32) + self.side_in[owner, side, 1].astype(jnp.float32)
+            ).astype(jnp.bfloat16)
+            self.half(owner, side).start()
+
+    def totals(self, turn):
+        cross, owner = self.cross, self.owner(turn)
+        found = []
+        if cross.square:
+            for side in range(2):
+                self.side(owner, side, 0).wait_recv()
+                self.half(owner, side).wait_recv()
+                rows = self.half_rows(side)
+                total = self.terms[owner, cross.fsdp, rows].astype(jnp.float32)
+                total = total + self.side_in[owner, side, 0].astype(jnp.float32)
+                total = total + self.half_in[owner, side].astype(jnp.float32)
+                found.append((rows, total))
+        else:
+            total = self.terms[owner, cross.fsdp].astype(jnp.float32)
+            for side in range(len(cross.sides)):
+                self.side(owner, side, 0).wait_recv()
+                total = total + self.side_in[owner, side].astype(jnp.float32)
+            found.append((pl.ds(0, self.rows), total))
+        return found
+
+    def ship(self, turn):
+        for rows, total in self.totals(turn):
+            self.row_out[turn + 1, rows] = total.astype(jnp.bfloat16)
+        self.row(turn + 1).start()
+
+    def block(self, owner):
+        return pl.ds(pl.multiple_of(owner * self.columns, 128), self.columns)
+
+    def keep(self, result):
+        cross = self.cross
+        for rows, total in self.totals(cross.seq_count - 1):
+            result[rows, self.block(cross.seq)] = total
+
+    def receive(self, step, result):
+        cross = self.cross
+        self.row(step).wait_recv()
+        owner = (cross.seq - step + cross.seq_count) % cross.seq_count
+        result[:, self.block(owner)] = self.row_in[step].astype(jnp.float32)
+
+    def finish(self):
+        cross = self.cross
+
+        @pl.loop(0, cross.seq_count)
+        def _(owner):
+            for side in range(len(cross.sides)):
+                for which in self.ways:
+                    self.side(owner, side, which).wait_send()
+                if cross.square:
+                    self.half(owner, side).wait_send()
+
+        @pl.loop(1, cross.seq_count)
+        def _(step):
+            self.row(step).wait_send()
+
+
+def bring_in_kernel(
+    chips,
+    fsdp_count,
+    inputs_ref,
+    query_ref,
+    key_ref,
+    value_ref,
+    output_ref,
+    gate_ref,
+    gains_ref,
+    inputs_out,
+    weights_out,
+    output_out,
+    gate_out,
+    gains_out,
+    outputs,
+    gains,
+    gain_row_send,
+    gain_row_recv,
+    gain_column_send,
+    gain_column_recv,
+    output_send,
+    output_recv,
+    store_sem,
+    *comm,
+):
+    line = Line(chips)
+    cross = Cross(2 * chips, fsdp_count)
+    gather = Gather(line, *comm[:5])
+    attention = Spread(cross, (query_ref, key_ref, value_ref), *comm[5:12])
+    gate = Spread(cross, (gate_ref,), *comm[12:])
+    seq_count, seq, fsdp = cross.seq_count, cross.seq, cross.fsdp
+
+    def gain_row(step):
+        return cross.remote(
+            gains_ref,
+            gains.at[seq, fsdp],
+            gain_row_send.at[step],
+            gain_row_recv.at[step],
+            cross.seq_peer(step),
+            fsdp,
+        )
+
+    def gain_column(owner, step):
+        ref = gains.at[owner, fsdp]
+        return cross.remote(
+            ref,
+            ref,
+            gain_column_send.at[owner, step],
+            gain_column_recv.at[owner, step],
+            seq,
+            cross.fsdp_peer(step),
+        )
+
+    def output_copy(step):
+        return cross.remote(
+            output_ref,
+            outputs.at[fsdp],
+            output_send.at[step],
+            output_recv.at[step],
+            seq,
+            cross.fsdp_peer(step),
+        )
+
+    greet_cross(seq_count, fsdp_count)
+    for step in range(1, seq_count):
+        gain_row(step).start()
+    attention.start()
+    gather.blocks[line.place * 2 + line.core] = inputs_ref[...]
+    gather.send(line.place)
+    gate.start()
+    gains[seq, fsdp] = gains_ref[...]
+    outputs[fsdp] = output_ref[...]
+    attention.own()
+    for step in range(1, fsdp_count):
+        gain_column(seq, step).start()
+
+    @pl.loop(1, seq_count)
+    def _(step):
+        attention.take(step)
+        gain_row(step).wait_recv()
+        for peer in range(1, fsdp_count):
+            gain_column(attention.owner(step), peer).start()
+
+    gate.own()
+    for step in range(1, fsdp_count):
+        output_copy(step).start()
+
+    @pl.loop(0, chips)
+    def _(step):
+        gather.step(step)
+        for late in range(2):
+            attention.relay(2 * step + late)
+
+            @pl.when(2 * step + late > 0)
+            def _():
+                gate.take(2 * step + late)
+
+    inputs_store = pltpu.make_async_copy(gather.blocks, inputs_out, store_sem.at[0])
+    inputs_store.start()
+
+    @pl.loop(0, seq_count)
+    def _(step):
+        gate.relay(step)
+        attention.settle(step)
+        for peer in range(1, fsdp_count):
+            gain_column(step, peer).wait_recv()
+
+    weights_store = pltpu.make_async_copy(attention.weights, weights_out, store_sem.at[1])
+    weights_store.start()
+    for step in range(1, fsdp_count):
+        output_copy(step).wait_recv()
+    output_store = pltpu.make_async_copy(outputs, output_out, store_sem.at[2])
+    output_store.start()
+    gains_out[...] = gains[...]
+
+    @pl.loop(0, seq_count)
+    def _(step):
+        gate.settle(step)
+
+    gate_store = pltpu.make_async_copy(gate.weights, gate_out, store_sem.at[3])
+    gate_store.start()
+    gather.finish()
+    attention.finish()
+    gate.finish()
+
+    @pl.loop(1, seq_count)
+    def _(step):
+        gain_row(step).wait_send()
+
+    @pl.loop(0, seq_count)
+    def _(owner):
+        for step in range(1, fsdp_count):
+            gain_column(owner, step).wait_send()
+
+    for step in range(1, fsdp_count):
+        output_copy(step).wait_send()
+    inputs_store.wait()
+    weights_store.wait()
+    output_store.wait()
+    gate_store.wait()
+
+
+def bring_in(local_in, query_weight, key_weight, value_weight, output_weight, gate_weight, gains):
+    rows, width = local_in.shape
+    slots = lax.axis_size("seq")
     fsdp_count = lax.axis_size("fsdp")
-    part = lax.all_to_all(weight, "seq", split_axis=1, concat_axis=0, tiled=True)
-    whole = lax.all_gather(part, "fsdp", axis=0, tiled=True)
-    return swap_blocks(whole, fsdp_count, seq_count)
-
-
-def columns_out(term):
-    seq_count = lax.axis_size("seq")
+    chips = slots // 2
+    own_rows, columns = query_weight.shape[0], query_weight.shape[1] // slots
+    units = gate_weight.shape[1] // slots
+    bf16, dma = jnp.bfloat16, pltpu.SemaphoreType.DMA
+    lanes = pl.cdiv(gains.shape[1], 128) * 128
+    padded = jnp.pad(gains, ((0, 16 - gains.shape[0]), (0, lanes - gains.shape[1])))
+    inputs_all, weights, outputs, gate, gains_all = pl.pallas_call(
+        functools.partial(bring_in_kernel, chips, fsdp_count),
+        out_shape=(
+            jax.ShapeDtypeStruct((slots, rows, width), bf16),
+            jax.ShapeDtypeStruct((3, slots, fsdp_count, own_rows, columns), bf16),
+            jax.ShapeDtypeStruct((fsdp_count, own_rows, width), bf16),
+            jax.ShapeDtypeStruct((1, slots, fsdp_count, own_rows, units), bf16),
+            jax.ShapeDtypeStruct((slots, fsdp_count, 16, lanes), bf16),
+        ),
+        in_specs=[whole_spec()] * 7,
+        out_specs=(far_spec(),) * 4 + (whole_spec(),),
+        scratch_shapes=[
+            pltpu.VMEM((fsdp_count, own_rows, width), bf16),
+            pltpu.VMEM((slots, fsdp_count, 16, lanes), bf16),
+            dma((slots,)),
+            dma((slots,)),
+            dma((slots, fsdp_count)),
+            dma((slots, fsdp_count)),
+            dma((fsdp_count,)),
+            dma((fsdp_count,)),
+            dma((4,)),
+        ]
+        + Gather.scratch(chips, rows, width)
+        + Spread.scratch(3, slots, fsdp_count, own_rows, columns)
+        + Spread.scratch(1, slots, fsdp_count, own_rows, units),
+        compiler_params=line_params(3),
+        name="bring_in",
+    )(local_in, query_weight, key_weight, value_weight, output_weight, gate_weight, padded)
+    gains_all = gains_all[:, :, : gains.shape[0], : gains.shape[1]]
+    return (
+        inputs_all.reshape(-1, width),
+        weights.reshape(3, -1, columns),
+        outputs.reshape(-1, width),
+        gate.reshape(-1, units),
+        gains_all.transpose(2, 0, 1, 3).reshape(gains.shape[0], -1),
+    )
+
+
+def product_terms(scatter, pairs, chip):
+    _, rows, width = scatter.fresh.shape
+    pair = pl.ds(chip * 2, 2)
+
+    @pl.loop(0, width // tile_of(width))
+    def _(tile):
+        columns = pl.ds(pl.multiple_of(tile * tile_of(width), 128), tile_of(width))
+        total = None
+        for left, right, across in pairs:
+            tokens = left[pair].reshape(2 * rows, -1)
+            if across:
+                term = dot_cols(tokens, right[columns, :])
+            else:
+                term = jnp.dot(tokens, right[:, columns], preferred_element_type=jnp.float32)
+            total = term if total is None else total + term
+        scatter.fresh[:, :, columns] = total.reshape(2, rows, -1)
+
+    scatter.after_term(chip)
+
+
+def project_kernel(
+    chips,
+    fsdp_count,
+    attended_ref,
+    output_ref,
+    up_ref,
+    down_ref,
+    result,
+    up_out,
+    down_out,
+    store_sem,
+    *comm,
+):
+    line = Line(chips)
+    cross = Cross(2 * chips, fsdp_count)
+    count = len(Scatter.scratch(chips, 4, 128))
+    scatter = Scatter(line, *comm[:count])
+    up = Spread(cross, (up_ref,), *comm[count : count + 7])
+    down = Spread(cross, (down_ref,), *comm[count + 7 :])
+    greet_cross(cross.seq_count, fsdp_count)
+    up.start()
+    up.own()
+
+    @pl.loop(0, chips)
+    def _(step):
+        product_terms(scatter, [(attended_ref, output_ref, False)], line.order(chips - 1 - step))
+
+    down.start()
+
+    @pl.loop(1, cross.seq_count)
+    def _(step):
+        up.take(step)
+        up.relay(step - 1)
+
+    down.own()
+
+    @pl.loop(0, chips)
+    def _(step):
+        scatter.hop(step)
+        for late in range(2):
+
+            @pl.when(2 * step + late > 0)
+            def _():
+                down.take(2 * step + late)
+
+    up.relay(cross.seq_count - 1)
+
+    @pl.loop(0, cross.seq_count)
+    def _(step):
+        down.relay(step)
+        up.settle(step)
+
+    up_store = pltpu.make_async_copy(up.weights, up_out, store_sem.at[0])
+    up_store.start()
+    scatter.settle(result)
+
+    @pl.loop(0, cross.seq_count)
+    def _(step):
+        down.settle(step)
+
+    down_store = pltpu.make_async_copy(down.weights, down_out, store_sem.at[1])
+    down_store.start()
+    scatter.finish()
+    up.finish()
+    down.finish()
+    up_store.wait()
+    down_store.wait()
+
+
+def project(attended, output_rows, up_weight, down_weight):
+    slots = lax.axis_size("seq")
     fsdp_count = lax.axis_size("fsdp")
-    swapped = swap_blocks(term, seq_count, fsdp_count).astype(jnp.bfloat16)
-    summed = lax.psum_scatter(swapped, "fsdp", scatter_dimension=0, tiled=True)
-    return lax.all_to_all(summed, "seq", split_axis=0, concat_axis=1, tiled=True).astype(
-        jnp.float32
-    )
+    chips = slots // 2
+    rows = attended.shape[0] // slots
+    width = output_rows.shape[1]
+    own_rows, units = up_weight.shape[0], up_weight.shape[1] // slots
+    weight = jax.ShapeDtypeStruct((1, slots, fsdp_count, own_rows, units), jnp.bfloat16)
+    projected, up, down = pl.pallas_call(
+        functools.partial(project_kernel, chips, fsdp_count),
+        out_shape=(jax.ShapeDtypeStruct((rows, width), jnp.float32), weight, weight),
+        in_specs=[whole_spec()] * 4,
+        out_specs=(whole_spec(), far_spec(), far_spec()),
+        scratch_shapes=[pltpu.SemaphoreType.DMA((2,))]
+        + Scatter.scratch(chips, rows, width)
+        + Spread.scratch(1, slots, fsdp_count, own_rows, units) * 2,
+        compiler_params=line_params(5),
+        name="project",
+    )(attended.reshape(slots, rows, -1), output_rows, up_weight, down_weight)
+    return projected, up.reshape(-1, units), down.reshape(-1, units)
+
+
+def gather_back_kernel(chips, fsdp_count, count, local_ref, *refs):
+    terms, refs = refs[:count], refs[count:]
+    out, results, store_sem, comm = refs[0], refs[1 : 1 + count], refs[1 + count], refs[2 + count :]
+    line = Line(chips)
+    cross = Cross(2 * chips, fsdp_count)
+    gather = Gather(line, *comm[:5])
+    collects = [
+        Collect(cross, terms[kind], *comm[5 + 11 * kind : 16 + 11 * kind]) for kind in range(count)
+    ]
+    seq_count = cross.seq_count
+    greet_cross(seq_count, fsdp_count)
+    gather.blocks[line.place * 2 + line.core] = local_ref[...]
+    gather.send(line.place)
+
+    def store(chip):
+        pair = pl.ds(chip * 2, 2)
+        return pltpu.make_async_copy(gather.blocks.at[pair], out.at[pair], store_sem.at[chip])
+
+    for collect in collects:
+
+        @pl.loop(0, seq_count)
+        def _(turn):
+            collect.send(turn)
+
+    store(gather.step(0)).start()
+    for kind, collect in enumerate(collects):
+        collect.middle(0)
+
+        @pl.loop(1, seq_count)
+        def _(turn):
+            collect.middle(turn)
+            collect.ship(turn - 1)
+            if kind == 0:
+
+                @pl.when((turn % 2 == 1) & ((turn + 1) // 2 < chips))
+                def _():
+                    store(gather.step((turn + 1) // 2)).start()
+
+        collect.keep(results[kind])
+
+    for kind, collect in enumerate(collects):
+
+        @pl.loop(1, seq_count)
+        def _(step):
+            collect.receive(step, results[kind])
+
+        collect.finish()
+
+    gather.finish()
+
+    @pl.loop(0, chips)
+    def _(chip):
+        store(chip).wait()
+
+
+def gather_back(local, terms):
+    rows, width = local.shape
+    slots = lax.axis_size("seq")
+    fsdp_count = lax.axis_size("fsdp")
+    chips = slots // 2
+    own = terms[0].shape[0] // (slots * fsdp_count)
+    units = terms[0].shape[1]
+    found = pl.pallas_call(
+        functools.partial(gather_back_kernel, chips, fsdp_count, len(terms)),
+        out_shape=(jax.ShapeDtypeStruct((slots, rows, width), jnp.bfloat16),)
+        + (jax.ShapeDtypeStruct((own, units * slots), jnp.float32),) * len(terms),
+        in_specs=[whole_spec()] * (1 + len(terms)),
+        out_specs=(far_spec(),) + (whole_spec(),) * len(terms),
+        scratch_shapes=[pltpu.SemaphoreType.DMA((chips,))]
+        + Gather.scratch(chips, rows, width)
+        + Collect.scratch(slots, fsdp_count, own, units) * len(terms),
+        compiler_params=line_params(6),
+        name="gather_back",
+    )(local, *[term.reshape(slots, fsdp_count, own, units) for term in terms])
+    return (found[0].reshape(-1, width),) + tuple(found[1:])
+
+
+def take_out_kernel(
+    chips,
+    fsdp_count,
+    *refs,
+):
+    lefts, rights, refs = refs[:3], refs[3:6], refs[6:]
+    terms, output_ref, gains_ref, refs = refs[0], refs[1], refs[2], refs[3:]
+    result, weight_out, output_out, gains_out, refs = refs[0], refs[1], refs[2], refs[3], refs[4:]
+    output_in, gain_in, gain_out, gain_rows, refs = refs[0], refs[1], refs[2], refs[3], refs[4:]
+    output_send, output_recv, gain_send, gain_recv, gain_row_send, gain_row_recv = refs[:6]
+    comm = refs[6:]
+    line = Line(chips)
+    cross = Cross(2 * chips, fsdp_count)
+    scatter = Scatter(line, *comm[:-11])
+    collect = Collect(cross, terms, *comm[-11:])
+    seq_count, seq, fsdp = cross.seq_count, cross.seq, cross.fsdp
+
+    def output_copy(step):
+        peer = cross.fsdp_peer(step)
+        return cross.remote(
+            output_ref.at[peer],
+            output_in.at[step],
+            output_send.at[step],
+            output_recv.at[step],
+            seq,
+            peer,
+        )
+
+    def gain_copy(step):
+        peer = cross.fsdp_peer(step)
+        return cross.remote(
+            gains_ref.at[peer], gain_in.at[step], gain_send.at[step], gain_recv.at[step], seq, peer
+        )
+
+    def gain_row(step):
+        peer = cross.seq_peer(step)
+        return cross.remote(
+            gain_out.at[peer],
+            gain_rows.at[step],
+            gain_row_send.at[step],
+            gain_row_recv.at[step],
+            peer,
+            fsdp,
+        )
+
+    greet_cross(seq_count, fsdp_count)
+    for step in range(1, fsdp_count):
+        gain_copy(step).start()
+
+    @pl.loop(0, seq_count)
+    def _(turn):
+        collect.send(turn)
+
+    for step in range(1, fsdp_count):
+        output_copy(step).start()
+
+    @pl.loop(0, chips)
+    def _(step):
+        product_terms(
+            scatter,
+            [(left, right, True) for left, right in zip(lefts, rights)],
+            line.order(chips - 1 - step),
+        )
+
+    total = gains_ref[fsdp]
+    for step in range(1, fsdp_count):
+        gain_copy(step).wait_recv()
+        total = total + gain_in[step]
+    gain_out[...] = total
+    for step in range(1, seq_count):
+        gain_row(step).start()
+
+    collect.middle(0)
+
+    @pl.loop(1, seq_count)
+    def _(turn):
+        collect.middle(turn)
+        collect.ship(turn - 1)
+
+        @pl.when(turn % 2 == 1)
+        def _():
+            scatter.hop(turn // 2)
+
+    collect.keep(weight_out)
+    total = output_ref[fsdp].astype(jnp.float32)
+    for step in range(1, fsdp_count):
+        output_copy(step).wait_recv()
+        total = total + output_in[step].astype(jnp.float32)
+    output_out[...] = total
+    scatter.settle(result)
+    total = gain_out[seq]
+    for step in range(1, seq_count):
+        gain_row(step).wait_recv()
+        total = total + gain_rows[step]
+    gains_out[...] = total
+
+    @pl.loop(1, seq_count)
+    def _(step):
+        collect.receive(step, weight_out)
+
+    scatter.finish()
+    collect.finish()
+
+    @pl.loop(1, seq_count)
+    def _(step):
+        gain_row(step).wait_send()
+
+    for step in range(1, fsdp_count):
+        output_copy(step).wait_send()
+        gain_copy(step).wait_send()
+
+
+def take_out(pairs, terms, output_term, gain_terms):
+    slots = lax.axis_size("seq")
+    fsdp_count = lax.axis_size("fsdp")
+    chips = slots // 2
+    width, columns = terms.shape
+    rows = pairs[0][0].shape[0] // slots
+    own = width // (slots * fsdp_count)
+    kinds = gain_terms.shape[0]
+    bf16, f32, dma = jnp.bfloat16, jnp.float32, pltpu.SemaphoreType.DMA
+    gains = gain_terms.reshape(kinds, slots, fsdp_count, own).transpose(2, 1, 0, 3)
+    lanes = pl.cdiv(own, 128) * 128
+    gains = jnp.pad(gains, ((0, 0), (0, 0), (0, 8 - kinds), (0, lanes - own)))
+    result, weights, output, gains = pl.pallas_call(
+        functools.partial(take_out_kernel, chips, fsdp_count),
+        out_shape=(
+            jax.ShapeDtypeStruct((rows, width), f32),
+            jax.ShapeDtypeStruct((own, columns * slots), f32),
+            jax.ShapeDtypeStruct((own, width), f32),
+            jax.ShapeDtypeStruct((8, lanes), f32),
+        ),
+        in_specs=[whole_spec()] * 9,
+        out_specs=(whole_spec(),) * 4,
+        scratch_shapes=[
+            pltpu.VMEM((fsdp_count, own, width), bf16),
+            pltpu.VMEM((fsdp_count, slots, 8, lanes), f32),
+            pltpu.VMEM((slots, 8, lanes), f32),
+            pltpu.VMEM((slots, 8, lanes), f32),
+            dma((fsdp_count,)),
+            dma((fsdp_count,)),
+            dma((fsdp_count,)),
+            dma((fsdp_count,)),
+            dma((slots,)),
+            dma((slots,)),
+        ]
+        + Scatter.scratch(chips, rows, width)
+        + Collect.scratch(slots, fsdp_count, own, columns),
+        compiler_params=line_params(4),
+        name="take_out",
+    )(
+        *[left.reshape(slots, rows, -1) for left, _ in pairs],
+        *[right for _, right in pairs],
+        terms.reshape(slots, fsdp_count, own, columns),
+        output_term.reshape(fsdp_count, own, width),
+        gains,
+    )
+    weights = weights.reshape(own, slots, 3, columns // 3)
+    weights = [weights[:, :, kind].reshape(own, -1) for kind in range(3)]
+    return result, weights, output, gains[:kinds, :own]
+
+
+def row_sum_kernel(seq_count, local_ref, result, every, send, recv):
+    seq, seq_peer = peers_of("seq", seq_count)
+    fsdp = lax.axis_index("fsdp")
+    barrier = pltpu.get_barrier_semaphore()
+    for step in range(1, seq_count):
+        pl.semaphore_signal(
+            barrier, inc=1, device_id=(seq_peer(step), fsdp), device_id_type=MESH
+        )
+    pl.semaphore_wait(barrier, seq_count - 1)
+    copies = [
+        pltpu.make_async_remote_copy(
+            src_ref=local_ref,
+            dst_ref=every.at[step],
+            send_sem=send.at[step],
+            recv_sem=recv.at[step],
+            device_id=(seq_peer(step), fsdp),
+            device_id_type=MESH,
+        )
+        for step in range(1, seq_count)
+    ]
+    for copy in copies:
+        copy.start()
+    total = local_ref[...]
+    for step in range(1, seq_count):
+        copies[step - 1].wait_recv()
+        total = total + every[step]
+    result[...] = total
+    for copy in copies:
+        copy.wait_send()
+
+
+def row_sum(collective_id, name, local):
+    slots = lax.axis_size("seq")
+    flat = local.reshape(-1, 128)
+    return pl.pallas_call(
+        functools.partial(row_sum_kernel, slots),
+        out_shape=jax.ShapeDtypeStruct(flat.shape, jnp.float32),
+        in_specs=[whole_spec()],
+        out_specs=whole_spec(),
+        scratch_shapes=[
+            pltpu.VMEM((slots,) + flat.shape, jnp.float32),
+            pltpu.SemaphoreType.DMA((slots,)),
+            pltpu.SemaphoreType.DMA((slots,)),
+        ],
+        compiler_params=line_params(collective_id),
+        name=name,
+    )(flat).reshape(local.shape)
 
 
 def rope_tables(row_count):
@@ -736,20 +1629,20 @@
     segment_row = segments[0]
     score_scale = DH ** (-0.5)
     seq_index = lax.axis_index("seq")
-    inputs_all = gather_seq(local_in)
+    inputs_all, attention_cols, output_rows, gate_cols, gains = bring_in(
+        local_in,
+        query_weight,
+        key_weight,
+        value_weight,
+        output_weight,
+        gate_weight,
+        jnp.stack([query_gain, key_gain, attention_gain, feedforward_gain]),
+    )
+    query_cols, key_cols, value_cols = attention_cols[0], attention_cols[1], attention_cols[2]
+    gains = gains.astype(jnp.float32)
     sequence_rows = inputs_all.shape[0]
-    query_cols = columns_in(query_weight)
-    key_cols = columns_in(key_weight)
-    value_cols = columns_in(value_weight)
     head_width = query_cols.shape[1]
     local_heads = head_width // DH
-    output_rows = lax.all_gather(output_weight, "fsdp", axis=0, tiled=True)
-    gains = lax.all_gather(
-        jnp.stack([query_gain, key_gain, attention_gain, feedforward_gain]),
-        ("seq", "fsdp"),
-        axis=1,
-        tiled=True,
-    ).astype(jnp.float32)
     query_scale = lax.dynamic_slice_in_dim(gains[0], seq_index * head_width, head_width, 0)
     key_scale = lax.dynamic_slice_in_dim(gains[1], seq_index * head_width, head_width, 0)
     attention_scale = gains[2]
@@ -759,9 +1652,10 @@
     values_low = jnp.dot(inputs_all, value_cols, preferred_element_type=jnp.float32).astype(
         jnp.bfloat16
     )
-    squares = lax.psum(
+    squares = row_sum(
+        7,
+        "square_sum",
         jnp.stack([jnp.sum(query_pre * query_pre, axis=-1), jnp.sum(key_pre * key_pre, axis=-1)]),
-        "seq",
     )
     inverse = lax.rsqrt(squares / width_all + eps_norm)
     query_unit = query_pre * inverse[0][:, None]
@@ -792,16 +1686,9 @@
 
     _, (out_blocks, log_totals) = lax.scan(attend_block, jnp.zeros((), jnp.int32), block_ids)
     attended_heads = out_blocks.reshape(sequence_rows, head_width)
-    projected = scatter_seq(
-        jnp.dot(attended_heads, output_rows, preferred_element_type=jnp.float32).astype(
-            jnp.bfloat16
-        )
-    ).astype(jnp.float32)
+    projected, up_cols, down_cols = project(attended_heads, output_rows, up_weight, down_weight)
     hidden = local_in.astype(jnp.float32) + rms_scale(projected, attention_scale)
     hidden_low = hidden.astype(jnp.bfloat16)
-    gate_cols = columns_in(gate_weight)
-    up_cols = columns_in(up_weight)
-    down_cols = columns_in(down_weight)
     mixed_pre, gate_linear, up_linear, activated, hidden_all = feed_forward(
         hidden_low, gate_cols, up_cols, down_cols
     )
@@ -818,18 +1705,17 @@
         grad_mixed_low, gate_cols, up_cols, down_cols, gate_linear, up_linear
     )
     grad_hidden = grad_result + hidden_term
-    gate_weight_grad = columns_out(contract_rows(hidden_all, grad_gate_low))
-    up_weight_grad = columns_out(contract_rows(hidden_all, grad_upward_low))
-    down_weight_grad = columns_out(contract_rows(grad_all, activated))
     _, branch_pull = jax.vjp(rms_scale, projected, attention_scale)
     grad_projected, grad_attention_gain = branch_pull(grad_hidden)
-    grad_projected_all = gather_seq(grad_projected.astype(jnp.bfloat16))
-    output_weight_grad = lax.psum_scatter(
-        contract_rows(attended_heads, grad_projected_all).astype(jnp.bfloat16),
-        "fsdp",
-        scatter_dimension=0,
-        tiled=True,
-    ).astype(jnp.float32)
+    grad_projected_all, gate_weight_grad, up_weight_grad, down_weight_grad = gather_back(
+        grad_projected.astype(jnp.bfloat16),
+        [
+            contract_rows(hidden_all, grad_gate_low).astype(jnp.bfloat16),
+            contract_rows(hidden_all, grad_upward_low).astype(jnp.bfloat16),
+            contract_rows(grad_all, activated).astype(jnp.bfloat16),
+        ],
+    )
+    output_term = contract_rows(attended_heads, grad_projected_all).astype(jnp.bfloat16)
     grad_attended = contract_cols(grad_projected_all, output_rows).astype(jnp.bfloat16)
     grad_out_heads = grad_attended.reshape(sequence_rows, local_heads, DH)
 
@@ -879,14 +1765,15 @@
     query_error = query_error * query_scale
     key_error = key_error * key_scale
     means = (
-        lax.psum(
+        row_sum(
+            8,
+            "mean_sum",
             jnp.stack(
                 [
                     jnp.sum(query_error * query_unit, axis=-1),
                     jnp.sum(key_error * key_unit, axis=-1),
                 ]
             ),
-            "seq",
         )
         / width_all
     )
@@ -896,25 +1783,25 @@
     grad_key_low = (inverse[1][:, None] * (key_error - key_unit * means[1][:, None])).astype(
         jnp.bfloat16
     )
-    grad_input = grad_hidden + scatter_seq(
-        (
-            contract_cols(grad_query_low, query_cols)
-            + contract_cols(grad_key_low, key_cols)
-            + contract_cols(grad_values, value_cols)
-        ).astype(jnp.bfloat16)
-    ).astype(jnp.float32)
-    query_weight_grad = columns_out(contract_rows(inputs_all, grad_query_low))
-    key_weight_grad = columns_out(contract_rows(inputs_all, grad_key_low))
-    value_weight_grad = columns_out(contract_rows(inputs_all, grad_values))
-    head_gains = lax.psum_scatter(
-        jnp.stack([grad_query_gain, grad_key_gain]), "fsdp", scatter_dimension=1, tiled=True
-    )
-    token_gains = lax.psum_scatter(
-        jnp.stack([grad_attention_gain, grad_feedforward_gain]),
-        ("seq", "fsdp"),
-        scatter_dimension=1,
-        tiled=True,
-    )
+    grads_low = jnp.concatenate([grad_query_low, grad_key_low, grad_values], axis=1)
+    attention_terms = contract_rows(inputs_all, grads_low).astype(jnp.bfloat16)
+    head_gains = lax.dynamic_update_slice_in_dim(
+        jnp.zeros((2, width_all), jnp.float32),
+        jnp.stack([grad_query_gain, grad_key_gain]),
+        seq_index * head_width,
+        1,
+    )
+    gain_terms = jnp.concatenate(
+        [head_gains, jnp.stack([grad_attention_gain, grad_feedforward_gain])], axis=0
+    )
+    input_term, attention_grads, output_weight_grad, gain_grads = take_out(
+        [(grad_query_low, query_cols), (grad_key_low, key_cols), (grad_values, value_cols)],
+        attention_terms,
+        output_term,
+        gain_terms,
+    )
+    query_weight_grad, key_weight_grad, value_weight_grad = attention_grads
+    grad_input = grad_hidden + input_term
     return (
         result,
         grad_input.reshape(1, token_count, width_all),
@@ -922,13 +1809,13 @@
         key_weight_grad,
         value_weight_grad,
         output_weight_grad,
-        head_gains[0],
-        head_gains[1],
-        token_gains[0],
+        gain_grads[0],
+        gain_grads[1],
+        gain_grads[2],
         gate_weight_grad,
         up_weight_grad,
         down_weight_grad,
-        token_gains[1],
+        gain_grads[3],
     )
 
 

time: 1230 us -> 843 us (0.69)
  waiting for transfers between devices: 585 us -> 0 us
  Pallas kernels: 157 us -> 664 us
  blocking collectives: 198 us -> 0 us
  local copies, waits for them, and re-layouts: 92.8 us -> 48 us
  starting transfers between devices: 32.6 us -> 0 us
  matrix products: 94.9 us -> 74.3 us
  between operations: 15.5 us -> 1.52 us
    pallas_call x0 -> x6, Pallas kernels: none -> 487 us  [the longest x1 171 us: gather_back(): pl.pallas_call(functools.partial(gather_back_kernel, chips, fsdp_count, l...]
    reduce_scatter x9 -> x0, waiting for transfers between devices: 266 us -> none  [the longest x6 149 us: columns_out(): summed = lax.psum_scatter(swapped, 'fsdp', scatter_dimension=0, tiled=True)]
    unnamed x22 -> x0, waiting for transfers between devices: 157 us -> none
    all_gather x9 -> x0, waiting for transfers between devices: 120 us -> none  [the longest x6 74.5 us: columns_in(): whole = lax.all_gather(part, 'fsdp', axis=0, tiled=True)]
    all_gather x1 -> x0, blocking collectives: 97.2 us -> none  [per_device(): lax.all_gather(jnp.stack([query_gain, key_gain, attention_gain, feedforwa...]
    all_to_all x4 -> x0, blocking collectives: 71.5 us -> none  [columns_in(): lax.all_to_all(weight, 'seq', split_axis=1, concat_axis=0, tiled=True)]
    all_to_all x8 -> x0, waiting for transfers between devices: 42.4 us -> none  [the longest x2 25.9 us: columns_in(): lax.all_to_all(weight, 'seq', split_axis=1, concat_axis=0, tiled=True)]
    all_to_all x8 -> x0, starting transfers between devices: 31.4 us -> none  [the longest x6 24.1 us: columns_out(): lax.all_to_all(summed, 'seq', split_axis=0, concat_axis=1, tiled=True)]
  transfers between devices with their start and end apart: 28 -> 0, of which waited for: 15 -> 0; matrix products, arithmetic and copies ran while one was open for 12% -> 0% of each run, Pallas kernels for 0% -> 0%
where the time goes in v4:
time: 843 us; the launch traced here: 836 us
  Pallas kernels  664 us (79%)
  matrix products  74.3 us (9%)
  local copies, waits for them, and re-layouts  48 us (6%)
  other arithmetic  40.3 us (5%)
    pallas_call x1, Pallas kernels, gather_back(): pl.pallas_call(functools.partial(gather_back_kernel, chips, fsdp_count, l...  171 us
    pallas_call x1, Pallas kernels, bring_in(): pl.pallas_call(functools.partial(bring_in_kernel, chips, fsdp_count), out...  110 us
    pallas_call x1, Pallas kernels, feed_forward(): pl.pallas_call(functools.partial(feed_forward_kernel, chips), out_shape=(...  99.5 us
    pallas_call x1, Pallas kernels, project(): pl.pallas_call(functools.partial(project_kernel, chips, fsdp_count), out_...  98.8 us
    pallas_call x1, Pallas kernels, take_out(): pl.pallas_call(functools.partial(take_out_kernel, chips, fsdp_count), out...  91.8 us
    pallas_call x1, Pallas kernels, feed_forward_back(): pl.pallas_call(functools.partial(feed_forward_back_kernel, chips), out_sh...  77.5 us
    dot_general x5, matrix products, contract_rows(): lax.dot_general(left, right, (((0,), (0,)), ((), ())), preferred_element_...  31.5 us

profile of v4, /device:TPU:0, one launch (start us, length us, event | category | flops | bytes accessed | tf_op | source)
XLA Modules:
  0.0 835.6 jit_solution(2666999776355450)
XLA Ops:
  0.6 1.3 fusion.68.gains_ref
  2.0 110.2 %bring_in.1 = (bf16[8,128,2048]{2,1,0:T(8,128)(2,1)}, bf16[3,8,4,64,256]{4,3,2,1,0:T(8,128)(2,1)}, bf16[4,64,2048]{2,1,0:T(8,128)(2,1)}, bf16[1,8,4,64,1024]{4,3,2,1,0:T(8,128)(2,1)}, bf16[8,4,16,128]{3,2,1,0:T(8,128)(2,1)}) custom-call(bf16[128,2048]{1,0:T(8,128)(2,1)} %bitcast.209, bf16[64,2048]{1,0:T(8,128)(2,1)} %query_ref.1, bf16[64,2048]{1,0:T(8,128)(2,1)} %key_ref.1, ...), custom_call_target="tpu_custom_call" | custom-call | tf_op jit(solution)/shard_map/bring_in/pallas_call | solution.py:1148
  112.2 3.3 fusion.75
  115.5 1.3 multiply_reduce_fusion.8
  116.8 1.3 multiply_reduce_fusion.7
  118.9 7.1 square_sum.1
  129.4 1.4 copy.79
  132.1 1.4 copy.80
  133.4 2.4 copy.81
  135.8 3.0 fusion.59
  138.8 2.0 subtract_convert_fusion
  141.8 1.3 convolution_convert_fusion.3
  143.4 12.7 %while.27 = (s32[]{:T(128)}, bf16[2,512,2,128]{3,2,1,0:T(2,128)(2,1)S(1)}, f32[2,2,512]{2,1,0:T(2,128)S(1)}, s32[2]{0:T(128)S(1)}, s32[1,1024]{1,0:T(1,128)S(1)}...) while((s32[]{:T(128)}, ...), condition=%wide.region_5.6_spmd, body=%wide.region_2.5_spmd.sunk | while | flops 551157248 | bytes 16824524 | solution.py:1687
  146.8 1.2 fusion.125
  148.0 1.7 fusion.126
  152.9 1.2 fusion.125
  154.1 1.7 fusion.126
  156.1 1.1 reshape_reshape.6.attended_ref
  157.3 98.8 %project.1 = (f32[128,2048]{1,0:T(8,128)}, bf16[1,8,4,64,1024]{4,3,2,1,0:T(8,128)(2,1)}, bf16[1,8,4,64,1024]{4,3,2,1,0:T(8,128)(2,1)}) custom-call(bf16[8,128,256]{2,1,0:T(8,128)(2,1)} %reshape_reshape.6.attended_ref, bf16[256,2048]{1,0:T(8,128)(2,1)} %bitcast.231, bf16[64,8192]{1,0:T(8,128)(2,1)} %up_ref.1, bf16[64,8192]{1,0:T(8,128)(2,1)} %down_ref.1), custom_call_target="tpu_custom_call" | custom-call | tf_op jit(solution)/shard_map/project/pallas_call | solution.py:1283
  256.0 1.4 multiply_reduce_fusion.6
  257.5 2.3 fusion.55.hidden_ref
  259.8 99.5 %feed_forward.1 = (f32[128,2048]{1,0:T(8,128)}, f32[8,128,1024]{2,1,0:T(8,128)}, f32[8,128,1024]{2,1,0:T(8,128)}, bf16[8,128,1024]{2,1,0:T(8,128)(2,1)}, bf16[8,128,2048]{2,1,0:T(8,128)(2,1)}) custom-call(bf16[128,2048]{1,0:T(8,128)(2,1)} %fusion.55.hidden_ref, bf16[2048,1024]{1,0:T(8,128)(2,1)} %bitcast.203, bf16[2048,1024]{1,0:T(8,128)(2,1)} %bitcast.205, ...), custom_call_target="tpu_custom_call" | custom-call | tf_op jit(solution)/shard_map/feed_forward/pallas_call | solution.py:604
  359.3 1.4 multiply_reduce_fusion.5
  360.8 1.6 fusion.52
  362.3 2.3 fusion.50.grad_ref
  364.6 77.5 %feed_forward_back.1 = (f32[128,2048]{1,0:T(8,128)}, bf16[8,128,1024]{2,1,0:T(8,128)(2,1)}, bf16[8,128,1024]{2,1,0:T(8,128)(2,1)}, bf16[8,128,2048]{2,1,0:T(8,128)(2,1)}) custom-call(bf16[128,2048]{1,0:T(8,128)(2,1)} %fusion.50.grad_ref, bf16[2048,1024]{1,0:T(8,128)(2,1)} %bitcast.204, bf16[2048,1024]{1,0:T(8,128)(2,1)} %bitcast.206, ...), custom_call_target="tpu_custom_call" | custom-call | tf_op jit(solution)/shard_map/feed_forward_back/pallas_call | solution.py:637
  442.1 9.5 %bitcast_convert_fusion = bf16[2048,1024]{1,0:T(8,128)(2,1)} fusion(bf16[8,128,2048]{2,1,0:T(8,128)(2,1)} %get-tuple-element.167, bf16[8,128,1024]{2,1,0:T(8,128)(2,1)} %get-tuple-element.168), kind=kOutput, calls=%fused_computation.52 | convolution fusion | flops 4297064448 | bytes 10485760 | tf_op jit(solution)/shard_map/dot_general | solution.py:52
  451.6 6.2 bitcast_convert_fusion.1
  457.9 6.2 bitcast_convert_fusion.2
  464.6 1.6 fusion.51
  466.2 171.1 %gather_back.1 = (bf16[8,128,2048]{2,1,0:T(8,128)(2,1)}, f32[64,8192]{1,0:T(8,128)}, f32[64,8192]{1,0:T(8,128)}, f32[64,8192]{1,0:T(8,128)}) custom-call(bf16[128,2048]{1,0:T(8,128)(2,1)} %get-tuple-element.333.local_ref, bf16[8,4,64,1024]{3,2,1,0:T(8,128)(2,1)} %bitcast.212, bf16[8,4,64,1024]{3,2,1,0:T(8,128)(2,1)} %bitcast.211, ...), custom_call_target="tpu_custom_call" | custom-call | tf_op jit(solution)/shard_map/gather_back/pallas_call | solution.py:1359
  637.3 3.8 convolution_convert_fusion.2
  641.1 40.8 %while.28 = (s32[]{:T(128)}, f32[1024,2,128]{0,2,1:T(8,128)}, f32[1024,2,128]{0,2,1:T(8,128)}, bf16[2,512,2,128]{3,1,0,2:T(8,128)(2,1)}, s32[2]{0:T(128)S(1)}, /...) while((s32[]{:T(128)}, f32[1024,2,128]{0,2,1:T(8,128)}, ...), condition=%wide.region_12.13_spmd.clone, body=%wide.region_10.12_spmd.clone.sunk | while | flops 1361051136 | bytes 86813704 | solution.py:1753
  643.1 2.7 fusion.136
  647.7 4.2 multiply_reduce_fusion.10
  652.0 1.4 multiply_convert_fusion.4
  653.4 2.6 fusion.138
  656.0 1.4 fusion.140
  657.4 3.5 fusion.139
  662.9 2.7 fusion.136
  667.6 4.2 multiply_reduce_fusion.10
  671.8 1.4 multiply_convert_fusion.4
  673.2 3.0 fusion.138
  676.2 1.4 fusion.140
  677.6 3.9 fusion.139
  681.9 1.6 copy.58
  684.7 1.9 multiply_subtract_fusion
  688.2 3.0 pad_maximum_fusion.1
  691.2 2.5 copy.59
  693.7 1.5 fusion.53
  696.3 4.6 convolution_convert_fusion.1
  701.5 7.8 mean_sum.1
  710.2 1.6 multiply_convert_fusion.1
  712.0 1.3 convert_element_type.159
  713.4 4.9 convolution_convert_fusion
  718.3 2.0 copy.61
  721.4 1.1 copy.72.refs_2_
  722.6 91.8 %take_out.1 = (f32[128,2048]{1,0:T(8,128)}, f32[64,6144]{1,0:T(8,128)}, f32[64,2048]{1,0:T(8,128)}, f32[8,128]{1,0:T(8,128)}) custom-call(bf16[8,128,256]{2,1,0:T(8,128)(2,1)} %bitcast.224, bf16[8,128,256]{2,1,0:T(8,128)(2,1)} %bitcast.223, bf16[8,128,256]{2,1,0:T(8,128)(2,1)} %copy.72.refs_2_, bf16[2048,256]{1,0:T(8,128)(2,1)} %bitcast.218, ...), custom_call_target="tpu_custom_call" | custom-call | tf_op jit(solution)/shard_map/take_out/pallas_call | solution.py:1498
  814.4 4.2 reshape.448
  818.6 7.5 slice_reduce_fusion
  829.0 1.1 add_bitcast_fusion
  831.5 1.3 copy.125
  832.8 1.3 copy.126
  834.1 1.3 copy.127
  (196 shorter events, 25.7 us)
Async XLA Ops:
  112.2 3.3 copy-start.42
  115.4 1.3 copy-start.21
  115.4 1.4 copy-start.20
  116.8 11.1 %copy-start.10 = (f32[1024,256]{0,1:T(8,128)}, f32[1024,256]{0,1:T(8,128)S(1)}, u32[]{:S(2)}) copy-start(f32[1024,256]{0,1:T(8,128)S(1)} %get-tuple-element.357) | copy-start | bytes 3145732
  118.2 12.8 %copy-start.12 = (f32[1024,256]{0,1:T(8,128)}, f32[1024,256]{0,1:T(8,128)S(1)}, u32[]{:S(2)}) copy-start(f32[1024,256]{0,1:T(8,128)S(1)} %get-tuple-element.355) | copy-start | bytes 3145732
  126.7 1.5 copy-start.33
  126.7 4.3 copy-start.35
  127.9 3.1 copy-start.37
  127.9 3.1 copy-start.39
  138.8 2.3 copy-start.16
  138.8 2.6 copy-start.19
  138.8 3.0 copy-start.43
  141.8 1.6 copy-start.30
  156.1 203.2 %copy-start.32 = (bf16[2,512,2,128]{3,2,1,0:T(2,128)(2,1)}, bf16[2,512,2,128]{3,2,1,0:T(2,128)(2,1)S(1)}, u32[]{:S(2)}) copy-start(bf16[2,512,2,128]{3,2,1,0:T(2,128)(2,1)S(1)} %get-tuple-element.153) | copy-start | bytes 1572868
  156.1 101.4 %copy-start.18 = (bf16[1,128,2048]{2,1,0:T(8,128)(2,1)S(1)}, bf16[1,128,2048]{2,1,0:T(8,128)(2,1)}, u32[]{:S(2)}) copy-start(bf16[1,128,2048]{2,1,0:T(8,128)(2,1)} %param.18) | copy-start | bytes 1572868
  259.8 101.0 %copy-start.8 = (bf16[1,128,2048]{2,1,0:T(8,128)(2,1)S(1)}, bf16[1,128,2048]{2,1,0:T(8,128)(2,1)}, u32[]{:S(2)}) copy-start(bf16[1,128,2048]{2,1,0:T(8,128)(2,1)} %param.31) | copy-start | bytes 1572868
  442.1 9.5 %copy-start.45 = (bf16[8,128,2048]{2,1,0:T(8,128)(2,1)S(1)}, bf16[8,128,2048]{2,1,0:T(8,128)(2,1)}, u32[]{:S(2)}) copy-start(bf16[8,128,2048]{2,1,0:T(8,128)(2,1)} %get-tuple-element.164) | copy-start | bytes 12582916
  442.1 9.5 %copy-start.47 = (bf16[8,128,1024]{2,1,0:T(8,128)(2,1)S(1)}, bf16[8,128,1024]{2,1,0:T(8,128)(2,1)}, u32[]{:S(2)}) copy-start(bf16[8,128,1024]{2,1,0:T(8,128)(2,1)} %get-tuple-element.166) | copy-start | bytes 6291460
  451.6 6.2 copy-start.46
  457.9 6.2 copy-start.6
  457.9 6.2 copy-start.14
  457.9 6.7 copy-start.7
  641.1 10.8 %copy-start.2 = (bf16[1024,2,128]{2,0,1:T(8,128)(2,1)}, bf16[1024,2,128]{2,0,1:T(8,128)(2,1)S(1)}, u32[]{:S(2)}) copy-start(bf16[1024,2,128]{2,0,1:T(8,128)(2,1)S(1)} %get-tuple-element.574) | copy-start | bytes 1572868 | tf_op jit(solution)/shard_map/while
  641.1 10.8 %copy-start.4 = (bf16[1024,2,128]{2,0,1:T(8,128)(2,1)}, bf16[1024,2,128]{2,0,1:T(8,128)(2,1)S(1)}, u32[]{:S(2)}) copy-start(bf16[1024,2,128]{2,0,1:T(8,128)(2,1)S(1)} %get-tuple-element.580) | copy-start | bytes 1572868 | tf_op jit(solution)/shard_map/while
  641.2 10.8 %copy-start.22 = (bf16[1024,2,128]{0,2,1:T(8,128)(2,1)}, bf16[1024,2,128]{0,2,1:T(8,128)(2,1)S(1)}, u32[]{:S(2)}) copy-start(bf16[1024,2,128]{0,2,1:T(8,128)(2,1)S(1)} %get-tuple-element.579) | copy-start | bytes 1572868 | tf_op jit(solution)/shard_map/while
  647.7 4.3 copy-start
  653.4 4.1 copy-start.1
  657.4 3.5 copy-start.3
  657.4 3.5 copy-start.5
  657.4 3.5 copy-start.23
  661.0 10.8 %copy-start.2 = (bf16[1024,2,128]{2,0,1:T(8,128)(2,1)}, bf16[1024,2,128]{2,0,1:T(8,128)(2,1)S(1)}, u32[]{:S(2)}) copy-start(bf16[1024,2,128]{2,0,1:T(8,128)(2,1)S(1)} %get-tuple-element.574) | copy-start | bytes 1572868 | tf_op jit(solution)/shard_map/while
  661.0 10.8 %copy-start.4 = (bf16[1024,2,128]{2,0,1:T(8,128)(2,1)}, bf16[1024,2,128]{2,0,1:T(8,128)(2,1)S(1)}, u32[]{:S(2)}) copy-start(bf16[1024,2,128]{2,0,1:T(8,128)(2,1)S(1)} %get-tuple-element.580) | copy-start | bytes 1572868 | tf_op jit(solution)/shard_map/while
  661.0 10.8 %copy-start.22 = (bf16[1024,2,128]{0,2,1:T(8,128)(2,1)}, bf16[1024,2,128]{0,2,1:T(8,128)(2,1)S(1)}, u32[]{:S(2)}) copy-start(bf16[1024,2,128]{0,2,1:T(8,128)(2,1)S(1)} %get-tuple-element.579) | copy-start | bytes 1572868 | tf_op jit(solution)/shard_map/while
  667.6 4.2 copy-start
  673.2 4.4 copy-start.1
  677.6 3.9 copy-start.3
  677.6 3.9 copy-start.5
  677.6 3.9 copy-start.23
  681.9 2.8 copy-start.17
  681.9 2.8 copy-start.24
  686.7 1.2 copy-start.11
  686.7 1.2 copy-start.34
  686.7 1.2 copy-start.38
  687.9 5.8 copy-start.13
  687.9 5.8 copy-start.36
  687.9 5.8 copy-start.40
  709.3 4.1 copy-start.44
  711.8 6.5 copy-start.25
  814.3 14.6 %copy-start.9 = (bf16[1,128,2048]{2,1,0:T(8,128)(2,1)S(1)}, bf16[1,128,2048]{2,1,0:T(8,128)(2,1)}, u32[]{:S(2)}) copy-start(bf16[1,128,2048]{2,1,0:T(8,128)(2,1)} %param.31) | copy-start | bytes 1572868
  814.4 14.6 %copy-start.15 = (f32[128,2048]{1,0:T(8,128)S(1)}, f32[128,2048]{1,0:T(8,128)}, u32[]{:S(2)}) copy-start(f32[128,2048]{1,0:T(8,128)} %get-tuple-element.162) | copy-start | bytes 3145732
  814.4 14.6 %copy-start.29 = (f32[128,2048]{1,0:T(8,128)S(1)}, f32[128,2048]{1,0:T(8,128)}, u32[]{:S(2)}) copy-start(f32[128,2048]{1,0:T(8,128)} %get-tuple-element.173) | copy-start | bytes 3145732
  826.1 4.1 copy-start.41
  826.1 4.6 copy-start.31
  826.1 5.4 copy-start.28
  829.0 3.8 copy-start.27
  831.5 2.6 copy-start.26

commit v5 on v4

--- a/solution.py
+++ b/solution.py
@@ -825,6 +825,10 @@
                     self.half(owner, side).wait_send()
 
 
+AHEAD = 2
+LAG = 3
+
+
 class Collect:
     def __init__(self, cross, terms, side_in, half_out, half_in, row_out, row_in, side_send, side_recv, half_send, half_recv, row_send, row_recv):
         self.cross, self.terms = cross, terms
@@ -834,10 +838,11 @@
         self.half_send, self.half_recv = half_send, half_recv
         self.row_send, self.row_recv = row_send, row_recv
         self.rows, self.columns = terms.shape[-2:]
-        self.kinds = terms.shape[:-4]
+        self.items = terms.shape[0] * cross.seq_count
 
     @staticmethod
-    def scratch(seq_count, fsdp_count, rows, columns):
+    def scratch(kinds, seq_count, fsdp_count, rows, columns):
+        seq_count = kinds * seq_count
         dma = pltpu.SemaphoreType.DMA
         vmem = pltpu.VMEM
         bf16 = jnp.bfloat16
@@ -869,127 +874,160 @@
     def half_rows(self, side):
         return pl.ds(side * (self.rows // 2), self.rows // 2)
 
-    def side(self, owner, side, which):
+    def side(self, turn, side, which):
         cross = self.cross
         if not cross.square:
             return cross.remote(
-                self.terms.at[owner, cross.sides[side]],
-                self.side_in.at[owner, side],
-                self.side_send.at[owner, side, 0],
-                self.side_recv.at[owner, side, 0],
+                self.terms.at[(*self.place(turn), cross.sides[side])],
+                self.side_in.at[turn, side],
+                self.side_send.at[turn, side, 0],
+                self.side_recv.at[turn, side, 0],
                 cross.seq,
                 cross.sides[side],
             )
         target = cross.sides[side] if which == 0 else cross.corner
         return cross.remote(
-            self.terms.at[owner, target, self.half_rows(side)],
-            self.side_in.at[owner, side, which],
-            self.side_send.at[owner, side, which],
-            self.side_recv.at[owner, side, which],
+            self.terms.at[(*self.place(turn), target, self.half_rows(side))],
+            self.side_in.at[turn, side, which],
+            self.side_send.at[turn, side, which],
+            self.side_recv.at[turn, side, which],
             cross.seq,
             cross.sides[side],
         )
 
-    def half(self, owner, side):
+    def half(self, turn, side):
         cross = self.cross
         return cross.remote(
-            self.half_out.at[owner, side],
-            self.half_in.at[owner, side],
-            self.half_send.at[owner, side],
-            self.half_recv.at[owner, side],
+            self.half_out.at[turn, side],
+            self.half_in.at[turn, side],
+            self.half_send.at[turn, side],
+            self.half_recv.at[turn, side],
             cross.seq,
             cross.sides[1 - side],
         )
 
-    def row(self, step):
+    def row(self, turn):
         cross = self.cross
         return cross.remote(
-            self.row_out.at[step],
-            self.row_in.at[step],
-            self.row_send.at[step],
-            self.row_recv.at[step],
-            cross.seq_peer(step),
+            self.row_out.at[turn],
+            self.row_in.at[turn],
+            self.row_send.at[turn],
+            self.row_recv.at[turn],
+            self.place(turn)[1],
             cross.fsdp,
         )
 
-    def owner(self, turn):
-        return self.cross.seq_peer(turn + 1)
+    def place(self, turn):
+        count = self.cross.seq_count
+        return turn // count, self.cross.seq_peer(turn % count + 1)
+
+    def is_own(self, turn):
+        return turn % self.cross.seq_count == self.cross.seq_count - 1
 
     @property
     def ways(self):
         return range(2) if self.cross.square else range(1)
 
     def send(self, turn):
-        owner = self.owner(turn)
         for which in reversed(self.ways):
             for side in range(len(self.cross.sides)):
-                self.side(owner, side, which).start()
+                self.side(turn, side, which).start()
 
     def middle(self, turn):
         if not self.cross.square:
             return
-        cross, owner = self.cross, self.owner(turn)
+        cross = self.cross
+        kind, owner = self.place(turn)
         for side in range(2):
-            self.side(owner, side, 1).wait_recv()
-            mine = self.terms[owner, cross.sides[1 - side], self.half_rows(side)]
-            self.half_out[owner, side] = (
-                mine.astype(jnp.float32) + self.side_in[owner, side, 1].astype(jnp.float32)
+            self.side(turn, side, 1).wait_recv()
+            mine = self.terms[kind, owner, cross.sides[1 - side], self.half_rows(side)]
+            self.half_out[turn, side] = (
+                mine.astype(jnp.float32) + self.side_in[turn, side, 1].astype(jnp.float32)
             ).astype(jnp.bfloat16)
-            self.half(owner, side).start()
+            self.half(turn, side).start()
 
     def totals(self, turn):
-        cross, owner = self.cross, self.owner(turn)
+        cross = self.cross
+        kind, owner = self.place(turn)
         found = []
         if cross.square:
             for side in range(2):
-                self.side(owner, side, 0).wait_recv()
-                self.half(owner, side).wait_recv()
+                self.side(turn, side, 0).wait_recv()
+                self.half(turn, side).wait_recv()
                 rows = self.half_rows(side)
-                total = self.terms[owner, cross.fsdp, rows].astype(jnp.float32)
-                total = total + self.side_in[owner, side, 0].astype(jnp.float32)
-                total = total + self.half_in[owner, side].astype(jnp.float32)
+                total = self.terms[kind, owner, cross.fsdp, rows].astype(jnp.float32)
+                total = total + self.side_in[turn, side, 0].astype(jnp.float32)
+                total = total + self.half_in[turn, side].astype(jnp.float32)
                 found.append((rows, total))
         else:
-            total = self.terms[owner, cross.fsdp].astype(jnp.float32)
+            total = self.terms[kind, owner, cross.fsdp].astype(jnp.float32)
             for side in range(len(cross.sides)):
-                self.side(owner, side, 0).wait_recv()
-                total = total + self.side_in[owner, side].astype(jnp.float32)
+                self.side(turn, side, 0).wait_recv()
+                total = total + self.side_in[turn, side].astype(jnp.float32)
             found.append((pl.ds(0, self.rows), total))
         return found
 
     def ship(self, turn):
-        for rows, total in self.totals(turn):
-            self.row_out[turn + 1, rows] = total.astype(jnp.bfloat16)
-        self.row(turn + 1).start()
-
-    def block(self, owner):
-        return pl.ds(pl.multiple_of(owner * self.columns, 128), self.columns)
-
-    def keep(self, result):
-        cross = self.cross
-        for rows, total in self.totals(cross.seq_count - 1):
-            result[rows, self.block(cross.seq)] = total
-
-    def receive(self, step, result):
-        cross = self.cross
-        self.row(step).wait_recv()
-        owner = (cross.seq - step + cross.seq_count) % cross.seq_count
-        result[:, self.block(owner)] = self.row_in[step].astype(jnp.float32)
+        own = self.is_own(turn)
+
+        @pl.when(own)
+        def _():
+            for rows, total in self.totals(turn):
+                self.row_in[turn, rows] = total.astype(jnp.bfloat16)
+
+        @pl.when(jnp.logical_not(own))
+        def _():
+            for rows, total in self.totals(turn):
+                self.row_out[turn, rows] = total.astype(jnp.bfloat16)
+            self.row(turn).start()
+
+    def beat(self, turn):
+        ahead = turn + AHEAD
+
+        @pl.when(ahead < self.items)
+        def _():
+            self.send(ahead)
+
+        @pl.when(turn < self.items)
+        def _():
+            self.middle(turn)
+
+        @pl.when(turn >= LAG)
+        def _():
+            self.ship(turn - LAG)
+
+    def begin(self):
+        for turn in range(min(AHEAD, self.items)):
+            self.send(turn)
+
+    @property
+    def beats(self):
+        return self.items + LAG
+
+    def receive(self, turn, put):
+        count = self.cross.seq_count
+
+        @pl.when(jnp.logical_not(self.is_own(turn)))
+        def _():
+            self.row(turn).wait_recv()
+
+        sender = (self.cross.seq - turn % count - 1 + count) % count
+        put(turn // count, sender, self.row_in[turn].astype(jnp.float32))
 
     def finish(self):
         cross = self.cross
 
-        @pl.loop(0, cross.seq_count)
-        def _(owner):
+        @pl.loop(0, self.items)
+        def _(turn):
             for side in range(len(cross.sides)):
                 for which in self.ways:
-                    self.side(owner, side, which).wait_send()
+                    self.side(turn, side, which).wait_send()
                 if cross.square:
-                    self.half(owner, side).wait_send()
-
-        @pl.loop(1, cross.seq_count)
-        def _(step):
-            self.row(step).wait_send()
+                    self.half(turn, side).wait_send()
+
+            @pl.when(jnp.logical_not(self.is_own(turn)))
+            def _():
+                self.row(turn).wait_send()
 
 
 def bring_in_kernel(
@@ -1060,9 +1098,9 @@
     for step in range(1, seq_count):
         gain_row(step).start()
     attention.start()
+    gate.start()
     gather.blocks[line.place * 2 + line.core] = inputs_ref[...]
     gather.send(line.place)
-    gate.start()
     gains[seq, fsdp] = gains_ref[...]
     outputs[fsdp] = output_ref[...]
     attention.own()
@@ -1075,27 +1113,31 @@
         gain_row(step).wait_recv()
         for peer in range(1, fsdp_count):
             gain_column(attention.owner(step), peer).start()
+        attention.relay(step - 1)
 
     gate.own()
+    attention.relay(seq_count - 1)
+    gather.step(0)
+
+    @pl.loop(1, seq_count)
+    def _(step):
+        gate.take(step)
+        gate.relay(step - 1)
+
+        @pl.when((step % 2 == 0) & (step > 2))
+        def _():
+            gather.step(step // 2 - 1)
+
     for step in range(1, fsdp_count):
         output_copy(step).start()
-
-    @pl.loop(0, chips)
-    def _(step):
-        gather.step(step)
-        for late in range(2):
-            attention.relay(2 * step + late)
-
-            @pl.when(2 * step + late > 0)
-            def _():
-                gate.take(2 * step + late)
-
+    gate.relay(seq_count - 1)
+    if chips > 1:
+        gather.step(chips - 1)
     inputs_store = pltpu.make_async_copy(gather.blocks, inputs_out, store_sem.at[0])
     inputs_store.start()
 
     @pl.loop(0, seq_count)
     def _(step):
-        gate.relay(step)
         attention.settle(step)
         for peer in range(1, fsdp_count):
             gain_column(step, peer).wait_recv()
@@ -1224,13 +1266,12 @@
     down = Spread(cross, (down_ref,), *comm[count + 7 :])
     greet_cross(cross.seq_count, fsdp_count)
     up.start()
+    down.start()
     up.own()
 
     @pl.loop(0, chips)
     def _(step):
         product_terms(scatter, [(attended_ref, output_ref, False)], line.order(chips - 1 - step))
-
-    down.start()
 
     @pl.loop(1, cross.seq_count)
     def _(step):
@@ -1238,21 +1279,22 @@
         up.relay(step - 1)
 
     down.own()
-
-    @pl.loop(0, chips)
+    up.relay(cross.seq_count - 1)
+    scatter.hop(0)
+
+    @pl.loop(1, cross.seq_count)
     def _(step):
-        scatter.hop(step)
-        for late in range(2):
-
-            @pl.when(2 * step + late > 0)
-            def _():
-                down.take(2 * step + late)
-
-    up.relay(cross.seq_count - 1)
+        down.take(step)
+        down.relay(step - 1)
+
+        @pl.when(step % 2 == 0)
+        def _():
+            scatter.hop(step // 2)
+
+    down.relay(cross.seq_count - 1)
 
     @pl.loop(0, cross.seq_count)
     def _(step):
-        down.relay(step)
         up.settle(step)
 
     up_store = pltpu.make_async_copy(up.weights, up_out, store_sem.at[0])
@@ -1295,16 +1337,15 @@
 
 
 def gather_back_kernel(chips, fsdp_count, count, local_ref, *refs):
-    terms, refs = refs[:count], refs[count:]
-    out, results, store_sem, comm = refs[0], refs[1 : 1 + count], refs[1 + count], refs[2 + count :]
+    sources, refs = refs[:count], refs[count:]
+    out, results, refs = refs[0], refs[1 : 1 + count], refs[1 + count :]
+    terms, load_sem, store_sem, comm = refs[0], refs[1], refs[2], refs[3:]
     line = Line(chips)
     cross = Cross(2 * chips, fsdp_count)
     gather = Gather(line, *comm[:5])
-    collects = [
-        Collect(cross, terms[kind], *comm[5 + 11 * kind : 16 + 11 * kind]) for kind in range(count)
-    ]
-    seq_count = cross.seq_count
-    greet_cross(seq_count, fsdp_count)
+    collect = Collect(cross, terms, *comm[5:])
+    copies = load([(sources[kind], terms.at[kind], load_sem.at[kind]) for kind in range(count)])
+    greet_cross(cross.seq_count, fsdp_count)
     gather.blocks[line.place * 2 + line.core] = local_ref[...]
     gather.send(line.place)
 
@@ -1312,36 +1353,32 @@
         pair = pl.ds(chip * 2, 2)
         return pltpu.make_async_copy(gather.blocks.at[pair], out.at[pair], store_sem.at[chip])
 
-    for collect in collects:
-
-        @pl.loop(0, seq_count)
-        def _(turn):
-            collect.send(turn)
-
+    for copy in copies:
+        copy.wait()
+    collect.begin()
     store(gather.step(0)).start()
-    for kind, collect in enumerate(collects):
-        collect.middle(0)
-
-        @pl.loop(1, seq_count)
-        def _(turn):
-            collect.middle(turn)
-            collect.ship(turn - 1)
-            if kind == 0:
-
-                @pl.when((turn % 2 == 1) & ((turn + 1) // 2 < chips))
-                def _():
-                    store(gather.step((turn + 1) // 2)).start()
-
-        collect.keep(results[kind])
-
-    for kind, collect in enumerate(collects):
-
-        @pl.loop(1, seq_count)
-        def _(step):
-            collect.receive(step, results[kind])
-
-        collect.finish()
-
+
+    @pl.loop(0, collect.beats)
+    def _(turn):
+        collect.beat(turn)
+
+        @pl.when((turn % 3 == 2) & (turn // 3 + 1 < chips))
+        def _():
+            store(gather.step(turn // 3 + 1)).start()
+
+    block = terms.shape[-1]
+
+    @pl.loop(0, cross.seq_count)
+    def _(turn):
+        for kind in range(count):
+
+            def put(_, sender, value):
+                columns = pl.ds(pl.multiple_of(sender * block, 128), block)
+                results[kind][:, columns] = value
+
+            collect.receive(kind * cross.seq_count + turn, put)
+
+    collect.finish()
     gather.finish()
 
     @pl.loop(0, chips)
@@ -1354,17 +1391,22 @@
     slots = lax.axis_size("seq")
     fsdp_count = lax.axis_size("fsdp")
     chips = slots // 2
+    count = len(terms)
     own = terms[0].shape[0] // (slots * fsdp_count)
     units = terms[0].shape[1]
     found = pl.pallas_call(
-        functools.partial(gather_back_kernel, chips, fsdp_count, len(terms)),
+        functools.partial(gather_back_kernel, chips, fsdp_count, count),
         out_shape=(jax.ShapeDtypeStruct((slots, rows, width), jnp.bfloat16),)
-        + (jax.ShapeDtypeStruct((own, units * slots), jnp.float32),) * len(terms),
-        in_specs=[whole_spec()] * (1 + len(terms)),
-        out_specs=(far_spec(),) + (whole_spec(),) * len(terms),
-        scratch_shapes=[pltpu.SemaphoreType.DMA((chips,))]
+        + (jax.ShapeDtypeStruct((own, units * slots), jnp.float32),) * count,
+        in_specs=[whole_spec()] + [far_spec()] * count,
+        out_specs=(far_spec(),) + (whole_spec(),) * count,
+        scratch_shapes=[
+            pltpu.VMEM((count, slots, fsdp_count, own, units), jnp.bfloat16),
+            pltpu.SemaphoreType.DMA((count,)),
+            pltpu.SemaphoreType.DMA((chips,)),
+        ]
         + Gather.scratch(chips, rows, width)
-        + Collect.scratch(slots, fsdp_count, own, units) * len(terms),
+        + Collect.scratch(count, slots, fsdp_count, own, units),
         compiler_params=line_params(6),
         name="gather_back",
     )(local, *[term.reshape(slots, fsdp_count, own, units) for term in terms])
@@ -1378,7 +1420,7 @@
 ):
     lefts, rights, refs = refs[:3], refs[3:6], refs[6:]
     terms, output_ref, gains_ref, refs = refs[0], refs[1], refs[2], refs[3:]
-    result, weight_out, output_out, gains_out, refs = refs[0], refs[1], refs[2], refs[3], refs[4:]
+    result, weight_outs, output_out, gains_out, refs = refs[0], refs[1:4], refs[4], refs[5], refs[6:]
     output_in, gain_in, gain_out, gain_rows, refs = refs[0], refs[1], refs[2], refs[3], refs[4:]
     output_send, output_recv, gain_send, gain_recv, gain_row_send, gain_row_recv = refs[:6]
     comm = refs[6:]
@@ -1420,12 +1462,7 @@
     for step in range(1, fsdp_count):
         gain_copy(step).start()
 
-    @pl.loop(0, seq_count)
-    def _(turn):
-        collect.send(turn)
-
-    for step in range(1, fsdp_count):
-        output_copy(step).start()
+    collect.begin()
 
     @pl.loop(0, chips)
     def _(step):
@@ -1443,18 +1480,19 @@
     for step in range(1, seq_count):
         gain_row(step).start()
 
-    collect.middle(0)
-
-    @pl.loop(1, seq_count)
+    @pl.loop(0, collect.beats)
     def _(turn):
-        collect.middle(turn)
-        collect.ship(turn - 1)
-
-        @pl.when(turn % 2 == 1)
+        collect.beat(turn)
+
+        @pl.when(turn == seq_count - AHEAD)
+        def _():
+            for step in range(1, fsdp_count):
+                output_copy(step).start()
+
+        @pl.when((turn % 2 == 0) & (turn < seq_count))
         def _():
             scatter.hop(turn // 2)
 
-    collect.keep(weight_out)
     total = output_ref[fsdp].astype(jnp.float32)
     for step in range(1, fsdp_count):
         output_copy(step).wait_recv()
@@ -1467,9 +1505,16 @@
         total = total + gain_rows[step]
     gains_out[...] = total
 
-    @pl.loop(1, seq_count)
-    def _(step):
-        collect.receive(step, weight_out)
+    columns = terms.shape[-1] // 3
+
+    def put(_, sender, value):
+        block = pl.ds(pl.multiple_of(sender * columns, 128), columns)
+        for kind in range(3):
+            weight_outs[kind][:, block] = value[:, kind * columns : (kind + 1) * columns]
+
+    @pl.loop(0, seq_count)
+    def _(turn):
+        collect.receive(turn, put)
 
     scatter.finish()
     collect.finish()
@@ -1495,16 +1540,18 @@
     gains = gain_terms.reshape(kinds, slots, fsdp_count, own).transpose(2, 1, 0, 3)
     lanes = pl.cdiv(own, 128) * 128
     gains = jnp.pad(gains, ((0, 0), (0, 0), (0, 8 - kinds), (0, lanes - own)))
-    result, weights, output, gains = pl.pallas_call(
+    result, query, key, value, output, gains = pl.pallas_call(
         functools.partial(take_out_kernel, chips, fsdp_count),
         out_shape=(
             jax.ShapeDtypeStruct((rows, width), f32),
-            jax.ShapeDtypeStruct((own, columns * slots), f32),
+            jax.ShapeDtypeStruct((own, columns // 3 * slots), f32),
+            jax.ShapeDtypeStruct((own, columns // 3 * slots), f32),
+            jax.ShapeDtypeStruct((own, columns // 3 * slots), f32),
             jax.ShapeDtypeStruct((own, width), f32),
             jax.ShapeDtypeStruct((8, lanes), f32),
         ),
         in_specs=[whole_spec()] * 9,
-        out_specs=(whole_spec(),) * 4,
+        out_specs=(whole_spec(),) * 6,
         scratch_shapes=[
             pltpu.VMEM((fsdp_count, own, width), bf16),
             pltpu.VMEM((fsdp_count, slots, 8, lanes), f32),
@@ -1518,19 +1565,17 @@
             dma((slots,)),
         ]
         + Scatter.scratch(chips, rows, width)
-        + Collect.scratch(slots, fsdp_count, own, columns),
+        + Collect.scratch(1, slots, fsdp_count, own, columns),
         compiler_params=line_params(4),
         name="take_out",
     )(
         *[left.reshape(slots, rows, -1) for left, _ in pairs],
         *[right for _, right in pairs],
-        terms.reshape(slots, fsdp_count, own, columns),
+        terms.reshape(1, slots, fsdp_count, own, columns),
         output_term.reshape(fsdp_count, own, width),
         gains,
     )
-    weights = weights.reshape(own, slots, 3, columns // 3)
-    weights = [weights[:, :, kind].reshape(own, -1) for kind in range(3)]
-    return result, weights, output, gains[:kinds, :own]
+    return result, (query, key, value), output, gains[:kinds, :own]
 
 
 def row_sum_kernel(seq_count, local_ref, result, every, send, recv):

time: 843 us -> 746 us (0.88)
  Pallas kernels: 664 us -> 573 us
  local copies, waits for them, and re-layouts: 48 us -> 37.9 us
    pallas_call x1, Pallas kernels: 171 us -> 127 us  [gather_back(): pl.pallas_call(functools.partial(gather_back_kernel, chips, fsdp_count, c...]
    pallas_call x1, Pallas kernels: 91.8 us -> 74.8 us  [take_out(): pl.pallas_call(functools.partial(take_out_kernel, chips, fsdp_count), out...]
    pallas_call x1, Pallas kernels: 99.5 us -> 86 us  [feed_forward(): pl.pallas_call(functools.partial(feed_forward_kernel, chips), out_shape=(...]
    pallas_call x1, Pallas kernels: 110 us -> 99.3 us  [bring_in(): pl.pallas_call(functools.partial(bring_in_kernel, chips, fsdp_count), out...]
where the time goes in v5:
time: 746 us; the launch traced here: 736 us
  Pallas kernels  573 us (77%)
  matrix products  74.3 us (10%)
  other arithmetic  41.7 us (6%)
  local copies, waits for them, and re-layouts  37.9 us (5%)
  loops' own time  7.55 us (1%)
    pallas_call x1, Pallas kernels, gather_back(): pl.pallas_call(functools.partial(gather_back_kernel, chips, fsdp_count, c...  127 us
    pallas_call x1, Pallas kernels, bring_in(): pl.pallas_call(functools.partial(bring_in_kernel, chips, fsdp_count), out...  99.3 us
    pallas_call x1, Pallas kernels, project(): pl.pallas_call(functools.partial(project_kernel, chips, fsdp_count), out_...  92.5 us
    pallas_call x1, Pallas kernels, feed_forward(): pl.pallas_call(functools.partial(feed_forward_kernel, chips), out_shape=(...  86 us
    pallas_call x1, Pallas kernels, feed_forward_back(): pl.pallas_call(functools.partial(feed_forward_back_kernel, chips), out_sh...  76.7 us
    pallas_call x1, Pallas kernels, take_out(): pl.pallas_call(functools.partial(take_out_kernel, chips, fsdp_count), out...  74.8 us
    dot_general x5, matrix products, contract_rows(): lax.dot_general(left, right, (((0,), (0,)), ((), ())), preferred_element_...  31.5 us
    pallas_call x2, Pallas kernels, row_sum(): pl.pallas_call(functools.partial(row_sum_kernel, slots), out_shape=jax.Sh...  16.6 us

profile of v5, /device:TPU:0, one launch (start us, length us, event | category | flops | bytes accessed | tf_op | source)
XLA Modules:
  0.0 736.3 jit_solution(14475201577964083403)
XLA Ops:
  0.6 1.3 fusion.68.gains_ref
  2.0 99.3 %bring_in.1 = (bf16[8,128,2048]{2,1,0:T(8,128)(2,1)}, bf16[3,8,4,64,256]{4,3,2,1,0:T(8,128)(2,1)}, bf16[4,64,2048]{2,1,0:T(8,128)(2,1)}, bf16[1,8,4,64,1024]{4,3,2,1,0:T(8,128)(2,1)}, bf16[8,4,16,128]{3,2,1,0:T(8,128)(2,1)}) custom-call(bf16[128,2048]{1,0:T(8,128)(2,1)} %bitcast.203, bf16[64,2048]{1,0:T(8,128)(2,1)} %query_ref.1, bf16[64,2048]{1,0:T(8,128)(2,1)} %key_ref.1, ...), custom_call_target="tpu_custom_call" | custom-call | tf_op jit(solution)/shard_map/bring_in/pallas_call | solution.py:1190
  101.3 3.3 fusion.75
  104.5 1.3 multiply_reduce_fusion.8
  105.9 1.3 multiply_reduce_fusion.7
  108.0 7.3 square_sum.1
  118.7 1.4 copy.79
  121.4 1.4 copy.80
  122.8 2.4 copy.81
  125.2 3.0 fusion.59
  128.1 2.0 subtract_convert_fusion
  131.1 1.3 convolution_convert_fusion.3
  132.8 12.6 %while.27 = (s32[]{:T(128)}, bf16[2,512,2,128]{3,2,1,0:T(2,128)(2,1)S(1)}, f32[2,2,512]{2,1,0:T(2,128)S(1)}, s32[2]{0:T(128)S(1)}, s32[1,1024]{1,0:T(1,128)S(1)}...) while((s32[]{:T(128)}, ...), condition=%wide.region_5.6_spmd, body=%wide.region_2.5_spmd.sunk | while | flops 551157248 | bytes 16824524 | solution.py:1732
  136.1 1.2 fusion.125
  137.3 1.7 fusion.126
  142.2 1.2 fusion.125
  143.4 1.7 fusion.126
  145.4 1.1 reshape_reshape.6.attended_ref
  146.5 92.5 %project.1 = (f32[128,2048]{1,0:T(8,128)}, bf16[1,8,4,64,1024]{4,3,2,1,0:T(8,128)(2,1)}, bf16[1,8,4,64,1024]{4,3,2,1,0:T(8,128)(2,1)}) custom-call(bf16[8,128,256]{2,1,0:T(8,128)(2,1)} %reshape_reshape.6.attended_ref, bf16[256,2048]{1,0:T(8,128)(2,1)} %bitcast.222, bf16[64,8192]{1,0:T(8,128)(2,1)} %up_ref.1, bf16[64,8192]{1,0:T(8,128)(2,1)} %down_ref.1), custom_call_target="tpu_custom_call" | custom-call | tf_op jit(solution)/shard_map/project/pallas_call | solution.py:1325
  239.1 1.4 multiply_reduce_fusion.6
  240.5 2.3 fusion.55.hidden_ref
  242.8 86.0 %feed_forward.1 = (f32[128,2048]{1,0:T(8,128)}, f32[8,128,1024]{2,1,0:T(8,128)}, f32[8,128,1024]{2,1,0:T(8,128)}, bf16[8,128,1024]{2,1,0:T(8,128)(2,1)}, bf16[8,128,2048]{2,1,0:T(8,128)(2,1)}) custom-call(bf16[128,2048]{1,0:T(8,128)(2,1)} %fusion.55.hidden_ref, bf16[2048,1024]{1,0:T(8,128)(2,1)} %bitcast.197, bf16[2048,1024]{1,0:T(8,128)(2,1)} %bitcast.199, ...), custom_call_target="tpu_custom_call" | custom-call | tf_op jit(solution)/shard_map/feed_forward/pallas_call | solution.py:604
  328.9 1.4 multiply_reduce_fusion.5
  330.3 1.6 fusion.52
  331.9 2.3 fusion.50.grad_ref
  334.2 76.7 %feed_forward_back.1 = (f32[128,2048]{1,0:T(8,128)}, bf16[8,128,1024]{2,1,0:T(8,128)(2,1)}, bf16[8,128,1024]{2,1,0:T(8,128)(2,1)}, bf16[8,128,2048]{2,1,0:T(8,128)(2,1)}) custom-call(bf16[128,2048]{1,0:T(8,128)(2,1)} %fusion.50.grad_ref, bf16[2048,1024]{1,0:T(8,128)(2,1)} %bitcast.198, bf16[2048,1024]{1,0:T(8,128)(2,1)} %bitcast.200, ...), custom_call_target="tpu_custom_call" | custom-call | tf_op jit(solution)/shard_map/feed_forward_back/pallas_call | solution.py:637
  410.9 9.5 %bitcast_convert_fusion = bf16[2048,1024]{1,0:T(8,128)(2,1)} fusion(bf16[8,128,2048]{2,1,0:T(8,128)(2,1)} %get-tuple-element.169, bf16[8,128,1024]{2,1,0:T(8,128)(2,1)} %get-tuple-element.170), kind=kOutput, calls=%fused_computation.52 | convolution fusion | flops 4297064448 | bytes 10485760 | tf_op jit(solution)/shard_map/dot_general | solution.py:52
  420.4 6.3 bitcast_convert_fusion.1
  426.7 6.2 bitcast_convert_fusion.2
  433.4 1.6 fusion.51
  435.0 127.3 %gather_back.1 = (bf16[8,128,2048]{2,1,0:T(8,128)(2,1)}, f32[64,8192]{1,0:T(8,128)}, f32[64,8192]{1,0:T(8,128)}, f32[64,8192]{1,0:T(8,128)}) custom-call(bf16[128,2048]{1,0:T(8,128)(2,1)} %get-tuple-element.334.local_ref, bf16[8,4,64,1024]{3,2,1,0:T(8,128)(2,1)} %bitcast.206, bf16[8,4,64,1024]{3,2,1,0:T(8,128)(2,1)} %bitcast.205, ...), custom_call_target="tpu_custom_call" | custom-call | tf_op jit(solution)/shard_map/gather_back/pallas_call | solution.py:1397
  562.2 3.8 convolution_convert_fusion.2
  566.1 40.7 %while.28 = (s32[]{:T(128)}, f32[1024,2,128]{0,2,1:T(8,128)}, f32[1024,2,128]{0,2,1:T(8,128)}, bf16[2,512,2,128]{3,1,0,2:T(8,128)(2,1)}, s32[2]{0:T(128)S(1)}, /...) while((s32[]{:T(128)}, f32[1024,2,128]{0,2,1:T(8,128)}, ...), condition=%wide.region_12.13_spmd.clone, body=%wide.region_10.12_spmd.clone.sunk | while | flops 1361051136 | bytes 86813704 | solution.py:1798
  568.0 2.7 fusion.136
  572.7 4.2 multiply_reduce_fusion.10
  576.9 1.4 multiply_convert_fusion.4
  578.3 2.6 fusion.138
  581.0 1.4 fusion.140
  582.4 3.5 fusion.139
  587.9 2.7 fusion.136
  592.5 4.2 multiply_reduce_fusion.10
  596.8 1.4 multiply_convert_fusion.4
  598.2 3.0 fusion.138
  601.2 1.4 fusion.140
  602.6 3.9 fusion.139
  606.7 1.6 copy.58
  609.6 1.9 multiply_subtract_fusion
  613.0 3.0 pad_maximum_fusion.1
  616.0 2.5 copy.59
  618.5 1.5 fusion.53
  621.1 4.6 convolution_convert_fusion.1
  626.3 9.2 %mean_sum.1 = f32[16,128]{1,0:T(8,128)} custom-call(f32[16,128]{1,0:T(8,128)} %reshape.437.local_ref), custom_call_target="tpu_custom_call" | custom-call | tf_op jit(solution)/shard_map/mean_sum/pallas_call | solution.py:1615
  636.4 1.6 multiply_convert_fusion.1
  638.3 1.3 convert_element_type.159
  639.6 4.9 convolution_convert_fusion
  644.5 2.0 copy.61
  647.7 1.1 copy.72.refs_2_
  648.8 74.8 %take_out.1 = (f32[128,2048]{1,0:T(8,128)}, f32[64,2048]{1,0:T(8,128)}, f32[64,2048]{1,0:T(8,128)}, f32[64,2048]{1,0:T(8,128)}, f32[64,2048]{1,0:T(8,128)}, /*index=5*/f32[8,128]{1,0:T(8,128)}) custom-call(bf16[8,128,256]{2,1,0:T(8,128)(2,1)} %bitcast.218, bf16[8,128,256]{2,1,0:T(8,128)(2,1)} %bitcast.217, bf16[8,128,256]{2,1,0:T(8,128)(2,1)} %copy.72.refs_2_, ...), custom_call_target="tpu_custom_call" | custom-call | tf_op jit(solution)/shard_map/take_out/pallas_call | solution.py:1543
  723.6 2.5 add_bitcast_fusion
  726.2 1.4 slice_bitcast_fusion.4
  727.5 2.0 copy.124
  731.9 1.3 copy.128
  733.3 1.3 copy.129
  734.6 1.3 copy.130
  (194 shorter events, 23.9 us)
Async XLA Ops:
  101.3 3.3 copy-start.42
  104.5 1.3 copy-start.21
  104.5 1.4 copy-start.20
  105.9 11.4 %copy-start.10 = (f32[1024,256]{0,1:T(8,128)}, f32[1024,256]{0,1:T(8,128)S(1)}, u32[]{:S(2)}) copy-start(f32[1024,256]{0,1:T(8,128)S(1)} %get-tuple-element.358) | copy-start | bytes 3145732
  107.2 13.0 %copy-start.12 = (f32[1024,256]{0,1:T(8,128)}, f32[1024,256]{0,1:T(8,128)S(1)}, u32[]{:S(2)}) copy-start(f32[1024,256]{0,1:T(8,128)S(1)} %get-tuple-element.356) | copy-start | bytes 3145732
  116.0 1.5 copy-start.34
  116.0 4.3 copy-start.36
  117.3 3.1 copy-start.38
  117.3 3.1 copy-start.40
  128.1 2.3 copy-start.16
  128.1 2.6 copy-start.19
  128.1 3.0 copy-start.43
  131.1 1.6 copy-start.29
  145.4 183.5 %copy-start.33 = (bf16[2,512,2,128]{3,2,1,0:T(2,128)(2,1)}, bf16[2,512,2,128]{3,2,1,0:T(2,128)(2,1)S(1)}, u32[]{:S(2)}) copy-start(bf16[2,512,2,128]{3,2,1,0:T(2,128)(2,1)S(1)} %get-tuple-element.155) | copy-start | bytes 1572868
  145.4 95.1 %copy-start.18 = (bf16[1,128,2048]{2,1,0:T(8,128)(2,1)S(1)}, bf16[1,128,2048]{2,1,0:T(8,128)(2,1)}, u32[]{:S(2)}) copy-start(bf16[1,128,2048]{2,1,0:T(8,128)(2,1)} %param.18) | copy-start | bytes 1572868
  242.8 87.5 %copy-start.8 = (bf16[1,128,2048]{2,1,0:T(8,128)(2,1)S(1)}, bf16[1,128,2048]{2,1,0:T(8,128)(2,1)}, u32[]{:S(2)}) copy-start(bf16[1,128,2048]{2,1,0:T(8,128)(2,1)} %param.31) | copy-start | bytes 1572868
  410.9 9.5 %copy-start.45 = (bf16[8,128,2048]{2,1,0:T(8,128)(2,1)S(1)}, bf16[8,128,2048]{2,1,0:T(8,128)(2,1)}, u32[]{:S(2)}) copy-start(bf16[8,128,2048]{2,1,0:T(8,128)(2,1)} %get-tuple-element.166) | copy-start | bytes 12582916
  410.9 9.5 %copy-start.47 = (bf16[8,128,1024]{2,1,0:T(8,128)(2,1)S(1)}, bf16[8,128,1024]{2,1,0:T(8,128)(2,1)}, u32[]{:S(2)}) copy-start(bf16[8,128,1024]{2,1,0:T(8,128)(2,1)} %get-tuple-element.168) | copy-start | bytes 6291460
  420.4 6.3 copy-start.46
  426.7 6.2 copy-start.6
  426.7 6.2 copy-start.14
  426.7 6.7 copy-start.7
  566.1 10.8 %copy-start.2 = (bf16[1024,2,128]{2,0,1:T(8,128)(2,1)}, bf16[1024,2,128]{2,0,1:T(8,128)(2,1)S(1)}, u32[]{:S(2)}) copy-start(bf16[1024,2,128]{2,0,1:T(8,128)(2,1)S(1)} %get-tuple-element.575) | copy-start | bytes 1572868 | tf_op jit(solution)/shard_map/while
  566.1 10.8 %copy-start.4 = (bf16[1024,2,128]{2,0,1:T(8,128)(2,1)}, bf16[1024,2,128]{2,0,1:T(8,128)(2,1)S(1)}, u32[]{:S(2)}) copy-start(bf16[1024,2,128]{2,0,1:T(8,128)(2,1)S(1)} %get-tuple-element.581) | copy-start | bytes 1572868 | tf_op jit(solution)/shard_map/while
  566.1 10.8 %copy-start.22 = (bf16[1024,2,128]{0,2,1:T(8,128)(2,1)}, bf16[1024,2,128]{0,2,1:T(8,128)(2,1)S(1)}, u32[]{:S(2)}) copy-start(bf16[1024,2,128]{0,2,1:T(8,128)(2,1)S(1)} %get-tuple-element.580) | copy-start | bytes 1572868 | tf_op jit(solution)/shard_map/while
  572.7 4.3 copy-start
  578.3 4.1 copy-start.1
  582.4 3.5 copy-start.3
  582.4 3.5 copy-start.5
  582.4 3.5 copy-start.23
  585.9 10.8 %copy-start.2 = (bf16[1024,2,128]{2,0,1:T(8,128)(2,1)}, bf16[1024,2,128]{2,0,1:T(8,128)(2,1)S(1)}, u32[]{:S(2)}) copy-start(bf16[1024,2,128]{2,0,1:T(8,128)(2,1)S(1)} %get-tuple-element.575) | copy-start | bytes 1572868 | tf_op jit(solution)/shard_map/while
  585.9 10.8 %copy-start.4 = (bf16[1024,2,128]{2,0,1:T(8,128)(2,1)}, bf16[1024,2,128]{2,0,1:T(8,128)(2,1)S(1)}, u32[]{:S(2)}) copy-start(bf16[1024,2,128]{2,0,1:T(8,128)(2,1)S(1)} %get-tuple-element.581) | copy-start | bytes 1572868 | tf_op jit(solution)/shard_map/while
  585.9 10.8 %copy-start.22 = (bf16[1024,2,128]{0,2,1:T(8,128)(2,1)}, bf16[1024,2,128]{0,2,1:T(8,128)(2,1)S(1)}, u32[]{:S(2)}) copy-start(bf16[1024,2,128]{0,2,1:T(8,128)(2,1)S(1)} %get-tuple-element.580) | copy-start | bytes 1572868 | tf_op jit(solution)/shard_map/while
  592.5 4.3 copy-start
  598.2 4.4 copy-start.1
  602.6 3.9 copy-start.3
  602.6 3.9 copy-start.5
  602.6 3.9 copy-start.23
  606.7 2.8 copy-start.17
  606.7 2.8 copy-start.24
  611.5 1.2 copy-start.11
  611.5 1.2 copy-start.35
  611.5 1.2 copy-start.39
  612.7 5.8 copy-start.13
  612.7 5.8 copy-start.37
  612.7 5.8 copy-start.41
  635.6 4.1 copy-start.44
  638.1 6.5 copy-start.25
  648.8 74.8 %copy-start.9 = (bf16[1,128,2048]{2,1,0:T(8,128)(2,1)S(1)}, bf16[1,128,2048]{2,1,0:T(8,128)(2,1)}, u32[]{:S(2)}) copy-start(bf16[1,128,2048]{2,1,0:T(8,128)(2,1)} %param.31) | copy-start | bytes 1572868
  648.8 74.8 %copy-start.15 = (f32[128,2048]{1,0:T(8,128)S(1)}, f32[128,2048]{1,0:T(8,128)}, u32[]{:S(2)}) copy-start(f32[128,2048]{1,0:T(8,128)} %get-tuple-element.164) | copy-start | bytes 3145732
  723.6 6.0 copy-start.32
  723.6 6.8 copy-start.31
  723.6 7.6 %copy-start.30 = (f32[64,2048]{1,0:T(8,128)S(1)}, f32[64,2048]{1,0:T(8,128)}, u32[]{:S(2)}) copy-start(f32[64,2048]{1,0:T(8,128)} %get-tuple-element.605) | copy-start | bytes 1572868
  723.6 8.3 %copy-start.28 = (f32[64,8192]{1,0:T(8,128)S(1)}, f32[64,8192]{1,0:T(8,128)}, u32[]{:S(2)}) copy-start(f32[64,8192]{1,0:T(8,128)} %get-tuple-element.609) | copy-start | bytes 6291460
  727.5 5.7 copy-start.27
  731.9 2.6 copy-start.26

commit v6 on v5

--- a/solution.py
+++ b/solution.py
@@ -591,7 +591,7 @@
 
 def line_params(collective_id):
     return pltpu.CompilerParams(
-        collective_id=collective_id, has_side_effects=True, vmem_limit_bytes=60 * 2**20
+        collective_id=collective_id, has_side_effects=True, vmem_limit_bytes=63 * 2**20
     )
 
 
@@ -827,48 +827,49 @@
 
 AHEAD = 2
 LAG = 3
+RING = 8
 
 
 class Collect:
-    def __init__(self, cross, terms, side_in, half_out, half_in, row_out, row_in, side_send, side_recv, half_send, half_recv, row_send, row_recv):
-        self.cross, self.terms = cross, terms
+    def __init__(self, cross, kinds, fill, terms, side_in, half_out, half_in, row_out, row_in, side_send, side_recv, half_send, half_recv, row_send, row_recv):
+        self.cross, self.fill, self.terms = cross, fill, terms
         self.side_in, self.half_out, self.half_in = side_in, half_out, half_in
         self.row_out, self.row_in = row_out, row_in
         self.side_send, self.side_recv = side_send, side_recv
         self.half_send, self.half_recv = half_send, half_recv
         self.row_send, self.row_recv = row_send, row_recv
         self.rows, self.columns = terms.shape[-2:]
-        self.items = terms.shape[0] * cross.seq_count
+        self.items = kinds * cross.seq_count
 
     @staticmethod
     def scratch(kinds, seq_count, fsdp_count, rows, columns):
-        seq_count = kinds * seq_count
         dma = pltpu.SemaphoreType.DMA
         vmem = pltpu.VMEM
         bf16 = jnp.bfloat16
+        items = kinds * seq_count
         if fsdp_count == 4:
             arrays = [
-                vmem((seq_count, 2, 2, rows // 2, columns), bf16),
-                vmem((seq_count, 2, rows // 2, columns), bf16),
-                vmem((seq_count, 2, rows // 2, columns), bf16),
+                vmem((items, 2, 2, rows // 2, columns), bf16),
+                vmem((RING, 2, rows // 2, columns), bf16),
+                vmem((items, 2, rows // 2, columns), bf16),
             ]
             sides = (2, 2)
         else:
             arrays = [
-                vmem((seq_count, fsdp_count - 1, rows, columns), bf16),
+                vmem((items, fsdp_count - 1, rows, columns), bf16),
                 vmem((1, 1, 16, 128), bf16),
                 vmem((1, 1, 16, 128), bf16),
             ]
             sides = (fsdp_count - 1, 1)
-        return arrays + [
-            vmem((seq_count, rows, columns), bf16),
-            vmem((seq_count, rows, columns), bf16),
-            dma((seq_count,) + sides),
-            dma((seq_count,) + sides),
-            dma((seq_count, 2)),
-            dma((seq_count, 2)),
-            dma((seq_count,)),
-            dma((seq_count,)),
+        return [vmem((RING, fsdp_count, rows, columns), bf16)] + arrays + [
+            vmem((RING, rows, columns), bf16),
+            vmem((items, rows, columns), bf16),
+            dma((items,) + sides),
+            dma((items,) + sides),
+            dma((items, 2)),
+            dma((items, 2)),
+            dma((items,)),
+            dma((items,)),
         ]
 
     def half_rows(self, side):
@@ -878,7 +879,7 @@
         cross = self.cross
         if not cross.square:
             return cross.remote(
-                self.terms.at[(*self.place(turn), cross.sides[side])],
+                self.terms.at[turn % RING, cross.sides[side]],
                 self.side_in.at[turn, side],
                 self.side_send.at[turn, side, 0],
                 self.side_recv.at[turn, side, 0],
@@ -887,7 +888,7 @@
             )
         target = cross.sides[side] if which == 0 else cross.corner
         return cross.remote(
-            self.terms.at[(*self.place(turn), target, self.half_rows(side))],
+            self.terms.at[turn % RING, target, self.half_rows(side)],
             self.side_in.at[turn, side, which],
             self.side_send.at[turn, side, which],
             self.side_recv.at[turn, side, which],
@@ -898,7 +899,7 @@
     def half(self, turn, side):
         cross = self.cross
         return cross.remote(
-            self.half_out.at[turn, side],
+            self.half_out.at[turn % RING, side],
             self.half_in.at[turn, side],
             self.half_send.at[turn, side],
             self.half_recv.at[turn, side],
@@ -909,7 +910,7 @@
     def row(self, turn):
         cross = self.cross
         return cross.remote(
-            self.row_out.at[turn],
+            self.row_out.at[turn % RING],
             self.row_in.at[turn],
             self.row_send.at[turn],
             self.row_recv.at[turn],
@@ -928,39 +929,58 @@
     def ways(self):
         return range(2) if self.cross.square else range(1)
 
-    def send(self, turn):
-        for which in reversed(self.ways):
-            for side in range(len(self.cross.sides)):
-                self.side(turn, side, which).start()
+    def sides(self, turn):
+        return [
+            self.side(turn, side, which)
+            for which in reversed(self.ways)
+            for side in range(len(self.cross.sides))
+        ]
+
+    def send(self, turn, first):
+        if not first:
+
+            @pl.when(turn >= RING)
+            def _():
+                for copy in self.sides(turn - RING):
+                    copy.wait_send()
+
+        kind, owner = self.place(turn)
+        self.fill(kind, owner, turn % RING)
+        for copy in self.sides(turn):
+            copy.start()
 
     def middle(self, turn):
         if not self.cross.square:
             return
         cross = self.cross
-        kind, owner = self.place(turn)
+
+        @pl.when(turn >= RING)
+        def _():
+            for side in range(2):
+                self.half(turn - RING, side).wait_send()
+
         for side in range(2):
             self.side(turn, side, 1).wait_recv()
-            mine = self.terms[kind, owner, cross.sides[1 - side], self.half_rows(side)]
-            self.half_out[turn, side] = (
+            mine = self.terms[turn % RING, cross.sides[1 - side], self.half_rows(side)]
+            self.half_out[turn % RING, side] = (
                 mine.astype(jnp.float32) + self.side_in[turn, side, 1].astype(jnp.float32)
             ).astype(jnp.bfloat16)
             self.half(turn, side).start()
 
     def totals(self, turn):
         cross = self.cross
-        kind, owner = self.place(turn)
         found = []
         if cross.square:
             for side in range(2):
                 self.side(turn, side, 0).wait_recv()
                 self.half(turn, side).wait_recv()
                 rows = self.half_rows(side)
-                total = self.terms[kind, owner, cross.fsdp, rows].astype(jnp.float32)
+                total = self.terms[turn % RING, cross.fsdp, rows].astype(jnp.float32)
                 total = total + self.side_in[turn, side, 0].astype(jnp.float32)
                 total = total + self.half_in[turn, side].astype(jnp.float32)
                 found.append((rows, total))
         else:
-            total = self.terms[kind, owner, cross.fsdp].astype(jnp.float32)
+            total = self.terms[turn % RING, cross.fsdp].astype(jnp.float32)
             for side in range(len(cross.sides)):
                 self.side(turn, side, 0).wait_recv()
                 total = total + self.side_in[turn, side].astype(jnp.float32)
@@ -969,6 +989,7 @@
 
     def ship(self, turn):
         own = self.is_own(turn)
+        self.free_row(turn - RING)
 
         @pl.when(own)
         def _():
@@ -978,15 +999,20 @@
         @pl.when(jnp.logical_not(own))
         def _():
             for rows, total in self.totals(turn):
-                self.row_out[turn, rows] = total.astype(jnp.bfloat16)
+                self.row_out[turn % RING, rows] = total.astype(jnp.bfloat16)
             self.row(turn).start()
+
+    def free_row(self, turn):
+        @pl.when((turn >= 0) & jnp.logical_not(self.is_own(turn)))
+        def _():
+            self.row(turn).wait_send()
 
     def beat(self, turn):
         ahead = turn + AHEAD
 
         @pl.when(ahead < self.items)
         def _():
-            self.send(ahead)
+            self.send(ahead, False)
 
         @pl.when(turn < self.items)
         def _():
@@ -997,8 +1023,9 @@
             self.ship(turn - LAG)
 
     def begin(self):
-        for turn in range(min(AHEAD, self.items)):
-            self.send(turn)
+        @pl.loop(0, min(AHEAD, self.items))
+        def _(turn):
+            self.send(turn, True)
 
     @property
     def beats(self):
@@ -1016,18 +1043,16 @@
 
     def finish(self):
         cross = self.cross
-
-        @pl.loop(0, self.items)
+        late = max(self.items - RING, 0)
+
+        @pl.loop(late, self.items)
         def _(turn):
-            for side in range(len(cross.sides)):
-                for which in self.ways:
-                    self.side(turn, side, which).wait_send()
-                if cross.square:
+            for copy in self.sides(turn):
+                copy.wait_send()
+            if cross.square:
+                for side in range(2):
                     self.half(turn, side).wait_send()
-
-            @pl.when(jnp.logical_not(self.is_own(turn)))
-            def _():
-                self.row(turn).wait_send()
+            self.free_row(turn)
 
 
 def bring_in_kernel(
@@ -1336,27 +1361,206 @@
     return projected, up.reshape(-1, units), down.reshape(-1, units)
 
 
-def gather_back_kernel(chips, fsdp_count, count, local_ref, *refs):
-    sources, refs = refs[:count], refs[count:]
-    out, results, refs = refs[0], refs[1 : 1 + count], refs[1 + count :]
-    terms, load_sem, store_sem, comm = refs[0], refs[1], refs[2], refs[3:]
+def dot_rows(left, right, precision=None):
+    return lax.dot_general(
+        left,
+        right,
+        (((0,), (0,)), ((), ())),
+        precision=precision,
+        preferred_element_type=jnp.float32,
+    )
+
+
+EXACT = lax.Precision.HIGHEST
+
+
+def turn_heads(tensor, cosine, sine):
+    heads = [
+        tensor[:, first : first + DH] * cosine
+        + pltpu.roll(tensor[:, first : first + DH], DH // 2, 1) * sine
+        for first in range(0, tensor.shape[1], DH)
+    ]
+    return jnp.concatenate(heads, axis=1) if len(heads) > 1 else heads[0]
+
+
+def attention_weights(queries, keys, first_row, segment_column, segment_row):
+    rows, count = queries.shape[0], keys.shape[0]
+    scores = dot_cols(queries, keys) * DH ** (-0.5)
+    query_place = first_row + lax.broadcasted_iota(jnp.int32, (rows, count), 0)
+    key_place = lax.broadcasted_iota(jnp.int32, (rows, count), 1)
+    allowed = (key_place <= query_place) & (segment_row == segment_column)
+    scores = jnp.where(allowed, scores, neg_fill)
+    expanded = jnp.exp(scores - jnp.max(scores, axis=-1, keepdims=True))
+    return expanded / jnp.sum(expanded, axis=-1, keepdims=True)
+
+
+class RowSum:
+    def __init__(self, cross, local, every, send_sem, recv_sem):
+        self.cross, self.local, self.every = cross, local, every
+        self.send_sem, self.recv_sem = send_sem, recv_sem
+
+    @staticmethod
+    def scratch(seq_count, shape):
+        dma = pltpu.SemaphoreType.DMA
+        return [
+            pltpu.VMEM(shape, jnp.float32),
+            pltpu.VMEM((seq_count,) + shape, jnp.float32),
+            dma((seq_count,)),
+            dma((seq_count,)),
+        ]
+
+    def copy(self, step):
+        cross = self.cross
+        return cross.remote(
+            self.local,
+            self.every.at[step],
+            self.send_sem.at[step],
+            self.recv_sem.at[step],
+            cross.seq_peer(step),
+            cross.fsdp,
+        )
+
+    def send(self, value):
+        self.local[...] = value
+        for step in range(1, self.cross.seq_count):
+            self.copy(step).start()
+
+    def receive(self):
+        total = self.local[...]
+        for step in range(1, self.cross.seq_count):
+            self.copy(step).wait_recv()
+            total = total + self.every[step]
+        return total
+
+    def finish(self):
+        for step in range(1, self.cross.seq_count):
+            self.copy(step).wait_send()
+
+
+def pick_row(row, shape):
+    return jnp.where(lax.broadcasted_iota(jnp.int32, shape, 0) == row, 1.0, 0.0)
+
+
+def gather_back_kernel(chips, fsdp_count, *refs):
+    local_ref, output_ref, gains_ref, inverse_ref, cosine_ref, sine_ref = refs[:6]
+    segment_column, segment_row = refs[6:8]
+    hidden_hbm, grad_hbm, gate_hbm, up_hbm, act_hbm = refs[8:13]
+    heads_hbm, pre_hbm = refs[13:15]
+    refs = refs[15:]
+    results, output_term, grads_out, gain_out = refs[:3], refs[3], refs[4], refs[5]
+    refs = refs[6:]
+    tokens, units, heads, pre, gathered, grad_query, grad_key, grad_value = refs[:8]
+    load_sem, refs = refs[8], refs[9:]
     line = Line(chips)
     cross = Cross(2 * chips, fsdp_count)
-    gather = Gather(line, *comm[:5])
-    collect = Collect(cross, terms, *comm[5:])
-    copies = load([(sources[kind], terms.at[kind], load_sem.at[kind]) for kind in range(count)])
+    gather = Gather(line, *refs[:5])
+    sums = RowSum(cross, *refs[5:9])
+    all_tokens, width = tokens.shape[1:]
+    block_units = units.shape[-1]
+    columns = output_ref.shape[0]
+    blocks = gather.blocks
+    rows = blocks.shape[1]
+
+    def fill(kind, owner, slot):
+        span = width // cross.seq_count
+        chosen = tokens[kind // 2, :, pl.ds(pl.multiple_of(owner * span, 128), span)]
+
+        @pl.loop(0, block_units // tile_of(block_units))
+        def _(tile):
+            part = pl.ds(pl.multiple_of(tile * tile_of(block_units), 128), tile_of(block_units))
+            term = dot_rows(chosen, units[kind, :, part]).astype(jnp.bfloat16)
+            collect.terms[slot, :, :, part] = term.reshape(fsdp_count, -1, term.shape[1])
+
+    collect = Collect(cross, 3, fill, *refs[9:])
+    copies = load(
+        [
+            (hidden_hbm, tokens.at[0], load_sem.at[0]),
+            (gate_hbm, units.at[0], load_sem.at[1]),
+            (up_hbm, units.at[1], load_sem.at[2]),
+            (grad_hbm, tokens.at[1], load_sem.at[3]),
+            (act_hbm, units.at[2], load_sem.at[4]),
+            (heads_hbm, heads, load_sem.at[5]),
+            (pre_hbm, pre, load_sem.at[6]),
+        ]
+    )
     greet_cross(cross.seq_count, fsdp_count)
-    gather.blocks[line.place * 2 + line.core] = local_ref[...]
+    blocks[line.place * 2 + line.core] = local_ref[...]
     gather.send(line.place)
-
-    def store(chip):
-        pair = pl.ds(chip * 2, 2)
-        return pltpu.make_async_copy(gather.blocks.at[pair], out.at[pair], store_sem.at[chip])
-
-    for copy in copies:
+    grad_key[...] = jnp.zeros_like(grad_key)
+    grad_value[...] = jnp.zeros_like(grad_value)
+    for copy in copies[:2]:
         copy.wait()
     collect.begin()
-    store(gather.step(0)).start()
+    for copy in copies[2:]:
+        copy.wait()
+
+    def arrive(step):
+        chip = gather.step(step)
+        whole = blocks[pl.ds(chip * 2, 2)].reshape(2 * rows, width)
+        found = dot_cols(whole, output_ref[...]).astype(jnp.bfloat16)
+        gathered[pl.ds(chip * 2 * rows, 2 * rows), :] = found
+
+    arrive(0)
+    query_rows = 128
+    blocks_of_rows = all_tokens // query_rows
+    first_beat = 3 * (chips - 1)
+
+    def attend(block):
+        first = pl.multiple_of(block * query_rows, query_rows)
+        span = pl.ds(first, query_rows)
+        for head in range(0, columns, DH):
+            part = pl.ds(head, DH)
+            queries, keys, values = heads[0, span, part], heads[1, :, part], heads[2, :, part]
+            outer = gathered[span, part]
+            probs = attention_weights(
+                queries, keys, first, segment_column[span, :], segment_row[...]
+            )
+            grad_value[:, part] += dot_rows(probs.astype(jnp.bfloat16), outer)
+            grad_probs = dot_cols(outer, values)
+            delta = jnp.sum(probs * grad_probs, axis=-1, keepdims=True)
+            grad_scores = (probs * (grad_probs - delta)).astype(jnp.bfloat16)
+            grad_query[span, part] = jnp.dot(
+                grad_scores, keys, preferred_element_type=jnp.float32
+            )
+            grad_key[:, part] += dot_rows(grad_scores, queries)
+
+    def errors(kind, grad):
+        scaled = (grad[...] * DH ** (-0.5)).astype(jnp.bfloat16).astype(jnp.float32)
+        error = turn_heads(scaled, cosine_ref[...], -sine_ref[...])
+        inverse = inverse_ref[:, kind : kind + 1]
+        return error, pre[kind] * inverse, inverse
+
+    def send_means():
+        total = None
+        for kind, grad in enumerate((grad_query, grad_key)):
+            error, unit, _ = errors(kind, grad)
+            product = error * unit
+            gain_out[kind : kind + 1, :] = jnp.sum(product, axis=0, keepdims=True)
+            row = lax.dot_general(
+                pick_row(kind, (8, columns)),
+                product * gains_ref[kind : kind + 1, :],
+                (((1,), (1,)), ((), ())),
+                precision=EXACT,
+                preferred_element_type=jnp.float32,
+            )
+            total = row if total is None else total + row
+        sums.send(total)
+        grads_out[2] = grad_value[...].astype(jnp.bfloat16)
+
+        @pl.loop(0, width // tile_of(width))
+        def _(tile):
+            part = pl.ds(pl.multiple_of(tile * tile_of(width), 128), tile_of(width))
+            outer = blocks[:, :, part].reshape(all_tokens, -1)
+            output_term[:, part] = dot_rows(heads[3], outer).astype(jnp.bfloat16)
+
+    def finish_grads():
+        means = sums.receive() / width
+        for kind, grad in enumerate((grad_query, grad_key)):
+            error, unit, inverse = errors(kind, grad)
+            mean = dot_rows(means, pick_row(kind, (8, 128)), EXACT)[:, :1]
+            grads_out[kind] = (
+                inverse * (error * gains_ref[kind : kind + 1, :] - unit * mean)
+            ).astype(jnp.bfloat16)
 
     @pl.loop(0, collect.beats)
     def _(turn):
@@ -1364,53 +1568,83 @@
 
         @pl.when((turn % 3 == 2) & (turn // 3 + 1 < chips))
         def _():
-            store(gather.step(turn // 3 + 1)).start()
-
-    block = terms.shape[-1]
+            arrive(turn // 3 + 1)
+
+        @pl.when((turn >= first_beat) & (turn < first_beat + blocks_of_rows))
+        def _():
+            attend(turn - first_beat)
+
+        @pl.when(turn == first_beat + blocks_of_rows)
+        def _():
+            send_means()
+
+        @pl.when(turn == first_beat + blocks_of_rows + 3)
+        def _():
+            finish_grads()
 
     @pl.loop(0, cross.seq_count)
     def _(turn):
-        for kind in range(count):
+        for kind in range(3):
 
             def put(_, sender, value):
-                columns = pl.ds(pl.multiple_of(sender * block, 128), block)
-                results[kind][:, columns] = value
+                part = pl.ds(pl.multiple_of(sender * block_units, 128), block_units)
+                results[kind][:, part] = value
 
             collect.receive(kind * cross.seq_count + turn, put)
 
     collect.finish()
     gather.finish()
-
-    @pl.loop(0, chips)
-    def _(chip):
-        store(chip).wait()
-
-
-def gather_back(local, terms):
+    sums.finish()
+
+
+def gather_back(local, output_rows, gains, inverse, tables, segment_row, far, heads, pre):
     rows, width = local.shape
     slots = lax.axis_size("seq")
     fsdp_count = lax.axis_size("fsdp")
     chips = slots // 2
-    count = len(terms)
-    own = terms[0].shape[0] // (slots * fsdp_count)
-    units = terms[0].shape[1]
+    own = width // (slots * fsdp_count)
+    units = far[2].shape[1]
+    _, tokens, columns = heads.shape
+    bf16, f32 = jnp.bfloat16, jnp.float32
     found = pl.pallas_call(
-        functools.partial(gather_back_kernel, chips, fsdp_count, count),
-        out_shape=(jax.ShapeDtypeStruct((slots, rows, width), jnp.bfloat16),)
-        + (jax.ShapeDtypeStruct((own, units * slots), jnp.float32),) * count,
-        in_specs=[whole_spec()] + [far_spec()] * count,
-        out_specs=(far_spec(),) + (whole_spec(),) * count,
+        functools.partial(gather_back_kernel, chips, fsdp_count),
+        out_shape=(jax.ShapeDtypeStruct((own, units * slots), f32),) * 3
+        + (
+            jax.ShapeDtypeStruct((columns, width), bf16),
+            jax.ShapeDtypeStruct((3, tokens, columns), bf16),
+            jax.ShapeDtypeStruct((8, columns), f32),
+        ),
+        in_specs=[whole_spec()] * 8 + [far_spec()] * 7,
+        out_specs=(whole_spec(),) * 6,
         scratch_shapes=[
-            pltpu.VMEM((count, slots, fsdp_count, own, units), jnp.bfloat16),
-            pltpu.SemaphoreType.DMA((count,)),
-            pltpu.SemaphoreType.DMA((chips,)),
+            pltpu.VMEM((2, tokens, width), bf16),
+            pltpu.VMEM((3, tokens, units), bf16),
+            pltpu.VMEM((4, tokens, columns), bf16),
+            pltpu.VMEM((2, tokens, columns), f32),
+            pltpu.VMEM((tokens, columns), bf16),
+            pltpu.VMEM((tokens, columns), f32),
+            pltpu.VMEM((tokens, columns), f32),
+            pltpu.VMEM((tokens, columns), f32),
+            pltpu.SemaphoreType.DMA((7,)),
         ]
         + Gather.scratch(chips, rows, width)
-        + Collect.scratch(count, slots, fsdp_count, own, units),
+        + RowSum.scratch(slots, (8, tokens))
+        + Collect.scratch(3, slots, fsdp_count, own, units),
         compiler_params=line_params(6),
         name="gather_back",
-    )(local, *[term.reshape(slots, fsdp_count, own, units) for term in terms])
-    return (found[0].reshape(-1, width),) + tuple(found[1:])
+    )(
+        local,
+        output_rows,
+        gains,
+        inverse,
+        *tables,
+        segment_row.reshape(tokens, 1),
+        segment_row.reshape(1, tokens),
+        *far,
+        heads,
+        pre,
+    )
+    return found[:3], found[3], found[4], found[5]
 
 
 def take_out_kernel(
@@ -1418,17 +1652,30 @@
     fsdp_count,
     *refs,
 ):
-    lefts, rights, refs = refs[:3], refs[3:6], refs[6:]
-    terms, output_ref, gains_ref, refs = refs[0], refs[1], refs[2], refs[3:]
+    grads_ref, rights, tokens_ref = refs[0], refs[1], refs[2]
+    output_ref, gains_ref, refs = refs[3], refs[4], refs[5:]
     result, weight_outs, output_out, gains_out, refs = refs[0], refs[1:4], refs[4], refs[5], refs[6:]
     output_in, gain_in, gain_out, gain_rows, refs = refs[0], refs[1], refs[2], refs[3], refs[4:]
     output_send, output_recv, gain_send, gain_recv, gain_row_send, gain_row_recv = refs[:6]
     comm = refs[6:]
     line = Line(chips)
     cross = Cross(2 * chips, fsdp_count)
-    scatter = Scatter(line, *comm[:-11])
-    collect = Collect(cross, terms, *comm[-11:])
     seq_count, seq, fsdp = cross.seq_count, cross.seq, cross.fsdp
+    scatter = Scatter(line, *comm[:-12])
+    columns = rights.shape[-1]
+    rows, width = scatter.fresh.shape[1:]
+
+    def fill(kind, owner, slot):
+        span = width // seq_count
+        part = pl.ds(pl.multiple_of(owner * span, 128), span)
+        chosen = tokens_ref[:, part]
+        for kind in range(3):
+            term = dot_rows(chosen, grads_ref[kind].reshape(-1, columns)).astype(jnp.bfloat16)
+            collect.terms[slot, :, :, kind * columns : (kind + 1) * columns] = term.reshape(
+                fsdp_count, -1, columns
+            )
+
+    collect = Collect(cross, 1, fill, *comm[-12:])
 
     def output_copy(step):
         peer = cross.fsdp_peer(step)
@@ -1468,7 +1715,7 @@
     def _(step):
         product_terms(
             scatter,
-            [(left, right, True) for left, right in zip(lefts, rights)],
+            [(grads_ref.at[kind], rights.at[kind], True) for kind in range(3)],
             line.order(chips - 1 - step),
         )
 
@@ -1505,8 +1752,6 @@
         total = total + gain_rows[step]
     gains_out[...] = total
 
-    columns = terms.shape[-1] // 3
-
     def put(_, sender, value):
         block = pl.ds(pl.multiple_of(sender * columns, 128), columns)
         for kind in range(3):
@@ -1528,12 +1773,12 @@
         gain_copy(step).wait_send()
 
 
-def take_out(pairs, terms, output_term, gain_terms):
+def take_out(grads, weights, tokens, output_term, gain_terms):
     slots = lax.axis_size("seq")
     fsdp_count = lax.axis_size("fsdp")
     chips = slots // 2
-    width, columns = terms.shape
-    rows = pairs[0][0].shape[0] // slots
+    _, width, columns = weights.shape
+    rows = tokens.shape[0] // slots
     own = width // (slots * fsdp_count)
     kinds = gain_terms.shape[0]
     bf16, f32, dma = jnp.bfloat16, jnp.float32, pltpu.SemaphoreType.DMA
@@ -1542,15 +1787,10 @@
     gains = jnp.pad(gains, ((0, 0), (0, 0), (0, 8 - kinds), (0, lanes - own)))
     result, query, key, value, output, gains = pl.pallas_call(
         functools.partial(take_out_kernel, chips, fsdp_count),
-        out_shape=(
-            jax.ShapeDtypeStruct((rows, width), f32),
-            jax.ShapeDtypeStruct((own, columns // 3 * slots), f32),
-            jax.ShapeDtypeStruct((own, columns // 3 * slots), f32),
-            jax.ShapeDtypeStruct((own, columns // 3 * slots), f32),
-            jax.ShapeDtypeStruct((own, width), f32),
-            jax.ShapeDtypeStruct((8, lanes), f32),
-        ),
-        in_specs=[whole_spec()] * 9,
+        out_shape=(jax.ShapeDtypeStruct((rows, width), f32),)
+        + (jax.ShapeDtypeStruct((own, columns * slots), f32),) * 3
+        + (jax.ShapeDtypeStruct((own, width), f32), jax.ShapeDtypeStruct((8, lanes), f32)),
+        in_specs=[whole_spec()] * 5,
         out_specs=(whole_spec(),) * 6,
         scratch_shapes=[
             pltpu.VMEM((fsdp_count, own, width), bf16),
@@ -1565,13 +1805,13 @@
             dma((slots,)),
         ]
         + Scatter.scratch(chips, rows, width)
-        + Collect.scratch(1, slots, fsdp_count, own, columns),
+        + Collect.scratch(1, slots, fsdp_count, own, 3 * columns),
         compiler_params=line_params(4),
         name="take_out",
     )(
-        *[left.reshape(slots, rows, -1) for left, _ in pairs],
-        *[right for _, right in pairs],
-        terms.reshape(1, slots, fsdp_count, own, columns),
+        grads.reshape(3, slots, rows, columns),
+        weights,
+        tokens,
         output_term.reshape(fsdp_count, own, width),
         gains,
     )
@@ -1631,24 +1871,20 @@
     half_width = DH // 2
     frequency = rope_base ** (-jnp.arange(half_width, dtype=jnp.float32) * 2.0 / DH)
     angles = jnp.arange(row_count, dtype=jnp.int32).astype(jnp.float32)[:, None] * frequency[None, :]
-    return jnp.cos(angles), jnp.sin(angles)
-
-
-def rotate(tensor, cosine, sine_table):
+    cosine, sine = jnp.cos(angles), jnp.sin(angles)
+    return (
+        jnp.concatenate([cosine, cosine], axis=1),
+        jnp.concatenate([-sine, sine], axis=1),
+    )
+
+
+def rotate(tensor, tables):
+    cosine, sine = tables
     row_count = tensor.shape[0]
     half_width = DH // 2
     grouped = tensor.reshape(row_count, -1, DH)
-    first_half = grouped[..., :half_width]
-    second_half = grouped[..., half_width:]
-    cosine = cosine[:, None, :]
-    sine_table = sine_table[:, None, :]
-    turned = jnp.concatenate(
-        [
-            first_half * cosine - second_half * sine_table,
-            second_half * cosine + first_half * sine_table,
-        ],
-        axis=-1,
-    )
+    swapped = jnp.concatenate([grouped[..., half_width:], grouped[..., :half_width]], axis=-1)
+    turned = grouped * cosine[:, None, :] + swapped * sine[:, None, :]
     return turned.reshape(tensor.shape)
 
 
@@ -1705,9 +1941,9 @@
     inverse = lax.rsqrt(squares / width_all + eps_norm)
     query_unit = query_pre * inverse[0][:, None]
     key_unit = key_pre * inverse[1][:, None]
-    cosine, sine_table = rope_tables(sequence_rows)
-    queries_low = rotate(query_unit * query_scale, cosine, sine_table).astype(jnp.bfloat16)
-    keys_low = rotate(key_unit * key_scale, cosine, sine_table).astype(jnp.bfloat16)
+    tables = rope_tables(sequence_rows)
+    queries_low = rotate(query_unit * query_scale, tables).astype(jnp.bfloat16)
+    keys_low = rotate(key_unit * key_scale, tables).astype(jnp.bfloat16)
     query_heads = queries_low.reshape(sequence_rows, local_heads, DH)
     key_heads = keys_low.reshape(sequence_rows, local_heads, DH)
     value_heads = values_low.reshape(sequence_rows, local_heads, DH)
@@ -1726,10 +1962,9 @@
         block_out = jnp.einsum(
             "hqk,khd->qhd", softmax_low, value_heads, preferred_element_type=jnp.float32
         )
-        log_total = (row_max + jnp.log(row_total))[..., 0]
-        return (loop_state, (block_out.astype(jnp.bfloat16), log_total))
-
-    _, (out_blocks, log_totals) = lax.scan(attend_block, jnp.zeros((), jnp.int32), block_ids)
+        return (loop_state, block_out.astype(jnp.bfloat16))
+
+    _, out_blocks = lax.scan(attend_block, jnp.zeros((), jnp.int32), block_ids)
     attended_heads = out_blocks.reshape(sequence_rows, head_width)
     projected, up_cols, down_cols = project(attended_heads, output_rows, up_weight, down_weight)
     hidden = local_in.astype(jnp.float32) + rms_scale(projected, attention_scale)
@@ -1752,100 +1987,31 @@
     grad_hidden = grad_result + hidden_term
     _, branch_pull = jax.vjp(rms_scale, projected, attention_scale)
     grad_projected, grad_attention_gain = branch_pull(grad_hidden)
-    grad_projected_all, gate_weight_grad, up_weight_grad, down_weight_grad = gather_back(
+    weight_grads, output_term, attention_grads, gain_rows = gather_back(
         grad_projected.astype(jnp.bfloat16),
-        [
-            contract_rows(hidden_all, grad_gate_low).astype(jnp.bfloat16),
-            contract_rows(hidden_all, grad_upward_low).astype(jnp.bfloat16),
-            contract_rows(grad_all, activated).astype(jnp.bfloat16),
-        ],
-    )
-    output_term = contract_rows(attended_heads, grad_projected_all).astype(jnp.bfloat16)
-    grad_attended = contract_cols(grad_projected_all, output_rows).astype(jnp.bfloat16)
-    grad_out_heads = grad_attended.reshape(sequence_rows, local_heads, DH)
-
-    def attend_back(loop_state, block_index):
-        key_total, value_total = loop_state
-        first_row = block_index * block_rows
-        query_block = lax.dynamic_slice_in_dim(query_heads, first_row, block_rows, 0)
-        grad_block = lax.dynamic_slice_in_dim(grad_out_heads, first_row, block_rows, 0)
-        log_block = lax.dynamic_index_in_dim(log_totals, block_index, 0, keepdims=False)
-        scores = masked_scores(query_block, key_heads, first_row, segment_row, score_scale)
-        probabilities = jnp.exp(scores - log_block[..., None])
-        softmax_low = probabilities.astype(jnp.bfloat16)
-        value_total = value_total + jnp.einsum(
-            "hqk,qhd->khd", softmax_low, grad_block, preferred_element_type=jnp.float32
-        )
-        grad_softmax = jnp.einsum(
-            "qhd,khd->hqk", grad_block, value_heads, preferred_element_type=jnp.float32
-        )
-        row_dot = jnp.sum(probabilities * grad_softmax, axis=-1, keepdims=True)
-        grad_scores = (probabilities * (grad_softmax - row_dot)).astype(jnp.bfloat16)
-        grad_query_block = (
-            jnp.einsum("hqk,khd->qhd", grad_scores, key_heads, preferred_element_type=jnp.float32)
-            * score_scale
-        )
-        key_total = (
-            key_total
-            + jnp.einsum(
-                "hqk,qhd->khd", grad_scores, query_block, preferred_element_type=jnp.float32
-            )
-            * score_scale
-        )
-        return ((key_total, value_total), grad_query_block.astype(jnp.bfloat16))
-
-    zero_heads = jnp.zeros((sequence_rows, local_heads, DH), jnp.float32)
-    (key_total, value_total), grad_query_blocks = lax.scan(
-        attend_back, (zero_heads, zero_heads), block_ids
-    )
-    grad_queries = grad_query_blocks.reshape(sequence_rows, head_width).astype(jnp.float32)
-    grad_keys = (
-        key_total.astype(jnp.bfloat16).reshape(sequence_rows, head_width).astype(jnp.float32)
-    )
-    grad_values = value_total.astype(jnp.bfloat16).reshape(sequence_rows, head_width)
-    query_error = rotate(grad_queries, cosine, -sine_table)
-    key_error = rotate(grad_keys, cosine, -sine_table)
-    grad_query_gain = jnp.sum(query_error * query_unit, axis=0)
-    grad_key_gain = jnp.sum(key_error * key_unit, axis=0)
-    query_error = query_error * query_scale
-    key_error = key_error * key_scale
-    means = (
-        row_sum(
-            8,
-            "mean_sum",
-            jnp.stack(
-                [
-                    jnp.sum(query_error * query_unit, axis=-1),
-                    jnp.sum(key_error * key_unit, axis=-1),
-                ]
-            ),
-        )
-        / width_all
-    )
-    grad_query_low = (
-        inverse[0][:, None] * (query_error - query_unit * means[0][:, None])
-    ).astype(jnp.bfloat16)
-    grad_key_low = (inverse[1][:, None] * (key_error - key_unit * means[1][:, None])).astype(
-        jnp.bfloat16
-    )
-    grads_low = jnp.concatenate([grad_query_low, grad_key_low, grad_values], axis=1)
-    attention_terms = contract_rows(inputs_all, grads_low).astype(jnp.bfloat16)
+        output_rows,
+        jnp.stack([query_scale, key_scale]),
+        inverse.T,
+        tables,
+        segment_row,
+        [hidden_all, grad_all, grad_gate_low, grad_upward_low, activated],
+        jnp.stack([queries_low, keys_low, values_low, attended_heads]),
+        jnp.stack([query_pre, key_pre]),
+    )
+    gate_weight_grad, up_weight_grad, down_weight_grad = weight_grads
     head_gains = lax.dynamic_update_slice_in_dim(
         jnp.zeros((2, width_all), jnp.float32),
-        jnp.stack([grad_query_gain, grad_key_gain]),
+        gain_rows[:2],
         seq_index * head_width,
         1,
     )
     gain_terms = jnp.concatenate(
         [head_gains, jnp.stack([grad_attention_gain, grad_feedforward_gain])], axis=0
     )
-    input_term, attention_grads, output_weight_grad, gain_grads = take_out(
-        [(grad_query_low, query_cols), (grad_key_low, key_cols), (grad_values, value_cols)],
-        attention_terms,
-        output_term,
-        gain_terms,
-    )
-    query_weight_grad, key_weight_grad, value_weight_grad = attention_grads
+    input_term, projection_grads, output_weight_grad, gain_grads = take_out(
+        attention_grads, attention_cols, inputs_all, output_term, gain_terms
+    )
+    query_weight_grad, key_weight_grad, value_weight_grad = projection_grads
     grad_input = grad_hidden + input_term
     return (
         result,

time: 746 us -> 677 us (0.908)
  matrix products: 74.3 us -> 23.6 us
  other arithmetic: 41.7 us -> 32.8 us
    dot_general x18 -> x0, matrix products: 67 us -> none  [the longest x5 31.5 us: contract_rows(): lax.dot_general(left, right, (((0,), (0,)), ((), ())), preferred_element_...]
    sub x0 -> x2, matrix products: none -> 9.46 us  [attend_block(): expanded = jnp.exp(scores - row_max)]
    pallas_call x2 -> x1, Pallas kernels: 16.6 us -> 7.19 us  [row_sum(): pl.pallas_call(functools.partial(row_sum_kernel, slots), out_shape=jax.Sh...]
    unnamed x92 -> x59, local copies, waits for them, and re-layouts: 14.9 us -> 9.77 us
where the time goes in v6:
time: 677 us; the launch traced here: 668 us
  Pallas kernels  575 us (85%)
  local copies, waits for them, and re-layouts  33.1 us (5%)
  other arithmetic  32.8 us (5%)
  matrix products  23.6 us (3%)
    pallas_call x1, Pallas kernels, gather_back(): pl.pallas_call(functools.partial(gather_back_kernel, chips, fsdp_count),...  131 us
    pallas_call x1, Pallas kernels, bring_in(): pl.pallas_call(functools.partial(bring_in_kernel, chips, fsdp_count), out...  99.3 us
    pallas_call x1, Pallas kernels, project(): pl.pallas_call(functools.partial(project_kernel, chips, fsdp_count), out_...  92.6 us
    pallas_call x1, Pallas kernels, feed_forward(): pl.pallas_call(functools.partial(feed_forward_kernel, chips), out_shape=(...  86.1 us
    pallas_call x1, Pallas kernels, take_out(): pl.pallas_call(functools.partial(take_out_kernel, chips, fsdp_count), out...  82 us
    pallas_call x1, Pallas kernels, feed_forward_back(): pl.pallas_call(functools.partial(feed_forward_back_kernel, chips), out_sh...  76.7 us

profile of v6, /device:TPU:0, one launch (start us, length us, event | category | flops | bytes accessed | tf_op | source)
XLA Modules:
  0.0 667.6 jit_solution(14186147974102106431)
XLA Ops:
  0.6 1.3 fusion.39.gains_ref
  2.0 99.3 %bring_in.1 = (bf16[8,128,2048]{2,1,0:T(8,128)(2,1)}, bf16[3,8,4,64,256]{4,3,2,1,0:T(8,128)(2,1)}, bf16[4,64,2048]{2,1,0:T(8,128)(2,1)}, bf16[1,8,4,64,1024]{4,3,2,1,0:T(8,128)(2,1)}, bf16[8,4,16,128]{3,2,1,0:T(8,128)(2,1)}) custom-call(bf16[128,2048]{1,0:T(8,128)(2,1)} %bitcast.131, bf16[64,2048]{1,0:T(8,128)(2,1)} %query_ref.1, bf16[64,2048]{1,0:T(8,128)(2,1)} %key_ref.1, ...), custom_call_target="tpu_custom_call" | custom-call | tf_op jit(solution)/shard_map/bring_in/pallas_call | solution.py:1215
  101.3 3.3 fusion.50
  104.5 2.3 multiply_reduce_fusion.5
  106.8 2.3 multiply_reduce_fusion.4
  109.1 0.6 reshape.249.local_ref
  109.7 7.2 %square_sum.1 = f32[16,128]{1,0:T(8,128)} custom-call(f32[16,128]{1,0:T(8,128)} %reshape.249.local_ref), custom_call_target="tpu_custom_call" | custom-call | tf_op jit(solution)/shard_map/square_sum/pallas_call | solution.py:1855
  116.9 0.7 add_rsqrt_fusion
  117.6 0.9 convert_bitcast_fusion
  118.8 1.6 copy.37
  120.6 0.5 reshape.250
  121.2 2.4 fusion.52
  124.0 1.3 multiply_multiply_fusion
  125.3 1.7 reshape.252
  127.1 1.1 fusion.51
  128.2 1.9 multiply_cosine_fusion
  130.1 0.3 pad_maximum_fusion.2
  130.5 0.8 copy-done.7
  131.3 2.5 maximum_multiply_fusion.1
  133.8 0.4 mul.266
  134.2 0.6 fusion.26
  134.8 0.9 copy_bitcast_fusion.1
  135.8 3.7 convolution_convert_fusion
  139.6 0.9 copy_bitcast_fusion
  140.6 20.1 %while.10 = (s32[]{:T(128)}, bf16[2,512,2,128]{3,2,1,0:T(2,128)(2,1)S(1)}, s32[2]{0:T(128)S(1)}, s32[1,1024]{1,0:T(1,128)S(1)}, s32[1024]{0:T(1024)S(1)}, /*inde...) while((s32[]{:T(128)}, ...), condition=%wide.region_5.6_spmd, body=%wide.region_2.5_spmd.sunk | while | flops 544867840 | bytes 14178523 | solution.py:1967
  140.6 0.6 dynamic_slice.25
  141.9 0.5 fusion.73
  142.6 4.7 fusion.74
  147.3 2.9 fusion.75
  150.6 0.6 dynamic_slice.25
  151.9 0.5 fusion.73
  152.6 4.7 fusion.74
  157.4 2.9 fusion.75
  160.6 0.3 stack_reshape.3
  161.0 0.4 copy-done.18
  161.4 2.7 pad_maximum_fusion.refs_13_
  164.1 1.1 reshape_reshape.3.attended_ref
  165.3 92.6 %project.1 = (f32[128,2048]{1,0:T(8,128)}, bf16[1,8,4,64,1024]{4,3,2,1,0:T(8,128)(2,1)}, bf16[1,8,4,64,1024]{4,3,2,1,0:T(8,128)(2,1)}) custom-call(bf16[8,128,256]{2,1,0:T(8,128)(2,1)} %reshape_reshape.3.attended_ref, bf16[256,2048]{1,0:T(8,128)(2,1)} %bitcast.136, bf16[64,8192]{1,0:T(8,128)(2,1)} %up_ref.1, bf16[64,8192]{1,0:T(8,128)(2,1)} %down_ref.1), custom_call_target="tpu_custom_call" | custom-call | tf_op jit(solution)/shard_map/project/pallas_call | solution.py:1350
  257.8 1.4 multiply_reduce_fusion.3
  259.3 2.3 fusion.28.hidden_ref
  261.6 86.1 %feed_forward.1 = (f32[128,2048]{1,0:T(8,128)}, f32[8,128,1024]{2,1,0:T(8,128)}, f32[8,128,1024]{2,1,0:T(8,128)}, bf16[8,128,1024]{2,1,0:T(8,128)(2,1)}, bf16[8,128,2048]{2,1,0:T(8,128)(2,1)}) custom-call(bf16[128,2048]{1,0:T(8,128)(2,1)} %fusion.28.hidden_ref, bf16[2048,1024]{1,0:T(8,128)(2,1)} %bitcast.122, bf16[2048,1024]{1,0:T(8,128)(2,1)} %bitcast.124, ...), custom_call_target="tpu_custom_call" | custom-call | tf_op jit(solution)/shard_map/feed_forward/pallas_call | solution.py:604
  347.7 1.4 multiply_reduce_fusion.2
  349.1 1.6 fusion.25
  350.7 2.3 fusion.23.grad_ref
  353.0 76.7 %feed_forward_back.1 = (f32[128,2048]{1,0:T(8,128)}, bf16[8,128,1024]{2,1,0:T(8,128)(2,1)}, bf16[8,128,1024]{2,1,0:T(8,128)(2,1)}, bf16[8,128,2048]{2,1,0:T(8,128)(2,1)}) custom-call(bf16[128,2048]{1,0:T(8,128)(2,1)} %fusion.23.grad_ref, bf16[2048,1024]{1,0:T(8,128)(2,1)} %bitcast.123, bf16[2048,1024]{1,0:T(8,128)(2,1)} %bitcast.125, ...), custom_call_target="tpu_custom_call" | custom-call | tf_op jit(solution)/shard_map/feed_forward_back/pallas_call | solution.py:637
  429.8 2.0 multiply_reduce_fusion
  431.8 3.5 fusion.24
  435.3 0.6 pad_maximum_fusion.5.refs_2_
  435.9 1.5 pad_maximum_fusion.1.refs_14_
  437.4 1.0 copy.44
  438.4 1.0 copy.48.refs_6_
  439.4 131.3 %gather_back.1 = (f32[64,8192]{1,0:T(8,128)}, f32[64,8192]{1,0:T(8,128)}, f32[64,8192]{1,0:T(8,128)}, bf16[256,2048]{1,0:T(8,128)(2,1)}, bf16[3,1024,256]{2,1,0:T(8,128)(2,1)}, /*index=5*/f32[8,256]{1,0:T(8,128)}) custom-call(bf16[128,2048]{1,0:T(8,128)(2,1)} %get-tuple-element.159.refs_0_, bf16[256,2048]{1,0:T(8,128)(2,1)} %bitcast.137, ...), custom_call_target="tpu_custom_call" | custom-call | tf_op jit(solution)/shard_map/gather_back/pallas_call | solution.py:1609
  570.7 0.7 slice_dynamic-update-slice_fusion
  571.8 0.7 pad.9.refs_4_
  572.5 82.0 %take_out.1 = (f32[128,2048]{1,0:T(8,128)}, f32[64,2048]{1,0:T(8,128)}, f32[64,2048]{1,0:T(8,128)}, f32[64,2048]{1,0:T(8,128)}, f32[64,2048]{1,0:T(8,128)}, /*index=5*/f32[8,128]{1,0:T(8,128)}) custom-call(bf16[3,8,128,256]{3,2,1,0:T(8,128)(2,1)} %bitcast.150, bf16[3,2048,256]{2,1,0:T(8,128)(2,1)} %bitcast.130, bf16[1024,2048]{1,0:T(8,128)(2,1)} %bitcast.139, ...), custom_call_target="tpu_custom_call" | custom-call | tf_op jit(solution)/shard_map/take_out/pallas_call | solution.py:1788
  654.6 2.9 add_bitcast_fusion
  657.4 1.3 slice_bitcast_fusion.2
  658.8 2.0 copy.100
  660.8 0.8 copy.101
  661.6 0.8 copy.102
  662.4 0.8 copy.103
  663.2 1.3 copy.104
  664.5 1.3 copy.105
  665.8 1.3 copy.106
  (90 shorter events, 3.0 us)
Async XLA Ops:
  101.3 3.3 copy-start.12
  120.4 13.8 %copy-start = (f32[1024,256]{1,0:T(8,128)}, f32[1024,256]{1,0:T(8,128)S(1)}, u32[]{:S(2)}) copy-start(f32[1024,256]{1,0:T(8,128)S(1)} %copy.37) | copy-start | bytes 3145732
  121.2 2.5 copy-start.21
  124.0 10.2 %copy-start.2 = (f32[1024,256]{1,0:T(8,128)}, f32[1024,256]{1,0:T(8,128)S(1)}, u32[]{:S(2)}) copy-start(f32[1024,256]{1,0:T(8,128)S(1)} %copy.38) | copy-start | bytes 3145732
  127.0 4.2 copy-start.13
  127.1 4.2 copy-start.14
  130.5 0.8 copy-start.7
  130.5 3.7 copy-start.6
  134.8 4.8 copy-start.8
  134.8 4.8 copy-start.10
  135.8 4.7 copy-start.26
  139.6 1.0 copy-start.20
  140.6 20.9 %copy-start.9 = (bf16[1024,256]{1,0:T(8,128)(2,1)S(1)}, bf16[1024,256]{1,0:T(8,128)(2,1)}, u32[]{:S(2)}) copy-start(bf16[1024,256]{1,0:T(8,128)(2,1)} %copy-done.8) | copy-start | bytes 1572868
  140.6 20.9 %copy-start.11 = (bf16[1024,256]{1,0:T(8,128)(2,1)S(1)}, bf16[1024,256]{1,0:T(8,128)(2,1)}, u32[]{:S(2)}) copy-start(bf16[1024,256]{1,0:T(8,128)(2,1)} %copy-done.10) | copy-start | bytes 1572868
  142.6 4.7 copy-start.22
  152.6 4.7 copy-start.22
  160.6 0.8 copy-start.18
  161.4 2.7 copy-start.19
  161.4 97.9 %copy-start.5 = (bf16[1,128,2048]{2,1,0:T(8,128)(2,1)S(1)}, bf16[1,128,2048]{2,1,0:T(8,128)(2,1)}, u32[]{:S(2)}) copy-start(bf16[1,128,2048]{2,1,0:T(8,128)(2,1)} %param.16) | copy-start | bytes 1572868
  261.6 87.6 %copy-start.4 = (bf16[1,128,2048]{2,1,0:T(8,128)(2,1)S(1)}, bf16[1,128,2048]{2,1,0:T(8,128)(2,1)}, u32[]{:S(2)}) copy-start(bf16[1,128,2048]{2,1,0:T(8,128)(2,1)} %param.29) | copy-start | bytes 1572868
  429.8 6.1 copy-start.1
  429.8 6.1 copy-start.3
  654.5 6.3 copy-start.25
  654.5 7.1 %copy-start.24 = (f32[64,2048]{1,0:T(8,128)S(1)}, f32[64,2048]{1,0:T(8,128)}, u32[]{:S(2)}) copy-start(f32[64,2048]{1,0:T(8,128)} %get-tuple-element.292) | copy-start | bytes 1572868
  654.6 7.8 %copy-start.23 = (f32[64,2048]{1,0:T(8,128)S(1)}, f32[64,2048]{1,0:T(8,128)}, u32[]{:S(2)}) copy-start(f32[64,2048]{1,0:T(8,128)} %get-tuple-element.293) | copy-start | bytes 1572868
  654.6 8.6 %copy-start.17 = (f32[64,8192]{1,0:T(8,128)S(1)}, f32[64,8192]{1,0:T(8,128)}, u32[]{:S(2)}) copy-start(f32[64,8192]{1,0:T(8,128)} %get-tuple-element.297) | copy-start | bytes 6291460
  658.8 5.7 copy-start.16
  663.2 2.6 copy-start.15

commit v7 on v6

--- a/solution.py
+++ b/solution.py
@@ -7,7 +7,6 @@
 from jax.experimental.pallas import tpu as pltpu
 from jax.sharding import PartitionSpec as P
 
-HEADS = 16
 DH = 128
 
 
@@ -18,62 +17,6 @@
 
 def rms_scale(tensor, gain):
     return tensor * lax.rsqrt(jnp.mean(tensor * tensor, axis=-1, keepdims=True) + eps_norm) * gain
-
-
-def rotary(tensor, positions):
-    row_count = tensor.shape[0]
-    grouped = tensor.reshape(row_count, HEADS, DH)
-    half_width = DH // 2
-    frequency = rope_base ** (-jnp.arange(half_width, dtype=jnp.float32) * 2.0 / DH)
-    angles = positions.astype(jnp.float32)[:, None] * frequency[None, :]
-    cosine = jnp.cos(angles)[:, None, :]
-    sine_table = jnp.sin(angles)[:, None, :]
-    first_half = grouped[..., :half_width]
-    second_half = grouped[..., half_width:]
-    turned = jnp.concatenate(
-        [
-            first_half * cosine - second_half * sine_table,
-            second_half * cosine + first_half * sine_table,
-        ],
-        axis=-1,
-    )
-    return turned.reshape(tensor.shape)
-
-
-def norm_rotary(tensor, gain, positions):
-    return rotary(rms_scale(tensor, gain), positions)
-
-
-def swiglu_act(gate_linear, up_linear):
-    return jax.nn.silu(gate_linear) * up_linear
-
-
-def contract_rows(left, right):
-    return lax.dot_general(
-        left, right, (((0,), (0,)), ((), ())), preferred_element_type=jnp.float32
-    )
-
-
-def contract_cols(left, right):
-    return lax.dot_general(
-        left, right, (((1,), (1,)), ((), ())), preferred_element_type=jnp.float32
-    )
-
-
-def masked_scores(query_block, key_heads, first_row, segment_row, score_scale):
-    block_rows = query_block.shape[0]
-    sequence_rows = key_heads.shape[0]
-    scores = (
-        jnp.einsum("qhd,khd->hqk", query_block, key_heads, preferred_element_type=jnp.float32)
-        * score_scale
-    )
-    query_pos = first_row + jnp.arange(block_rows, dtype=jnp.int32)
-    key_pos = jnp.arange(sequence_rows, dtype=jnp.int32)
-    query_seg = lax.dynamic_slice_in_dim(segment_row, first_row, block_rows, 0)
-    allowed = (key_pos[None, :] <= query_pos[:, None]) & (
-        segment_row[None, :] == query_seg[:, None]
-    )
-    return jnp.where(allowed[None], scores, neg_fill)
 
 
 MESH = pl.DeviceIdType.MESH
@@ -711,26 +654,28 @@
 
 
 class Spread:
-    def __init__(self, cross, sources, weights, row_send, row_recv, side_send, side_recv, half_send, half_recv):
-        self.cross, self.sources, self.weights = cross, sources, weights
+    def __init__(self, cross, group, stack, weights, row_send, row_recv, side_send, side_recv, half_send, half_recv):
+        self.cross, self.group, self.stack, self.weights = cross, group, stack, weights
         self.row_send, self.row_recv = row_send, row_recv
         self.side_send, self.side_recv = side_send, side_recv
         self.half_send, self.half_recv = half_send, half_recv
-        self.kinds, self.columns = len(sources), weights.shape[-1]
-        self.rows = weights.shape[-2]
+        self.columns, self.rows = weights.shape[-1], weights.shape[-2]
+        self.items = weights.shape[0] // group * cross.seq_count
 
     @staticmethod
-    def scratch(kinds, seq_count, fsdp_count, rows, columns):
+    def scratch(kinds, group, seq_count, fsdp_count, rows, columns):
         dma = pltpu.SemaphoreType.DMA
         sides = 2 if fsdp_count == 4 else fsdp_count - 1
+        items = kinds // group * seq_count
         return [
+            pltpu.VMEM((kinds, rows, seq_count * columns), jnp.bfloat16),
             pltpu.VMEM((kinds, seq_count, fsdp_count, rows, columns), jnp.bfloat16),
             dma((kinds, seq_count)),
             dma((kinds, seq_count)),
-            dma((seq_count, sides)),
-            dma((seq_count, sides)),
-            dma((seq_count, 2)),
-            dma((seq_count, 2)),
+            dma((items, sides)),
+            dma((items, sides)),
+            dma((items, 2)),
+            dma((items, 2)),
         ]
 
     def block(self, owner):
@@ -740,7 +685,7 @@
         cross = self.cross
         peer = cross.seq_peer(step)
         return cross.remote(
-            self.sources[kind].at[:, self.block(peer)],
+            self.stack.at[kind, :, self.block(peer)],
             self.weights.at[kind, cross.seq, cross.fsdp],
             self.row_send.at[kind, step],
             self.row_recv.at[kind, step],
@@ -748,81 +693,91 @@
             cross.fsdp,
         )
 
-    def side(self, owner, side):
+    def place(self, item):
+        count = self.cross.seq_count
+        step = item % count
+        return item // count * self.group, step, (self.cross.seq - step + count) % count
+
+    def side(self, item, side):
         cross = self.cross
-        ref = self.weights.at[:, owner, cross.fsdp]
+        first, _, owner = self.place(item)
+        ref = self.weights.at[pl.ds(first, self.group), owner, cross.fsdp]
         return cross.remote(
             ref,
             ref,
-            self.side_send.at[owner, side],
-            self.side_recv.at[owner, side],
+            self.side_send.at[item, side],
+            self.side_recv.at[item, side],
             cross.seq,
             cross.sides[side],
         )
 
-    def half(self, owner, side):
+    def half(self, item, side):
         cross = self.cross
+        first, _, owner = self.place(item)
         rows = pl.ds(side * (self.rows // 2), self.rows // 2)
-        ref = self.weights.at[:, owner, cross.sides[side], rows]
+        ref = self.weights.at[pl.ds(first, self.group), owner, cross.sides[side], rows]
         return cross.remote(
             ref,
             ref,
-            self.half_send.at[owner, side],
-            self.half_recv.at[owner, side],
+            self.half_send.at[item, side],
+            self.half_recv.at[item, side],
             cross.seq,
             cross.sides[1 - side],
         )
 
-    def start(self):
+    def send_rows(self, item):
+        first, step, _ = self.place(item)
+
+        @pl.when(step > 0)
+        def _():
+            for kind in range(self.group):
+                self.row(first + kind, step).start()
+
+    def take(self, item):
         cross = self.cross
-        for step in range(1, cross.seq_count):
-            for kind in range(self.kinds):
-                self.row(kind, step).start()
-
-    def own(self):
-        cross = self.cross
-        for kind in range(self.kinds):
-            self.weights[kind, cross.seq, cross.fsdp] = self.sources[kind][:, self.block(cross.seq)]
-        self.pass_on(0)
-
-    def owner(self, step):
-        return (self.cross.seq - step + self.cross.seq_count) % self.cross.seq_count
-
-    def take(self, step):
-        for kind in range(self.kinds):
-            self.row(kind, step).wait_recv()
-        self.pass_on(step)
-
-    def pass_on(self, step):
+        first, step, _ = self.place(item)
+
+        @pl.when(step > 0)
+        def _():
+            for kind in range(self.group):
+                self.row(first + kind, step).wait_recv()
+
+        @pl.when(step == 0)
+        def _():
+            for kind in range(self.group):
+                own = self.stack[first + kind, :, self.block(cross.seq)]
+                self.weights[first + kind, cross.seq, cross.fsdp] = own
+
+        for side in range(len(cross.sides)):
+            self.side(item, side).start()
+
+    def relay(self, item):
         for side in range(len(self.cross.sides)):
-            self.side(self.owner(step), side).start()
-
-    def relay(self, step):
-        owner = self.owner(step)
-        for side in range(len(self.cross.sides)):
-            self.side(owner, side).wait_recv()
+            self.side(item, side).wait_recv()
             if self.cross.square:
-                self.half(owner, side).start()
-
-    def settle(self, step):
+                self.half(item, side).start()
+
+    def settle(self, item):
         if self.cross.square:
             for side in range(2):
-                self.half(self.owner(step), side).wait_recv()
+                self.half(item, side).wait_recv()
 
     def finish(self):
         cross = self.cross
 
-        @pl.loop(1, cross.seq_count)
-        def _(step):
-            for kind in range(self.kinds):
-                self.row(kind, step).wait_send()
-
-        @pl.loop(0, cross.seq_count)
-        def _(owner):
+        @pl.loop(0, self.items)
+        def _(item):
+            first, step, _ = self.place(item)
+
+            @pl.when(step > 0)
+            def _():
+                for kind in range(self.group):
+                    self.row(first + kind, step).wait_send()
+
             for side in range(len(cross.sides)):
-                self.side(owner, side).wait_send()
+                self.side(item, side).wait_send()
                 if cross.square:
-                    self.half(owner, side).wait_send()
+                    self.half(item, side).wait_send()
 
 
 AHEAD = 2
@@ -1055,38 +1010,131 @@
             self.free_row(turn)
 
 
-def bring_in_kernel(
-    chips,
-    fsdp_count,
-    inputs_ref,
-    query_ref,
-    key_ref,
-    value_ref,
-    output_ref,
-    gate_ref,
-    gains_ref,
-    inputs_out,
-    weights_out,
-    output_out,
-    gate_out,
-    gains_out,
-    outputs,
-    gains,
-    gain_row_send,
-    gain_row_recv,
-    gain_column_send,
-    gain_column_recv,
-    output_send,
-    output_recv,
-    store_sem,
-    *comm,
-):
+def dot_rows(left, right, precision=None):
+    return lax.dot_general(
+        left,
+        right,
+        (((0,), (0,)), ((), ())),
+        precision=precision,
+        preferred_element_type=jnp.float32,
+    )
+
+
+EXACT = lax.Precision.HIGHEST
+
+
+def turn_heads(tensor, cosine, sine):
+    heads = [
+        tensor[:, first : first + DH] * cosine
+        + pltpu.roll(tensor[:, first : first + DH], DH // 2, 1) * sine
+        for first in range(0, tensor.shape[1], DH)
+    ]
+    return jnp.concatenate(heads, axis=1) if len(heads) > 1 else heads[0]
+
+
+def attention_weights(queries, keys, first_row, segment_column, segment_row):
+    rows, count = queries.shape[0], keys.shape[0]
+    scores = dot_cols(queries, keys) * DH ** (-0.5)
+    query_place = first_row + lax.broadcasted_iota(jnp.int32, (rows, count), 0)
+    key_place = lax.broadcasted_iota(jnp.int32, (rows, count), 1)
+    allowed = (key_place <= query_place) & (segment_row == segment_column)
+    scores = jnp.where(allowed, scores, neg_fill)
+    expanded = jnp.exp(scores - jnp.max(scores, axis=-1, keepdims=True))
+    return expanded / jnp.sum(expanded, axis=-1, keepdims=True)
+
+
+class RowSum:
+    def __init__(self, cross, local, every, send_sem, recv_sem):
+        self.cross, self.local, self.every = cross, local, every
+        self.send_sem, self.recv_sem = send_sem, recv_sem
+
+    @staticmethod
+    def scratch(seq_count, shape):
+        dma = pltpu.SemaphoreType.DMA
+        return [
+            pltpu.VMEM(shape, jnp.float32),
+            pltpu.VMEM((seq_count,) + shape, jnp.float32),
+            dma((seq_count,)),
+            dma((seq_count,)),
+        ]
+
+    def copy(self, step):
+        cross = self.cross
+        return cross.remote(
+            self.local,
+            self.every.at[step],
+            self.send_sem.at[step],
+            self.recv_sem.at[step],
+            cross.seq_peer(step),
+            cross.fsdp,
+        )
+
+    def send(self, value):
+        self.local[...] = value
+        for step in range(1, self.cross.seq_count):
+            self.copy(step).start()
+
+    def receive(self):
+        total = self.local[...]
+        for step in range(1, self.cross.seq_count):
+            self.copy(step).wait_recv()
+            total = total + self.every[step]
+        return total
+
+    def finish(self):
+        for step in range(1, self.cross.seq_count):
+            self.copy(step).wait_send()
+
+
+def pick_row(row, shape):
+    return jnp.where(lax.broadcasted_iota(jnp.int32, shape, 0) == row, 1.0, 0.0)
+
+
+def product_terms(scatter, pairs, chip):
+    _, rows, width = scatter.fresh.shape
+    pair = pl.ds(chip * 2, 2)
+
+    @pl.loop(0, width // tile_of(width))
+    def _(tile):
+        columns = pl.ds(pl.multiple_of(tile * tile_of(width), 128), tile_of(width))
+        total = None
+        for left, right, across in pairs:
+            tokens = left[pair].reshape(2 * rows, -1)
+            if across:
+                term = dot_cols(tokens, right[columns, :])
+            else:
+                term = jnp.dot(tokens, right(columns), preferred_element_type=jnp.float32)
+            total = term if total is None else total + term
+        scatter.fresh[:, :, columns] = total.reshape(2, rows, -1)
+
+    scatter.after_term(chip)
+
+
+EARLY = 6
+LEAD = 2
+HOPPING = 4
+
+
+def bring_in_kernel(chips, fsdp_count, *refs):
+    inputs_ref, gains_ref, cosine_ref, sine_ref, segment_column, segment_row = refs[:6]
+    sources, output_ref, refs = refs[6:12], refs[12], refs[13:]
+    projected, inverse_out, own_gains, gains_out = refs[:4]
+    inputs_out, attention_out, output_out, units_out, heads_out, pre_out = refs[4:10]
+    outputs, gains, heads, pre, refs = refs[10], refs[11], refs[12], refs[13], refs[14:]
+    gain_row_send, gain_row_recv, gain_column_send, gain_column_recv = refs[:4]
+    output_send, output_recv, load_sem, store_sem, refs = refs[4], refs[5], refs[6], refs[7], refs[8:]
     line = Line(chips)
     cross = Cross(2 * chips, fsdp_count)
-    gather = Gather(line, *comm[:5])
-    attention = Spread(cross, (query_ref, key_ref, value_ref), *comm[5:12])
-    gate = Spread(cross, (gate_ref,), *comm[12:])
+    gather, refs = Gather(line, *refs[:5]), refs[5:]
+    sums, refs = RowSum(cross, *refs[:4]), refs[4:]
+    attention, refs = Spread(cross, 3, *refs[:8]), refs[8:]
+    units, refs = Spread(cross, 1, *refs[:8]), refs[8:]
+    scatter = Scatter(line, *refs)
     seq_count, seq, fsdp = cross.seq_count, cross.seq, cross.fsdp
+    blocks = gather.blocks
+    _, rows, width = blocks.shape
+    columns = attention.columns
+    tokens = seq_count * rows
 
     def gain_row(step):
         return cross.remote(
@@ -1119,71 +1167,215 @@
             cross.fsdp_peer(step),
         )
 
+    stacks = [attention.stack.at[kind] for kind in range(3)]
+    stacks += [units.stack.at[kind] for kind in range(3)]
+    copies = load(
+        [(source, stack, load_sem.at[i]) for i, (source, stack) in enumerate(zip(sources, stacks))]
+    )
     greet_cross(seq_count, fsdp_count)
+    for copy in copies:
+        copy.wait()
+
+    @pl.loop(0, attention.items)
+    def _(item):
+        attention.send_rows(item)
+
     for step in range(1, seq_count):
         gain_row(step).start()
-    attention.start()
-    gate.start()
-    gather.blocks[line.place * 2 + line.core] = inputs_ref[...]
+    blocks[line.place * 2 + line.core] = inputs_ref[...]
     gather.send(line.place)
+
+    @pl.loop(0, EARLY)
+    def _(item):
+        units.send_rows(item)
+
     gains[seq, fsdp] = gains_ref[...]
     outputs[fsdp] = output_ref[...]
-    attention.own()
     for step in range(1, fsdp_count):
         gain_column(seq, step).start()
+
+    attention.take(0)
 
     @pl.loop(1, seq_count)
     def _(step):
         attention.take(step)
         gain_row(step).wait_recv()
+        owner = (seq - step + seq_count) % seq_count
         for peer in range(1, fsdp_count):
-            gain_column(attention.owner(step), peer).start()
+            gain_column(owner, peer).start()
         attention.relay(step - 1)
 
-    gate.own()
-    attention.relay(seq_count - 1)
-    gather.step(0)
-
-    @pl.loop(1, seq_count)
-    def _(step):
-        gate.take(step)
-        gate.relay(step - 1)
-
-        @pl.when((step % 2 == 0) & (step > 2))
-        def _():
-            gather.step(step // 2 - 1)
-
-    for step in range(1, fsdp_count):
-        output_copy(step).start()
-    gate.relay(seq_count - 1)
-    if chips > 1:
-        gather.step(chips - 1)
-    inputs_store = pltpu.make_async_copy(gather.blocks, inputs_out, store_sem.at[0])
-    inputs_store.start()
-
-    @pl.loop(0, seq_count)
-    def _(step):
-        attention.settle(step)
-        for peer in range(1, fsdp_count):
-            gain_column(step, peer).wait_recv()
-
-    weights_store = pltpu.make_async_copy(attention.weights, weights_out, store_sem.at[1])
-    weights_store.start()
-    for step in range(1, fsdp_count):
-        output_copy(step).wait_recv()
+    def project_inputs(step):
+        chip = gather.step(step)
+        pair = pl.ds(chip * 2, 2)
+        whole = blocks[pair].reshape(2 * rows, width)
+        for kind in range(3):
+            weight = attention.weights[kind].reshape(width, columns)
+            found = jnp.dot(whole, weight, preferred_element_type=jnp.float32)
+            if kind < 2:
+                pre[kind, pl.ds(chip * 2 * rows, 2 * rows)] = found
+            else:
+                heads[2, pair] = found.astype(jnp.bfloat16).reshape(2, rows, columns)
+
+    def weights_arrived():
+        attention.relay(seq_count - 1)
+        for step in range(1, fsdp_count):
+            output_copy(step).start()
+
+        @pl.loop(0, seq_count)
+        def _(item):
+            attention.settle(item)
+            for peer in range(1, fsdp_count):
+                gain_column(item, peer).wait_recv()
+
+        gains_out[...] = gains[...]
+        lanes = gains.shape[-1]
+        own = columns // fsdp_count
+        lane = lax.broadcasted_iota(jnp.int32, (lanes, columns), 0)
+        column = lax.broadcasted_iota(jnp.int32, (lanes, columns), 1)
+        total = None
+        for peer in range(fsdp_count):
+            place = (column == lane + peer * own) & (lane < own)
+            term = jnp.dot(
+                gains[seq, peer],
+                jnp.where(place, 1.0, 0.0).astype(jnp.bfloat16),
+                preferred_element_type=jnp.float32,
+            )
+            total = term if total is None else total + term
+        own_gains[...] = total
+        project_inputs(0)
+
+    def send_squares():
+        total = None
+        for kind in range(2):
+            row = lax.dot_general(
+                pick_row(kind, (8, columns)),
+                pre[kind] * pre[kind],
+                (((1,), (1,)), ((), ())),
+                precision=EXACT,
+                preferred_element_type=jnp.float32,
+            )
+            total = row if total is None else total + row
+        sums.send(total)
+
+    def make_heads():
+        squares = sums.receive()
+        for kind in range(2):
+            mean = dot_rows(squares, pick_row(kind, (8, 128)), EXACT) / width
+            inverse = lax.rsqrt(mean + eps_norm)
+            inverse_out[:, kind : kind + 1] = inverse[:, :1]
+            for first in range(0, columns, DH):
+                part = pl.ds(first, DH)
+                scaled = pre[kind, :, part] * inverse * own_gains[kind : kind + 1, part]
+                turned = turn_heads(scaled, cosine_ref[...], sine_ref[...])
+                heads[kind, :, :, part] = turned.astype(jnp.bfloat16).reshape(seq_count, rows, DH)
+
+    def attend(step):
+        chip = line.order(chips - 1 - step)
+
+        @pl.loop(0, 2)
+        def _(core):
+            slot = chip * 2 + core
+            first = pl.multiple_of(slot * rows, rows)
+            for head in range(0, columns, DH):
+                part = pl.ds(head, DH)
+                probs = attention_weights(
+                    heads[0, slot, :, part],
+                    heads[1, :, :, part].reshape(tokens, DH),
+                    first,
+                    segment_column[pl.ds(first, rows), :],
+                    segment_row[...],
+                )
+                heads[3, slot, :, part] = jnp.dot(
+                    probs.astype(jnp.bfloat16),
+                    heads[2, :, :, part].reshape(tokens, DH),
+                    preferred_element_type=jnp.float32,
+                ).astype(jnp.bfloat16)
+
+        product_terms(
+            scatter,
+            [(heads.at[3], lambda part: outputs[:, :, part].reshape(columns, -1), False)],
+            chip,
+        )
+
+    inputs_store = pltpu.make_async_copy(blocks, inputs_out, store_sem.at[0])
+    attention_store = pltpu.make_async_copy(attention.weights, attention_out, store_sem.at[1])
     output_store = pltpu.make_async_copy(outputs, output_out, store_sem.at[2])
-    output_store.start()
-    gains_out[...] = gains[...]
-
-    @pl.loop(0, seq_count)
-    def _(step):
-        gate.settle(step)
-
-    gate_store = pltpu.make_async_copy(gate.weights, gate_out, store_sem.at[3])
-    gate_store.start()
+    heads_store = pltpu.make_async_copy(heads, heads_out, store_sem.at[3])
+    pre_store = pltpu.make_async_copy(pre, pre_out, store_sem.at[4])
+
+    def units_store(kind):
+        return pltpu.make_async_copy(units.weights.at[kind], units_out.at[kind], store_sem.at[5 + kind])
+
+    @pl.loop(0, LEAD)
+    def _(item):
+        units.take(item)
+
+    arrived = 1
+    after_gather = 4 * (chips - 1) - 1
+    attending = after_gather + 3
+    hopping = attending + chips
+    beats = max(units.items + 1, hopping + 2 * chips)
+
+    @pl.loop(0, beats)
+    def _(beat):
+        @pl.when(beat + EARLY < units.items)
+        def _():
+            units.send_rows(beat + EARLY)
+
+        @pl.when(beat + LEAD < units.items)
+        def _():
+            units.take(beat + LEAD)
+
+        @pl.when((beat > 0) & (beat <= units.items))
+        def _():
+            units.relay(beat - 1)
+
+        @pl.when(beat == arrived)
+        def _():
+            weights_arrived()
+            attention_store.start()
+
+        @pl.when((beat % 4 == 2) & (beat // 4 + 1 < chips))
+        def _():
+            project_inputs(beat // 4 + 1)
+
+        @pl.when(beat == after_gather)
+        def _():
+            inputs_store.start()
+            pre_store.start()
+            send_squares()
+            for step in range(1, fsdp_count):
+                output_copy(step).wait_recv()
+            output_store.start()
+
+        @pl.when(beat == after_gather + 2)
+        def _():
+            make_heads()
+
+        @pl.when((beat >= attending) & (beat < attending + chips))
+        def _():
+            attend(beat - attending)
+
+        @pl.when((beat >= hopping) & ((beat - hopping) % 2 == 0) & (beat < hopping + 2 * chips))
+        def _():
+            scatter.hop(chips - 1 - (beat - hopping) // 2)
+
+    heads_store.start()
+    scatter.settle(projected)
+    for kind in range(3):
+
+        @pl.loop(0, seq_count)
+        def _(step):
+            units.settle(kind * seq_count + step)
+
+        units_store(kind).start()
+
+    scatter.finish()
     gather.finish()
+    sums.finish()
     attention.finish()
-    gate.finish()
+    units.finish()
 
     @pl.loop(1, seq_count)
     def _(step):
@@ -1196,249 +1388,85 @@
 
     for step in range(1, fsdp_count):
         output_copy(step).wait_send()
-    inputs_store.wait()
-    weights_store.wait()
-    output_store.wait()
-    gate_store.wait()
-
-
-def bring_in(local_in, query_weight, key_weight, value_weight, output_weight, gate_weight, gains):
+    for store in (inputs_store, attention_store, output_store, heads_store, pre_store):
+        store.wait()
+    for kind in range(3):
+        units_store(kind).wait()
+
+
+def bring_in(local_in, attention_rows, unit_rows, output_weight, gains, tables, segment_row):
     rows, width = local_in.shape
     slots = lax.axis_size("seq")
     fsdp_count = lax.axis_size("fsdp")
     chips = slots // 2
-    own_rows, columns = query_weight.shape[0], query_weight.shape[1] // slots
-    units = gate_weight.shape[1] // slots
-    bf16, dma = jnp.bfloat16, pltpu.SemaphoreType.DMA
+    tokens = slots * rows
+    own, columns = attention_rows[0].shape[0], attention_rows[0].shape[1] // slots
+    units = unit_rows[0].shape[1] // slots
+    bf16, f32, dma = jnp.bfloat16, jnp.float32, pltpu.SemaphoreType.DMA
     lanes = pl.cdiv(gains.shape[1], 128) * 128
     padded = jnp.pad(gains, ((0, 16 - gains.shape[0]), (0, lanes - gains.shape[1])))
-    inputs_all, weights, outputs, gate, gains_all = pl.pallas_call(
+    found = pl.pallas_call(
         functools.partial(bring_in_kernel, chips, fsdp_count),
         out_shape=(
+            jax.ShapeDtypeStruct((rows, width), f32),
+            jax.ShapeDtypeStruct((tokens, 8), f32),
+            jax.ShapeDtypeStruct((16, columns), f32),
+            jax.ShapeDtypeStruct((slots, fsdp_count, 16, lanes), bf16),
             jax.ShapeDtypeStruct((slots, rows, width), bf16),
-            jax.ShapeDtypeStruct((3, slots, fsdp_count, own_rows, columns), bf16),
-            jax.ShapeDtypeStruct((fsdp_count, own_rows, width), bf16),
-            jax.ShapeDtypeStruct((1, slots, fsdp_count, own_rows, units), bf16),
-            jax.ShapeDtypeStruct((slots, fsdp_count, 16, lanes), bf16),
+            jax.ShapeDtypeStruct((3, slots, fsdp_count, own, columns), bf16),
+            jax.ShapeDtypeStruct((fsdp_count, own, width), bf16),
+            jax.ShapeDtypeStruct((3, slots, fsdp_count, own, units), bf16),
+            jax.ShapeDtypeStruct((4, slots, rows, columns), bf16),
+            jax.ShapeDtypeStruct((2, tokens, columns), f32),
         ),
-        in_specs=[whole_spec()] * 7,
-        out_specs=(far_spec(),) * 4 + (whole_spec(),),
+        in_specs=[whole_spec()] * 6 + [far_spec()] * 6 + [whole_spec()],
+        out_specs=(whole_spec(),) * 4 + (far_spec(),) * 6,
         scratch_shapes=[
-            pltpu.VMEM((fsdp_count, own_rows, width), bf16),
+            pltpu.VMEM((fsdp_count, own, width), bf16),
             pltpu.VMEM((slots, fsdp_count, 16, lanes), bf16),
+            pltpu.VMEM((4, slots, rows, columns), bf16),
+            pltpu.VMEM((2, tokens, columns), f32),
             dma((slots,)),
             dma((slots,)),
             dma((slots, fsdp_count)),
             dma((slots, fsdp_count)),
             dma((fsdp_count,)),
             dma((fsdp_count,)),
-            dma((4,)),
+            dma((6,)),
+            dma((8,)),
         ]
         + Gather.scratch(chips, rows, width)
-        + Spread.scratch(3, slots, fsdp_count, own_rows, columns)
-        + Spread.scratch(1, slots, fsdp_count, own_rows, units),
+        + RowSum.scratch(slots, (8, tokens))
+        + Spread.scratch(3, 3, slots, fsdp_count, own, columns)
+        + Spread.scratch(3, 1, slots, fsdp_count, own, units)
+        + Scatter.scratch(chips, rows, width),
         compiler_params=line_params(3),
         name="bring_in",
-    )(local_in, query_weight, key_weight, value_weight, output_weight, gate_weight, padded)
-    gains_all = gains_all[:, :, : gains.shape[0], : gains.shape[1]]
+    )(
+        local_in,
+        padded,
+        *tables,
+        segment_row.reshape(tokens, 1),
+        segment_row.reshape(1, tokens),
+        *attention_rows,
+        *unit_rows,
+        output_weight,
+    )
+    projected, inverse, own_gains, every_gain = found[:4]
+    inputs_all, weights, outputs, unit_columns, heads, pre = found[4:]
+    every_gain = every_gain[:, :, : gains.shape[0], : gains.shape[1]]
     return (
+        projected,
         inputs_all.reshape(-1, width),
         weights.reshape(3, -1, columns),
         outputs.reshape(-1, width),
-        gate.reshape(-1, units),
-        gains_all.transpose(2, 0, 1, 3).reshape(gains.shape[0], -1),
-    )
-
-
-def product_terms(scatter, pairs, chip):
-    _, rows, width = scatter.fresh.shape
-    pair = pl.ds(chip * 2, 2)
-
-    @pl.loop(0, width // tile_of(width))
-    def _(tile):
-        columns = pl.ds(pl.multiple_of(tile * tile_of(width), 128), tile_of(width))
-        total = None
-        for left, right, across in pairs:
-            tokens = left[pair].reshape(2 * rows, -1)
-            if across:
-                term = dot_cols(tokens, right[columns, :])
-            else:
-                term = jnp.dot(tokens, right[:, columns], preferred_element_type=jnp.float32)
-            total = term if total is None else total + term
-        scatter.fresh[:, :, columns] = total.reshape(2, rows, -1)
-
-    scatter.after_term(chip)
-
-
-def project_kernel(
-    chips,
-    fsdp_count,
-    attended_ref,
-    output_ref,
-    up_ref,
-    down_ref,
-    result,
-    up_out,
-    down_out,
-    store_sem,
-    *comm,
-):
-    line = Line(chips)
-    cross = Cross(2 * chips, fsdp_count)
-    count = len(Scatter.scratch(chips, 4, 128))
-    scatter = Scatter(line, *comm[:count])
-    up = Spread(cross, (up_ref,), *comm[count : count + 7])
-    down = Spread(cross, (down_ref,), *comm[count + 7 :])
-    greet_cross(cross.seq_count, fsdp_count)
-    up.start()
-    down.start()
-    up.own()
-
-    @pl.loop(0, chips)
-    def _(step):
-        product_terms(scatter, [(attended_ref, output_ref, False)], line.order(chips - 1 - step))
-
-    @pl.loop(1, cross.seq_count)
-    def _(step):
-        up.take(step)
-        up.relay(step - 1)
-
-    down.own()
-    up.relay(cross.seq_count - 1)
-    scatter.hop(0)
-
-    @pl.loop(1, cross.seq_count)
-    def _(step):
-        down.take(step)
-        down.relay(step - 1)
-
-        @pl.when(step % 2 == 0)
-        def _():
-            scatter.hop(step // 2)
-
-    down.relay(cross.seq_count - 1)
-
-    @pl.loop(0, cross.seq_count)
-    def _(step):
-        up.settle(step)
-
-    up_store = pltpu.make_async_copy(up.weights, up_out, store_sem.at[0])
-    up_store.start()
-    scatter.settle(result)
-
-    @pl.loop(0, cross.seq_count)
-    def _(step):
-        down.settle(step)
-
-    down_store = pltpu.make_async_copy(down.weights, down_out, store_sem.at[1])
-    down_store.start()
-    scatter.finish()
-    up.finish()
-    down.finish()
-    up_store.wait()
-    down_store.wait()
-
-
-def project(attended, output_rows, up_weight, down_weight):
-    slots = lax.axis_size("seq")
-    fsdp_count = lax.axis_size("fsdp")
-    chips = slots // 2
-    rows = attended.shape[0] // slots
-    width = output_rows.shape[1]
-    own_rows, units = up_weight.shape[0], up_weight.shape[1] // slots
-    weight = jax.ShapeDtypeStruct((1, slots, fsdp_count, own_rows, units), jnp.bfloat16)
-    projected, up, down = pl.pallas_call(
-        functools.partial(project_kernel, chips, fsdp_count),
-        out_shape=(jax.ShapeDtypeStruct((rows, width), jnp.float32), weight, weight),
-        in_specs=[whole_spec()] * 4,
-        out_specs=(whole_spec(), far_spec(), far_spec()),
-        scratch_shapes=[pltpu.SemaphoreType.DMA((2,))]
-        + Scatter.scratch(chips, rows, width)
-        + Spread.scratch(1, slots, fsdp_count, own_rows, units) * 2,
-        compiler_params=line_params(5),
-        name="project",
-    )(attended.reshape(slots, rows, -1), output_rows, up_weight, down_weight)
-    return projected, up.reshape(-1, units), down.reshape(-1, units)
-
-
-def dot_rows(left, right, precision=None):
-    return lax.dot_general(
-        left,
-        right,
-        (((0,), (0,)), ((), ())),
-        precision=precision,
-        preferred_element_type=jnp.float32,
-    )
-
-
-EXACT = lax.Precision.HIGHEST
-
-
-def turn_heads(tensor, cosine, sine):
-    heads = [
-        tensor[:, first : first + DH] * cosine
-        + pltpu.roll(tensor[:, first : first + DH], DH // 2, 1) * sine
-        for first in range(0, tensor.shape[1], DH)
-    ]
-    return jnp.concatenate(heads, axis=1) if len(heads) > 1 else heads[0]
-
-
-def attention_weights(queries, keys, first_row, segment_column, segment_row):
-    rows, count = queries.shape[0], keys.shape[0]
-    scores = dot_cols(queries, keys) * DH ** (-0.5)
-    query_place = first_row + lax.broadcasted_iota(jnp.int32, (rows, count), 0)
-    key_place = lax.broadcasted_iota(jnp.int32, (rows, count), 1)
-    allowed = (key_place <= query_place) & (segment_row == segment_column)
-    scores = jnp.where(allowed, scores, neg_fill)
-    expanded = jnp.exp(scores - jnp.max(scores, axis=-1, keepdims=True))
-    return expanded / jnp.sum(expanded, axis=-1, keepdims=True)
-
-
-class RowSum:
-    def __init__(self, cross, local, every, send_sem, recv_sem):
-        self.cross, self.local, self.every = cross, local, every
-        self.send_sem, self.recv_sem = send_sem, recv_sem
-
-    @staticmethod
-    def scratch(seq_count, shape):
-        dma = pltpu.SemaphoreType.DMA
-        return [
-            pltpu.VMEM(shape, jnp.float32),
-            pltpu.VMEM((seq_count,) + shape, jnp.float32),
-            dma((seq_count,)),
-            dma((seq_count,)),
-        ]
-
-    def copy(self, step):
-        cross = self.cross
-        return cross.remote(
-            self.local,
-            self.every.at[step],
-            self.send_sem.at[step],
-            self.recv_sem.at[step],
-            cross.seq_peer(step),
-            cross.fsdp,
-        )
-
-    def send(self, value):
-        self.local[...] = value
-        for step in range(1, self.cross.seq_count):
-            self.copy(step).start()
-
-    def receive(self):
-        total = self.local[...]
-        for step in range(1, self.cross.seq_count):
-            self.copy(step).wait_recv()
-            total = total + self.every[step]
-        return total
-
-    def finish(self):
-        for step in range(1, self.cross.seq_count):
-            self.copy(step).wait_send()
-
-
-def pick_row(row, shape):
-    return jnp.where(lax.broadcasted_iota(jnp.int32, shape, 0) == row, 1.0, 0.0)
+        [unit_columns[kind].reshape(-1, units) for kind in range(3)],
+        heads.reshape(4, tokens, columns),
+        pre,
+        inverse,
+        own_gains,
+        every_gain.transpose(2, 0, 1, 3).reshape(gains.shape[0], -1),
+    )
 
 
 def gather_back_kernel(chips, fsdp_count, *refs):
@@ -1736,9 +1764,9 @@
             for step in range(1, fsdp_count):
                 output_copy(step).start()
 
-        @pl.when((turn % 2 == 0) & (turn < seq_count))
-        def _():
-            scatter.hop(turn // 2)
+        @pl.when((turn >= HOPPING) & (turn < HOPPING + chips))
+        def _():
+            scatter.hop(chips - 1 - (turn - HOPPING))
 
     total = output_ref[fsdp].astype(jnp.float32)
     for step in range(1, fsdp_count):
@@ -1818,55 +1846,6 @@
     return result, (query, key, value), output, gains[:kinds, :own]
 
 
-def row_sum_kernel(seq_count, local_ref, result, every, send, recv):
-    seq, seq_peer = peers_of("seq", seq_count)
-    fsdp = lax.axis_index("fsdp")
-    barrier = pltpu.get_barrier_semaphore()
-    for step in range(1, seq_count):
-        pl.semaphore_signal(
-            barrier, inc=1, device_id=(seq_peer(step), fsdp), device_id_type=MESH
-        )
-    pl.semaphore_wait(barrier, seq_count - 1)
-    copies = [
-        pltpu.make_async_remote_copy(
-            src_ref=local_ref,
-            dst_ref=every.at[step],
-            send_sem=send.at[step],
-            recv_sem=recv.at[step],
-            device_id=(seq_peer(step), fsdp),
-            device_id_type=MESH,
-        )
-        for step in range(1, seq_count)
-    ]
-    for copy in copies:
-        copy.start()
-    total = local_ref[...]
-    for step in range(1, seq_count):
-        copies[step - 1].wait_recv()
-        total = total + every[step]
-    result[...] = total
-    for copy in copies:
-        copy.wait_send()
-
-
-def row_sum(collective_id, name, local):
-    slots = lax.axis_size("seq")
-    flat = local.reshape(-1, 128)
-    return pl.pallas_call(
-        functools.partial(row_sum_kernel, slots),
-        out_shape=jax.ShapeDtypeStruct(flat.shape, jnp.float32),
-        in_specs=[whole_spec()],
-        out_specs=whole_spec(),
-        scratch_shapes=[
-            pltpu.VMEM((slots,) + flat.shape, jnp.float32),
-            pltpu.SemaphoreType.DMA((slots,)),
-            pltpu.SemaphoreType.DMA((slots,)),
-        ],
-        compiler_params=line_params(collective_id),
-        name=name,
-    )(flat).reshape(local.shape)
-
-
 def rope_tables(row_count):
     half_width = DH // 2
     frequency = rope_base ** (-jnp.arange(half_width, dtype=jnp.float32) * 2.0 / DH)
@@ -1876,16 +1855,6 @@
         jnp.concatenate([cosine, cosine], axis=1),
         jnp.concatenate([-sine, sine], axis=1),
     )
-
-
-def rotate(tensor, tables):
-    cosine, sine = tables
-    row_count = tensor.shape[0]
-    half_width = DH // 2
-    grouped = tensor.reshape(row_count, -1, DH)
-    swapped = jnp.concatenate([grouped[..., half_width:], grouped[..., :half_width]], axis=-1)
-    turned = grouped * cosine[:, None, :] + swapped * sine[:, None, :]
-    return turned.reshape(tensor.shape)
 
 
 def per_device(
@@ -1908,65 +1877,33 @@
     width_all = inputs.shape[2]
     local_in = inputs.reshape(token_count, width_all)
     segment_row = segments[0]
-    score_scale = DH ** (-0.5)
     seq_index = lax.axis_index("seq")
-    inputs_all, attention_cols, output_rows, gate_cols, gains = bring_in(
+    tables = rope_tables(segment_row.shape[0])
+    (
+        projected,
+        inputs_all,
+        attention_cols,
+        output_rows,
+        unit_cols,
+        heads,
+        pre,
+        inverse,
+        own_gains,
+        gains,
+    ) = bring_in(
         local_in,
-        query_weight,
-        key_weight,
-        value_weight,
+        [query_weight, key_weight, value_weight],
+        [gate_weight, up_weight, down_weight],
         output_weight,
-        gate_weight,
         jnp.stack([query_gain, key_gain, attention_gain, feedforward_gain]),
-    )
-    query_cols, key_cols, value_cols = attention_cols[0], attention_cols[1], attention_cols[2]
+        tables,
+        segment_row,
+    )
+    gate_cols, up_cols, down_cols = unit_cols
+    head_width = heads.shape[2]
     gains = gains.astype(jnp.float32)
-    sequence_rows = inputs_all.shape[0]
-    head_width = query_cols.shape[1]
-    local_heads = head_width // DH
-    query_scale = lax.dynamic_slice_in_dim(gains[0], seq_index * head_width, head_width, 0)
-    key_scale = lax.dynamic_slice_in_dim(gains[1], seq_index * head_width, head_width, 0)
     attention_scale = gains[2]
     feedforward_scale = gains[3]
-    query_pre = jnp.dot(inputs_all, query_cols, preferred_element_type=jnp.float32)
-    key_pre = jnp.dot(inputs_all, key_cols, preferred_element_type=jnp.float32)
-    values_low = jnp.dot(inputs_all, value_cols, preferred_element_type=jnp.float32).astype(
-        jnp.bfloat16
-    )
-    squares = row_sum(
-        7,
-        "square_sum",
-        jnp.stack([jnp.sum(query_pre * query_pre, axis=-1), jnp.sum(key_pre * key_pre, axis=-1)]),
-    )
-    inverse = lax.rsqrt(squares / width_all + eps_norm)
-    query_unit = query_pre * inverse[0][:, None]
-    key_unit = key_pre * inverse[1][:, None]
-    tables = rope_tables(sequence_rows)
-    queries_low = rotate(query_unit * query_scale, tables).astype(jnp.bfloat16)
-    keys_low = rotate(key_unit * key_scale, tables).astype(jnp.bfloat16)
-    query_heads = queries_low.reshape(sequence_rows, local_heads, DH)
-    key_heads = keys_low.reshape(sequence_rows, local_heads, DH)
-    value_heads = values_low.reshape(sequence_rows, local_heads, DH)
-    block_rows = min(512, sequence_rows)
-    block_count = sequence_rows // block_rows
-    block_ids = jnp.arange(block_count, dtype=jnp.int32)
-
-    def attend_block(loop_state, block_index):
-        first_row = block_index * block_rows
-        query_block = lax.dynamic_slice_in_dim(query_heads, first_row, block_rows, 0)
-        scores = masked_scores(query_block, key_heads, first_row, segment_row, score_scale)
-        row_max = jnp.max(scores, axis=-1, keepdims=True)
-        expanded = jnp.exp(scores - row_max)
-        row_total = jnp.sum(expanded, axis=-1, keepdims=True)
-        softmax_low = (expanded / row_total).astype(jnp.bfloat16)
-        block_out = jnp.einsum(
-            "hqk,khd->qhd", softmax_low, value_heads, preferred_element_type=jnp.float32
-        )
-        return (loop_state, block_out.astype(jnp.bfloat16))
-
-    _, out_blocks = lax.scan(attend_block, jnp.zeros((), jnp.int32), block_ids)
-    attended_heads = out_blocks.reshape(sequence_rows, head_width)
-    projected, up_cols, down_cols = project(attended_heads, output_rows, up_weight, down_weight)
     hidden = local_in.astype(jnp.float32) + rms_scale(projected, attention_scale)
     hidden_low = hidden.astype(jnp.bfloat16)
     mixed_pre, gate_linear, up_linear, activated, hidden_all = feed_forward(
@@ -1990,13 +1927,13 @@
     weight_grads, output_term, attention_grads, gain_rows = gather_back(
         grad_projected.astype(jnp.bfloat16),
         output_rows,
-        jnp.stack([query_scale, key_scale]),
-        inverse.T,
+        own_gains,
+        inverse,
         tables,
         segment_row,
         [hidden_all, grad_all, grad_gate_low, grad_upward_low, activated],
-        jnp.stack([queries_low, keys_low, values_low, attended_heads]),
-        jnp.stack([query_pre, key_pre]),
+        heads,
+        pre,
     )
     gate_weight_grad, up_weight_grad, down_weight_grad = weight_grads
     head_gains = lax.dynamic_update_slice_in_dim(

time: 677 us -> 595 us (0.88)
  Pallas kernels: 575 us -> 547 us
  matrix products: 23.6 us -> 0 us
  local copies, waits for them, and re-layouts: 33.1 us -> 21.6 us
  other arithmetic: 32.8 us -> 21.9 us
    pallas_call x2 -> x0, Pallas kernels: 99.8 us -> none  [the longest x1 92.6 us: project(): pl.pallas_call(functools.partial(project_kernel, chips, fsdp_count), out_...]
    pallas_call x1, Pallas kernels: 99.3 us -> 179 us  [bring_in(): pl.pallas_call(functools.partial(bring_in_kernel, chips, fsdp_count), out...]
    dot_general x5 -> x0, matrix products: 14.2 us -> none  [the longest x2 5.89 us: attend_block(): jnp.einsum('hqk,khd->qhd', softmax_low, value_heads, preferred_element_ty...]
    sub x2 -> x0, matrix products: 9.46 us -> none  [attend_block(): expanded = jnp.exp(scores - row_max)]
where the time goes in v7:
time: 595 us; the launch traced here: 591 us
  Pallas kernels  547 us (92%)
  other arithmetic  21.9 us (4%)
  local copies, waits for them, and re-layouts  21.6 us (4%)
    pallas_call x1, Pallas kernels, bring_in(): pl.pallas_call(functools.partial(bring_in_kernel, chips, fsdp_count), out...  179 us
    pallas_call x1, Pallas kernels, gather_back(): pl.pallas_call(functools.partial(gather_back_kernel, chips, fsdp_count),...  131 us
    pallas_call x1, Pallas kernels, feed_forward(): pl.pallas_call(functools.partial(feed_forward_kernel, chips), out_shape=(...  83.1 us
    pallas_call x1, Pallas kernels, feed_forward_back(): pl.pallas_call(functools.partial(feed_forward_back_kernel, chips), out_sh...  77.8 us
    pallas_call x1, Pallas kernels, take_out(): pl.pallas_call(functools.partial(take_out_kernel, chips, fsdp_count), out...  75.8 us

profile of v7, /device:TPU:0, one launch (start us, length us, event | category | flops | bytes accessed | tf_op | source)
XLA Modules:
  0.0 591.1 jit_solution(18138168985886239740)
XLA Ops:
  0.6 0.0 copy-start.8
  0.7 0.0 copy-start.12
  0.7 0.0 copy-start.11
  0.7 0.0 copy-start.10
  0.7 0.0 copy-start.9
  0.7 1.9 fusion.8
  2.6 1.3 pad_maximum_fusion
  3.9 0.0 copy-start.1
  3.9 0.0 copy-done.8
  3.9 1.0 copy.27.refs_4_.refs_6_
  5.0 0.0 copy-done.12
  5.0 0.0 copy-done.11
  5.0 0.0 copy-done.10
  5.0 0.0 copy-done.9
  5.0 0.6 fusion.17.refs_1_
  5.6 179.3 %bring_in.1 = (f32[128,2048]{1,0:T(8,128)}, f32[1024,8]{1,0:T(8,128)}, f32[16,256]{1,0:T(8,128)}, bf16[8,4,16,128]{3,2,1,0:T(8,128)(2,1)}, bf16[8,128,2048]{2,1,...) custom-call(bf16[128,2048]{1,0:T(8,128)(2,1)} %bitcast.58, ...), custom_call_target="tpu_custom_call" | custom-call | tf_op jit(solution)/shard_map/bring_in/pallas_call | solution.py:1408
  184.9 1.4 multiply_reduce_fusion.3
  186.3 0.9 convert_bitcast_fusion
  187.2 0.1 slice_reduce_fusion
  187.3 0.1 mul.163
  187.4 0.0 copy-done.1
  187.4 2.2 fusion.6.hidden_ref
  189.6 8.8 %fusion.23 = (bf16[1,8,4,64,1024]{4,3,2,1,0:T(8,128)(2,1)}, bf16[1,8,4,64,1024]{4,3,2,1,0:T(8,128)(2,1)}, bf16[1,8,4,64,1024]{4,3,2,1,0:T(8,128)(2,1)}) fusion(bf16[3,8,4,64,1024]{4,3,2,1,0:T(8,128)(2,1)} %get-tuple-element.46), kind=kLoop, calls=%fused_computation.56 | loop fusion | bytes 25165824 | tf_op jit(solution)/shard_map/slice | solution.py:1463
  198.5 0.0 copy-start
  198.5 83.1 %feed_forward.1 = (f32[128,2048]{1,0:T(8,128)}, f32[8,128,1024]{2,1,0:T(8,128)}, f32[8,128,1024]{2,1,0:T(8,128)}, bf16[8,128,1024]{2,1,0:T(8,128)(2,1)}, bf16[8,128,2048]{2,1,0:T(8,128)(2,1)}) custom-call(bf16[128,2048]{1,0:T(8,128)(2,1)} %fusion.6.hidden_ref, bf16[2048,1024]{1,0:T(8,128)(2,1)} %bitcast.56, bf16[2048,1024]{1,0:T(8,128)(2,1)} %bitcast.54, ...), custom_call_target="tpu_custom_call" | custom-call | tf_op jit(solution)/shard_map/feed_forward/pallas_call | solution.py:547
  281.6 1.4 multiply_reduce_fusion.2
  283.0 0.1 mul.169
  283.1 0.0 copy-done
  283.1 1.6 fusion.5
  284.6 2.3 fusion.3.grad_ref
  286.9 77.8 %feed_forward_back.1 = (f32[128,2048]{1,0:T(8,128)}, bf16[8,128,1024]{2,1,0:T(8,128)(2,1)}, bf16[8,128,1024]{2,1,0:T(8,128)(2,1)}, bf16[8,128,2048]{2,1,0:T(8,128)(2,1)}) custom-call(bf16[128,2048]{1,0:T(8,128)(2,1)} %fusion.3.grad_ref, bf16[2048,1024]{1,0:T(8,128)(2,1)} %bitcast.57, bf16[2048,1024]{1,0:T(8,128)(2,1)} %bitcast.55, ...), custom_call_target="tpu_custom_call" | custom-call | tf_op jit(solution)/shard_map/feed_forward_back/pallas_call | solution.py:580
  364.7 1.9 multiply_reduce_fusion
  366.6 3.5 fusion.4
  370.1 130.7 %gather_back.1 = (f32[64,8192]{1,0:T(8,128)}, f32[64,8192]{1,0:T(8,128)}, f32[64,8192]{1,0:T(8,128)}, bf16[256,2048]{1,0:T(8,128)(2,1)}, bf16[3,1024,256]{2,1,0:T(8,128)(2,1)}, /*index=5*/f32[8,256]{1,0:T(8,128)}) custom-call(bf16[128,2048]{1,0:T(8,128)(2,1)} %get-tuple-element.84.refs_0_, bf16[256,2048]{1,0:T(8,128)(2,1)} %bitcast.69, ...), custom_call_target="tpu_custom_call" | custom-call | tf_op jit(solution)/shard_map/gather_back/pallas_call | solution.py:1637
  500.8 0.7 slice_dynamic-update-slice_fusion
  501.6 0.1 concatenate.18
  501.7 0.1 concatenate.19
  501.8 0.1 concatenate.20
  501.9 0.1 maximum_bitcast_fusion
  502.0 0.7 pad.9.refs_4_
  502.6 75.8 %take_out.1 = (f32[128,2048]{1,0:T(8,128)}, f32[64,2048]{1,0:T(8,128)}, f32[64,2048]{1,0:T(8,128)}, f32[64,2048]{1,0:T(8,128)}, f32[64,2048]{1,0:T(8,128)}, /*index=5*/f32[8,128]{1,0:T(8,128)}) custom-call(bf16[3,8,128,256]{3,2,1,0:T(8,128)(2,1)} %bitcast.67, bf16[3,2048,256]{2,1,0:T(8,128)(2,1)} %bitcast.62, bf16[1024,2048]{1,0:T(8,128)(2,1)} %bitcast.59, ...), custom_call_target="tpu_custom_call" | custom-call | tf_op jit(solution)/shard_map/take_out/pallas_call | solution.py:1816
  578.5 0.0 copy-start.7
  578.5 0.0 copy-start.6
  578.5 0.0 copy-start.5
  578.5 0.0 copy-start.4
  578.5 2.9 add_bitcast_fusion
  581.4 1.4 slice_bitcast_fusion
  582.7 0.0 copy-start.3
  582.7 2.0 copy.40
  584.7 0.0 copy-done.7
  584.7 0.8 copy.41
  585.5 0.0 copy-done.6
  585.5 0.8 copy.42
  586.3 0.0 copy-done.5
  586.3 0.8 copy.43
  587.1 0.0 copy-done.4
  587.1 0.0 copy-start.2
  587.1 1.3 copy.44
  588.4 0.0 copy-done.3
  588.4 1.3 copy.45
  589.8 0.0 copy-done.2
  589.8 1.3 copy.46
  (10 shorter events, 0.1 us)
Async XLA Ops:
  0.6 3.3 copy-start.8
  0.7 4.3 copy-start.12
  0.7 4.3 copy-start.11
  0.7 4.3 copy-start.10
  0.7 4.3 copy-start.9
  3.9 183.4 %copy-start.1 = (bf16[1,128,2048]{2,1,0:T(8,128)(2,1)S(1)}, bf16[1,128,2048]{2,1,0:T(8,128)(2,1)}, u32[]{:S(2)}) copy-start(bf16[1,128,2048]{2,1,0:T(8,128)(2,1)} %param.14) | copy-start | bytes 1572868
  198.5 84.6 %copy-start = (bf16[1,128,2048]{2,1,0:T(8,128)(2,1)S(1)}, bf16[1,128,2048]{2,1,0:T(8,128)(2,1)}, u32[]{:S(2)}) copy-start(bf16[1,128,2048]{2,1,0:T(8,128)(2,1)} %param.27) | copy-start | bytes 1572868
  578.5 6.3 %copy-start.7 = (f32[64,2048]{1,0:T(8,128)S(1)}, f32[64,2048]{1,0:T(8,128)}, u32[]{:S(2)}) copy-start(f32[64,2048]{1,0:T(8,128)} %get-tuple-element.111) | copy-start | bytes 1572868
  578.5 7.1 %copy-start.6 = (f32[64,2048]{1,0:T(8,128)S(1)}, f32[64,2048]{1,0:T(8,128)}, u32[]{:S(2)}) copy-start(f32[64,2048]{1,0:T(8,128)} %get-tuple-element.112) | copy-start | bytes 1572868
  578.5 7.8 %copy-start.5 = (f32[64,2048]{1,0:T(8,128)S(1)}, f32[64,2048]{1,0:T(8,128)}, u32[]{:S(2)}) copy-start(f32[64,2048]{1,0:T(8,128)} %get-tuple-element.113) | copy-start | bytes 1572868
  578.5 8.6 %copy-start.4 = (f32[64,8192]{1,0:T(8,128)S(1)}, f32[64,8192]{1,0:T(8,128)}, u32[]{:S(2)}) copy-start(f32[64,8192]{1,0:T(8,128)} %get-tuple-element.117) | copy-start | bytes 6291460
  582.7 5.7 copy-start.3
  587.1 2.6 copy-start.2

commit v8 on v7

--- a/solution.py
+++ b/solution.py
@@ -228,17 +228,20 @@
             total = total + self.inward[way, chip, rows].astype(jnp.float32)
         return rows, total
 
-    def pass_on(self, chip, upward, first):
+    def pass_part(self, chip, part, upward, first):
         target = self.line.above if upward else self.line.below
+        if not first:
+            self.part(chip, part, upward, target).wait_recv()
+        rows, total = self.total(chip, part, () if first else (upward,))
+        self.out[chip, rows] = total.astype(jnp.bfloat16)
+        self.part(chip, part, upward, target).start()
+
+    def hand_on(self, chip, upward, first):
         self.side(chip).wait_recv()
 
         @pl.loop(0, RS_PARTS)
         def _(part):
-            if not first:
-                self.part(chip, part, upward, target).wait_recv()
-            rows, total = self.total(chip, part, () if first else (upward,))
-            self.out[chip, rows] = total.astype(jnp.bfloat16)
-            self.part(chip, part, upward, target).start()
+            self.pass_part(chip, part, upward, first)
 
     def after_term(self, chip):
         line = self.line
@@ -246,11 +249,11 @@
 
         @pl.when((chip < line.place) & jnp.logical_not(line.has_above))
         def _():
-            self.pass_on(chip, 0, True)
+            self.hand_on(chip, 0, True)
 
         @pl.when((chip > line.place) & jnp.logical_not(line.has_below))
         def _():
-            self.pass_on(chip, 1, True)
+            self.hand_on(chip, 1, True)
 
     def hop(self, step):
         line = self.line
@@ -261,15 +264,15 @@
 
         @pl.when(go_up & lower)
         def _():
-            self.pass_on(up_chip, 1, False)
+            self.hand_on(up_chip, 1, False)
 
         @pl.when(go_down)
         def _():
-            self.pass_on(down_chip, 0, False)
+            self.hand_on(down_chip, 0, False)
 
         @pl.when(go_up & jnp.logical_not(lower))
         def _():
-            self.pass_on(up_chip, 1, False)
+            self.hand_on(up_chip, 1, False)
 
     def settle(self, result):
         line = self.line
@@ -337,193 +340,6 @@
     return copies
 
 
-def feed_forward_kernel(
-    chips,
-    hidden_ref,
-    gate_hbm,
-    up_hbm,
-    down_hbm,
-    mixed_ref,
-    gate_out,
-    up_out,
-    act_out,
-    all_out,
-    gate_w,
-    up_w,
-    down_w,
-    gate_keep,
-    up_keep,
-    act_keep,
-    load_sem,
-    store_sem,
-    *comm,
-):
-    line = Line(chips)
-    gather = Gather(line, *comm[:5])
-    scatter = Scatter(line, *comm[5:])
-    blocks, fresh = gather.blocks, scatter.fresh
-    _, rows, width = blocks.shape
-    units = gate_w.shape[1]
-    copies = load(
-        [
-            (gate_hbm, gate_w, load_sem.at[0]),
-            (up_hbm, up_w, load_sem.at[1]),
-            (down_hbm, down_w, load_sem.at[2]),
-        ]
-    )
-    line.greet()
-    blocks[line.place * 2 + line.core] = hidden_ref[...]
-    gather.send(line.place)
-
-    def stores(chip):
-        pair = pl.ds(chip * 2, 2)
-        return [
-            pltpu.make_async_copy(gate_keep.at[pair], gate_out.at[pair], store_sem.at[0, chip]),
-            pltpu.make_async_copy(up_keep.at[pair], up_out.at[pair], store_sem.at[1, chip]),
-            pltpu.make_async_copy(act_keep.at[pair], act_out.at[pair], store_sem.at[2, chip]),
-            pltpu.make_async_copy(blocks.at[pair], all_out.at[pair], store_sem.at[3, chip]),
-        ]
-
-    for copy in copies:
-        copy.wait()
-
-    @pl.loop(0, chips)
-    def _(step):
-        chip = gather.step(step)
-        pair = pl.ds(chip * 2, 2)
-
-        @pl.loop(0, units // tile_of(units))
-        def _(tile):
-            columns = pl.ds(pl.multiple_of(tile * tile_of(units), 128), tile_of(units))
-            tokens = blocks[pair].reshape(2 * rows, width)
-            gate = jnp.dot(tokens, gate_w[:, columns], preferred_element_type=jnp.float32)
-            up = jnp.dot(tokens, up_w[:, columns], preferred_element_type=jnp.float32)
-            gate_keep[pair, :, columns] = gate.reshape(2, rows, -1)
-            up_keep[pair, :, columns] = up.reshape(2, rows, -1)
-            act_keep[pair, :, columns] = (
-                (gate / (1.0 + jnp.exp(-gate)) * up).astype(jnp.bfloat16).reshape(2, rows, -1)
-            )
-
-        @pl.loop(0, width // tile_of(width))
-        def _(tile):
-            columns = pl.ds(pl.multiple_of(tile * tile_of(width), 128), tile_of(width))
-            act = act_keep[pair].reshape(2 * rows, units)
-            fresh[:, :, columns] = dot_cols(act, down_w[columns, :]).reshape(2, rows, -1)
-
-        for copy in stores(chip):
-            copy.start()
-        scatter.after_term(chip)
-
-    scatter.hops()
-    scatter.settle(mixed_ref)
-    scatter.finish()
-    gather.finish()
-
-    @pl.loop(0, chips)
-    def _(chip):
-        for copy in stores(chip):
-            copy.wait()
-
-
-def feed_forward_back_kernel(
-    chips,
-    grad_ref,
-    gate_hbm,
-    up_hbm,
-    down_hbm,
-    gate_lin_hbm,
-    up_lin_hbm,
-    hidden_grad_ref,
-    gate_out,
-    up_out,
-    all_out,
-    gate_w,
-    up_w,
-    down_w,
-    gate_lin,
-    up_lin,
-    gate_keep,
-    up_keep,
-    load_sem,
-    store_sem,
-    *comm,
-):
-    line = Line(chips)
-    gather = Gather(line, *comm[:5])
-    scatter = Scatter(line, *comm[5:])
-    blocks, fresh = gather.blocks, scatter.fresh
-    _, rows, width = blocks.shape
-    units = gate_w.shape[1]
-    copies = load(
-        [
-            (down_hbm, down_w, load_sem.at[0]),
-            (gate_lin_hbm, gate_lin, load_sem.at[1]),
-            (up_lin_hbm, up_lin, load_sem.at[2]),
-            (gate_hbm, gate_w, load_sem.at[3]),
-            (up_hbm, up_w, load_sem.at[4]),
-        ]
-    )
-    line.greet()
-    blocks[line.place * 2 + line.core] = grad_ref[...]
-    gather.send(line.place)
-
-    def stores(chip):
-        pair = pl.ds(chip * 2, 2)
-        return [
-            pltpu.make_async_copy(gate_keep.at[pair], gate_out.at[pair], store_sem.at[0, chip]),
-            pltpu.make_async_copy(up_keep.at[pair], up_out.at[pair], store_sem.at[1, chip]),
-            pltpu.make_async_copy(blocks.at[pair], all_out.at[pair], store_sem.at[2, chip]),
-        ]
-
-    for copy in copies:
-        copy.wait()
-
-    @pl.loop(0, chips)
-    def _(step):
-        chip = gather.step(step)
-        pair = pl.ds(chip * 2, 2)
-
-        @pl.loop(0, units // tile_of(units))
-        def _(tile):
-            columns = pl.ds(pl.multiple_of(tile * tile_of(units), 128), tile_of(units))
-            tokens = blocks[pair].reshape(2 * rows, width)
-            grad = jnp.dot(tokens, down_w[:, columns], preferred_element_type=jnp.float32)
-            gate = gate_lin[pair, :, columns].reshape(2 * rows, -1)
-            up = up_lin[pair, :, columns].reshape(2 * rows, -1)
-            sig = 1.0 / (1.0 + jnp.exp(-gate))
-            gate_keep[pair, :, columns] = (
-                (grad * up * sig * (1.0 + gate * (1.0 - sig)))
-                .astype(jnp.bfloat16)
-                .reshape(2, rows, -1)
-            )
-            up_keep[pair, :, columns] = (
-                (grad * (gate * sig)).astype(jnp.bfloat16).reshape(2, rows, -1)
-            )
-
-        @pl.loop(0, width // tile_of(width))
-        def _(tile):
-            columns = pl.ds(pl.multiple_of(tile * tile_of(width), 128), tile_of(width))
-            gate = gate_keep[pair].reshape(2 * rows, units)
-            up = up_keep[pair].reshape(2 * rows, units)
-            fresh[:, :, columns] = (
-                dot_cols(gate, gate_w[columns, :]) + dot_cols(up, up_w[columns, :])
-            ).reshape(2, rows, -1)
-
-        for copy in stores(chip):
-            copy.start()
-        scatter.after_term(chip)
-
-    scatter.hops()
-    scatter.settle(hidden_grad_ref)
-    scatter.finish()
-    gather.finish()
-
-    @pl.loop(0, chips)
-    def _(chip):
-        for copy in stores(chip):
-            copy.wait()
-
-
 def whole_spec():
     return pl.BlockSpec(memory_space=pltpu.VMEM)
 
@@ -534,78 +350,7 @@
 
 def line_params(collective_id):
     return pltpu.CompilerParams(
-        collective_id=collective_id, has_side_effects=True, vmem_limit_bytes=63 * 2**20
-    )
-
-
-def feed_forward(hidden_low, gate_cols, up_cols, down_cols):
-    rows, width = hidden_low.shape
-    units = gate_cols.shape[1]
-    slots = lax.axis_size("seq")
-    chips = slots // 2
-    weights = [pltpu.VMEM((width, units), jnp.bfloat16)] * 3
-    mixed, gate, up, act, every = pl.pallas_call(
-        functools.partial(feed_forward_kernel, chips),
-        out_shape=(
-            jax.ShapeDtypeStruct((rows, width), jnp.float32),
-            jax.ShapeDtypeStruct((slots, rows, units), jnp.float32),
-            jax.ShapeDtypeStruct((slots, rows, units), jnp.float32),
-            jax.ShapeDtypeStruct((slots, rows, units), jnp.bfloat16),
-            jax.ShapeDtypeStruct((slots, rows, width), jnp.bfloat16),
-        ),
-        in_specs=[whole_spec()] + [far_spec()] * 3,
-        out_specs=(whole_spec(),) + (far_spec(),) * 4,
-        scratch_shapes=weights
-        + [
-            pltpu.VMEM((slots, rows, units), jnp.float32),
-            pltpu.VMEM((slots, rows, units), jnp.float32),
-            pltpu.VMEM((slots, rows, units), jnp.bfloat16),
-            pltpu.SemaphoreType.DMA((3,)),
-            pltpu.SemaphoreType.DMA((4, chips)),
-        ]
-        + Gather.scratch(chips, rows, width)
-        + Scatter.scratch(chips, rows, width),
-        compiler_params=line_params(1),
-        name="feed_forward",
-    )(hidden_low, gate_cols, up_cols, down_cols)
-    return mixed, gate, up, act.reshape(-1, units), every.reshape(-1, width)
-
-
-def feed_forward_back(grad_low, gate_cols, up_cols, down_cols, gate, up):
-    rows, width = grad_low.shape
-    units = gate_cols.shape[1]
-    slots = lax.axis_size("seq")
-    chips = slots // 2
-    weights = [pltpu.VMEM((width, units), jnp.bfloat16)] * 3
-    hidden_grad, gate_grad, up_grad, every = pl.pallas_call(
-        functools.partial(feed_forward_back_kernel, chips),
-        out_shape=(
-            jax.ShapeDtypeStruct((rows, width), jnp.float32),
-            jax.ShapeDtypeStruct((slots, rows, units), jnp.bfloat16),
-            jax.ShapeDtypeStruct((slots, rows, units), jnp.bfloat16),
-            jax.ShapeDtypeStruct((slots, rows, width), jnp.bfloat16),
-        ),
-        in_specs=[whole_spec()] + [far_spec()] * 5,
-        out_specs=(whole_spec(),) + (far_spec(),) * 3,
-        scratch_shapes=weights
-        + [
-            pltpu.VMEM((slots, rows, units), jnp.float32),
-            pltpu.VMEM((slots, rows, units), jnp.float32),
-            pltpu.VMEM((slots, rows, units), jnp.bfloat16),
-            pltpu.VMEM((slots, rows, units), jnp.bfloat16),
-            pltpu.SemaphoreType.DMA((5,)),
-            pltpu.SemaphoreType.DMA((3, chips)),
-        ]
-        + Gather.scratch(chips, rows, width)
-        + Scatter.scratch(chips, rows, width),
-        compiler_params=line_params(2),
-        name="feed_forward_back",
-    )(grad_low, gate_cols, up_cols, down_cols, gate, up)
-    return (
-        hidden_grad,
-        gate_grad.reshape(-1, units),
-        up_grad.reshape(-1, units),
-        every.reshape(-1, width),
+        collective_id=collective_id, has_side_effects=True, vmem_limit_bytes=67_043_328
     )
 
 
@@ -748,7 +493,10 @@
                 own = self.stack[first + kind, :, self.block(cross.seq)]
                 self.weights[first + kind, cross.seq, cross.fsdp] = own
 
-        for side in range(len(cross.sides)):
+        self.pass_on(item)
+
+    def pass_on(self, item):
+        for side in range(len(self.cross.sides)):
             self.side(item, side).start()
 
     def relay(self, item):
@@ -774,10 +522,13 @@
                 for kind in range(self.group):
                     self.row(first + kind, step).wait_send()
 
-            for side in range(len(cross.sides)):
-                self.side(item, side).wait_send()
-                if cross.square:
-                    self.half(item, side).wait_send()
+            self.finish_item(item)
+
+    def finish_item(self, item):
+        for side in range(len(self.cross.sides)):
+            self.side(item, side).wait_send()
+            if self.cross.square:
+                self.half(item, side).wait_send()
 
 
 AHEAD = 2
@@ -973,7 +724,7 @@
         def _():
             self.middle(turn)
 
-        @pl.when(turn >= LAG)
+        @pl.when((turn >= LAG) & (turn < self.beats))
         def _():
             self.ship(turn - LAG)
 
@@ -994,7 +745,7 @@
             self.row(turn).wait_recv()
 
         sender = (self.cross.seq - turn % count - 1 + count) % count
-        put(turn // count, sender, self.row_in[turn].astype(jnp.float32))
+        put(turn // count, sender, self.row_in[turn])
 
     def finish(self):
         cross = self.cross
@@ -1119,8 +870,8 @@
     inputs_ref, gains_ref, cosine_ref, sine_ref, segment_column, segment_row = refs[:6]
     sources, output_ref, refs = refs[6:12], refs[12], refs[13:]
     projected, inverse_out, own_gains, gains_out = refs[:4]
-    inputs_out, attention_out, output_out, units_out, heads_out, pre_out = refs[4:10]
-    outputs, gains, heads, pre, refs = refs[10], refs[11], refs[12], refs[13], refs[14:]
+    inputs_out, attention_out, output_out, heads_out, pre_out = refs[4:9]
+    units_out, outputs, gains, heads, pre, refs = refs[9:12], refs[12], refs[13], refs[14], refs[15], refs[16:]
     gain_row_send, gain_row_recv, gain_column_send, gain_column_recv = refs[:4]
     output_send, output_recv, load_sem, store_sem, refs = refs[4], refs[5], refs[6], refs[7], refs[8:]
     line = Line(chips)
@@ -1305,7 +1056,7 @@
     pre_store = pltpu.make_async_copy(pre, pre_out, store_sem.at[4])
 
     def units_store(kind):
-        return pltpu.make_async_copy(units.weights.at[kind], units_out.at[kind], store_sem.at[5 + kind])
+        return pltpu.make_async_copy(units.weights.at[kind], units_out[kind], store_sem.at[5 + kind])
 
     @pl.loop(0, LEAD)
     def _(item):
@@ -1415,12 +1166,12 @@
             jax.ShapeDtypeStruct((slots, rows, width), bf16),
             jax.ShapeDtypeStruct((3, slots, fsdp_count, own, columns), bf16),
             jax.ShapeDtypeStruct((fsdp_count, own, width), bf16),
-            jax.ShapeDtypeStruct((3, slots, fsdp_count, own, units), bf16),
             jax.ShapeDtypeStruct((4, slots, rows, columns), bf16),
             jax.ShapeDtypeStruct((2, tokens, columns), f32),
-        ),
+        )
+        + (jax.ShapeDtypeStruct((slots, fsdp_count, own, units), bf16),) * 3,
         in_specs=[whole_spec()] * 6 + [far_spec()] * 6 + [whole_spec()],
-        out_specs=(whole_spec(),) * 4 + (far_spec(),) * 6,
+        out_specs=(whole_spec(),) * 4 + (far_spec(),) * 8,
         scratch_shapes=[
             pltpu.VMEM((fsdp_count, own, width), bf16),
             pltpu.VMEM((slots, fsdp_count, 16, lanes), bf16),
@@ -1453,14 +1204,14 @@
         output_weight,
     )
     projected, inverse, own_gains, every_gain = found[:4]
-    inputs_all, weights, outputs, unit_columns, heads, pre = found[4:]
+    inputs_all, weights, outputs, heads, pre = found[4:9]
     every_gain = every_gain[:, :, : gains.shape[0], : gains.shape[1]]
     return (
         projected,
         inputs_all.reshape(-1, width),
         weights.reshape(3, -1, columns),
         outputs.reshape(-1, width),
-        [unit_columns[kind].reshape(-1, units) for kind in range(3)],
+        [columns_of.reshape(-1, units) for columns_of in found[9:]],
         heads.reshape(4, tokens, columns),
         pre,
         inverse,
@@ -1472,18 +1223,17 @@
 def gather_back_kernel(chips, fsdp_count, *refs):
     local_ref, output_ref, gains_ref, inverse_ref, cosine_ref, sine_ref = refs[:6]
     segment_column, segment_row = refs[6:8]
-    hidden_hbm, grad_hbm, gate_hbm, up_hbm, act_hbm = refs[8:13]
-    heads_hbm, pre_hbm = refs[13:15]
-    refs = refs[15:]
-    results, output_term, grads_out, gain_out = refs[:3], refs[3], refs[4], refs[5]
-    refs = refs[6:]
+    hidden_hbm, gate_hbm, up_hbm, heads_hbm, pre_hbm = refs[8:13]
+    refs = refs[13:]
+    results, output_term, grads_out, gain_out = refs[:2], refs[2], refs[3], refs[4]
+    refs = refs[5:]
     tokens, units, heads, pre, gathered, grad_query, grad_key, grad_value = refs[:8]
     load_sem, refs = refs[8], refs[9:]
     line = Line(chips)
     cross = Cross(2 * chips, fsdp_count)
     gather = Gather(line, *refs[:5])
     sums = RowSum(cross, *refs[5:9])
-    all_tokens, width = tokens.shape[1:]
+    all_tokens, width = tokens.shape
     block_units = units.shape[-1]
     columns = output_ref.shape[0]
     blocks = gather.blocks
@@ -1491,7 +1241,7 @@
 
     def fill(kind, owner, slot):
         span = width // cross.seq_count
-        chosen = tokens[kind // 2, :, pl.ds(pl.multiple_of(owner * span, 128), span)]
+        chosen = tokens[:, pl.ds(pl.multiple_of(owner * span, 128), span)]
 
         @pl.loop(0, block_units // tile_of(block_units))
         def _(tile):
@@ -1499,16 +1249,14 @@
             term = dot_rows(chosen, units[kind, :, part]).astype(jnp.bfloat16)
             collect.terms[slot, :, :, part] = term.reshape(fsdp_count, -1, term.shape[1])
 
-    collect = Collect(cross, 3, fill, *refs[9:])
+    collect = Collect(cross, 2, fill, *refs[9:])
     copies = load(
         [
-            (hidden_hbm, tokens.at[0], load_sem.at[0]),
+            (hidden_hbm, tokens, load_sem.at[0]),
             (gate_hbm, units.at[0], load_sem.at[1]),
             (up_hbm, units.at[1], load_sem.at[2]),
-            (grad_hbm, tokens.at[1], load_sem.at[3]),
-            (act_hbm, units.at[2], load_sem.at[4]),
-            (heads_hbm, heads, load_sem.at[5]),
-            (pre_hbm, pre, load_sem.at[6]),
+            (heads_hbm, heads, load_sem.at[3]),
+            (pre_hbm, pre, load_sem.at[4]),
         ]
     )
     greet_cross(cross.seq_count, fsdp_count)
@@ -1529,13 +1277,9 @@
         gathered[pl.ds(chip * 2 * rows, 2 * rows), :] = found
 
     arrive(0)
-    query_rows = 128
-    blocks_of_rows = all_tokens // query_rows
-    first_beat = 3 * (chips - 1)
-
-    def attend(block):
-        first = pl.multiple_of(block * query_rows, query_rows)
-        span = pl.ds(first, query_rows)
+    def attend(slot):
+        first = pl.multiple_of(slot * rows, rows)
+        span = pl.ds(first, rows)
         for head in range(0, columns, DH):
             part = pl.ds(head, DH)
             queries, keys, values = heads[0, span, part], heads[1, :, part], heads[2, :, part]
@@ -1590,29 +1334,31 @@
                 inverse * (error * gains_ref[kind : kind + 1, :] - unit * mean)
             ).astype(jnp.bfloat16)
 
-    @pl.loop(0, collect.beats)
+    attended = 3 * chips - 1
+
+    @pl.loop(0, max(collect.beats, attended + 4))
     def _(turn):
         collect.beat(turn)
 
+        @pl.when((turn % 3 < 2) & (turn // 3 < chips))
+        def _():
+            attend(line.order(turn // 3) * 2 + turn % 3)
+
         @pl.when((turn % 3 == 2) & (turn // 3 + 1 < chips))
         def _():
             arrive(turn // 3 + 1)
 
-        @pl.when((turn >= first_beat) & (turn < first_beat + blocks_of_rows))
-        def _():
-            attend(turn - first_beat)
-
-        @pl.when(turn == first_beat + blocks_of_rows)
+        @pl.when(turn == attended)
         def _():
             send_means()
 
-        @pl.when(turn == first_beat + blocks_of_rows + 3)
+        @pl.when(turn == attended + 3)
         def _():
             finish_grads()
 
     @pl.loop(0, cross.seq_count)
     def _(turn):
-        for kind in range(3):
+        for kind in range(2):
 
             def put(_, sender, value):
                 part = pl.ds(pl.multiple_of(sender * block_units, 128), block_units)
@@ -1631,33 +1377,33 @@
     fsdp_count = lax.axis_size("fsdp")
     chips = slots // 2
     own = width // (slots * fsdp_count)
-    units = far[2].shape[1]
+    units = far[1].shape[1]
     _, tokens, columns = heads.shape
     bf16, f32 = jnp.bfloat16, jnp.float32
     found = pl.pallas_call(
         functools.partial(gather_back_kernel, chips, fsdp_count),
-        out_shape=(jax.ShapeDtypeStruct((own, units * slots), f32),) * 3
+        out_shape=(jax.ShapeDtypeStruct((own, units * slots), bf16),) * 2
         + (
             jax.ShapeDtypeStruct((columns, width), bf16),
             jax.ShapeDtypeStruct((3, tokens, columns), bf16),
             jax.ShapeDtypeStruct((8, columns), f32),
         ),
-        in_specs=[whole_spec()] * 8 + [far_spec()] * 7,
-        out_specs=(whole_spec(),) * 6,
+        in_specs=[whole_spec()] * 8 + [far_spec()] * 5,
+        out_specs=(whole_spec(),) * 5,
         scratch_shapes=[
-            pltpu.VMEM((2, tokens, width), bf16),
-            pltpu.VMEM((3, tokens, units), bf16),
+            pltpu.VMEM((tokens, width), bf16),
+            pltpu.VMEM((2, tokens, units), bf16),
             pltpu.VMEM((4, tokens, columns), bf16),
             pltpu.VMEM((2, tokens, columns), f32),
             pltpu.VMEM((tokens, columns), bf16),
             pltpu.VMEM((tokens, columns), f32),
             pltpu.VMEM((tokens, columns), f32),
             pltpu.VMEM((tokens, columns), f32),
-            pltpu.SemaphoreType.DMA((7,)),
+            pltpu.SemaphoreType.DMA((5,)),
         ]
         + Gather.scratch(chips, rows, width)
         + RowSum.scratch(slots, (8, tokens))
-        + Collect.scratch(3, slots, fsdp_count, own, units),
+        + Collect.scratch(2, slots, fsdp_count, own, units),
         compiler_params=line_params(6),
         name="gather_back",
     )(
@@ -1672,7 +1418,7 @@
         heads,
         pre,
     )
-    return found[:3], found[3], found[4], found[5]
+    return found[:2], found[2], found[3], found[4]
 
 
 def take_out_kernel(
@@ -1816,7 +1562,7 @@
     result, query, key, value, output, gains = pl.pallas_call(
         functools.partial(take_out_kernel, chips, fsdp_count),
         out_shape=(jax.ShapeDtypeStruct((rows, width), f32),)
-        + (jax.ShapeDtypeStruct((own, columns * slots), f32),) * 3
+        + (jax.ShapeDtypeStruct((own, columns * slots), bf16),) * 3
         + (jax.ShapeDtypeStruct((own, width), f32), jax.ShapeDtypeStruct((8, lanes), f32)),
         in_specs=[whole_spec()] * 5,
         out_specs=(whole_spec(),) * 6,
@@ -1844,6 +1590,311 @@
         gains,
     )
     return result, (query, key, value), output, gains[:kinds, :own]
+
+
+def feed_forward_kernel(
+    chips,
+    hidden_ref,
+    gate_hbm,
+    up_hbm,
+    down_hbm,
+    stream_ref,
+    cotangent_ref,
+    gain_ref,
+    result_ref,
+    grad_ref,
+    gain_grad_ref,
+    gate_out,
+    up_out,
+    act_out,
+    all_out,
+    gate_w,
+    up_w,
+    down_w,
+    gate_keep,
+    up_keep,
+    act_keep,
+    load_sem,
+    store_sem,
+    mixed_ref,
+    *comm,
+):
+    line = Line(chips)
+    gather = Gather(line, *comm[:5])
+    scatter = Scatter(line, *comm[5:])
+    blocks, fresh = gather.blocks, scatter.fresh
+    _, rows, width = blocks.shape
+    units = gate_w.shape[1]
+    copies = load(
+        [
+            (gate_hbm, gate_w, load_sem.at[0]),
+            (up_hbm, up_w, load_sem.at[1]),
+            (down_hbm, down_w, load_sem.at[2]),
+        ]
+    )
+    line.greet()
+    blocks[line.place * 2 + line.core] = hidden_ref[...]
+    gather.send(line.place)
+
+    def stores(chip):
+        pair = pl.ds(chip * 2, 2)
+        return [
+            pltpu.make_async_copy(gate_keep.at[pair], gate_out.at[pair], store_sem.at[0, chip]),
+            pltpu.make_async_copy(up_keep.at[pair], up_out.at[pair], store_sem.at[1, chip]),
+            pltpu.make_async_copy(act_keep.at[pair], act_out.at[pair], store_sem.at[2, chip]),
+            pltpu.make_async_copy(blocks.at[pair], all_out.at[pair], store_sem.at[3, chip]),
+        ]
+
+    for copy in copies:
+        copy.wait()
+
+    @pl.loop(0, chips)
+    def _(step):
+        chip = gather.step(step)
+        pair = pl.ds(chip * 2, 2)
+
+        @pl.loop(0, units // tile_of(units))
+        def _(tile):
+            columns = pl.ds(pl.multiple_of(tile * tile_of(units), 128), tile_of(units))
+            tokens = blocks[pair].reshape(2 * rows, width)
+            gate = jnp.dot(tokens, gate_w[:, columns], preferred_element_type=jnp.float32)
+            up = jnp.dot(tokens, up_w[:, columns], preferred_element_type=jnp.float32)
+            gate_keep[pair, :, columns] = gate.reshape(2, rows, -1)
+            up_keep[pair, :, columns] = up.reshape(2, rows, -1)
+            act_keep[pair, :, columns] = (
+                (gate / (1.0 + jnp.exp(-gate)) * up).astype(jnp.bfloat16).reshape(2, rows, -1)
+            )
+
+        @pl.loop(0, width // tile_of(width))
+        def _(tile):
+            columns = pl.ds(pl.multiple_of(tile * tile_of(width), 128), tile_of(width))
+            act = act_keep[pair].reshape(2 * rows, units)
+            fresh[:, :, columns] = dot_cols(act, down_w[columns, :]).reshape(2, rows, -1)
+
+        for copy in stores(chip):
+            copy.start()
+        scatter.after_term(chip)
+
+    scatter.hops()
+    scatter.settle(mixed_ref)
+    gain_grad_ref[...] = jnp.zeros_like(gain_grad_ref)
+    part_rows = min(32, rows)
+
+    @pl.loop(0, rows // part_rows)
+    def _(part):
+        span = pl.ds(pl.multiple_of(part * part_rows, part_rows), part_rows)
+        mixed, outer, gain = mixed_ref[span], cotangent_ref[span].astype(jnp.float32), gain_ref[0:1]
+        inverse = lax.rsqrt(jnp.mean(mixed * mixed, axis=-1, keepdims=True) + eps_norm)
+        unit = mixed * inverse
+        result_ref[span] = (stream_ref[span] + unit * gain).astype(jnp.bfloat16)
+        gain_grad_ref[0:1] += jnp.sum(outer * unit, axis=0, keepdims=True)
+        outer = outer * gain
+        mean = jnp.mean(outer * unit, axis=-1, keepdims=True)
+        grad_ref[span] = (inverse * (outer - unit * mean)).astype(jnp.bfloat16)
+
+    scatter.finish()
+    gather.finish()
+
+    @pl.loop(0, chips)
+    def _(chip):
+        for copy in stores(chip):
+            copy.wait()
+
+
+def feed_forward(hidden_low, gate_cols, up_cols, down_cols, stream, cotangent, gain):
+    rows, width = hidden_low.shape
+    units = gate_cols.shape[1]
+    slots = lax.axis_size("seq")
+    chips = slots // 2
+    weights = [pltpu.VMEM((width, units), jnp.bfloat16)] * 3
+    result, grad, gain_grad, gate, up, act, every = pl.pallas_call(
+        functools.partial(feed_forward_kernel, chips),
+        out_shape=(
+            jax.ShapeDtypeStruct((rows, width), jnp.bfloat16),
+            jax.ShapeDtypeStruct((rows, width), jnp.bfloat16),
+            jax.ShapeDtypeStruct((8, width), jnp.float32),
+            jax.ShapeDtypeStruct((slots, rows, units), jnp.float32),
+            jax.ShapeDtypeStruct((slots, rows, units), jnp.float32),
+            jax.ShapeDtypeStruct((slots, rows, units), jnp.bfloat16),
+            jax.ShapeDtypeStruct((slots, rows, width), jnp.bfloat16),
+        ),
+        in_specs=[whole_spec()] + [far_spec()] * 3 + [whole_spec()] * 3,
+        out_specs=(whole_spec(),) * 3 + (far_spec(),) * 4,
+        scratch_shapes=weights
+        + [
+            pltpu.VMEM((slots, rows, units), jnp.float32),
+            pltpu.VMEM((slots, rows, units), jnp.float32),
+            pltpu.VMEM((slots, rows, units), jnp.bfloat16),
+            pltpu.SemaphoreType.DMA((3,)),
+            pltpu.SemaphoreType.DMA((4, chips)),
+            pltpu.VMEM((rows, width), jnp.float32),
+        ]
+        + Gather.scratch(chips, rows, width)
+        + Scatter.scratch(chips, rows, width),
+        compiler_params=line_params(1),
+        name="feed_forward",
+    )(hidden_low, gate_cols, up_cols, down_cols, stream, cotangent, gain.reshape(1, width))
+    return (
+        result,
+        grad,
+        gain_grad[0],
+        gate,
+        up,
+        act.reshape(-1, units),
+        every.reshape(-1, width),
+    )
+
+
+def feed_forward_back_kernel(chips, fsdp_count, *refs):
+    grad_ref, gate_hbm, up_hbm, down_hbm, gate_lin_hbm, up_lin_hbm, act_hbm = refs[:7]
+    hidden_grad_ref, gate_out, up_out, down_grad, refs = *refs[7:11], refs[11:]
+    gate_w, up_w, down_w, gate_lin, up_lin, gate_keep, up_keep, act, refs = *refs[:8], refs[8:]
+    load_sem, store_sem, refs = refs[0], refs[1], refs[2:]
+    line = Line(chips)
+    cross = Cross(2 * chips, fsdp_count)
+    gather = Gather(line, *refs[:5])
+    scatter = Scatter(line, *refs[5:15])
+    blocks, fresh = gather.blocks, scatter.fresh
+    _, rows, width = blocks.shape
+    units = gate_w.shape[1]
+    all_tokens = cross.seq_count * rows
+
+    def fill(kind, owner, slot):
+        span = width // cross.seq_count
+        part = pl.ds(pl.multiple_of(owner * span, 128), span)
+        chosen = blocks[:, :, part].reshape(all_tokens, span)
+
+        @pl.loop(0, units // tile_of(units))
+        def _(tile):
+            columns = pl.ds(pl.multiple_of(tile * tile_of(units), 128), tile_of(units))
+            term = dot_rows(chosen, act[:, columns]).astype(jnp.bfloat16)
+            collect.terms[slot, :, :, columns] = term.reshape(fsdp_count, -1, term.shape[1])
+
+    collect = Collect(cross, 1, fill, *refs[15:])
+    copies = load(
+        [
+            (down_hbm, down_w, load_sem.at[0]),
+            (gate_lin_hbm, gate_lin, load_sem.at[1]),
+            (up_lin_hbm, up_lin, load_sem.at[2]),
+            (gate_hbm, gate_w, load_sem.at[3]),
+            (up_hbm, up_w, load_sem.at[4]),
+            (act_hbm, act, load_sem.at[5]),
+        ]
+    )
+    greet_cross(cross.seq_count, fsdp_count)
+    blocks[line.place * 2 + line.core] = grad_ref[...]
+    gather.send(line.place)
+
+    def stores(chip):
+        pair = pl.ds(chip * 2, 2)
+        return [
+            pltpu.make_async_copy(gate_keep.at[pair], gate_out.at[pair], store_sem.at[0, chip]),
+            pltpu.make_async_copy(up_keep.at[pair], up_out.at[pair], store_sem.at[1, chip]),
+        ]
+
+    for copy in copies:
+        copy.wait()
+
+    @pl.loop(0, chips)
+    def _(step):
+        chip = gather.step(step)
+        pair = pl.ds(chip * 2, 2)
+
+        @pl.loop(0, units // tile_of(units))
+        def _(tile):
+            columns = pl.ds(pl.multiple_of(tile * tile_of(units), 128), tile_of(units))
+            tokens = blocks[pair].reshape(2 * rows, width)
+            grad = jnp.dot(tokens, down_w[:, columns], preferred_element_type=jnp.float32)
+            gate = gate_lin[pair, :, columns].reshape(2 * rows, -1)
+            up = up_lin[pair, :, columns].reshape(2 * rows, -1)
+            sig = 1.0 / (1.0 + jnp.exp(-gate))
+            gate_keep[pair, :, columns] = (
+                (grad * up * sig * (1.0 + gate * (1.0 - sig)))
+                .astype(jnp.bfloat16)
+                .reshape(2, rows, -1)
+            )
+            up_keep[pair, :, columns] = (
+                (grad * (gate * sig)).astype(jnp.bfloat16).reshape(2, rows, -1)
+            )
+
+        @pl.loop(0, width // tile_of(width))
+        def _(tile):
+            columns = pl.ds(pl.multiple_of(tile * tile_of(width), 128), tile_of(width))
+            gate = gate_keep[pair].reshape(2 * rows, units)
+            up = up_keep[pair].reshape(2 * rows, units)
+            fresh[:, :, columns] = (
+                dot_cols(gate, gate_w[columns, :]) + dot_cols(up, up_w[columns, :])
+            ).reshape(2, rows, -1)
+
+        for copy in stores(chip):
+            copy.start()
+        scatter.after_term(chip)
+
+    collect.begin()
+
+    @pl.loop(0, collect.beats)
+    def _(turn):
+        collect.beat(turn)
+
+        @pl.when(turn < chips)
+        def _():
+            scatter.hop(turn)
+
+    scatter.settle(hidden_grad_ref)
+
+    def put(_, sender, value):
+        columns = pl.ds(pl.multiple_of(sender * units, 128), units)
+        down_grad[:, columns] = value
+
+    @pl.loop(0, cross.seq_count)
+    def _(turn):
+        collect.receive(turn, put)
+
+    scatter.finish()
+    gather.finish()
+    collect.finish()
+
+    @pl.loop(0, chips)
+    def _(chip):
+        for copy in stores(chip):
+            copy.wait()
+
+
+def feed_forward_back(grad_low, gate_cols, up_cols, down_cols, gate, up, act):
+    rows, width = grad_low.shape
+    units = gate_cols.shape[1]
+    slots = lax.axis_size("seq")
+    fsdp_count = lax.axis_size("fsdp")
+    chips = slots // 2
+    own = width // (slots * fsdp_count)
+    bf16, f32 = jnp.bfloat16, jnp.float32
+    hidden_grad, gate_grad, up_grad, down_grad = pl.pallas_call(
+        functools.partial(feed_forward_back_kernel, chips, fsdp_count),
+        out_shape=(
+            jax.ShapeDtypeStruct((rows, width), f32),
+            jax.ShapeDtypeStruct((slots, rows, units), bf16),
+            jax.ShapeDtypeStruct((slots, rows, units), bf16),
+            jax.ShapeDtypeStruct((own, units * slots), bf16),
+        ),
+        in_specs=[whole_spec()] + [far_spec()] * 6,
+        out_specs=(whole_spec(), far_spec(), far_spec(), whole_spec()),
+        scratch_shapes=[pltpu.VMEM((width, units), bf16)] * 3
+        + [
+            pltpu.VMEM((slots, rows, units), f32),
+            pltpu.VMEM((slots, rows, units), f32),
+            pltpu.VMEM((slots, rows, units), bf16),
+            pltpu.VMEM((slots, rows, units), bf16),
+            pltpu.VMEM((slots * rows, units), bf16),
+            pltpu.SemaphoreType.DMA((6,)),
+            pltpu.SemaphoreType.DMA((2, chips)),
+        ]
+        + Gather.scratch(chips, rows, width)
+        + Scatter.scratch(chips, rows, width)
+        + Collect.scratch(1, slots, fsdp_count, own, units),
+        compiler_params=line_params(2),
+        name="feed_forward_back",
+    )(grad_low, gate_cols, up_cols, down_cols, gate, up, act)
+    return hidden_grad, gate_grad.reshape(-1, units), up_grad.reshape(-1, units), down_grad
 
 
 def rope_tables(row_count):
@@ -1906,22 +1957,17 @@
     feedforward_scale = gains[3]
     hidden = local_in.astype(jnp.float32) + rms_scale(projected, attention_scale)
     hidden_low = hidden.astype(jnp.bfloat16)
-    mixed_pre, gate_linear, up_linear, activated, hidden_all = feed_forward(
-        hidden_low, gate_cols, up_cols, down_cols
-    )
-    result = (
-        (hidden + rms_scale(mixed_pre, feedforward_scale))
-        .astype(jnp.bfloat16)
-        .reshape(1, token_count, width_all)
-    )
-    grad_result = cotangent.reshape(token_count, width_all).astype(jnp.float32)
-    _, mixed_pull = jax.vjp(rms_scale, mixed_pre, feedforward_scale)
-    grad_mixed, grad_feedforward_gain = mixed_pull(grad_result)
-    grad_mixed_low = grad_mixed.astype(jnp.bfloat16)
-    hidden_term, grad_gate_low, grad_upward_low, grad_all = feed_forward_back(
-        grad_mixed_low, gate_cols, up_cols, down_cols, gate_linear, up_linear
-    )
-    grad_hidden = grad_result + hidden_term
+    grad_result = cotangent.reshape(token_count, width_all)
+    result, grad_mixed_low, grad_feedforward_gain, gate_linear, up_linear, activated, hidden_all = (
+        feed_forward(
+            hidden_low, gate_cols, up_cols, down_cols, hidden, grad_result, feedforward_scale
+        )
+    )
+    result = result.reshape(1, token_count, width_all)
+    hidden_term, grad_gate_low, grad_upward_low, down_weight_grad = feed_forward_back(
+        grad_mixed_low, gate_cols, up_cols, down_cols, gate_linear, up_linear, activated
+    )
+    grad_hidden = grad_result.astype(jnp.float32) + hidden_term
     _, branch_pull = jax.vjp(rms_scale, projected, attention_scale)
     grad_projected, grad_attention_gain = branch_pull(grad_hidden)
     weight_grads, output_term, attention_grads, gain_rows = gather_back(
@@ -1931,11 +1977,11 @@
         inverse,
         tables,
         segment_row,
-        [hidden_all, grad_all, grad_gate_low, grad_upward_low, activated],
+        [hidden_all, grad_gate_low, grad_upward_low],
         heads,
         pre,
     )
-    gate_weight_grad, up_weight_grad, down_weight_grad = weight_grads
+    gate_weight_grad, up_weight_grad = weight_grads
     head_gains = lax.dynamic_update_slice_in_dim(
         jnp.zeros((2, width_all), jnp.float32),
         gain_rows[:2],
@@ -1953,16 +1999,16 @@
     return (
         result,
         grad_input.reshape(1, token_count, width_all),
-        query_weight_grad,
-        key_weight_grad,
-        value_weight_grad,
+        query_weight_grad.astype(jnp.float32),
+        key_weight_grad.astype(jnp.float32),
+        value_weight_grad.astype(jnp.float32),
         output_weight_grad,
         gain_grads[0],
         gain_grads[1],
         gain_grads[2],
-        gate_weight_grad,
-        up_weight_grad,
-        down_weight_grad,
+        gate_weight_grad.astype(jnp.float32),
+        up_weight_grad.astype(jnp.float32),
+        down_weight_grad.astype(jnp.float32),
         gain_grads[3],
     )
 

time: 595 us -> 572 us (0.961)
  local copies, waits for them, and re-layouts: 21.6 us -> 8.13 us
  Pallas kernels: 547 us -> 539 us
    pallas_call x1, Pallas kernels: 131 us -> 105 us  [gather_back(): pl.pallas_call(functools.partial(gather_back_kernel, chips, fsdp_count),...]
    pallas_call x1, Pallas kernels: 77.8 us -> 96.6 us  [feed_forward_back(): pl.pallas_call(functools.partial(feed_forward_back_kernel, chips, fsdp_co...]
    slice x1, local copies, waits for them, and re-layouts: 8.84 us -> 0.86 us  [feed_forward(): gain_grad[0]]
    unnamed x33 -> x48, local copies, waits for them, and re-layouts: 8.41 us -> 2.43 us
where the time goes in v8:
time: 572 us; the launch traced here: 570 us
  Pallas kernels  539 us (94%)
  other arithmetic  22.5 us (4%)
  local copies, waits for them, and re-layouts  8.13 us (1%)
    pallas_call x1, Pallas kernels, bring_in(): pl.pallas_call(functools.partial(bring_in_kernel, chips, fsdp_count), out...  179 us
    pallas_call x1, Pallas kernels, gather_back(): pl.pallas_call(functools.partial(gather_back_kernel, chips, fsdp_count),...  105 us
    pallas_call x1, Pallas kernels, feed_forward_back(): pl.pallas_call(functools.partial(feed_forward_back_kernel, chips, fsdp_co...  96.6 us
    pallas_call x1, Pallas kernels, feed_forward(): pl.pallas_call(functools.partial(feed_forward_kernel, chips), out_shape=(...  84.5 us
    pallas_call x1, Pallas kernels, take_out(): pl.pallas_call(functools.partial(take_out_kernel, chips, fsdp_count), out...  73.7 us

profile of v8, /device:TPU:0, one launch (start us, length us, event | category | flops | bytes accessed | tf_op | source)
XLA Modules:
  0.0 570.5 jit_solution(16401405488468035204)
XLA Ops:
  0.7 0.0 copy-start.13
  0.7 0.0 copy-start.19
  0.7 0.0 copy-start.20
  0.7 0.0 copy-start.21
  0.7 0.0 copy-start.22
  0.7 1.9 fusion.1
  2.6 1.3 pad_maximum_fusion
  3.9 0.0 copy-done.13
  3.9 1.0 copy.27.refs_4_.refs_6_
  5.0 0.0 copy-done.19
  5.0 0.0 copy-done.20
  5.0 0.0 copy-done.21
  5.0 0.0 copy-done.22
  5.0 0.6 fusion.10.refs_1_
  5.6 179.4 %bring_in.1 = (f32[128,2048]{1,0:T(8,128)}, f32[1024,8]{1,0:T(8,128)}, f32[16,256]{1,0:T(8,128)}, bf16[8,4,16,128]{3,2,1,0:T(8,128)(2,1)}, bf16[8,128,2048]{2,1,...) custom-call(bf16[128,2048]{1,0:T(8,128)(2,1)} %bitcast.52, ...), custom_call_target="tpu_custom_call" | custom-call | tf_op jit(solution)/shard_map/bring_in/pallas_call | solution.py:1159
  185.0 1.4 multiply_reduce_fusion.2
  186.3 0.0 copy-start.14
  186.4 0.9 convert_bitcast_fusion
  187.2 0.1 slice_reduce_fusion
  187.3 0.0 copy-done.17
  187.3 0.1 mul.106
  187.4 0.6 copy-done.11
  188.0 2.7 fusion.15
  190.7 0.7 slice.39.gain_ref
  191.4 0.0 copy-done.14
  191.4 84.5 %feed_forward.1 = (bf16[128,2048]{1,0:T(8,128)(2,1)}, bf16[128,2048]{1,0:T(8,128)(2,1)}, f32[8,2048]{1,0:T(8,128)}, f32[8,128,1024]{2,1,0:T(8,128)}, f32[8,128,1...) custom-call(bf16[128,2048]{1,0:T(8,128)(2,1)} %get-tuple-element.85.hidden_ref, ...), custom_call_target="tpu_custom_call" | custom-call | tf_op jit(solution)/shard_map/feed_forward/pallas_call | solution.py:1710
  276.0 96.6 %feed_forward_back.1 = (f32[128,2048]{1,0:T(8,128)}, bf16[8,128,1024]{2,1,0:T(8,128)(2,1)}, bf16[8,128,1024]{2,1,0:T(8,128)(2,1)}, bf16[64,8192]{1,0:T(8,128)(2,1)}) custom-call(bf16[128,2048]{1,0:T(8,128)(2,1)} %get-tuple-element.53.refs_0_, bf16[2048,1024]{1,0:T(8,128)(2,1)} %bitcast.42, bf16[2048,1024]{1,0:T(8,128)(2,1)} %bitcast.44, ...), custom_call_target="tpu_custom_call" | custom-call | tf_op jit(solution)/shard_map/feed_forward_back/pallas_call | solution.py:1871
  372.5 0.0 copy-start.18
  372.5 0.0 copy-start
  372.6 0.0 copy-start.1
  372.6 0.0 copy-start.2
  372.6 0.0 copy-start.12
  372.6 0.0 copy-start.15
  372.6 2.8 multiply_reduce_fusion
  375.4 0.0 copy-done.18
  375.4 0.0 copy-done
  375.4 0.0 copy-done.1
  375.4 0.0 copy-done.2
  375.4 0.0 copy-done.12
  375.4 0.0 copy-done.15
  375.4 1.1 fusion.refs_0_
  376.5 104.8 %gather_back.1 = (bf16[64,8192]{1,0:T(8,128)(2,1)}, bf16[64,8192]{1,0:T(8,128)(2,1)}, bf16[256,2048]{1,0:T(8,128)(2,1)}, bf16[3,1024,256]{2,1,0:T(8,128)(2,1)}, f32[8,256]{1,0:T(8,128)}) custom-call(bf16[128,2048]{1,0:T(8,128)(2,1)} %fusion.refs_0_, bf16[256,2048]{1,0:T(8,128)(2,1)} %bitcast.58, f32[16,256]{1,0:T(8,128)} %get-tuple-element.59.refs_2_, ...), custom_call_target="tpu_custom_call" | custom-call | tf_op jit(solution)/shard_map/gather_back/pallas_call | solution.py:1383
  481.3 0.7 slice_dynamic-update-slice_fusion
  482.0 0.1 concatenate.18
  482.1 0.8 concatenate.19
  482.9 0.9 slice_reduce_fusion.2
  483.8 0.1 concatenate.20
  483.9 0.1 maximum_bitcast_fusion
  484.0 0.7 pad.9.refs_4_
  484.6 73.7 %take_out.1 = (f32[128,2048]{1,0:T(8,128)}, bf16[64,2048]{1,0:T(8,128)(2,1)}, bf16[64,2048]{1,0:T(8,128)(2,1)}, bf16[64,2048]{1,0:T(8,128)(2,1)}, f32[64,2048]{1,0:T(8,128)}, /*index=5*/f32[8,128]{1,0:T(8,128)}) custom-call(bf16[3,8,128,256]{3,2,1,0:T(8,128)(2,1)} %bitcast.56, bf16[3,2048,256]{2,1,0:T(8,128)(2,1)} %bitcast.50, bf16[1024,2048]{1,0:T(8,128)(2,1)} %bitcast.48, ...), custom_call_target="tpu_custom_call" | custom-call | tf_op jit(solution)/shard_map/take_out/pallas_call | solution.py:1562
  558.4 0.0 copy-start.10
  558.4 0.0 copy-start.9
  558.4 0.0 copy-start.8
  558.4 2.9 add_bitcast_fusion
  561.3 0.8 convert_element_type.61
  562.2 0.8 convert_element_type.62
  563.0 0.8 convert_element_type.63
  563.8 0.5 slice_bitcast_fusion
  564.4 1.5 convert_element_type.64
  565.8 1.5 convert_element_type.65
  567.3 0.1 copy-done.3
  567.4 1.5 convert_element_type.66
  568.9 0.8 copy.35
  569.7 0.8 copy.36
  (24 shorter events, 0.1 us)
Async XLA Ops:
  0.7 3.3 copy-start.13
  0.7 4.3 copy-start.19
  0.7 4.3 copy-start.20
  0.7 4.3 copy-start.21
  0.7 4.3 copy-start.22
  186.3 1.0 copy-start.17
  186.3 5.1 copy-start.14
  187.4 0.6 copy-start.11
  372.5 2.8 copy-start.18
  372.5 2.8 copy-start
  372.6 2.8 copy-start.1
  372.6 2.8 copy-start.2
  372.6 2.8 copy-start.12
  372.6 2.8 copy-start.15
  558.4 2.9 copy-start.10
  558.4 3.8 copy-start.9
  558.4 4.6 copy-start.8
  561.3 2.5 copy-start.16
  561.3 3.0 copy-start.5
  563.0 2.8 copy-start.4
  565.8 1.6 copy-start.3
  567.3 1.6 copy-start.6
  567.4 2.3 copy-start.7

commit v9 on v8

--- a/solution.py
+++ b/solution.py
@@ -863,7 +863,7 @@
 
 EARLY = 6
 LEAD = 2
-HOPPING = 4
+HOPPING = 1
 
 
 def bring_in_kernel(chips, fsdp_count, *refs):
@@ -1058,6 +1058,13 @@
     def units_store(kind):
         return pltpu.make_async_copy(units.weights.at[kind], units_out[kind], store_sem.at[5 + kind])
 
+    def settle_units(kind):
+        @pl.loop(0, seq_count)
+        def _(step):
+            units.settle(kind * seq_count + step)
+
+        units_store(kind).start()
+
     @pl.loop(0, LEAD)
     def _(item):
         units.take(item)
@@ -1108,20 +1115,19 @@
         def _():
             attend(beat - attending)
 
-        @pl.when((beat >= hopping) & ((beat - hopping) % 2 == 0) & (beat < hopping + 2 * chips))
-        def _():
-            scatter.hop(chips - 1 - (beat - hopping) // 2)
+        for kind in range(2):
+
+            @pl.when(beat == (kind + 1) * seq_count + 3)
+            def _():
+                settle_units(kind)
+
+        @pl.when((beat >= hopping) & (beat < hopping + chips))
+        def _():
+            scatter.hop(chips - 1 - (beat - hopping))
 
     heads_store.start()
     scatter.settle(projected)
-    for kind in range(3):
-
-        @pl.loop(0, seq_count)
-        def _(step):
-            units.settle(kind * seq_count + step)
-
-        units_store(kind).start()
-
+    settle_units(2)
     scatter.finish()
     gather.finish()
     sums.finish()

time: 572 us -> 563 us (0.984)
  Pallas kernels: 539 us -> 529 us
    pallas_call x1, Pallas kernels: 73.7 us -> 64.2 us  [take_out(): pl.pallas_call(functools.partial(take_out_kernel, chips, fsdp_count), out...]
where the time goes in v9:
time: 563 us; the launch traced here: 560 us
  Pallas kernels  529 us (94%)
  other arithmetic  22.5 us (4%)
  local copies, waits for them, and re-layouts  8.13 us (1%)
    pallas_call x1, Pallas kernels, bring_in(): pl.pallas_call(functools.partial(bring_in_kernel, chips, fsdp_count), out...  179 us
    pallas_call x1, Pallas kernels, gather_back(): pl.pallas_call(functools.partial(gather_back_kernel, chips, fsdp_count),...  105 us
    pallas_call x1, Pallas kernels, feed_forward_back(): pl.pallas_call(functools.partial(feed_forward_back_kernel, chips, fsdp_co...  96.5 us
    pallas_call x1, Pallas kernels, feed_forward(): pl.pallas_call(functools.partial(feed_forward_kernel, chips), out_shape=(...  84.3 us
    pallas_call x1, Pallas kernels, take_out(): pl.pallas_call(functools.partial(take_out_kernel, chips, fsdp_count), out...  64.2 us

profile of v9, /device:TPU:0, one launch (start us, length us, event | category | flops | bytes accessed | tf_op | source)
XLA Modules:
  0.0 560.5 jit_solution(4744539871552677925)
XLA Ops:
  0.7 0.0 copy-start.13
  0.7 0.0 copy-start.19
  0.7 0.0 copy-start.20
  0.7 0.0 copy-start.21
  0.7 0.0 copy-start.22
  0.7 1.9 fusion.1
  2.6 1.3 pad_maximum_fusion
  3.9 0.0 copy-done.13
  3.9 1.0 copy.27.refs_4_.refs_6_
  5.0 0.0 copy-done.19
  5.0 0.0 copy-done.20
  5.0 0.0 copy-done.21
  5.0 0.0 copy-done.22
  5.0 0.6 fusion.10.refs_1_
  5.6 179.4 %bring_in.1 = (f32[128,2048]{1,0:T(8,128)}, f32[1024,8]{1,0:T(8,128)}, f32[16,256]{1,0:T(8,128)}, bf16[8,4,16,128]{3,2,1,0:T(8,128)(2,1)}, bf16[8,128,2048]{2,1,...) custom-call(bf16[128,2048]{1,0:T(8,128)(2,1)} %bitcast.52, ...), custom_call_target="tpu_custom_call" | custom-call | tf_op jit(solution)/shard_map/bring_in/pallas_call | solution.py:1165
  185.0 1.4 multiply_reduce_fusion.2
  186.4 0.0 copy-start.14
  186.4 0.9 convert_bitcast_fusion
  187.2 0.1 slice_reduce_fusion
  187.4 0.0 copy-done.17
  187.4 0.1 mul.106
  187.5 0.6 copy-done.11
  188.1 2.7 fusion.15
  190.8 0.7 slice.39.gain_ref
  191.5 0.0 copy-done.14
  191.5 84.3 %feed_forward.1 = (bf16[128,2048]{1,0:T(8,128)(2,1)}, bf16[128,2048]{1,0:T(8,128)(2,1)}, f32[8,2048]{1,0:T(8,128)}, f32[8,128,1024]{2,1,0:T(8,128)}, f32[8,128,1...) custom-call(bf16[128,2048]{1,0:T(8,128)(2,1)} %get-tuple-element.85.hidden_ref, ...), custom_call_target="tpu_custom_call" | custom-call | tf_op jit(solution)/shard_map/feed_forward/pallas_call | solution.py:1716
  275.7 96.5 %feed_forward_back.1 = (f32[128,2048]{1,0:T(8,128)}, bf16[8,128,1024]{2,1,0:T(8,128)(2,1)}, bf16[8,128,1024]{2,1,0:T(8,128)(2,1)}, bf16[64,8192]{1,0:T(8,128)(2,1)}) custom-call(bf16[128,2048]{1,0:T(8,128)(2,1)} %get-tuple-element.53.refs_0_, bf16[2048,1024]{1,0:T(8,128)(2,1)} %bitcast.42, bf16[2048,1024]{1,0:T(8,128)(2,1)} %bitcast.44, ...), custom_call_target="tpu_custom_call" | custom-call | tf_op jit(solution)/shard_map/feed_forward_back/pallas_call | solution.py:1877
  372.2 0.0 copy-start.18
  372.2 0.0 copy-start
  372.3 0.0 copy-start.1
  372.3 0.0 copy-start.2
  372.3 0.0 copy-start.12
  372.3 0.0 copy-start.15
  372.3 2.8 multiply_reduce_fusion
  375.1 0.0 copy-done.18
  375.1 0.0 copy-done
  375.1 0.0 copy-done.1
  375.1 0.0 copy-done.2
  375.1 1.1 fusion.refs_0_
  376.2 104.6 %gather_back.1 = (bf16[64,8192]{1,0:T(8,128)(2,1)}, bf16[64,8192]{1,0:T(8,128)(2,1)}, bf16[256,2048]{1,0:T(8,128)(2,1)}, bf16[3,1024,256]{2,1,0:T(8,128)(2,1)}, f32[8,256]{1,0:T(8,128)}) custom-call(bf16[128,2048]{1,0:T(8,128)(2,1)} %fusion.refs_0_, bf16[256,2048]{1,0:T(8,128)(2,1)} %bitcast.58, f32[16,256]{1,0:T(8,128)} %get-tuple-element.59.refs_2_, ...), custom_call_target="tpu_custom_call" | custom-call | tf_op jit(solution)/shard_map/gather_back/pallas_call | solution.py:1389
  480.8 0.7 slice_dynamic-update-slice_fusion
  481.5 0.1 concatenate.18
  481.7 0.8 concatenate.19
  482.5 0.9 slice_reduce_fusion.2
  483.3 0.1 concatenate.20
  483.4 0.1 maximum_bitcast_fusion
  483.5 0.7 pad.9.refs_4_
  484.2 64.2 %take_out.1 = (f32[128,2048]{1,0:T(8,128)}, bf16[64,2048]{1,0:T(8,128)(2,1)}, bf16[64,2048]{1,0:T(8,128)(2,1)}, bf16[64,2048]{1,0:T(8,128)(2,1)}, f32[64,2048]{1,0:T(8,128)}, /*index=5*/f32[8,128]{1,0:T(8,128)}) custom-call(bf16[3,8,128,256]{3,2,1,0:T(8,128)(2,1)} %bitcast.56, bf16[3,2048,256]{2,1,0:T(8,128)(2,1)} %bitcast.50, bf16[1024,2048]{1,0:T(8,128)(2,1)} %bitcast.48, ...), custom_call_target="tpu_custom_call" | custom-call | tf_op jit(solution)/shard_map/take_out/pallas_call | solution.py:1568
  548.4 0.0 copy-start.10
  548.4 0.0 copy-start.9
  548.4 0.0 copy-start.8
  548.4 2.9 add_bitcast_fusion
  551.3 0.8 convert_element_type.61
  552.2 0.8 convert_element_type.62
  553.0 0.8 convert_element_type.63
  553.8 0.0 copy-done.16
  553.8 0.5 slice_bitcast_fusion
  554.4 1.5 convert_element_type.64
  555.8 0.0 copy-done.4
  555.8 1.5 convert_element_type.65
  557.3 0.1 copy-done.3
  557.4 1.5 convert_element_type.66
  558.9 0.8 copy.35
  559.7 0.8 copy.36
  (24 shorter events, 0.1 us)
Async XLA Ops:
  0.7 3.3 copy-start.13
  0.7 4.3 copy-start.19
  0.7 4.3 copy-start.20
  0.7 4.3 copy-start.21
  0.7 4.3 copy-start.22
  186.4 1.0 copy-start.17
  186.4 5.1 copy-start.14
  187.5 0.6 copy-start.11
  372.2 2.8 copy-start.18
  372.2 2.8 copy-start
  372.3 2.8 copy-start.1
  372.3 2.8 copy-start.2
  372.3 2.8 copy-start.12
  372.3 2.8 copy-start.15
  548.4 2.9 copy-start.10
  548.4 3.8 copy-start.9
  548.4 4.6 copy-start.8
  551.3 2.5 copy-start.16
  551.3 3.0 copy-start.5
  553.0 2.8 copy-start.4
  555.8 1.6 copy-start.3
  557.3 1.6 copy-start.6
  557.4 2.3 copy-start.7

commit v10 on v9

--- a/solution.py
+++ b/solution.py
@@ -1432,12 +1432,11 @@
     fsdp_count,
     *refs,
 ):
-    grads_ref, rights, tokens_ref = refs[0], refs[1], refs[2]
-    output_ref, gains_ref, refs = refs[3], refs[4], refs[5:]
+    sources, output_ref, gains_ref, refs = refs[:3], refs[3], refs[4], refs[5:]
     result, weight_outs, output_out, gains_out, refs = refs[0], refs[1:4], refs[4], refs[5], refs[6:]
     output_in, gain_in, gain_out, gain_rows, refs = refs[0], refs[1], refs[2], refs[3], refs[4:]
     output_send, output_recv, gain_send, gain_recv, gain_row_send, gain_row_recv = refs[:6]
-    comm = refs[6:]
+    grads_ref, rights, tokens_ref, load_sem, comm = *refs[6:10], refs[10:]
     line = Line(chips)
     cross = Cross(2 * chips, fsdp_count)
     seq_count, seq, fsdp = cross.seq_count, cross.seq, cross.fsdp
@@ -1485,10 +1484,18 @@
             fsdp,
         )
 
+    copies = load(
+        [
+            (source, target, load_sem.at[i])
+            for i, (source, target) in enumerate(zip(sources, (grads_ref, rights, tokens_ref)))
+        ]
+    )
     greet_cross(seq_count, fsdp_count)
     for step in range(1, fsdp_count):
         gain_copy(step).start()
 
+    for copy in copies:
+        copy.wait()
     collect.begin()
 
     @pl.loop(0, chips)
@@ -1570,7 +1577,7 @@
         out_shape=(jax.ShapeDtypeStruct((rows, width), f32),)
         + (jax.ShapeDtypeStruct((own, columns * slots), bf16),) * 3
         + (jax.ShapeDtypeStruct((own, width), f32), jax.ShapeDtypeStruct((8, lanes), f32)),
-        in_specs=[whole_spec()] * 5,
+        in_specs=[far_spec()] * 3 + [whole_spec()] * 2,
         out_specs=(whole_spec(),) * 6,
         scratch_shapes=[
             pltpu.VMEM((fsdp_count, own, width), bf16),
@@ -1583,6 +1590,10 @@
             dma((fsdp_count,)),
             dma((slots,)),
             dma((slots,)),
+            pltpu.VMEM((3, slots, rows, columns), bf16),
+            pltpu.VMEM((3, width, columns), bf16),
+            pltpu.VMEM((slots * rows, width), bf16),
+            dma((3,)),
         ]
         + Scatter.scratch(chips, rows, width)
         + Collect.scratch(1, slots, fsdp_count, own, 3 * columns),
@@ -1600,13 +1611,13 @@
 
 def feed_forward_kernel(
     chips,
-    hidden_ref,
+    projected_ref,
+    inputs_ref,
     gate_hbm,
     up_hbm,
     down_hbm,
-    stream_ref,
     cotangent_ref,
-    gain_ref,
+    gains_ref,
     result_ref,
     grad_ref,
     gain_grad_ref,
@@ -1623,6 +1634,7 @@
     load_sem,
     store_sem,
     mixed_ref,
+    stream_ref,
     *comm,
 ):
     line = Line(chips)
@@ -1638,8 +1650,19 @@
             (down_hbm, down_w, load_sem.at[2]),
         ]
     )
+    part_rows = min(32, rows)
+    own_slot = line.place * 2 + line.core
+
+    @pl.loop(0, rows // part_rows)
+    def _(part):
+        span = pl.ds(pl.multiple_of(part * part_rows, part_rows), part_rows)
+        value = projected_ref[span]
+        inverse = lax.rsqrt(jnp.mean(value * value, axis=-1, keepdims=True) + eps_norm)
+        stream = inputs_ref[span].astype(jnp.float32) + value * inverse * gains_ref[0:1]
+        stream_ref[span] = stream
+        blocks[own_slot, span] = stream.astype(jnp.bfloat16)
+
     line.greet()
-    blocks[line.place * 2 + line.core] = hidden_ref[...]
     gather.send(line.place)
 
     def stores(chip):
@@ -1684,12 +1707,11 @@
     scatter.hops()
     scatter.settle(mixed_ref)
     gain_grad_ref[...] = jnp.zeros_like(gain_grad_ref)
-    part_rows = min(32, rows)
 
     @pl.loop(0, rows // part_rows)
     def _(part):
         span = pl.ds(pl.multiple_of(part * part_rows, part_rows), part_rows)
-        mixed, outer, gain = mixed_ref[span], cotangent_ref[span].astype(jnp.float32), gain_ref[0:1]
+        mixed, outer, gain = mixed_ref[span], cotangent_ref[span].astype(jnp.float32), gains_ref[1:2]
         inverse = lax.rsqrt(jnp.mean(mixed * mixed, axis=-1, keepdims=True) + eps_norm)
         unit = mixed * inverse
         result_ref[span] = (stream_ref[span] + unit * gain).astype(jnp.bfloat16)
@@ -1707,8 +1729,8 @@
             copy.wait()
 
 
-def feed_forward(hidden_low, gate_cols, up_cols, down_cols, stream, cotangent, gain):
-    rows, width = hidden_low.shape
+def feed_forward(projected, inputs, gate_cols, up_cols, down_cols, cotangent, gains):
+    rows, width = projected.shape
     units = gate_cols.shape[1]
     slots = lax.axis_size("seq")
     chips = slots // 2
@@ -1724,7 +1746,7 @@
             jax.ShapeDtypeStruct((slots, rows, units), jnp.bfloat16),
             jax.ShapeDtypeStruct((slots, rows, width), jnp.bfloat16),
         ),
-        in_specs=[whole_spec()] + [far_spec()] * 3 + [whole_spec()] * 3,
+        in_specs=[whole_spec()] * 2 + [far_spec()] * 3 + [whole_spec()] * 2,
         out_specs=(whole_spec(),) * 3 + (far_spec(),) * 4,
         scratch_shapes=weights
         + [
@@ -1734,12 +1756,13 @@
             pltpu.SemaphoreType.DMA((3,)),
             pltpu.SemaphoreType.DMA((4, chips)),
             pltpu.VMEM((rows, width), jnp.float32),
+            pltpu.VMEM((rows, width), jnp.float32),
         ]
         + Gather.scratch(chips, rows, width)
         + Scatter.scratch(chips, rows, width),
         compiler_params=line_params(1),
         name="feed_forward",
-    )(hidden_low, gate_cols, up_cols, down_cols, stream, cotangent, gain.reshape(1, width))
+    )(projected, inputs, gate_cols, up_cols, down_cols, cotangent, gains)
     return (
         result,
         grad,
@@ -1960,13 +1983,10 @@
     head_width = heads.shape[2]
     gains = gains.astype(jnp.float32)
     attention_scale = gains[2]
-    feedforward_scale = gains[3]
-    hidden = local_in.astype(jnp.float32) + rms_scale(projected, attention_scale)
-    hidden_low = hidden.astype(jnp.bfloat16)
     grad_result = cotangent.reshape(token_count, width_all)
     result, grad_mixed_low, grad_feedforward_gain, gate_linear, up_linear, activated, hidden_all = (
         feed_forward(
-            hidden_low, gate_cols, up_cols, down_cols, hidden, grad_result, feedforward_scale
+            projected, local_in, gate_cols, up_cols, down_cols, grad_result, gains[2:4]
         )
     )
     result = result.reshape(1, token_count, width_all)

time: 563 us -> 563 us (level)
  no operation moved by 1% of the time
where the time goes in v10:
time: 563 us; the launch traced here: 559 us
  Pallas kernels  527 us (94%)
  other arithmetic  21.5 us (4%)
  local copies, waits for them, and re-layouts  9.52 us (2%)
    pallas_call x1, Pallas kernels, bring_in(): pl.pallas_call(functools.partial(bring_in_kernel, chips, fsdp_count), out...  179 us
    pallas_call x1, Pallas kernels, gather_back(): pl.pallas_call(functools.partial(gather_back_kernel, chips, fsdp_count),...  104 us
    pallas_call x1, Pallas kernels, feed_forward_back(): pl.pallas_call(functools.partial(feed_forward_back_kernel, chips, fsdp_co...  96.8 us
    pallas_call x1, Pallas kernels, feed_forward(): pl.pallas_call(functools.partial(feed_forward_kernel, chips), out_shape=(...  85.4 us
    pallas_call x1, Pallas kernels, take_out(): pl.pallas_call(functools.partial(take_out_kernel, chips, fsdp_count), out...  61.8 us

profile of v10, /device:TPU:0, one launch (start us, length us, event | category | flops | bytes accessed | tf_op | source)
XLA Modules:
  0.0 559.1 jit_solution(11698185648388980906)
XLA Ops:
  0.7 1.3 fusion.10.refs_1_
  2.0 1.7 copy.28.refs_4_.refs_6_
  3.7 1.9 fusion.1
  5.6 1.3 pad_maximum_fusion
  6.9 179.4 %bring_in.1 = (f32[128,2048]{1,0:T(8,128)}, f32[1024,8]{1,0:T(8,128)}, f32[16,256]{1,0:T(8,128)}, bf16[8,4,16,128]{3,2,1,0:T(8,128)(2,1)}, bf16[8,128,2048]{2,1,...) custom-call(bf16[128,2048]{1,0:T(8,128)(2,1)} %bitcast.50, ...), custom_call_target="tpu_custom_call" | custom-call | tf_op jit(solution)/shard_map/bring_in/pallas_call | solution.py:1165
  186.3 1.4 multiply_reduce_fusion.2
  187.7 0.0 copy-start.14
  187.7 0.5 fusion.14
  188.2 0.8 convert_bitcast_fusion
  189.0 0.0 copy-done.14
  189.1 0.1 slice_reduce_fusion
  189.1 0.7 mul.92
  189.8 0.7 slice.38.gains_ref
  190.5 85.4 %feed_forward.1 = (bf16[128,2048]{1,0:T(8,128)(2,1)}, bf16[128,2048]{1,0:T(8,128)(2,1)}, f32[8,2048]{1,0:T(8,128)}, f32[8,128,1024]{2,1,0:T(8,128)}, f32[8,128,1...) custom-call(f32[128,2048]{1,0:T(8,128)} %get-tuple-element.47.projected_ref, ...), custom_call_target="tpu_custom_call" | custom-call | tf_op jit(solution)/shard_map/feed_forward/pallas_call | solution.py:1738
  276.0 96.8 %feed_forward_back.1 = (f32[128,2048]{1,0:T(8,128)}, bf16[8,128,1024]{2,1,0:T(8,128)(2,1)}, bf16[8,128,1024]{2,1,0:T(8,128)(2,1)}, bf16[64,8192]{1,0:T(8,128)(2,1)}) custom-call(bf16[128,2048]{1,0:T(8,128)(2,1)} %get-tuple-element.53.refs_0_, bf16[2048,1024]{1,0:T(8,128)(2,1)} %bitcast.40, bf16[2048,1024]{1,0:T(8,128)(2,1)} %bitcast.42, ...), custom_call_target="tpu_custom_call" | custom-call | tf_op jit(solution)/shard_map/feed_forward_back/pallas_call | solution.py:1900
  372.7 0.0 copy-start.15
  372.8 0.0 copy-start
  372.8 0.0 copy-start.1
  372.8 0.0 copy-start.2
  372.8 0.0 copy-start.11
  372.8 0.0 copy-start.12
  372.8 1.0 slice_reduce_fusion.1
  373.8 0.1 concatenate.20
  373.9 0.6 copy.33
  374.5 2.6 multiply_reduce_fusion
  377.2 0.0 copy-done.15
  377.2 0.0 copy-done
  377.2 0.0 copy-done.1
  377.2 0.0 copy-done.2
  377.2 0.0 copy-done.11
  377.2 0.0 copy-done.12
  377.2 1.1 fusion.refs_0_
  378.3 103.7 %gather_back.1 = (bf16[64,8192]{1,0:T(8,128)(2,1)}, bf16[64,8192]{1,0:T(8,128)(2,1)}, bf16[256,2048]{1,0:T(8,128)(2,1)}, bf16[3,1024,256]{2,1,0:T(8,128)(2,1)}, f32[8,256]{1,0:T(8,128)}) custom-call(bf16[128,2048]{1,0:T(8,128)(2,1)} %fusion.refs_0_, bf16[256,2048]{1,0:T(8,128)(2,1)} %bitcast.57, f32[16,256]{1,0:T(8,128)} %get-tuple-element.59.refs_2_, ...), custom_call_target="tpu_custom_call" | custom-call | tf_op jit(solution)/shard_map/gather_back/pallas_call | solution.py:1389
  482.0 0.7 slice_dynamic-update-slice_fusion
  482.7 0.8 concatenate.19
  483.5 0.1 concatenate.18
  483.7 0.8 maximum_bitcast_fusion
  484.5 0.7 pad.9.refs_4_
  485.1 61.8 %take_out.1 = (f32[128,2048]{1,0:T(8,128)}, bf16[64,2048]{1,0:T(8,128)(2,1)}, bf16[64,2048]{1,0:T(8,128)(2,1)}, bf16[64,2048]{1,0:T(8,128)(2,1)}, f32[64,2048]{1,0:T(8,128)}, /*index=5*/f32[8,128]{1,0:T(8,128)}) custom-call(bf16[3,8,128,256]{3,2,1,0:T(8,128)(2,1)} %bitcast.55, bf16[3,2048,256]{2,1,0:T(8,128)(2,1)} %bitcast.48, bf16[1024,2048]{1,0:T(8,128)(2,1)} %bitcast.46, ...), custom_call_target="tpu_custom_call" | custom-call | tf_op jit(solution)/shard_map/take_out/pallas_call | solution.py:1575
  547.0 0.0 copy-start.13
  547.0 0.0 copy-start.10
  547.0 0.0 copy-start.9
  547.0 0.0 copy-start.8
  547.0 2.9 add_bitcast_fusion
  549.9 0.0 copy-done.13
  549.9 0.0 copy-start.5
  549.9 0.5 slice_bitcast_fusion
  550.4 0.0 copy-done.10
  550.4 0.8 convert_element_type.53
  551.3 0.0 copy-done.9
  551.3 0.8 convert_element_type.54
  552.1 0.0 copy-done.8
  552.1 0.0 copy-start.4
  552.1 0.8 convert_element_type.55
  552.9 0.0 copy-done.5
  552.9 1.5 convert_element_type.56
  554.4 0.0 copy-done.4
  554.4 1.5 convert_element_type.57
  555.9 0.1 copy-done.3
  556.0 1.5 convert_element_type.58
  557.5 0.0 copy-done.6
  557.5 0.8 copy.37
  558.3 0.0 copy-done.7
  558.3 0.8 copy.38
  (11 shorter events, 0.1 us)
Async XLA Ops:
  187.7 1.4 copy-start.14
  372.7 4.4 copy-start.15
  372.8 4.4 copy-start
  372.8 4.4 copy-start.1
  372.8 4.4 copy-start.2
  372.8 4.4 copy-start.11
  372.8 4.4 copy-start.12
  547.0 2.9 copy-start.13
  547.0 3.5 copy-start.10
  547.0 4.3 copy-start.9
  547.0 5.1 copy-start.8
  549.9 3.0 copy-start.5
  552.1 2.3 copy-start.4
  554.4 1.6 copy-start.3
  556.0 1.5 copy-start.6
  556.0 2.3 copy-start.7
